TPU v7x, 256 devices: a whole 4x4x8 slice. The times are simulated.
256 devices in a mesh: chan: 64 (over y, x_lo, z), beam: 4 (over x_hi, core).
Axes of the slice: x: 4 (x_hi: 2, x_lo: 2; x = x_hi * 2 + x_lo), y: 4, z: 8, core: 2. Of those that a mesh axis runs over, the one named last changes fastest.
Arguments:
- signals: bfloat16 [16384, 8192], P('chan', 'beam'), may hold values from -6 to 6
- weights: bfloat16 [3, 2, 512, 16384], P(None, None, 'beam', 'chan'), may hold values from -0.046875 to 0.046875
- bin_group: int32 [2048], replicated, may hold values from 0 to 2
Outputs:
- formed: float32 [2048, 2, 512], P('chan', None, 'beam')
All inputs are finite; a program needn't handle non-finite values.
Results may differ from a plain program's by a relative error of at most 0.0042.
Values may be sent and summed in bfloat16 or wider, within the bound.
No kernel may reach another device: no remote copies, remote signals or barrier semaphores. Data moves between devices by JAX's collectives and lax.ppermute only.
A program may use at most 64 MiB of HBM per device.

v0:
```python
import math

import jax
import jax.numpy as jnp
from jax import lax
from jax.sharding import PartitionSpec as P


def cut_along(shard, dim, count):
    before, after = (shard.shape[:dim], shard.shape[dim + 1 :])
    return jnp.moveaxis(shard.reshape(*before, count, -1, *after), dim, 0)


def sum_at_owner(shard, axis, dim):
    count = lax.axis_size(axis)
    tiles = lax.all_to_all(cut_along(shard, dim, count), axis, 0, 0, tiled=True)
    return jnp.sum(tiles.astype(jnp.float32), axis=0)


def complex_terms(weight_block, spec_block, onehot):
    selected = onehot[:, :, None, None] * spec_block[:, None, :, :]
    products = jnp.einsum(
        "gpbc,fgqc->fpqb", weight_block, selected, preferred_element_type=jnp.float32
    )
    real_part = products[:, 0, 0] - products[:, 1, 1]
    imag_part = products[:, 0, 1] + products[:, 1, 0]
    return jnp.stack([real_part, imag_part], 1)


def transform(samples, first_sample, span, total_samples, bin_count):
    block = 512
    frequency = jnp.arange(1, bin_count + 1, dtype=jnp.int32)

    def add_block(step, running):
        start = step * block
        piece = lax.dynamic_slice_in_dim(samples, start, block, 1)
        sample_index = first_sample + start + jnp.arange(block, dtype=jnp.int32)
        phases = frequency[:, None] * sample_index[None, :] % total_samples
        angles = 2.0 * math.pi / total_samples * phases.astype(jnp.float32)
        twiddle = jnp.stack([jnp.cos(angles), -jnp.sin(angles)], 1).astype(jnp.bfloat16)
        return running + lax.dot_general(
            twiddle, piece, (((2,), (1,)), ((), ())), preferred_element_type=jnp.float32
        )

    empty = jnp.zeros((bin_count, 2, samples.shape[0]), jnp.float32)
    return lax.fori_loop(0, span // block, add_block, empty)


def shards(signals, weights, bin_group):
    samples_dev = signals.shape[1]
    total_samples = samples_dev * lax.axis_size("beam")
    bin_count = bin_group.shape[0]
    set_count = weights.shape[0]
    scale = 1.0 / math.sqrt(total_samples)
    partial_value = transform(
        signals, lax.axis_index("beam") * samples_dev, samples_dev, total_samples, bin_count
    )
    summed = lax.psum(partial_value, "beam")
    spectrum = (summed * scale).astype(jnp.bfloat16)
    set_ids = jnp.arange(set_count, dtype=jnp.int32)
    onehot_all = (bin_group[:, None] == set_ids[None, :]).astype(jnp.bfloat16)
    return sum_at_owner(
        complex_terms(weights, spectrum, onehot_all).astype(jnp.bfloat16), "chan", 0
    )


def solution(mesh):
    in_specs = (P("chan", "beam"), P(None, None, "beam", "chan"), P())
    out_specs = P("chan", None, "beam")
    return jax.shard_map(shards, mesh=mesh, in_specs=in_specs, out_specs=out_specs, check_vma=False)
```

profile of v0, /device:TPU:1, one launch (start us, length us, event | category | flops | bytes accessed | tf_op | source)
XLA Modules:
  0.0 258.0 jit_solution(7029655484710082618)
XLA Ops:
  6.5 0.0 all-reduce.2.cloned.1.call-start
  6.5 99.6 %while.16 = (s32[]{:T(128)}, f32[2048,2,256]{2,0,1:T(8,128)}, s32[]{:T(128)}, bf16[256,2048]{1,0:T(8,128)(2,1)}, s32[]{:T(128)}, /*index=5*/s32[]{:T(128)}, s32[]{:T(128)}, s32[]{:T(128)}) while((s32[]{:T(128)}, f32[2048,2,256]{2,0,1:T(8,128)}, s32[]{:T(128)}, bf16[256,2048]{1,0:T(8,128)(2,1)}, s32[]{:T(128)}, ...), condition=%wide.region_1.2_spmd.clone, body=%wide.region_0.1_spmd.clone.sunk | while | flops 1095764480 | bytes 17060000 | solution.py:46
  6.5 19.1 %cosine_convert_fusion.2 = (bf16[2048,1,512]{2,0,1:T(8,128)(2,1)S(1)}, bf16[2048,1,512]{2,0,1:T(8,128)(2,1)}) fusion(s32[512]{0:T(512)S(1)} %iota_add_fusion.4, s32[2048]{0:T(1024)S(1)} %iota_add_fusion.5), kind=kLoop, calls=%fused_computation.15.clone.1 | loop fusion | flops 17825792 | bytes 4204544 | tf_op jit(solution)/shard_map/convert
  25.7 4.8 %select_add_fusion.2 = f32[2048,2,256]{2,0,1:T(8,128)} fusion(f32[2048,2,256]{2,0,1:T(8,128)} %get-tuple-element.206, bf16[2048,1,512]{2,0,1:T(8,128)(2,1)} %get-tuple-element.195, bf16[2048,1,512]{2,0,1:T(8,128)(2,1)S(1)} %get-tuple-element.196, pred[]{:T(512)S(6)} %compare.10, bf16[256,2048]{1,0:T(8,128)(2,1)} %get-tuple-element.216, s32[]{:T(128)S(6)} %select_n.60), kind=kOutput, calls=%fused_computation.13.clone.1 | convolution fusion | flops 1077936128 | bytes 12845061 | tf_op jit(solution)/shard_map/while/body/eval_jaxpr/dot_general | solution.py:41
  30.5 19.1 %cosine_convert_fusion.2 = (bf16[2048,1,512]{2,0,1:T(8,128)(2,1)S(1)}, bf16[2048,1,512]{2,0,1:T(8,128)(2,1)}) fusion(s32[512]{0:T(512)S(1)} %iota_add_fusion.4, s32[2048]{0:T(1024)S(1)} %iota_add_fusion.5), kind=kLoop, calls=%fused_computation.15.clone.1 | loop fusion | flops 17825792 | bytes 4204544 | tf_op jit(solution)/shard_map/convert
  49.6 6.1 %select_add_fusion.2 = f32[2048,2,256]{2,0,1:T(8,128)} fusion(f32[2048,2,256]{2,0,1:T(8,128)} %get-tuple-element.206, bf16[2048,1,512]{2,0,1:T(8,128)(2,1)} %get-tuple-element.195, bf16[2048,1,512]{2,0,1:T(8,128)(2,1)S(1)} %get-tuple-element.196, pred[]{:T(512)S(6)} %compare.10, bf16[256,2048]{1,0:T(8,128)(2,1)} %get-tuple-element.216, s32[]{:T(128)S(6)} %select_n.60), kind=kOutput, calls=%fused_computation.13.clone.1 | convolution fusion | flops 1077936128 | bytes 12845061 | tf_op jit(solution)/shard_map/while/body/eval_jaxpr/dot_general | solution.py:41
  55.7 19.1 %cosine_convert_fusion.2 = (bf16[2048,1,512]{2,0,1:T(8,128)(2,1)S(1)}, bf16[2048,1,512]{2,0,1:T(8,128)(2,1)}) fusion(s32[512]{0:T(512)S(1)} %iota_add_fusion.4, s32[2048]{0:T(1024)S(1)} %iota_add_fusion.5), kind=kLoop, calls=%fused_computation.15.clone.1 | loop fusion | flops 17825792 | bytes 4204544 | tf_op jit(solution)/shard_map/convert
  74.8 6.1 %select_add_fusion.2 = f32[2048,2,256]{2,0,1:T(8,128)} fusion(f32[2048,2,256]{2,0,1:T(8,128)} %get-tuple-element.206, bf16[2048,1,512]{2,0,1:T(8,128)(2,1)} %get-tuple-element.195, bf16[2048,1,512]{2,0,1:T(8,128)(2,1)S(1)} %get-tuple-element.196, pred[]{:T(512)S(6)} %compare.10, bf16[256,2048]{1,0:T(8,128)(2,1)} %get-tuple-element.216, s32[]{:T(128)S(6)} %select_n.60), kind=kOutput, calls=%fused_computation.13.clone.1 | convolution fusion | flops 1077936128 | bytes 12845061 | tf_op jit(solution)/shard_map/while/body/eval_jaxpr/dot_general | solution.py:41
  81.0 19.1 %cosine_convert_fusion.2 = (bf16[2048,1,512]{2,0,1:T(8,128)(2,1)S(1)}, bf16[2048,1,512]{2,0,1:T(8,128)(2,1)}) fusion(s32[512]{0:T(512)S(1)} %iota_add_fusion.4, s32[2048]{0:T(1024)S(1)} %iota_add_fusion.5), kind=kLoop, calls=%fused_computation.15.clone.1 | loop fusion | flops 17825792 | bytes 4204544 | tf_op jit(solution)/shard_map/convert
  100.0 6.1 %select_add_fusion.2 = f32[2048,2,256]{2,0,1:T(8,128)} fusion(f32[2048,2,256]{2,0,1:T(8,128)} %get-tuple-element.206, bf16[2048,1,512]{2,0,1:T(8,128)(2,1)} %get-tuple-element.195, bf16[2048,1,512]{2,0,1:T(8,128)(2,1)S(1)} %get-tuple-element.196, pred[]{:T(512)S(6)} %compare.10, bf16[256,2048]{1,0:T(8,128)(2,1)} %get-tuple-element.216, s32[]{:T(128)S(6)} %select_n.60), kind=kOutput, calls=%fused_computation.13.clone.1 | convolution fusion | flops 1077936128 | bytes 12845061 | tf_op jit(solution)/shard_map/while/body/eval_jaxpr/dot_general | solution.py:41
  106.2 0.0 copy-start
  106.2 0.0 all-reduce.2.cloned.1.call-update
  106.2 0.7 copy-done
  106.9 0.0 copy-start.1
  106.9 101.6 %all-reduce.2.cloned.1.call-done = f32[2048,2,256]{2,0,1:T(8,128)} async-done(((f32[2048,2,256]{2,0,1:T(8,128)}), f32[2048,2,256]{2,0,1:T(8,128)}) %all-reduce.2.cloned.1.call-update) | async-done | bytes 4194320 | tf_op jit(solution)/shard_map/psum | solution.py:58
  208.5 2.6 %multiply_convert_fusion = bf16[2048,2,256]{2,0,1:T(8,128)(2,1)S(1)} fusion(f32[2048,2,256]{2,0,1:T(8,128)} %all-reduce.2.cloned.1.call-done), kind=kLoop, calls=%fused_computation.25 | loop fusion | flops 2097152 | bytes 6291456 | tf_op jit(solution)/shard_map/convert_element_type | solution.py:59
  211.1 0.0 copy-done.1
  211.1 2.0 fusion.18
  213.1 0.2 fusion.24
  213.3 0.1 pad_maximum_fusion
  213.4 36.9 %all_to_all.5 = bf16[64,32,2,128]{3,1,2,0:T(8,128)(2,1)S(1)} all-to-all(bf16[64,32,2,128]{3,1,2,0:T(8,128)(2,1)S(1)} %pad_maximum_fusion), channel_id=1, replica_groups=mesh['chan'=64,'beam'=4] {'chan'}, dimensions={0} | all-to-all | bytes 2097152 | tf_op jit(solution)/shard_map/all_to_all | solution.py:16
  250.3 0.2 convert_reduce_fusion
  250.5 0.6 copy.9
  (10 shorter events, 0.0 us)
Async XLA Ops:
  6.5 201.9 %all-reduce.2.cloned.1.call-start = ((), (), s32[]{:S(2)}) async-start(), calls=%async_computation.1 | async-start | bytes 8388608 | tf_op jit(solution)/shard_map/psum | solution.py:58
  106.2 0.7 copy-start
  106.9 104.2 %copy-start.1 = (bf16[3,2,128,256]{3,2,1,0:T(8,128)(2,1)S(1)}, bf16[3,2,128,256]{3,2,1,0:T(8,128)(2,1)}, u32[]{:S(2)}) copy-start(bf16[3,2,128,256]{3,2,1,0:T(8,128)(2,1)} %param.6) | copy-start | bytes 1179652
Sparse Core Ops, SparseCore 0:
  106.3 102.1 all-reduce.1
where the time goes:
time: 259 us; the launch traced here: 258 us
  waiting for transfers between devices  102 us (39%)
  other arithmetic  79.5 us (31%)
  blocking collectives  36.9 us (14%)
  matrix products  25.2 us (10%)
  between operations  13.4 us (5%)
    psum x1, waiting for transfers between devices, shards(): summed = lax.psum(partial_value, 'beam')  102 us
    another operation x5, other arithmetic  76.6 us
    all_to_all x1, blocking collectives, sum_at_owner(): tiles = lax.all_to_all(cut_along(shard, dim, count), axis, 0, 0, tiled=True)  36.9 us
    dot_general x4, matrix products, add_block(): lax.dot_general(twiddle, piece, (((2,), (1,)), ((), ())), preferred_eleme...  23.2 us
  transfers between devices with their start and end apart: 1, of which 1 were waited for; matrix products, arithmetic and copies ran while one was open for 0% of the time, Pallas kernels for 0%

commit v1 on v0

v1 whole, which is shorter than its diff:
```python
import math

import jax
import jax.numpy as jnp
from jax import lax
from jax.experimental import pallas as pl
from jax.experimental.pallas import tpu as pltpu
from jax.sharding import PartitionSpec as P

F32 = jnp.float32
BF16 = jnp.bfloat16

STRIDE = 8
LANES = 128


def unit_root(numer, denom):
    angle = 2.0 * math.pi / denom * (numer % denom).astype(F32)
    return jnp.cos(angle), -jnp.sin(angle)


def transform_tables(samples, time_half):
    inner = samples // STRIDE
    lane = jnp.arange(inner // 2, dtype=jnp.int32)
    k = jnp.arange(32, dtype=jnp.int32)
    row = jnp.arange(32, dtype=jnp.int32)
    coarse = jnp.stack(unit_root(k[:, None] * (32 * lane)[None, :], inner))
    fine = jnp.stack(unit_root((row + 1)[:, None] * lane[None, :], inner))
    fine = fine.reshape(2, 4, 8, -1).transpose(1, 0, 2, 3)
    j = jnp.arange(4, dtype=jnp.int32)
    r = jnp.arange(8, dtype=jnp.int32)
    f1 = (32 * k[None, :, None] + 8 * j[:, None, None] + r[None, None, :] + 1).reshape(4, 256, 1)
    s = jnp.arange(LANES, dtype=jnp.int32)[None, None, :]
    numer = f1 * (s % STRIDE + samples // 2 * time_half)
    angle = 2.0 * math.pi / samples * (numer % samples).astype(F32)
    outer = jnp.where(s < STRIDE, jnp.cos(angle), -jnp.sin(angle)) * (1.0 / math.sqrt(samples))
    return coarse, fine, outer


def dft_kernel(ids_ref, own_ref, other_ref, coarse_ref, fine_ref, outer_ref, out_ref, xs_ref, t_ref, f_ref):
    step = pl.program_id(0)

    @pl.when(step == 0)
    def _():
        core = ids_ref[0]
        n_in = lax.broadcasted_iota(jnp.int32, (1024, 1024), 0)
        n_out = lax.broadcasted_iota(jnp.int32, (1024, 1024), 1)
        source = (n_out % LANES) * STRIDE + n_out // LANES
        perm = jnp.where(n_in == source, 1.0, 0.0).astype(BF16)
        rows = jnp.concatenate(
            [own_ref[:, 0:1024], own_ref[:, 1024:2048], other_ref[:, 0:1024], other_ref[:, 1024:2048]], 0
        )
        split = jnp.dot(rows, perm, preferred_element_type=F32).astype(BF16)
        for part in range(4):
            place = core if part < 2 else 1 - core
            lane0 = pl.multiple_of((place * 2 + part % 2) * LANES, LANES)
            for s in range(STRIDE):
                xs_ref[s * 128 : (s + 1) * 128, pl.ds(lane0, LANES)] = split[
                    part * 128 : (part + 1) * 128, s * 128 : (s + 1) * 128
                ]

    quarter = ids_ref[1 + step]
    fr = fine_ref[quarter, 0]
    fi = fine_ref[quarter, 1]

    def make_rows(pair, carry):
        re, im = [], []
        for h in range(2):
            cr = coarse_ref[0, pl.ds(2 * pair + h, 1), :]
            ci = coarse_ref[1, pl.ds(2 * pair + h, 1), :]
            re.append(cr * fr - ci * fi)
            im.append(cr * fi + ci * fr)
        row0 = pl.multiple_of(pair * 16, 16)
        t_ref[pl.ds(row0, 16), :] = jnp.concatenate(re, 0).astype(BF16)
        t_ref[pl.ds(row0 + 256, 16), :] = jnp.concatenate(im, 0).astype(BF16)
        return carry

    lax.fori_loop(0, 16, make_rows, 0)
    f_ref[...] = lax.dot_general(
        t_ref[...], xs_ref[...], (((1,), (1,)), ((), ())), preferred_element_type=F32
    )

    half = math.sqrt(0.5)

    def combine(chunk, carry):
        row0 = pl.multiple_of(chunk * 16, 16)
        gr, gi = [], []
        outer = outer_ref[quarter, pl.ds(row0, 16), :]
        for s in range(STRIDE):
            a = f_ref[pl.ds(row0, 16), s * 128 : (s + 1) * 128]
            b = f_ref[pl.ds(row0 + 256, 16), s * 128 : (s + 1) * 128]
            wr = outer[:, s : s + 1]
            wi = outer[:, STRIDE + s : STRIDE + s + 1]
            gr.append(wr * a - wi * b)
            gi.append(wr * b + wi * a)
        pr = [gr[s] + gr[s + 4] for s in range(4)]
        pi = [gi[s] + gi[s + 4] for s in range(4)]
        mr = [gr[s] - gr[s + 4] for s in range(4)]
        mi = [gi[s] - gi[s + 4] for s in range(4)]
        low_r = (pr[0] + pr[2]) + (pr[1] + pr[3])
        low_i = (pi[0] + pi[2]) + (pi[1] + pi[3])
        er, ei = mr[0] + mi[2], mi[0] - mr[2]
        dr, di = mr[1] + mi[3], mi[1] - mr[3]
        high_r = er + half * (dr + di)
        high_i = ei + half * (di - dr)
        out_ref[0, pl.ds(row0, 16), :] = low_r.astype(BF16)
        out_ref[0, pl.ds(row0 + 256, 16), :] = high_r.astype(BF16)
        out_ref[0, pl.ds(row0 + 512, 16), :] = low_i.astype(BF16)
        out_ref[0, pl.ds(row0 + 768, 16), :] = high_i.astype(BF16)
        return carry

    lax.fori_loop(0, 16, combine, 0)


def dft(ids, own, other, tables, count):
    return pl.pallas_call(
        dft_kernel,
        grid=(count,),
        in_specs=[
            pl.BlockSpec(memory_space=pltpu.SMEM),
            pl.BlockSpec((128, 2048), lambda i: (0, 0)),
            pl.BlockSpec((128, 2048), lambda i: (0, 0)),
            pl.BlockSpec((2, 32, 512), lambda i: (0, 0, 0)),
            pl.BlockSpec((4, 2, 8, 512), lambda i: (0, 0, 0, 0)),
            pl.BlockSpec((4, 256, 128), lambda i: (0, 0, 0)),
        ],
        out_specs=pl.BlockSpec((1, 1024, 128), lambda i: (i, 0, 0)),
        out_shape=jax.ShapeDtypeStruct((count, 1024, 128), BF16),
        scratch_shapes=[
            pltpu.VMEM((1024, 512), BF16),
            pltpu.VMEM((512, 512), BF16),
            pltpu.VMEM((512, 1024), F32),
        ],
        name="dft",
    )(ids, own, other, *tables)


def form_kernel(ids_ref, spec_ref, onehot_ref, w0_ref, w1_ref, out_ref, l_ref):
    me = ids_ref[0]
    for core in range(2):
        spec = spec_ref[core].astype(F32) + spec_ref[2 + core].astype(F32)
        cols = slice(core * 128, core * 128 + 128)
        spec = spec.astype(BF16)
        sr, si = spec[:512], spec[512:]
        for g in range(3):
            m = onehot_ref[:, g : g + 1].astype(BF16)
            mr, mi = sr * m, si * m
            base = g * 512
            c0 = slice(base + cols.start, base + cols.stop)
            c1 = slice(base + 256 + cols.start, base + 256 + cols.stop)
            l_ref[0:512, c0] = mr
            l_ref[0:512, c1] = -mi
            l_ref[512:1024, c0] = mi
            l_ref[512:1024, c1] = mr
    for sib in range(2):
        acc = jnp.zeros((1024, 256), F32)
        for g in range(3):
            for p in range(2):
                w = jnp.concatenate(
                    [w0_ref[g, p], w1_ref[0, g, p]] if sib == 0 else [w1_ref[1, g, p], w1_ref[2, g, p]], 0
                )
                col = (g * 2 + p) * 256
                acc = acc + lax.dot_general(
                    l_ref[:, col : col + 256], w, (((1,), (1,)), ((), ())), preferred_element_type=F32
                )
        for peer in range(2):
            block = me ^ (sib + 2 * peer)
            part = acc[:, peer * 128 : peer * 128 + 128]
            re = part[:512].reshape(64, 8, 128)
            im = part[512:].reshape(64, 8, 128)
            both = jnp.concatenate([re, im], 1).astype(BF16)
            out_ref[:, pl.ds(block, 1)] = both[:, None]


def form(ids, spec, onehot, w_own, w_rest):
    vm = pl.BlockSpec(memory_space=pltpu.VMEM)
    return pl.pallas_call(
        form_kernel,
        in_specs=[pl.BlockSpec(memory_space=pltpu.SMEM), vm, vm, vm, vm],
        out_specs=vm,
        out_shape=jax.ShapeDtypeStruct((64, 4, 16, 128), BF16),
        scratch_shapes=[pltpu.VMEM((1024, 1536), BF16)],
        name="form",
    )(ids, spec, onehot, w_own, w_rest)


def shards(signals, weights, bin_group):
    samples = signals.shape[1] * lax.axis_size("beam")
    me = lax.axis_index("beam")
    core = me % 2
    swap_core = [(0, 1), (1, 0), (2, 3), (3, 2)]
    swap_half = [(0, 2), (2, 0), (1, 3), (3, 1)]
    halves = signals.reshape(2, 128, -1)
    mine = lax.dynamic_index_in_dim(halves, core, 0, keepdims=False)
    theirs = lax.dynamic_index_in_dim(halves, 1 - core, 0, keepdims=False)
    other = lax.ppermute(theirs, "beam", swap_core)

    w_peer = lax.ppermute(weights, "beam", swap_half)
    w_sib = lax.ppermute(weights, "beam", swap_core)
    w_sib_peer = lax.ppermute(w_peer, "beam", swap_core)
    w_rest = jnp.stack([w_peer, w_sib, w_sib_peer])

    tables = transform_tables(samples, me // 2)
    ids = jnp.stack([core, *[jnp.int32(q) for q in range(4)]])
    partial = dft(ids, mine, other, tables, 4)
    spec = lax.all_to_all(partial, "beam", 0, 0, tiled=True)

    mine_bins = lax.dynamic_index_in_dim(bin_group.reshape(64, 4, 8), me, 1, keepdims=False).reshape(512, 1)
    onehot = (mine_bins == jnp.arange(3, dtype=jnp.int32)[None, :]).astype(F32)
    parts = form(me[None], spec, onehot, weights, w_rest).reshape(256, 16, 128)
    got = lax.all_to_all(parts, ("chan", "beam"), 0, 0, tiled=True)
    summed = jnp.sum(got.reshape(64, 4, 2, 8, 128).astype(F32), axis=0)
    return summed.transpose(0, 2, 1, 3).reshape(32, 2, 128)


def solution(mesh):
    in_specs = (P("chan", "beam"), P(None, None, "beam", "chan"), P())
    out_specs = P("chan", None, "beam")
    return jax.shard_map(shards, mesh=mesh, in_specs=in_specs, out_specs=out_specs, check_vma=False)
```

time: 259 us -> 99.6 us (0.38)
  waiting for transfers between devices: 102 us -> 12.1 us
  other arithmetic: 79.5 us -> 7.37 us
  matrix products: 25.2 us -> 0 us
  Pallas kernels: 0 us -> 20.3 us
  between operations: 13.4 us -> 0.1 us
  starting transfers between devices: 0.01 us -> 8.64 us
  blocking collectives: 36.9 us -> 44.9 us
  local copies, waits for them, and re-layouts: 1.32 us -> 5.89 us
    psum x1 -> x0, waiting for transfers between devices: 102 us -> none  [shards(): summed = lax.psum(partial_value, 'beam')]
    another operation x6 -> x2, other arithmetic: 76.7 us -> 1.8 us  [the longest x1 1.15 us: shards(): w_rest = jnp.stack([w_peer, w_sib, w_sib_peer])]
    dot_general x5 -> x0, matrix products: 25.2 us -> none  [the longest x4 23.2 us: add_block(): lax.dot_general(twiddle, piece, (((2,), (1,)), ((), ())), preferred_eleme...]
    pallas_call x0 -> x2, Pallas kernels: none -> 20.3 us  [the longest x1 15.5 us: dft(): pl.pallas_call(dft_kernel, grid=(count,), in_specs=[pl.BlockSpec(memory_s...]
    all_to_all x0 -> x1, waiting for transfers between devices: none -> 11.3 us  [shards(): spec = lax.all_to_all(partial, 'beam', 0, 0, tiled=True)]
    all_to_all x1, blocking collectives: 36.9 us -> 44.9 us  [shards(): got = lax.all_to_all(parts, ('chan', 'beam'), 0, 0, tiled=True)]
    ppermute x0 -> x4, starting transfers between devices: none -> 4.75 us  [the longest x1 3.2 us: shards(): other = lax.ppermute(theirs, 'beam', swap_core)]
    all_to_all x0 -> x1, starting transfers between devices: none -> 3.89 us  [shards(): spec = lax.all_to_all(partial, 'beam', 0, 0, tiled=True)]
  transfers between devices with their start and end apart: 1 -> 5, of which waited for: 1 -> 3; matrix products, arithmetic and copies ran while one was open for 0% -> 9% of each run, Pallas kernels for 0% -> 16%
where the time goes in v1:
time: 99.6 us; the launch traced here: 99.3 us
  blocking collectives  44.9 us (45%)
  Pallas kernels  20.3 us (20%)
  waiting for transfers between devices  12.1 us (12%)
  starting transfers between devices  8.64 us (9%)
  other arithmetic  7.37 us (7%)
  local copies, waits for them, and re-layouts  5.89 us (6%)
    all_to_all x1, blocking collectives, shards(): got = lax.all_to_all(parts, ('chan', 'beam'), 0, 0, tiled=True)  44.9 us
    pallas_call x1, Pallas kernels, dft(): pl.pallas_call(dft_kernel, grid=(count,), in_specs=[pl.BlockSpec(memory_s...  15.5 us
    all_to_all x1, waiting for transfers between devices, shards(): spec = lax.all_to_all(partial, 'beam', 0, 0, tiled=True)  11.3 us
    pallas_call x1, Pallas kernels, form(): pl.pallas_call(form_kernel, in_specs=[pl.BlockSpec(memory_space=pltpu.SME...  4.87 us
    all_to_all x1, starting transfers between devices, shards(): spec = lax.all_to_all(partial, 'beam', 0, 0, tiled=True)  3.89 us
    ppermute x1, starting transfers between devices, shards(): other = lax.ppermute(theirs, 'beam', swap_core)  3.2 us
    mul x1, other arithmetic, transform_tables(): jnp.where(s < STRIDE, jnp.cos(angle), -jnp.sin(angle))  3.16 us
    squeeze x1, local copies, waits for them, and re-layouts, shards(): theirs = lax.dynamic_index_in_dim(halves, 1 - core, 0, keepdims=False)  2.13 us
  transfers between devices with their start and end apart: 5, of which 3 were waited for; matrix products, arithmetic and copies ran while one was open for 9% of the time, Pallas kernels for 16%

profile of v1, /device:TPU:1, one launch (start us, length us, event | category | flops | bytes accessed | tf_op | source)
XLA Modules:
  0.0 99.3 jit_solution(1022870197512613663)
XLA Ops:
  0.0 2.1 %dynamic-slice_bitcast_fusion = (bf16[128,2048]{1,0:T(8,128)(2,1)S(1)}, bf16[128,2048]{1,0:T(8,128)(2,1)}) fusion(bf16[2,128,2048]{2,1,0:T(8,128)(2,1)} %bitcast.22, s32[]{:T(128)S(6)} %select_n.83, s32[]{:T(128)S(6)} %select_n.82), kind=kLoop, calls=%fused_computation.11 | loop fusion | bytes 2097160 | tf_op jit(solution)/shard_map/jit(dynamic_index_in_dim)/squeeze | solution.py:195
  2.1 3.2 %collective-permute-start = (bf16[128,2048]{1,0:T(8,128)(2,1)S(1)}, bf16[128,2048]{1,0:T(8,128)(2,1)S(1)}, u32[]{:S(2)}, u32[]{:S(2)}) collective-permute-start(bf16[128,2048]{1,0:T(8,128)(2,1)S(1)} %get-tuple-element.5), channel_id=1, source_target_pairs={{0,1},{1,0},{2,3},{3,2},{4,5},{5,4},{6,7},{7,6},{8,9},{9,8},{10,11... | collective-permute-start | bytes 1572872 | tf_op jit(solution)/shard_map/ppermute | solution.py:196
  5.3 1.0 %collective-permute-start.1 = (bf16[3,2,128,256]{3,2,1,0:T(8,128)(2,1)S(1)}, bf16[3,2,128,256]{3,2,1,0:T(8,128)(2,1)S(1)}, u32[]{:S(2)}, u32[]{:S(2)}) collective-permute-start(bf16[3,2,128,256]{3,2,1,0:T(8,128)(2,1)S(1)} %copy-done.2), channel_id=1, source_target_pairs={{0,2},{2,0},{1,3},{3,1},{4,6},{6,4},{5,7},{7,5},{8,10},{10,8},{9,1... | collective-permute-start | bytes 1179656 | tf_op jit(solution)/shard_map/ppermute | solution.py:198
  6.4 0.1 broadcast_add_fusion
  6.5 0.1 add.157
  6.6 0.1 add.158
  6.7 0.1 add.160
  6.8 0.3 fusion.16
  7.1 0.3 fusion.17
  7.4 3.2 %select_multiply_fusion.outer_ref = f32[4,256,128]{2,1,0:T(8,128)} fusion(s32[128]{0:T(128)S(1)} %fusion.18, s32[4,256]{1,0:T(4,128)S(1)} %add_add_fusion, pred[128]{0:T(512)(128)(4,1)S(1)} %iota_compare_fusion.1), kind=kLoop, calls=%fused_computation.10 | loop fusion | flops 2228224 | bytes 529024 | tf_op jit(solution)/shard_map/mul | solution.py:36
  10.6 0.7 maximum_bitcast_fusion.fine_ref
  11.3 0.7 stack.29.ids_ref
  11.9 0.7 pad_maximum_fusion.1.coarse_ref
  12.6 0.0 collective-permute-done.other_ref
  12.6 0.8 copy-done.1
  13.4 15.5 %dft.1 = bf16[4,1024,128]{2,1,0:T(8,128)(2,1)} custom-call(s32[5]{0:T(128)} %stack.29.ids_ref, bf16[128,2048]{1,0:T(8,128)(2,1)} %get-tuple-element.6.own_ref, bf16[128,2048]{1,0:T(8,128)(2,1)} %copy-done.1, f32[2,32,512]{2,1,0:T(8,128)} %pad_maximum_fusion.1.coarse_ref, f32[4,2,8,512]{3,2,1,0:T(8,128)} %maximum_bitcast_fusion.fine_ref, ...), custom_call_target="tpu_custom_call" | custom-call | tf_op jit(solution)/shard_map/dft/pallas_call | solution.py:116
  28.8 3.9 %all-to-all-start = ((bf16[4,1024,128]{2,1,0:T(8,128)(2,1)}), bf16[4,1024,128]{2,1,0:T(8,128)(2,1)S(1)}, u32[]{:S(2)}, u32[]{:S(2)}) async-start(bf16[4,1024,128]{2,1,0:T(8,128)(2,1)} %dft.1), calls=%async_computation | async-start | bytes 2097152 | tf_op jit(solution)/shard_map/all_to_all | solution.py:206
  32.7 0.1 collective-permute-start.2
  32.9 0.4 collective-permute-start.3
  33.3 0.2 reshape.294
  33.4 0.1 dynamic-slice_reduce_fusion
  33.6 0.1 eq.24
  33.6 0.9 fusion.3.onehot_ref
  34.5 0.2 collective-permute-done.2
  34.7 0.6 collective-permute-done.3
  35.2 1.1 %pad_maximum_fusion.w1_ref = bf16[3,3,2,128,256]{4,3,2,1,0:T(8,128)(2,1)} fusion(bf16[1,3,2,128,256]{4,3,2,1,0:T(8,128)(2,1)S(1)} %bitcast.25, bf16[1,3,2,128,256]{4,3,2,1,0:T(8,128)(2,1)S(1)} %bitcast.24, bf16[1,3,2,128,256]{4,3,2,1,0:T(8,128)(2,1)S(1)} %bitcast.23), kind=kLoop, calls=%fused_computation.1 | loop fusion | flops 1179648 | bytes 2359296 | tf_op jit(solution)/shard_map/stack | solution.py:201
  36.4 11.3 %all-to-all-done.spec_ref = bf16[4,1024,128]{2,1,0:T(8,128)(2,1)S(1)} async-done(((bf16[4,1024,128]{2,1,0:T(8,128)(2,1)}), bf16[4,1024,128]{2,1,0:T(8,128)(2,1)S(1)}, u32[]{:S(2)}, u32[]{:S(2)}) %all-to-all-start) | async-done | bytes 1048608 | tf_op jit(solution)/shard_map/all_to_all | solution.py:206
  47.7 1.0 copy-done
  48.7 4.9 %form.1 = bf16[64,4,16,128]{3,2,1,0:T(8,128)(2,1)} custom-call(s32[1]{0:T(128)} %bitcast.ids_ref, bf16[4,1024,128]{2,1,0:T(8,128)(2,1)} %copy-done, f32[512,3]{1,0:T(8,128)} %fusion.3.onehot_ref, bf16[3,2,128,256]{3,2,1,0:T(8,128)(2,1)} %w0_ref.1, bf16[3,3,2,128,256]{4,3,2,1,0:T(8,128)(2,1)} %pad_maximum_fusion.w1_ref), custom_call_target="tpu_custom_call" | custom-call | tf_op jit(solution)/shard_map/form/pallas_call | solution.py:177
  53.6 44.9 %all_to_all.10 = bf16[256,16,128]{2,1,0:T(8,128)(2,1)S(1)} all-to-all(bf16[256,16,128]{2,1,0:T(8,128)(2,1)} %bitcast.21), channel_id=1, replica_groups=mesh['chan'=64,'beam'=4] {'chan','beam'}, dimensions={0} | all-to-all | bytes 2097152 | tf_op jit(solution)/shard_map/all_to_all | solution.py:211
  98.5 0.2 convert_reduce_fusion
  98.7 0.6 copy.5
  (16 shorter events, 0.1 us)
Async XLA Ops:
  0.0 5.3 %copy-start.2 = (bf16[3,2,128,256]{3,2,1,0:T(8,128)(2,1)S(1)}, bf16[3,2,128,256]{3,2,1,0:T(8,128)(2,1)}, u32[]{:S(2)}) copy-start(bf16[3,2,128,256]{3,2,1,0:T(8,128)(2,1)} %w0_ref.1) | copy-start | bytes 1179652
  2.1 10.4 %collective-permute-start = (bf16[128,2048]{1,0:T(8,128)(2,1)S(1)}, bf16[128,2048]{1,0:T(8,128)(2,1)S(1)}, u32[]{:S(2)}, u32[]{:S(2)}) collective-permute-start(bf16[128,2048]{1,0:T(8,128)(2,1)S(1)} %get-tuple-element.5), channel_id=1, source_target_pairs={{0,1},{1,0},{2,3},{3,2},{4,5},{5,4},{6,7},{7,6},{8,9},{9,8},{10,11... | collective-permute-start | bytes 1572872 | tf_op jit(solution)/shard_map/ppermute | solution.py:196
  5.3 27.5 %collective-permute-start.1 = (bf16[3,2,128,256]{3,2,1,0:T(8,128)(2,1)S(1)}, bf16[3,2,128,256]{3,2,1,0:T(8,128)(2,1)S(1)}, u32[]{:S(2)}, u32[]{:S(2)}) collective-permute-start(bf16[3,2,128,256]{3,2,1,0:T(8,128)(2,1)S(1)} %copy-done.2), channel_id=1, source_target_pairs={{0,2},{2,0},{1,3},{3,1},{4,6},{6,4},{5,7},{7,5},{8,10},{10,8},{9,1... | collective-permute-start | bytes 1179656 | tf_op jit(solution)/shard_map/ppermute | solution.py:198
  12.6 0.8 copy-start.1
  28.8 4.4 %copy-start.3 = (s32[2048]{0:T(1024)S(1)}, s32[2048]{0:T(1024)}, u32[]{:S(2)}) copy-start(s32[2048]{0:T(1024)} %param.5) | copy-start | bytes 24580
  28.8 18.9 %all-to-all-start = ((bf16[4,1024,128]{2,1,0:T(8,128)(2,1)}), bf16[4,1024,128]{2,1,0:T(8,128)(2,1)S(1)}, u32[]{:S(2)}, u32[]{:S(2)}) async-start(bf16[4,1024,128]{2,1,0:T(8,128)(2,1)} %dft.1), calls=%async_computation | async-start | bytes 2097152 | tf_op jit(solution)/shard_map/all_to_all | solution.py:206
  32.7 1.9 %collective-permute-start.2 = (bf16[3,2,128,256]{3,2,1,0:T(8,128)(2,1)S(1)}, bf16[3,2,128,256]{3,2,1,0:T(8,128)(2,1)S(1)}, u32[]{:S(2)}, u32[]{:S(2)}) collective-permute-start(bf16[3,2,128,256]{3,2,1,0:T(8,128)(2,1)S(1)} %copy-done.2), channel_id=1, source_target_pairs={{0,1},{1,0},{2,3},{3,2},{4,5},{5,4},{6,7},{7,6},{8,9},{9,8},{10,11... | collective-permute-start | bytes 1179656 | tf_op jit(solution)/shard_map/ppermute | solution.py:199
  32.9 2.4 %collective-permute-start.3 = (bf16[3,2,128,256]{3,2,1,0:T(8,128)(2,1)S(1)}, bf16[3,2,128,256]{3,2,1,0:T(8,128)(2,1)S(1)}, u32[]{:S(2)}, u32[]{:S(2)}) collective-permute-start(bf16[3,2,128,256]{3,2,1,0:T(8,128)(2,1)S(1)} %collective-permute-done.1), channel_id=1, source_target_pairs={{0,1},{1,0},{2,3},{3,2},{4,5},{5,4},{6,7},{7,6},{8,9},{9,8},{10,11... | collective-permute-start | bytes 1179656 | tf_op jit(solution)/shard_map/ppermute | solution.py:200
  47.7 1.0 copy-start

commit v2 on v0

v2 whole, which is shorter than its diff:
```python
import math

import jax
import jax.numpy as jnp
from jax import lax
from jax.experimental import pallas as pl
from jax.experimental.pallas import tpu as pltpu
from jax.sharding import Mesh, PartitionSpec as P

F32 = jnp.float32
BF16 = jnp.bfloat16
I32 = jnp.int32

STRIDE = 8
SAMPLES = 8192
LIMIT = 24 * 1024 * 1024


def root(numer, denom):
    angle = 2.0 * math.pi / denom * (numer & (denom - 1)).astype(F32)
    return jnp.cos(angle), -jnp.sin(angle)


def iota(shape, dim):
    return lax.broadcasted_iota(I32, shape, dim)


def deinterleave(x, perm):
    out = []
    rows = jnp.concatenate([x[:, :1024], x[:, 1024:]], 0)
    split = jnp.dot(rows, perm, preferred_element_type=F32).astype(BF16)
    for s in range(STRIDE):
        cols = split[:, s * 128 : (s + 1) * 128]
        out.append(jnp.concatenate([cols[:128], cols[128:]], 1))
    return out


def prep_kernel(ids_ref, own_ref, xs_ref, perm_ref, t_ref, outer_ref):
    core, half, low = ids_ref[0], ids_ref[1], ids_ref[2]
    lane = iota((32, 512), 1)
    part = lane // 128
    u = jnp.where(part < 2, 2 * core + part, 2 * (1 - core) + part - 2)
    m = u * 128 + (lane & 127)
    ar, ai = root(iota((32, 128), 0) * iota((32, 128), 1), 32)
    br, bi = root((iota((32, 512), 0) + 1) * m, 1024)
    s = iota((32, 128), 1) & (STRIDE - 1)
    imag = (iota((32, 128), 1) & STRIDE) != 0
    oar, oai = root(iota((32, 128), 0) * s * 32, SAMPLES)
    obr, obi = root((iota((32, 128), 0) + 1) * (s + SAMPLES // 2 * half), SAMPLES)
    scale = 1.0 / math.sqrt(SAMPLES)
    ob1 = jnp.where(imag, obi, obr) * scale
    ob2 = jnp.where(imag, obr, -obi) * scale
    tile = lambda row: jnp.concatenate([row] * 4, 1)
    for tl in range(2):
        for th in range(2):
            slot = {(0, 1): 0, (1, 0): 1, (1, 1): 2, (0, 0): 3}[(tl, th)]
            swap_h = half if th == 0 else 1 - half
            swap_l = low if tl == 0 else 1 - low
            pick = lambda a: jnp.where(swap_h == 1, a[16:], a[:16])
            fr, fi, o1, o2 = pick(br), pick(bi), pick(ob1), pick(ob2)
            for t in range(16):
                k0 = (t // 8) * 16 + t % 8
                sel = lambda a: jnp.where(swap_l == 1, a[k0 + 8 : k0 + 9], a[k0 : k0 + 1])
                cr, ci = tile(sel(ar)), tile(sel(ai))
                row = slot * 512 + t * 16
                t_ref[row : row + 16, :] = (cr * fr - ci * fi).astype(BF16)
                t_ref[row + 256 : row + 272, :] = (cr * fi + ci * fr).astype(BF16)
                outer_ref[slot, t * 16 : t * 16 + 16, :] = sel(oar) * o1 + sel(oai) * o2
    offset = iota((1024, 128), 0) - STRIDE * iota((1024, 128), 1)
    for s in range(STRIDE):
        perm_ref[:, s * 128 : (s + 1) * 128] = jnp.where(offset == s, 1.0, 0.0).astype(BF16)
    for s, rows in enumerate(deinterleave(own_ref[...], perm_ref[...])):
        xs_ref[s * 128 : (s + 1) * 128, :] = rows


def prep(ids, signals):
    full = lambda *shape: pl.BlockSpec(shape, lambda i, ids: (0,) * len(shape))
    return pl.pallas_call(
        prep_kernel,
        grid_spec=pltpu.PrefetchScalarGridSpec(
            num_scalar_prefetch=1,
            grid=(1,),
            in_specs=[pl.BlockSpec((128, 2048), lambda i, ids: (ids[0], 0))],
            out_specs=[full(1024, 256), full(1024, 1024), full(2048, 512), full(4, 256, 128)],
        ),
        out_shape=[
            jax.ShapeDtypeStruct((1024, 256), BF16),
            jax.ShapeDtypeStruct((1024, 1024), BF16),
            jax.ShapeDtypeStruct((2048, 512), BF16),
            jax.ShapeDtypeStruct((4, 256, 128), F32),
        ],
        compiler_params=pltpu.CompilerParams(vmem_limit_bytes=LIMIT),
        name="prep",
    )(ids, signals)


def combine(f_ref, outer_ref, slot, out_ref, index):
    half = math.sqrt(0.5)

    def step(chunk, carry):
        row0 = pl.multiple_of(chunk * 16, 16)
        gr, gi = [], []
        outer = outer_ref[slot, pl.ds(row0, 16), :]
        for s in range(STRIDE):
            a = f_ref[pl.ds(row0, 16), s * 128 : (s + 1) * 128]
            b = f_ref[pl.ds(row0 + 256, 16), s * 128 : (s + 1) * 128]
            wr = outer[:, s : s + 1]
            wi = outer[:, STRIDE + s : STRIDE + s + 1]
            gr.append(wr * a - wi * b)
            gi.append(wr * b + wi * a)
        pr = [gr[s] + gr[s + 4] for s in range(4)]
        pi = [gi[s] + gi[s + 4] for s in range(4)]
        mr = [gr[s] - gr[s + 4] for s in range(4)]
        mi = [gi[s] - gi[s + 4] for s in range(4)]
        er, ei = mr[0] + mi[2], mi[0] - mr[2]
        dr, di = mr[1] + mi[3], mi[1] - mr[3]
        results = (
            (pr[0] + pr[2]) + (pr[1] + pr[3]),
            er + half * (dr + di),
            (pi[0] + pi[2]) + (pi[1] + pi[3]),
            ei + half * (di - dr),
        )
        for place, value in enumerate(results):
            out_ref[index, pl.ds(row0 + 256 * place, 16), :] = value.astype(out_ref.dtype)
        return carry

    lax.fori_loop(0, 16, step, 0, unroll=4)


def first_kernel(other_ref, own_ref, perm_ref, t_ref, outer_ref, out_ref, xs_ref, f_ref):
    xs_ref[:, 0:256] = own_ref[...]
    for s, rows in enumerate(deinterleave(other_ref[...], perm_ref[...])):
        xs_ref[s * 128 : (s + 1) * 128, 256:512] = rows
    f_ref[...] = lax.dot_general(
        t_ref[0:512, :], xs_ref[...], (((1,), (1,)), ((), ())), preferred_element_type=F32
    )
    combine(f_ref, outer_ref, 0, out_ref, 0)


def next_kernel(slots, xs_ref, t_ref, outer_ref, out_ref, f_ref):
    for index, slot in enumerate(slots):
        buf = f_ref.at[index]
        buf[...] = lax.dot_general(
            t_ref[slot * 512 : slot * 512 + 512, :],
            xs_ref[...],
            (((1,), (1,)), ((), ())),
            preferred_element_type=F32,
        )
        combine(buf, outer_ref, slot, out_ref, index)


VM = pl.BlockSpec(memory_space=pltpu.VMEM)


def dft_first(other, own, perm, table, outer):
    return pl.pallas_call(
        first_kernel,
        in_specs=[VM] * 5,
        out_specs=[VM, VM],
        out_shape=[jax.ShapeDtypeStruct((1, 1024, 128), BF16), jax.ShapeDtypeStruct((1024, 512), BF16)],
        scratch_shapes=[pltpu.VMEM((512, 1024), F32)],
        compiler_params=pltpu.CompilerParams(vmem_limit_bytes=LIMIT),
        name="dft_first",
    )(other, own, perm, table, outer)


def dft_next(xs, table, outer, slots, dtype):
    return pl.pallas_call(
        lambda *refs: next_kernel(slots, *refs),
        in_specs=[VM] * 3,
        out_specs=VM,
        out_shape=jax.ShapeDtypeStruct((len(slots), 1024, 128), dtype),
        scratch_shapes=[pltpu.VMEM((len(slots), 512, 1024), F32)],
        compiler_params=pltpu.CompilerParams(vmem_limit_bytes=LIMIT),
        name="dft_next",
    )(xs, table, outer)


def form_kernel(ids_ref, mine_ref, sib_ref, group_ref, w0_ref, w1_ref, w2_ref, w3_ref, out_ref, l_ref, w_ref):
    core, half = ids_ref[0], ids_ref[1]
    for src, place in ((mine_ref, core), (sib_ref, 1 - core)):
        for xl in range(2):
            lane0 = pl.multiple_of(xl * 256 + place * 128, 128)
            sr, si = src[xl, 0:512, :], src[xl, 512:1024, :]
            l_ref[0:512, pl.ds(lane0, 128)] = sr
            l_ref[0:512, pl.ds(lane0 + 512, 128)] = -si
            l_ref[512:1024, pl.ds(lane0, 128)] = si
            l_ref[512:1024, pl.ds(lane0 + 512, 128)] = sr
    for g in range(3):
        for p in range(2):
            for b, xl, ref in ((0, 0, w0_ref), (0, 1, w1_ref), (1, 0, w2_ref), (1, 1, w3_ref)):
                row, col = g * 256 + b * 128, p * 512 + xl * 256
                w_ref[row : row + 128, col : col + 256] = ref[g, p]
    total = jnp.zeros((2, 512, 256), F32)
    groups = group_ref[...]
    for g in range(3):
        acc = lax.dot_general(
            l_ref[...], w_ref[g * 256 : g * 256 + 256, :], (((1,), (1,)), ((), ())), preferred_element_type=F32
        )
        total = jnp.where((groups == g)[None], acc.reshape(2, 512, 256), total)
    for b in range(2):
        part = total[:, :, b * 128 : b * 128 + 128]
        re = part[0].reshape(4, 8, 16, 128)
        im = part[1].reshape(4, 8, 16, 128)
        both = jnp.concatenate([re, im], 2).astype(BF16)
        out_ref[:, :, pl.ds(half if b == 0 else 1 - half, 1)] = both[:, :, None]


def form(ids, mine, sib, group, weights):
    return pl.pallas_call(
        form_kernel,
        in_specs=[pl.BlockSpec(memory_space=pltpu.SMEM)] + [VM] * 7,
        out_specs=VM,
        out_shape=jax.ShapeDtypeStruct((4, 8, 2, 32, 128), BF16),
        scratch_shapes=[pltpu.VMEM((1024, 1024), BF16), pltpu.VMEM((768, 1024), BF16)],
        compiler_params=pltpu.CompilerParams(vmem_limit_bytes=LIMIT),
        name="form",
    )(ids, mine, sib, group, *weights)


def shards(signals, weights, bin_group):
    half, core, low = lax.axis_index("xhi"), lax.axis_index("core"), lax.axis_index("xlo")
    ring = ("xlo", "xhi", "core")

    def exchange(value, flip):
        return lax.ppermute(value, ring, [(i, i ^ flip) for i in range(8)])

    ids = jnp.stack([core, half, low])
    theirs = lax.dynamic_slice_in_dim(signals, (1 - core) * 128, 128, 0)
    other = exchange(theirs, 1)
    own, perm, table, outer = prep(ids, signals)
    peers = [exchange(weights, flip) for flip in (4, 2, 6)]

    spec0, xs = dft_first(other, own, perm, table, outer)
    got0 = exchange(spec0[0], 2)
    spec12 = dft_next(xs, table, outer, (1, 2), BF16)
    got1 = exchange(spec12[0], 4)
    got2 = exchange(spec12[1], 6)
    spec3 = dft_next(xs, table, outer, (3,), F32)
    same = spec3[0] + got0.astype(F32)
    cross = got1.astype(F32) + got2.astype(F32)
    mine = jnp.stack([same, cross]).astype(BF16)
    sib = exchange(mine, 1)

    owned = lax.dynamic_index_in_dim(bin_group.reshape(4, 2, 8, 2, 16), low, 1, keepdims=False)
    owned = lax.dynamic_index_in_dim(owned, half, 2, keepdims=False).reshape(512, 1)
    parts = form(ids, mine, sib, owned, [weights] + peers).reshape(64, 32, 128)
    got = lax.all_to_all(parts, ("y", "z", "xhi"), 0, 0, tiled=True)
    summed = jnp.sum(got.reshape(32, 2, 2, 16, 128).astype(F32), axis=0)
    return summed.transpose(0, 2, 1, 3).reshape(32, 2, 128)


def solution(mesh):
    fine = Mesh(mesh.devices.reshape(4, 2, 8, 2, 2), ("y", "xlo", "z", "xhi", "core"))
    chan, beam = ("y", "xlo", "z"), ("xhi", "core")
    in_specs = (P(chan, beam), P(None, None, beam, chan), P())
    out_specs = P(chan, None, beam)
    return jax.shard_map(shards, mesh=fine, in_specs=in_specs, out_specs=out_specs, check_vma=False)
```

time: 259 us -> 83.1 us (0.32)
  the two profiles are of different devices: /device:TPU:1 before, /device:TPU:2 now
where the time goes in v2:
time: 83.1 us; the launch traced here: 82.9 us
  blocking collectives  33.2 us (40%)
  waiting for transfers between devices  24 us (29%)
  Pallas kernels  13.6 us (16%)
  starting transfers between devices  8.25 us (10%)
  local copies, waits for them, and re-layouts  3.34 us (4%)
    all_to_all x1, blocking collectives, shards(): got = lax.all_to_all(parts, ('y', 'z', 'xhi'), 0, 0, tiled=True)  33.2 us
    ppermute x8, waiting for transfers between devices, exchange(): return lax.ppermute(value, ring, [(i, i ^ flip) for i in range(8)])  24 us
    ppermute x8, starting transfers between devices, exchange(): return lax.ppermute(value, ring, [(i, i ^ flip) for i in range(8)])  8.25 us
    pallas_call x2, Pallas kernels, dft_next(): pl.pallas_call(lambda *refs: next_kernel(slots, *refs), in_specs=[VM] * 3...  5.66 us
    pallas_call x1, Pallas kernels, form(): pl.pallas_call(form_kernel, in_specs=[pl.BlockSpec(memory_space=pltpu.SME...  2.95 us
    pallas_call x1, Pallas kernels, prep(): pl.pallas_call(prep_kernel, grid_spec=pltpu.PrefetchScalarGridSpec(num_sc...  2.61 us
    pallas_call x1, Pallas kernels, dft_first(): pl.pallas_call(first_kernel, in_specs=[VM] * 5, out_specs=[VM, VM], out_s...  2.42 us
  transfers between devices with their start and end apart: 8, of which 5 were waited for; matrix products, arithmetic and copies ran while one was open for 1% of the time, Pallas kernels for 10%

profile of v2, /device:TPU:2, one launch (start us, length us, event | category | flops | bytes accessed | tf_op | source)
XLA Modules:
  0.0 82.9 jit_solution(3781838731045392102)
XLA Ops:
  0.0 1.1 %constant_dynamic-slice_fusion = bf16[128,2048]{1,0:T(8,128)(2,1)S(1)} fusion(bf16[256,2048]{1,0:T(8,128)(2,1)} %own_ref.1, s32[]{:T(128)S(6)} %select_n.15), kind=kLoop, calls=%fused_computation.11 | loop fusion | bytes 1048580 | tf_op jit(solution)/shard_map/dynamic_slice | solution.py:229
  1.1 0.1 collective-permute-start
  1.2 0.1 pad_add_fusion.ids_ref
  1.3 1.2 %copy-done = bf16[256,2048]{1,0:T(8,128)(2,1)S(1)} copy-done((bf16[256,2048]{1,0:T(8,128)(2,1)S(1)}, bf16[256,2048]{1,0:T(8,128)(2,1)}, u32[]{:S(2)}) %copy-start) | copy-done | bytes 1048600
  2.5 2.6 %prep.1 = (bf16[1024,256]{1,0:T(8,128)(2,1)S(1)}, bf16[1024,1024]{1,0:T(8,128)(2,1)S(1)}, bf16[2048,512]{1,0:T(8,128)(2,1)S(1)}, f32[4,256,128]{2,1,0:T(8,128)S(1)}) custom-call(s32[3]{0:T(128)S(1)} %pad_add_fusion.ids_ref, bf16[256,2048]{1,0:T(8,128)(2,1)S(1)} %copy-done), custom_call_target="tpu_custom_call" | custom-call | tf_op jit(solution)/shard_map/prep/pallas_call | solution.py:78
  5.1 2.4 %dft_first.1 = (bf16[1,1024,128]{2,1,0:T(8,128)(2,1)S(1)}, bf16[1024,512]{1,0:T(8,128)(2,1)S(1)}) custom-call(bf16[128,2048]{1,0:T(8,128)(2,1)S(1)} %collective-permute-done.other_ref, bf16[1024,256]{1,0:T(8,128)(2,1)S(1)} %get-tuple-element.11.own_ref, bf16[1024,1024]{1,0:T(8,128)(2,1)S(1)} %get-tuple-element.12.perm_ref, ...), custom_call_target="tpu_custom_call" | custom-call | tf_op jit(solution)/shard_map/dft_first/pallas_call | solution.py:156
  7.5 2.2 %collective-permute-start.1 = (bf16[1024,128]{1,0:T(8,128)(2,1)S(1)}, bf16[1024,128]{1,0:T(8,128)(2,1)S(1)}, u32[]{:S(2)}, u32[]{:S(2)}) collective-permute-start(bf16[1024,128]{1,0:T(8,128)(2,1)S(1)} %bitcast.24), channel_id=1, source_target_pairs={{0,2},{1,3},{2,0},{3,1},{32,34},{33,35},{34,32},{35,33},{4,6},{5,7... | collective-permute-start | bytes 786440 | tf_op jit(solution)/shard_map/ppermute | solution.py:226
  9.8 3.8 %dft_next.3 = bf16[2,1024,128]{2,1,0:T(8,128)(2,1)S(1)} custom-call(bf16[1024,512]{1,0:T(8,128)(2,1)S(1)} %get-tuple-element.15.refs_0_, bf16[2048,512]{1,0:T(8,128)(2,1)S(1)} %get-tuple-element.13.t_ref.refs_1_, f32[4,256,128]{2,1,0:T(8,128)S(1)} %get-tuple-element.14.outer_ref.refs_2_), custom_call_target="tpu_custom_call" | custom-call | tf_op jit(solution)/shard_map/dft_next/pallas_call | solution.py:168
  13.6 1.5 %collective-permute-start.2 = (bf16[1024,128]{1,0:T(8,128)(2,1)S(1)}, bf16[1024,128]{1,0:T(8,128)(2,1)S(1)}, u32[]{:S(2)}, u32[]{:S(2)}) collective-permute-start(bf16[1024,128]{1,0:T(8,128)(2,1)S(1)} %get-tuple-element.17), channel_id=1, source_target_pairs={{0,32},{1,33},{2,34},{3,35},{32,0},{33,1},{34,2},{35,3},{4,36},{5,... | collective-permute-start | bytes 786440 | tf_op jit(solution)/shard_map/ppermute | solution.py:226
  15.1 0.5 collective-permute-start.3
  15.6 1.9 %dft_next.2 = f32[1,1024,128]{2,1,0:T(8,128)S(1)} custom-call(bf16[1024,512]{1,0:T(8,128)(2,1)S(1)} %get-tuple-element.15.refs_0_, bf16[2048,512]{1,0:T(8,128)(2,1)S(1)} %get-tuple-element.13.t_ref.refs_1_, f32[4,256,128]{2,1,0:T(8,128)S(1)} %get-tuple-element.14.outer_ref.refs_2_), custom_call_target="tpu_custom_call" | custom-call | tf_op jit(solution)/shard_map/dft_next/pallas_call | solution.py:168
  17.5 0.0 copy-start.1
  17.5 0.7 collective-permute-done.1
  18.2 0.1 fusion.2
  18.3 5.2 %collective-permute-done.2 = bf16[1024,128]{1,0:T(8,128)(2,1)S(1)} collective-permute-done((bf16[1024,128]{1,0:T(8,128)(2,1)S(1)}, bf16[1024,128]{1,0:T(8,128)(2,1)S(1)}, u32[]{:S(2)}, u32[]{:S(2)}) %collective-permute-start.2) | collective-permute-done | bytes 262176 | tf_op jit(solution)/shard_map/ppermute | solution.py:226
  23.5 0.0 collective-permute-done.3
  23.5 0.1 fusion.1
  23.6 0.1 pad_maximum_fusion.mine_ref
  23.7 0.1 collective-permute-start.4
  23.8 2.2 %collective-permute-start.5 = (bf16[3,2,128,256]{3,2,1,0:T(8,128)(2,1)S(1)}, bf16[3,2,128,256]{3,2,1,0:T(8,128)(2,1)S(1)}, u32[]{:S(2)}, u32[]{:S(2)}) collective-permute-start(bf16[3,2,128,256]{3,2,1,0:T(8,128)(2,1)S(1)} %copy-done.1), channel_id=1, source_target_pairs={{0,32},{1,33},{2,34},{3,35},{32,0},{33,1},{34,2},{35,3},{4,36},{5,... | collective-permute-start | bytes 1179656 | tf_op jit(solution)/shard_map/ppermute | solution.py:226
  26.0 0.7 collective-permute-start.6
  26.8 0.8 %collective-permute-start.7 = (bf16[3,2,128,256]{3,2,1,0:T(8,128)(2,1)S(1)}, bf16[3,2,128,256]{3,2,1,0:T(8,128)(2,1)S(1)}, u32[]{:S(2)}, u32[]{:S(2)}) collective-permute-start(bf16[3,2,128,256]{3,2,1,0:T(8,128)(2,1)S(1)} %copy-done.1), channel_id=1, source_target_pairs={{0,34},{1,35},{2,32},{3,33},{32,2},{33,3},{34,0},{35,1},{4,38},{5,... | collective-permute-start | bytes 1179656 | tf_op jit(solution)/shard_map/ppermute | solution.py:226
  27.6 0.1 reshape.18
  27.7 0.1 dynamic-slice_reduce_fusion
  27.8 0.2 reshape.23.group_ref
  28.0 8.0 %collective-permute-done.5.w1_ref = bf16[3,2,128,256]{3,2,1,0:T(8,128)(2,1)S(1)} collective-permute-done((bf16[3,2,128,256]{3,2,1,0:T(8,128)(2,1)S(1)}, bf16[3,2,128,256]{3,2,1,0:T(8,128)(2,1)S(1)}, u32[]{:S(2)}, u32[]{:S(2)}) %collective-permute-start.5) | collective-permute-done | bytes 393248 | tf_op jit(solution)/shard_map/ppermute | solution.py:226
  36.0 8.7 %collective-permute-done.6.w2_ref = bf16[3,2,128,256]{3,2,1,0:T(8,128)(2,1)S(1)} collective-permute-done((bf16[3,2,128,256]{3,2,1,0:T(8,128)(2,1)S(1)}, bf16[3,2,128,256]{3,2,1,0:T(8,128)(2,1)S(1)}, u32[]{:S(2)}, u32[]{:S(2)}) %collective-permute-start.6) | collective-permute-done | bytes 393248 | tf_op jit(solution)/shard_map/ppermute | solution.py:226
  44.7 1.4 %collective-permute-done.7.w3_ref = bf16[3,2,128,256]{3,2,1,0:T(8,128)(2,1)S(1)} collective-permute-done((bf16[3,2,128,256]{3,2,1,0:T(8,128)(2,1)S(1)}, bf16[3,2,128,256]{3,2,1,0:T(8,128)(2,1)S(1)}, u32[]{:S(2)}, u32[]{:S(2)}) %collective-permute-start.7) | collective-permute-done | bytes 393248 | tf_op jit(solution)/shard_map/ppermute | solution.py:226
  46.0 3.0 %form.1 = bf16[4,8,2,32,128]{4,3,2,1,0:T(8,128)(2,1)S(1)} custom-call(s32[3]{0:T(128)S(1)} %pad_add_fusion.ids_ref, bf16[2,1024,128]{2,1,0:T(8,128)(2,1)S(1)} %pad_maximum_fusion.mine_ref, bf16[2,1024,128]{2,1,0:T(8,128)(2,1)S(1)} %collective-permute-done.4.sib_ref, s32[512,1]{1,0:T(8,128)S(1)} %reshape.23.group_ref, bf16[3,2,128,256]{3,2,1,0:T(8,128)(2,1)S(1)} %copy-done.1, ...), custom_call_target="tpu_custom_call" | custom-call | tf_op jit(solution)/shard_map/form/pallas_call | solution.py:210
  49.0 33.2 %all_to_all.5 = bf16[64,32,128]{2,1,0:T(8,128)(2,1)S(1)} all-to-all(bf16[64,32,128]{2,1,0:T(8,128)(2,1)S(1)} %bitcast.23), channel_id=1, replica_groups=mesh['y'=4,'xlo'=2,'z'=8,'xhi'=2,'core'=2] {'y','z','xhi'}, dimensions={0} | all-to-all | bytes 1048576 | tf_op jit(solution)/shard_map/all_to_all | solution.py:248
  82.2 0.1 convert_reduce_fusion
  82.3 0.6 copy.8
  (8 shorter events, 0.1 us)
Async XLA Ops:
  1.1 4.0 %collective-permute-start = (bf16[128,2048]{1,0:T(8,128)(2,1)S(1)}, bf16[128,2048]{1,0:T(8,128)(2,1)S(1)}, u32[]{:S(2)}, u32[]{:S(2)}) collective-permute-start(bf16[128,2048]{1,0:T(8,128)(2,1)S(1)} %constant_dynamic-slice_fusion), channel_id=1, source_target_pairs={{0,1},{1,0},{2,3},{3,2},{32,33},{33,32},{34,35},{35,34},{4,5},{5,4... | collective-permute-start | bytes 1572872 | tf_op jit(solution)/shard_map/ppermute | solution.py:226
  1.3 1.2 %copy-start = (bf16[256,2048]{1,0:T(8,128)(2,1)S(1)}, bf16[256,2048]{1,0:T(8,128)(2,1)}, u32[]{:S(2)}) copy-start(bf16[256,2048]{1,0:T(8,128)(2,1)} %own_ref.1) | copy-start | bytes 3145732
  7.5 10.7 %collective-permute-start.1 = (bf16[1024,128]{1,0:T(8,128)(2,1)S(1)}, bf16[1024,128]{1,0:T(8,128)(2,1)S(1)}, u32[]{:S(2)}, u32[]{:S(2)}) collective-permute-start(bf16[1024,128]{1,0:T(8,128)(2,1)S(1)} %bitcast.24), channel_id=1, source_target_pairs={{0,2},{1,3},{2,0},{3,1},{32,34},{33,35},{34,32},{35,33},{4,6},{5,7... | collective-permute-start | bytes 786440 | tf_op jit(solution)/shard_map/ppermute | solution.py:226
  13.6 9.9 %collective-permute-start.2 = (bf16[1024,128]{1,0:T(8,128)(2,1)S(1)}, bf16[1024,128]{1,0:T(8,128)(2,1)S(1)}, u32[]{:S(2)}, u32[]{:S(2)}) collective-permute-start(bf16[1024,128]{1,0:T(8,128)(2,1)S(1)} %get-tuple-element.17), channel_id=1, source_target_pairs={{0,32},{1,33},{2,34},{3,35},{32,0},{33,1},{34,2},{35,3},{4,36},{5,... | collective-permute-start | bytes 786440 | tf_op jit(solution)/shard_map/ppermute | solution.py:226
  15.1 8.4 %collective-permute-start.3 = (bf16[1024,128]{1,0:T(8,128)(2,1)S(1)}, bf16[1024,128]{1,0:T(8,128)(2,1)S(1)}, u32[]{:S(2)}, u32[]{:S(2)}) collective-permute-start(bf16[1024,128]{1,0:T(8,128)(2,1)S(1)} %get-tuple-element.18), channel_id=1, source_target_pairs={{0,34},{1,35},{2,32},{3,33},{32,2},{33,3},{34,0},{35,1},{4,38},{5,... | collective-permute-start | bytes 786440 | tf_op jit(solution)/shard_map/ppermute | solution.py:226
  17.5 6.3 %copy-start.1 = (bf16[3,2,128,256]{3,2,1,0:T(8,128)(2,1)S(1)}, bf16[3,2,128,256]{3,2,1,0:T(8,128)(2,1)}, u32[]{:S(2)}) copy-start(bf16[3,2,128,256]{3,2,1,0:T(8,128)(2,1)} %w0_ref.1) | copy-start | bytes 1179652
  17.5 10.1 %copy-start.2 = (s32[2048]{0:T(1024)S(1)}, s32[2048]{0:T(1024)}, u32[]{:S(2)}) copy-start(s32[2048]{0:T(1024)} %param.5) | copy-start | bytes 24580
  23.7 22.4 %collective-permute-start.4 = (bf16[2,1024,128]{2,1,0:T(8,128)(2,1)S(1)}, bf16[2,1024,128]{2,1,0:T(8,128)(2,1)S(1)}, u32[]{:S(2)}, u32[]{:S(2)}) collective-permute-start(bf16[2,1024,128]{2,1,0:T(8,128)(2,1)S(1)} %pad_maximum_fusion.mine_ref), channel_id=1, source_target_pairs={{0,1},{1,0},{2,3},{3,2},{32,33},{33,32},{34,35},{35,34},{4,5},{5,4... | collective-permute-start | bytes 1572872 | tf_op jit(solution)/shard_map/ppermute | solution.py:226
  23.8 12.2 %collective-permute-start.5 = (bf16[3,2,128,256]{3,2,1,0:T(8,128)(2,1)S(1)}, bf16[3,2,128,256]{3,2,1,0:T(8,128)(2,1)S(1)}, u32[]{:S(2)}, u32[]{:S(2)}) collective-permute-start(bf16[3,2,128,256]{3,2,1,0:T(8,128)(2,1)S(1)} %copy-done.1), channel_id=1, source_target_pairs={{0,32},{1,33},{2,34},{3,35},{32,0},{33,1},{34,2},{35,3},{4,36},{5,... | collective-permute-start | bytes 1179656 | tf_op jit(solution)/shard_map/ppermute | solution.py:226
  26.0 18.6 %collective-permute-start.6 = (bf16[3,2,128,256]{3,2,1,0:T(8,128)(2,1)S(1)}, bf16[3,2,128,256]{3,2,1,0:T(8,128)(2,1)S(1)}, u32[]{:S(2)}, u32[]{:S(2)}) collective-permute-start(bf16[3,2,128,256]{3,2,1,0:T(8,128)(2,1)S(1)} %copy-done.1), channel_id=1, source_target_pairs={{0,2},{1,3},{2,0},{3,1},{32,34},{33,35},{34,32},{35,33},{4,6},{5,7... | collective-permute-start | bytes 1179656 | tf_op jit(solution)/shard_map/ppermute | solution.py:226
  26.8 19.3 %collective-permute-start.7 = (bf16[3,2,128,256]{3,2,1,0:T(8,128)(2,1)S(1)}, bf16[3,2,128,256]{3,2,1,0:T(8,128)(2,1)S(1)}, u32[]{:S(2)}, u32[]{:S(2)}) collective-permute-start(bf16[3,2,128,256]{3,2,1,0:T(8,128)(2,1)S(1)} %copy-done.1), channel_id=1, source_target_pairs={{0,34},{1,35},{2,32},{3,33},{32,2},{33,3},{34,0},{35,1},{4,38},{5,... | collective-permute-start | bytes 1179656 | tf_op jit(solution)/shard_map/ppermute | solution.py:226

commit v3 on v2

--- a/solution.py
+++ b/solution.py
@@ -94,7 +94,7 @@
     )(ids, signals)
 
 
-def combine(f_ref, outer_ref, slot, out_ref, index):
+def combine(f_ref, outer_ref, slot, out_ref):
     half = math.sqrt(0.5)
 
     def step(chunk, carry):
@@ -121,7 +121,7 @@
             ei + half * (di - dr),
         )
         for place, value in enumerate(results):
-            out_ref[index, pl.ds(row0 + 256 * place, 16), :] = value.astype(out_ref.dtype)
+            out_ref[pl.ds(row0 + 256 * place, 16), :] = value.astype(out_ref.dtype)
         return carry
 
     lax.fori_loop(0, 16, step, 0, unroll=4)
@@ -134,10 +134,11 @@
     f_ref[...] = lax.dot_general(
         t_ref[0:512, :], xs_ref[...], (((1,), (1,)), ((), ())), preferred_element_type=F32
     )
-    combine(f_ref, outer_ref, 0, out_ref, 0)
-
-
-def next_kernel(slots, xs_ref, t_ref, outer_ref, out_ref, f_ref):
+    combine(f_ref, outer_ref, 0, out_ref)
+
+
+def next_kernel(slots, xs_ref, t_ref, outer_ref, *rest):
+    outs, f_ref = rest[:-1], rest[-1]
     for index, slot in enumerate(slots):
         buf = f_ref.at[index]
         buf[...] = lax.dot_general(
@@ -146,7 +147,7 @@
             (((1,), (1,)), ((), ())),
             preferred_element_type=F32,
         )
-        combine(buf, outer_ref, slot, out_ref, index)
+        combine(buf, outer_ref, slot, outs[index])
 
 
 VM = pl.BlockSpec(memory_space=pltpu.VMEM)
@@ -157,7 +158,7 @@
         first_kernel,
         in_specs=[VM] * 5,
         out_specs=[VM, VM],
-        out_shape=[jax.ShapeDtypeStruct((1, 1024, 128), BF16), jax.ShapeDtypeStruct((1024, 512), BF16)],
+        out_shape=[jax.ShapeDtypeStruct((1024, 128), BF16), jax.ShapeDtypeStruct((1024, 512), BF16)],
         scratch_shapes=[pltpu.VMEM((512, 1024), F32)],
         compiler_params=pltpu.CompilerParams(vmem_limit_bytes=LIMIT),
         name="dft_first",
@@ -168,29 +169,31 @@
     return pl.pallas_call(
         lambda *refs: next_kernel(slots, *refs),
         in_specs=[VM] * 3,
-        out_specs=VM,
-        out_shape=jax.ShapeDtypeStruct((len(slots), 1024, 128), dtype),
+        out_specs=[VM] * len(slots),
+        out_shape=[jax.ShapeDtypeStruct((1024, 128), dtype)] * len(slots),
         scratch_shapes=[pltpu.VMEM((len(slots), 512, 1024), F32)],
         compiler_params=pltpu.CompilerParams(vmem_limit_bytes=LIMIT),
-        name="dft_next",
     )(xs, table, outer)
 
 
-def form_kernel(ids_ref, mine_ref, sib_ref, group_ref, w0_ref, w1_ref, w2_ref, w3_ref, out_ref, l_ref, w_ref):
+def form_kernel(ids_ref, s0_ref, s1_ref, p0_ref, p1_ref, group_ref, w0_ref, w1_ref, w2a_ref, w2b_ref, w3_ref, out_ref, l_ref, w_ref):
     core, half = ids_ref[0], ids_ref[1]
-    for src, place in ((mine_ref, core), (sib_ref, 1 - core)):
+    for srcs, place in (((s0_ref, s1_ref), core), ((p0_ref, p1_ref), 1 - core)):
         for xl in range(2):
             lane0 = pl.multiple_of(xl * 256 + place * 128, 128)
-            sr, si = src[xl, 0:512, :], src[xl, 512:1024, :]
+            src = srcs[xl]
+            sr, si = src[0:512, :], src[512:1024, :]
             l_ref[0:512, pl.ds(lane0, 128)] = sr
             l_ref[0:512, pl.ds(lane0 + 512, 128)] = -si
             l_ref[512:1024, pl.ds(lane0, 128)] = si
             l_ref[512:1024, pl.ds(lane0 + 512, 128)] = sr
     for g in range(3):
         for p in range(2):
-            for b, xl, ref in ((0, 0, w0_ref), (0, 1, w1_ref), (1, 0, w2_ref), (1, 1, w3_ref)):
+            i = g * 2 + p
+            w2 = w2a_ref[i] if i < 3 else w2b_ref[i - 3]
+            for b, xl, w in ((0, 0, w0_ref[i]), (0, 1, w1_ref[i]), (1, 0, w2), (1, 1, w3_ref[i])):
                 row, col = g * 256 + b * 128, p * 512 + xl * 256
-                w_ref[row : row + 128, col : col + 256] = ref[g, p]
+                w_ref[row : row + 128, col : col + 256] = w
     total = jnp.zeros((2, 512, 256), F32)
     groups = group_ref[...]
     for g in range(3):
@@ -206,16 +209,16 @@
         out_ref[:, :, pl.ds(half if b == 0 else 1 - half, 1)] = both[:, :, None]
 
 
-def form(ids, mine, sib, group, weights):
+def form(ids, spec, group, weights):
     return pl.pallas_call(
         form_kernel,
-        in_specs=[pl.BlockSpec(memory_space=pltpu.SMEM)] + [VM] * 7,
+        in_specs=[pl.BlockSpec(memory_space=pltpu.SMEM)] + [VM] * 10,
         out_specs=VM,
         out_shape=jax.ShapeDtypeStruct((4, 8, 2, 32, 128), BF16),
         scratch_shapes=[pltpu.VMEM((1024, 1024), BF16), pltpu.VMEM((768, 1024), BF16)],
         compiler_params=pltpu.CompilerParams(vmem_limit_bytes=LIMIT),
         name="form",
-    )(ids, mine, sib, group, *weights)
+    )(ids, *spec, group, *weights)
 
 
 def shards(signals, weights, bin_group):
@@ -228,24 +231,28 @@
     ids = jnp.stack([core, half, low])
     theirs = lax.dynamic_slice_in_dim(signals, (1 - core) * 128, 128, 0)
     other = exchange(theirs, 1)
-    own, perm, table, outer = prep(ids, signals)
-    peers = [exchange(weights, flip) for flip in (4, 2, 6)]
+    blocks = weights.reshape(6, 128, 256)
+    w1 = exchange(blocks, 4)
+    w3 = exchange(blocks, 6)
+    own, perm, table, outer = prep(ids, pltpu.with_memory_space_constraint(signals, pltpu.HBM))
 
     spec0, xs = dft_first(other, own, perm, table, outer)
-    got0 = exchange(spec0[0], 2)
-    spec12 = dft_next(xs, table, outer, (1, 2), BF16)
-    got1 = exchange(spec12[0], 4)
-    got2 = exchange(spec12[1], 6)
-    spec3 = dft_next(xs, table, outer, (3,), F32)
-    same = spec3[0] + got0.astype(F32)
-    cross = got1.astype(F32) + got2.astype(F32)
-    mine = jnp.stack([same, cross]).astype(BF16)
-    sib = exchange(mine, 1)
+    got0 = exchange(spec0, 2)
+    spec1, spec2 = dft_next(xs, table, outer, (1, 2), BF16)
+    got1 = exchange(spec1, 4)
+    got2 = exchange(spec2, 6)
+    w2a = exchange(w1[:3], 6)
+    w2b = exchange(w3[3:], 4)
+    (spec3,) = dft_next(xs, table, outer, (3,), F32)
+    same = (spec3 + got0.astype(F32)).astype(BF16)
+    same_sib = exchange(same, 1)
+    cross = (got1.astype(F32) + got2.astype(F32)).astype(BF16)
+    cross_sib = exchange(cross, 1)
 
     owned = lax.dynamic_index_in_dim(bin_group.reshape(4, 2, 8, 2, 16), low, 1, keepdims=False)
     owned = lax.dynamic_index_in_dim(owned, half, 2, keepdims=False).reshape(512, 1)
-    parts = form(ids, mine, sib, owned, [weights] + peers).reshape(64, 32, 128)
-    got = lax.all_to_all(parts, ("y", "z", "xhi"), 0, 0, tiled=True)
+    parts = form(ids, (same, cross, same_sib, cross_sib), owned, (blocks, w1, w2a, w2b, w3))
+    got = lax.all_to_all(parts.reshape(64, 32, 128), ("y", "z", "xhi"), 0, 0, tiled=True)
     summed = jnp.sum(got.reshape(32, 2, 2, 16, 128).astype(F32), axis=0)
     return summed.transpose(0, 2, 1, 3).reshape(32, 2, 128)
 

time: 83.1 us -> 77.4 us (0.931)
  waiting for transfers between devices: 24 us -> 18.4 us
  starting transfers between devices: 8.25 us -> 10.6 us
  blocking collectives: 33.2 us -> 31 us
  local copies, waits for them, and re-layouts: 3.34 us -> 2.11 us
  Pallas kernels: 13.6 us -> 14.7 us
    ppermute x8 -> x10, waiting for transfers between devices: 24 us -> 18.4 us  [exchange(): return lax.ppermute(value, ring, [(i, i ^ flip) for i in range(8)])]
    ppermute x8 -> x10, starting transfers between devices: 8.25 us -> 10.6 us  [exchange(): return lax.ppermute(value, ring, [(i, i ^ flip) for i in range(8)])]
    all_to_all x1, blocking collectives: 33.2 us -> 31 us  [shards(): lax.all_to_all(parts.reshape(64, 32, 128), ('y', 'z', 'xhi'), 0, 0, tiled...]
    unnamed x6 -> x4, local copies, waits for them, and re-layouts: 1.24 us -> 0.01 us
    pallas_call x1, Pallas kernels: 2.61 us -> 3.66 us  [prep(): pl.pallas_call(prep_kernel, grid_spec=pltpu.PrefetchScalarGridSpec(num_sc...]
  transfers between devices with their start and end apart: 8 -> 10, of which waited for: 5 -> 6; matrix products, arithmetic and copies ran while one was open for 1% -> 1% of each run, Pallas kernels for 10% -> 7%
where the time goes in v3:
time: 77.4 us; the launch traced here: 77.2 us
  blocking collectives  31 us (40%)
  waiting for transfers between devices  18.4 us (24%)
  Pallas kernels  14.7 us (19%)
  starting transfers between devices  10.6 us (14%)
  local copies, waits for them, and re-layouts  2.11 us (3%)
    all_to_all x1, blocking collectives, shards(): lax.all_to_all(parts.reshape(64, 32, 128), ('y', 'z', 'xhi'), 0, 0, tiled...  31 us
    ppermute x10, waiting for transfers between devices, exchange(): return lax.ppermute(value, ring, [(i, i ^ flip) for i in range(8)])  18.4 us
    ppermute x10, starting transfers between devices, exchange(): return lax.ppermute(value, ring, [(i, i ^ flip) for i in range(8)])  10.6 us
    pallas_call x2, Pallas kernels, dft_next(): pl.pallas_call(lambda *refs: next_kernel(slots, *refs), in_specs=[VM] * 3...  5.66 us
    pallas_call x1, Pallas kernels, prep(): pl.pallas_call(prep_kernel, grid_spec=pltpu.PrefetchScalarGridSpec(num_sc...  3.66 us
    pallas_call x1, Pallas kernels, form(): pl.pallas_call(form_kernel, in_specs=[pl.BlockSpec(memory_space=pltpu.SME...  2.96 us
    pallas_call x1, Pallas kernels, dft_first(): pl.pallas_call(first_kernel, in_specs=[VM] * 5, out_specs=[VM, VM], out_s...  2.43 us
  transfers between devices with their start and end apart: 10, of which 6 were waited for; matrix products, arithmetic and copies ran while one was open for 1% of the time, Pallas kernels for 7%

profile of v3, /device:TPU:2, one launch (start us, length us, event | category | flops | bytes accessed | tf_op | source)
XLA Modules:
  0.0 77.2 jit_solution(2371998612555113364)
XLA Ops:
  0.0 1.1 %constant_dynamic-slice_fusion = bf16[128,2048]{1,0:T(8,128)(2,1)S(1)} fusion(bf16[256,2048]{1,0:T(8,128)(2,1)} %own_ref.1, s32[]{:T(128)S(6)} %select_n.15), kind=kLoop, calls=%fused_computation.5 | loop fusion | bytes 1048580 | tf_op jit(solution)/shard_map/dynamic_slice | solution.py:232
  1.1 0.1 collective-permute-start
  1.2 0.1 pad_add_fusion.ids_ref
  1.3 3.7 %prep.1 = (bf16[1024,256]{1,0:T(8,128)(2,1)S(1)}, bf16[1024,1024]{1,0:T(8,128)(2,1)S(1)}, bf16[2048,512]{1,0:T(8,128)(2,1)S(1)}, f32[4,256,128]{2,1,0:T(8,128)S(1)}) custom-call(s32[3]{0:T(128)S(1)} %pad_add_fusion.ids_ref, bf16[256,2048]{1,0:T(8,128)(2,1)} %own_ref.1), custom_call_target="tpu_custom_call" | custom-call | tf_op jit(solution)/shard_map/prep/pallas_call | solution.py:78
  4.9 2.4 %dft_first.1 = (bf16[1024,128]{1,0:T(8,128)(2,1)S(1)}, bf16[1024,512]{1,0:T(8,128)(2,1)S(1)}) custom-call(bf16[128,2048]{1,0:T(8,128)(2,1)S(1)} %collective-permute-done.other_ref, bf16[1024,256]{1,0:T(8,128)(2,1)S(1)} %get-tuple-element.13.own_ref, bf16[1024,1024]{1,0:T(8,128)(2,1)S(1)} %get-tuple-element.14.perm_ref, ...), custom_call_target="tpu_custom_call" | custom-call | tf_op jit(solution)/shard_map/dft_first/pallas_call | solution.py:157
  7.4 3.8 %shard_map.38 = (bf16[1024,128]{1,0:T(8,128)(2,1)S(1)}, bf16[1024,128]{1,0:T(8,128)(2,1)S(1)}) custom-call(bf16[1024,512]{1,0:T(8,128)(2,1)S(1)} %get-tuple-element.17.refs_0_, bf16[2048,512]{1,0:T(8,128)(2,1)S(1)} %get-tuple-element.15.t_ref.refs_1_, f32[4,256,128]{2,1,0:T(8,128)S(1)} %get-tuple-element.16.outer_ref.refs_2_), custom_call_target="tpu_custom_call" | custom-call | tf_op jit(solution)/shard_map/pallas_call | solution.py:169
  11.2 2.3 %collective-permute-start.2 = (bf16[1024,128]{1,0:T(8,128)(2,1)S(1)}, bf16[1024,128]{1,0:T(8,128)(2,1)S(1)}, u32[]{:S(2)}, u32[]{:S(2)}) collective-permute-start(bf16[1024,128]{1,0:T(8,128)(2,1)S(1)} %get-tuple-element.19), channel_id=1, source_target_pairs={{0,32},{1,33},{2,34},{3,35},{32,0},{33,1},{34,2},{35,3},{4,36},{5,... | collective-permute-start | bytes 786440 | tf_op jit(solution)/shard_map/ppermute | solution.py:229
  13.5 0.5 collective-permute-start.3
  14.0 1.7 %collective-permute-start.1 = (bf16[1024,128]{1,0:T(8,128)(2,1)S(1)}, bf16[1024,128]{1,0:T(8,128)(2,1)S(1)}, u32[]{:S(2)}, u32[]{:S(2)}) collective-permute-start(bf16[1024,128]{1,0:T(8,128)(2,1)S(1)} %get-tuple-element.18), channel_id=1, source_target_pairs={{0,2},{1,3},{2,0},{3,1},{32,34},{33,35},{34,32},{35,33},{4,6},{5,7... | collective-permute-start | bytes 786440 | tf_op jit(solution)/shard_map/ppermute | solution.py:229
  15.7 1.9 %collective-permute-start.6 = (bf16[6,128,256]{2,1,0:T(8,128)(2,1)S(1)}, bf16[6,128,256]{2,1,0:T(8,128)(2,1)S(1)}, u32[]{:S(2)}, u32[]{:S(2)}) collective-permute-start(bf16[6,128,256]{2,1,0:T(8,128)(2,1)S(1)} %bitcast.10), channel_id=1, source_target_pairs={{0,32},{1,33},{2,34},{3,35},{32,0},{33,1},{34,2},{35,3},{4,36},{5,... | collective-permute-start | bytes 1179656 | tf_op jit(solution)/shard_map/ppermute | solution.py:229
  17.6 0.5 collective-permute-start.8
  18.1 1.9 %shard_map.37 = f32[1024,128]{1,0:T(8,128)S(1)} custom-call(bf16[1024,512]{1,0:T(8,128)(2,1)S(1)} %get-tuple-element.17.refs_0_, bf16[2048,512]{1,0:T(8,128)(2,1)S(1)} %get-tuple-element.15.t_ref.refs_1_, f32[4,256,128]{2,1,0:T(8,128)S(1)} %get-tuple-element.16.outer_ref.refs_2_), custom_call_target="tpu_custom_call" | custom-call | tf_op jit(solution)/shard_map/pallas_call | solution.py:169
  19.9 0.0 copy-start.1
  20.0 0.7 collective-permute-done.2
  20.7 7.6 %collective-permute-done.3 = bf16[1024,128]{1,0:T(8,128)(2,1)S(1)} collective-permute-done((bf16[1024,128]{1,0:T(8,128)(2,1)S(1)}, bf16[1024,128]{1,0:T(8,128)(2,1)S(1)}, u32[]{:S(2)}, u32[]{:S(2)}) %collective-permute-start.3) | collective-permute-done | bytes 262176 | tf_op jit(solution)/shard_map/ppermute | solution.py:229
  28.3 0.1 add_convert_fusion.s1_ref
  28.4 0.1 collective-permute-start.5
  28.5 0.1 add_convert_fusion.1.s0_ref
  28.5 0.6 collective-permute-start.4
  29.1 5.4 %collective-permute-done.6.w1_ref = bf16[6,128,256]{2,1,0:T(8,128)(2,1)S(1)} collective-permute-done((bf16[6,128,256]{2,1,0:T(8,128)(2,1)S(1)}, bf16[6,128,256]{2,1,0:T(8,128)(2,1)S(1)}, u32[]{:S(2)}, u32[]{:S(2)}) %collective-permute-start.6) | collective-permute-done | bytes 393248 | tf_op jit(solution)/shard_map/ppermute | solution.py:229
  34.6 1.1 %collective-permute-start.7 = (bf16[3,128,256]{2,1,0:T(8,128)(2,1)S(1)}, bf16[3,128,256]{2,1,0:T(8,128)(2,1)S(1)}, u32[]{:S(2)}, u32[]{:S(2)}) collective-permute-start(bf16[3,128,256]{2,1,0:T(8,128)(2,1)S(1)} %slice.8), channel_id=1, source_target_pairs={{0,34},{1,35},{2,32},{3,33},{32,2},{33,3},{34,0},{35,1},{4,38},{5,... | collective-permute-start | bytes 589832 | tf_op jit(solution)/shard_map/ppermute | solution.py:229
  35.6 0.3 collective-permute-done.8.w3_ref
  36.0 1.9 %collective-permute-start.9 = (bf16[3,128,256]{2,1,0:T(8,128)(2,1)S(1)}, bf16[3,128,256]{2,1,0:T(8,128)(2,1)S(1)}, u32[]{:S(2)}, u32[]{:S(2)}) collective-permute-start(bf16[3,128,256]{2,1,0:T(8,128)(2,1)S(1)} %slice.9), channel_id=1, source_target_pairs={{0,32},{1,33},{2,34},{3,35},{32,0},{33,1},{34,2},{35,3},{4,36},{5,... | collective-permute-start | bytes 589832 | tf_op jit(solution)/shard_map/ppermute | solution.py:229
  37.8 0.1 reshape.21
  38.0 0.1 dynamic-slice_reduce_fusion
  38.0 0.2 reshape.27.group_ref
  38.2 3.2 %collective-permute-done.7.w2a_ref = bf16[3,128,256]{2,1,0:T(8,128)(2,1)S(1)} collective-permute-done((bf16[3,128,256]{2,1,0:T(8,128)(2,1)S(1)}, bf16[3,128,256]{2,1,0:T(8,128)(2,1)S(1)}, u32[]{:S(2)}, u32[]{:S(2)}) %collective-permute-start.7) | collective-permute-done | bytes 196640 | tf_op jit(solution)/shard_map/ppermute | solution.py:229
  41.4 1.2 %collective-permute-done.9.w2b_ref = bf16[3,128,256]{2,1,0:T(8,128)(2,1)S(1)} collective-permute-done((bf16[3,128,256]{2,1,0:T(8,128)(2,1)S(1)}, bf16[3,128,256]{2,1,0:T(8,128)(2,1)S(1)}, u32[]{:S(2)}, u32[]{:S(2)}) %collective-permute-start.9) | collective-permute-done | bytes 196640 | tf_op jit(solution)/shard_map/ppermute | solution.py:229
  42.6 3.0 %form.1 = bf16[4,8,2,32,128]{4,3,2,1,0:T(8,128)(2,1)S(1)} custom-call(s32[3]{0:T(128)S(1)} %pad_add_fusion.ids_ref, bf16[1024,128]{1,0:T(8,128)(2,1)S(1)} %add_convert_fusion.1.s0_ref, bf16[1024,128]{1,0:T(8,128)(2,1)S(1)} %add_convert_fusion.s1_ref, bf16[1024,128]{1,0:T(8,128)(2,1)S(1)} %collective-permute-done.4.p0_ref, ...), custom_call_target="tpu_custom_call" | custom-call | tf_op jit(solution)/shard_map/form/pallas_call | solution.py:213
  45.5 31.0 %all_to_all.5 = bf16[64,32,128]{2,1,0:T(8,128)(2,1)S(1)} all-to-all(bf16[64,32,128]{2,1,0:T(8,128)(2,1)S(1)} %bitcast.9), channel_id=1, replica_groups=mesh['y'=4,'xlo'=2,'z'=8,'xhi'=2,'core'=2] {'y','z','xhi'}, dimensions={0} | all-to-all | bytes 1048576 | tf_op jit(solution)/shard_map/all_to_all | solution.py:255
  76.5 0.1 convert_reduce_fusion
  76.6 0.6 copy.8
  (10 shorter events, 0.1 us)
Async XLA Ops:
  1.1 3.9 %collective-permute-start = (bf16[128,2048]{1,0:T(8,128)(2,1)S(1)}, bf16[128,2048]{1,0:T(8,128)(2,1)S(1)}, u32[]{:S(2)}, u32[]{:S(2)}) collective-permute-start(bf16[128,2048]{1,0:T(8,128)(2,1)S(1)} %constant_dynamic-slice_fusion), channel_id=1, source_target_pairs={{0,1},{1,0},{2,3},{3,2},{32,33},{33,32},{34,35},{35,34},{4,5},{5,4... | collective-permute-start | bytes 1572872 | tf_op jit(solution)/shard_map/ppermute | solution.py:229
  7.4 8.3 %copy-start = (bf16[3,2,128,256]{3,2,1,0:T(8,128)(2,1)S(1)}, bf16[3,2,128,256]{3,2,1,0:T(8,128)(2,1)}, u32[]{:S(2)}) copy-start(bf16[3,2,128,256]{3,2,1,0:T(8,128)(2,1)} %param.4) | copy-start | bytes 1179652
  11.2 9.5 %collective-permute-start.2 = (bf16[1024,128]{1,0:T(8,128)(2,1)S(1)}, bf16[1024,128]{1,0:T(8,128)(2,1)S(1)}, u32[]{:S(2)}, u32[]{:S(2)}) collective-permute-start(bf16[1024,128]{1,0:T(8,128)(2,1)S(1)} %get-tuple-element.19), channel_id=1, source_target_pairs={{0,32},{1,33},{2,34},{3,35},{32,0},{33,1},{34,2},{35,3},{4,36},{5,... | collective-permute-start | bytes 786440 | tf_op jit(solution)/shard_map/ppermute | solution.py:229
  13.5 14.8 %collective-permute-start.3 = (bf16[1024,128]{1,0:T(8,128)(2,1)S(1)}, bf16[1024,128]{1,0:T(8,128)(2,1)S(1)}, u32[]{:S(2)}, u32[]{:S(2)}) collective-permute-start(bf16[1024,128]{1,0:T(8,128)(2,1)S(1)} %get-tuple-element.20), channel_id=1, source_target_pairs={{0,34},{1,35},{2,32},{3,33},{32,2},{33,3},{34,0},{35,1},{4,38},{5,... | collective-permute-start | bytes 786440 | tf_op jit(solution)/shard_map/ppermute | solution.py:229
  14.0 14.5 %collective-permute-start.1 = (bf16[1024,128]{1,0:T(8,128)(2,1)S(1)}, bf16[1024,128]{1,0:T(8,128)(2,1)S(1)}, u32[]{:S(2)}, u32[]{:S(2)}) collective-permute-start(bf16[1024,128]{1,0:T(8,128)(2,1)S(1)} %get-tuple-element.18), channel_id=1, source_target_pairs={{0,2},{1,3},{2,0},{3,1},{32,34},{33,35},{34,32},{35,33},{4,6},{5,7... | collective-permute-start | bytes 786440 | tf_op jit(solution)/shard_map/ppermute | solution.py:229
  15.7 18.9 %collective-permute-start.6 = (bf16[6,128,256]{2,1,0:T(8,128)(2,1)S(1)}, bf16[6,128,256]{2,1,0:T(8,128)(2,1)S(1)}, u32[]{:S(2)}, u32[]{:S(2)}) collective-permute-start(bf16[6,128,256]{2,1,0:T(8,128)(2,1)S(1)} %bitcast.10), channel_id=1, source_target_pairs={{0,32},{1,33},{2,34},{3,35},{32,0},{33,1},{34,2},{35,3},{4,36},{5,... | collective-permute-start | bytes 1179656 | tf_op jit(solution)/shard_map/ppermute | solution.py:229
  17.6 18.4 %collective-permute-start.8 = (bf16[6,128,256]{2,1,0:T(8,128)(2,1)S(1)}, bf16[6,128,256]{2,1,0:T(8,128)(2,1)S(1)}, u32[]{:S(2)}, u32[]{:S(2)}) collective-permute-start(bf16[6,128,256]{2,1,0:T(8,128)(2,1)S(1)} %bitcast.11), channel_id=1, source_target_pairs={{0,34},{1,35},{2,32},{3,33},{32,2},{33,3},{34,0},{35,1},{4,38},{5,... | collective-permute-start | bytes 1179656 | tf_op jit(solution)/shard_map/ppermute | solution.py:229
  19.9 17.9 %copy-start.1 = (s32[2048]{0:T(1024)S(1)}, s32[2048]{0:T(1024)}, u32[]{:S(2)}) copy-start(s32[2048]{0:T(1024)} %param.5) | copy-start | bytes 24580
  28.4 14.2 %collective-permute-start.5 = (bf16[1024,128]{1,0:T(8,128)(2,1)S(1)}, bf16[1024,128]{1,0:T(8,128)(2,1)S(1)}, u32[]{:S(2)}, u32[]{:S(2)}) collective-permute-start(bf16[1024,128]{1,0:T(8,128)(2,1)S(1)} %add_convert_fusion.s1_ref), channel_id=1, source_target_pairs={{0,1},{1,0},{2,3},{3,2},{32,33},{33,32},{34,35},{35,34},{4,5},{5,4... | collective-permute-start | bytes 786440 | tf_op jit(solution)/shard_map/ppermute | solution.py:229
  28.5 14.0 %collective-permute-start.4 = (bf16[1024,128]{1,0:T(8,128)(2,1)S(1)}, bf16[1024,128]{1,0:T(8,128)(2,1)S(1)}, u32[]{:S(2)}, u32[]{:S(2)}) collective-permute-start(bf16[1024,128]{1,0:T(8,128)(2,1)S(1)} %add_convert_fusion.1.s0_ref), channel_id=1, source_target_pairs={{0,1},{1,0},{2,3},{3,2},{32,33},{33,32},{34,35},{35,34},{4,5},{5,4... | collective-permute-start | bytes 786440 | tf_op jit(solution)/shard_map/ppermute | solution.py:229
  34.6 6.8 %collective-permute-start.7 = (bf16[3,128,256]{2,1,0:T(8,128)(2,1)S(1)}, bf16[3,128,256]{2,1,0:T(8,128)(2,1)S(1)}, u32[]{:S(2)}, u32[]{:S(2)}) collective-permute-start(bf16[3,128,256]{2,1,0:T(8,128)(2,1)S(1)} %slice.8), channel_id=1, source_target_pairs={{0,34},{1,35},{2,32},{3,33},{32,2},{33,3},{34,0},{35,1},{4,38},{5,... | collective-permute-start | bytes 589832 | tf_op jit(solution)/shard_map/ppermute | solution.py:229
  36.0 6.6 %collective-permute-start.9 = (bf16[3,128,256]{2,1,0:T(8,128)(2,1)S(1)}, bf16[3,128,256]{2,1,0:T(8,128)(2,1)S(1)}, u32[]{:S(2)}, u32[]{:S(2)}) collective-permute-start(bf16[3,128,256]{2,1,0:T(8,128)(2,1)S(1)} %slice.9), channel_id=1, source_target_pairs={{0,32},{1,33},{2,34},{3,35},{32,0},{33,1},{34,2},{35,3},{4,36},{5,... | collective-permute-start | bytes 589832 | tf_op jit(solution)/shard_map/ppermute | solution.py:229

commit v4 on v2

v4 whole, which is shorter than its diff:
```python
import math

import jax
import jax.numpy as jnp
from jax import lax
from jax.experimental import pallas as pl
from jax.experimental.pallas import tpu as pltpu
from jax.sharding import Mesh, PartitionSpec as P

F32 = jnp.float32
BF16 = jnp.bfloat16
I32 = jnp.int32

STRIDE = 8
SAMPLES = 8192
LIMIT = 24 * 1024 * 1024


def root(numer, denom):
    angle = 2.0 * math.pi / denom * (numer & (denom - 1)).astype(F32)
    return jnp.cos(angle), -jnp.sin(angle)


def iota(shape, dim):
    return lax.broadcasted_iota(I32, shape, dim)


def deinterleave(x, perm):
    out = []
    rows = jnp.concatenate([x[:, :1024], x[:, 1024:]], 0)
    split = jnp.dot(rows, perm, preferred_element_type=F32).astype(BF16)
    for s in range(STRIDE):
        cols = split[:, s * 128 : (s + 1) * 128]
        out.append(jnp.concatenate([cols[:128], cols[128:]], 1))
    return out


def prep_kernel(ids_ref, own_ref, xs_ref, perm_ref, t_ref, outer_ref):
    core, half = ids_ref[0], ids_ref[1]
    lane = iota((32, 512), 1)
    part = lane // 128
    u = jnp.where(part < 2, 2 * core + part, 2 * (1 - core) + part - 2)
    m = u * 128 + (lane & 127)
    ar, ai = root(iota((32, 128), 0) * iota((32, 128), 1), 32)
    br, bi = root((iota((32, 512), 0) + 1) * m, 1024)
    s = iota((32, 128), 1) & (STRIDE - 1)
    imag = (iota((32, 128), 1) & STRIDE) != 0
    oar, oai = root(iota((32, 128), 0) * s * 32, SAMPLES)
    obr, obi = root((iota((32, 128), 0) + 1) * (s + SAMPLES // 2 * half), SAMPLES)
    scale = 1.0 / math.sqrt(SAMPLES)
    ob1 = jnp.where(imag, obi, obr) * scale
    ob2 = jnp.where(imag, obr, -obi) * scale
    tile = lambda row: jnp.concatenate([row] * 4, 1)
    for slot in range(4):
        side = (1 - half) if slot < 2 else half
        pick = lambda a: jnp.where(side == 1, a[16:], a[:16])
        fr, fi, o1, o2 = pick(br), pick(bi), pick(ob1), pick(ob2)
        for t in range(16):
            k = (slot % 2) * 16 + t
            cr, ci = tile(ar[k : k + 1]), tile(ai[k : k + 1])
            row = slot * 512 + t * 16
            t_ref[row : row + 16, :] = (cr * fr - ci * fi).astype(BF16)
            t_ref[row + 256 : row + 272, :] = (cr * fi + ci * fr).astype(BF16)
            outer_ref[slot, t * 16 : t * 16 + 16, :] = oar[k : k + 1] * o1 + oai[k : k + 1] * o2
    offset = iota((1024, 128), 0) - STRIDE * iota((1024, 128), 1)
    for s in range(STRIDE):
        perm_ref[:, s * 128 : (s + 1) * 128] = jnp.where(offset == s, 1.0, 0.0).astype(BF16)
    for s, rows in enumerate(deinterleave(own_ref[...], perm_ref[...])):
        xs_ref[s * 128 : (s + 1) * 128, :] = rows


def prep(ids, signals):
    full = lambda *shape: pl.BlockSpec(shape, lambda i, ids: (0,) * len(shape))
    return pl.pallas_call(
        prep_kernel,
        grid_spec=pltpu.PrefetchScalarGridSpec(
            num_scalar_prefetch=1,
            grid=(1,),
            in_specs=[pl.BlockSpec((128, 2048), lambda i, ids: (ids[0], 0))],
            out_specs=[full(1024, 256), full(1024, 1024), full(2048, 512), full(4, 256, 128)],
        ),
        out_shape=[
            jax.ShapeDtypeStruct((1024, 256), BF16),
            jax.ShapeDtypeStruct((1024, 1024), BF16),
            jax.ShapeDtypeStruct((2048, 512), BF16),
            jax.ShapeDtypeStruct((4, 256, 128), F32),
        ],
        compiler_params=pltpu.CompilerParams(vmem_limit_bytes=LIMIT),
        name="prep",
    )(ids, signals)


def combine(f_ref, outer_ref, slot, *out_refs):
    half = math.sqrt(0.5)

    def step(chunk, carry):
        row0 = pl.multiple_of(chunk * 16, 16)
        gr, gi = [], []
        outer = outer_ref[slot, pl.ds(row0, 16), :]
        for s in range(STRIDE):
            a = f_ref[pl.ds(row0, 16), s * 128 : (s + 1) * 128]
            b = f_ref[pl.ds(row0 + 256, 16), s * 128 : (s + 1) * 128]
            wr = outer[:, s : s + 1]
            wi = outer[:, STRIDE + s : STRIDE + s + 1]
            gr.append(wr * a - wi * b)
            gi.append(wr * b + wi * a)
        pr = [gr[s] + gr[s + 4] for s in range(4)]
        pi = [gi[s] + gi[s + 4] for s in range(4)]
        mr = [gr[s] - gr[s + 4] for s in range(4)]
        mi = [gi[s] - gi[s + 4] for s in range(4)]
        er, ei = mr[0] + mi[2], mi[0] - mr[2]
        dr, di = mr[1] + mi[3], mi[1] - mr[3]
        results = (
            (pr[0] + pr[2]) + (pr[1] + pr[3]),
            er + half * (dr + di),
            (pi[0] + pi[2]) + (pi[1] + pi[3]),
            ei + half * (di - dr),
        )
        for place, value in enumerate(results):
            for out_ref in out_refs:
                out_ref[pl.ds(row0 + 256 * place, 16), :] = value.astype(out_ref.dtype)
        return carry

    lax.fori_loop(0, 16, step, 0, unroll=4)


def first_kernel(other_ref, own_ref, perm_ref, t_ref, outer_ref, out_ref, xs_ref, f_ref):
    xs_ref[:, 0:256] = own_ref[...]
    for s, rows in enumerate(deinterleave(other_ref[...], perm_ref[...])):
        xs_ref[s * 128 : (s + 1) * 128, 256:512] = rows
    f_ref[...] = lax.dot_general(
        t_ref[0:512, :], xs_ref[...], (((1,), (1,)), ((), ())), preferred_element_type=F32
    )
    combine(f_ref, outer_ref, 0, out_ref)


def spectrum(slot, xs_ref, t_ref, f_ref):
    f_ref[...] = lax.dot_general(
        t_ref[slot * 512 : slot * 512 + 512, :], xs_ref[...], (((1,), (1,)), ((), ())), preferred_element_type=F32
    )


def second_kernel(xs_ref, t_ref, outer_ref, out_ref, f_ref):
    spectrum(1, xs_ref, t_ref, f_ref)
    combine(f_ref, outer_ref, 1, out_ref)


def own_kernel(xs_ref, t_ref, outer_ref, owned_ref, wide_ref, out_ref, f_ref):
    for index in range(2):
        spectrum(2 + index, xs_ref, t_ref, f_ref.at[index])
        combine(f_ref.at[index], outer_ref, 2 + index, wide_ref.at[index], out_ref.at[index])


VM = pl.BlockSpec(memory_space=pltpu.VMEM)


def dft_first(other, own, perm, table, outer):
    return pl.pallas_call(
        first_kernel,
        in_specs=[VM] * 5,
        out_specs=[VM, VM],
        out_shape=[jax.ShapeDtypeStruct((1024, 128), BF16), jax.ShapeDtypeStruct((1024, 512), BF16)],
        scratch_shapes=[pltpu.VMEM((512, 1024), F32)],
        compiler_params=pltpu.CompilerParams(vmem_limit_bytes=LIMIT),
        name="dft_first",
    )(other, own, perm, table, outer)


def dft_second(xs, table, outer):
    return pl.pallas_call(
        second_kernel,
        in_specs=[VM] * 3,
        out_specs=VM,
        out_shape=jax.ShapeDtypeStruct((1024, 128), BF16),
        scratch_shapes=[pltpu.VMEM((512, 1024), F32)],
        compiler_params=pltpu.CompilerParams(vmem_limit_bytes=LIMIT),
        name="dft_second",
    )(xs, table, outer)


def dft_own(xs, table, outer, owned):
    return pl.pallas_call(
        own_kernel,
        in_specs=[VM] * 4,
        out_specs=[VM, VM],
        out_shape=[jax.ShapeDtypeStruct((2, 1024, 128), F32), jax.ShapeDtypeStruct((2, 1024, 128), BF16)],
        scratch_shapes=[pltpu.VMEM((2, 512, 1024), F32)],
        compiler_params=pltpu.CompilerParams(vmem_limit_bytes=LIMIT),
        name="dft_own",
    )(xs, table, outer, owned)


def form_kernel(part, ids_ref, wide_ref, got_ref, sib_ref, sib_got_ref, group_ref, w0_ref, w1_ref, *rest):
    out_ref, l_ref, w_ref = rest[-3:]
    core, half = ids_ref[0], ids_ref[1]
    for mine, theirs, place in ((wide_ref, got_ref, core), (sib_ref, sib_got_ref, 1 - core)):
        lane0 = pl.multiple_of(place * 128, 128)
        both = (mine[part].astype(F32) + theirs[...].astype(F32)).astype(BF16)
        sr, si = both[0:512], both[512:1024]
        l_ref[0:512, pl.ds(lane0, 128)] = sr
        l_ref[0:512, pl.ds(lane0 + 256, 128)] = -si
        l_ref[512:1024, pl.ds(lane0, 128)] = si
        l_ref[512:1024, pl.ds(lane0 + 256, 128)] = sr
    for g in range(3):
        for p in range(2):
            for b, ref in ((0, w0_ref), (1, w1_ref)):
                row, col = g * 256 + b * 128, p * 256
                w_ref[row : row + 128, col : col + 256] = ref[g * 2 + p]
    total = jnp.zeros((2, 512, 256), F32)
    groups = group_ref[part]
    for g in range(3):
        acc = lax.dot_general(
            l_ref[...], w_ref[g * 256 : g * 256 + 256, :], (((1,), (1,)), ((), ())), preferred_element_type=F32
        )
        total = jnp.where((groups == g)[None], acc.reshape(2, 512, 256), total)
    for b in range(2):
        block = total[:, :, b * 128 : b * 128 + 128]
        re = block[0].reshape(2, 2, 8, 16, 128)
        im = block[1].reshape(2, 2, 8, 16, 128)
        pair = jnp.concatenate([re, im], 3).astype(BF16)
        side = half if b == 0 else 1 - half
        for f2 in range(2):
            out_ref[2 * f2 + part, :, pl.ds(side, 1)] = pair[f2][:, None]


def form(part, ids, spec, group, weights, begun=()):
    return pl.pallas_call(
        lambda *refs: form_kernel(part, *refs),
        in_specs=[pl.BlockSpec(memory_space=pltpu.SMEM)] + [VM] * (7 + len(begun)),
        out_specs=VM,
        out_shape=jax.ShapeDtypeStruct((4, 2, 2, 8, 32, 128), BF16),
        input_output_aliases={8: 0} if begun else {},
        scratch_shapes=[pltpu.VMEM((1024, 512), BF16), pltpu.VMEM((768, 512), BF16)],
        compiler_params=pltpu.CompilerParams(vmem_limit_bytes=LIMIT),
        name="form_b" if part else "form_a",
    )(ids, *spec, group, *weights, *begun)


def add_first_kernel(got_ref, out_ref):
    for z in range(8):
        for side in range(2):
            total = got_ref[side, z].astype(F32)
            for src in range(1, 8):
                total = total + got_ref[2 * src + side, z].astype(F32)
            out_ref[z, side] = total


def add_last_kernel(got_ref, out_ref):
    for side in range(2):
        total = got_ref[0, side]
        for src in range(1, 8):
            total = total + got_ref[src, side]
        for p in range(2):
            out_ref[side * 16 : side * 16 + 16, p, :] = total[p * 16 : p * 16 + 16]


def add_first(got):
    return pl.pallas_call(
        add_first_kernel,
        in_specs=[VM],
        out_specs=VM,
        out_shape=jax.ShapeDtypeStruct((8, 2, 32, 128), F32),
        compiler_params=pltpu.CompilerParams(vmem_limit_bytes=LIMIT),
        name="add_first",
    )(got)


def add_last(got):
    return pl.pallas_call(
        add_last_kernel,
        in_specs=[VM],
        out_specs=VM,
        out_shape=jax.ShapeDtypeStruct((32, 2, 128), F32),
        compiler_params=pltpu.CompilerParams(vmem_limit_bytes=LIMIT),
        name="add_last",
    )(got)


def shards(signals, weights, bin_group):
    half, core = lax.axis_index("xhi"), lax.axis_index("core")

    def exchange(value, flip):
        return lax.ppermute(value, ("xhi", "core"), [(i, i ^ flip) for i in range(4)])

    ids = jnp.stack([core, half])
    blocks = weights.reshape(6, 128, 256)
    w_far = exchange(blocks, 2)
    theirs = lax.dynamic_slice_in_dim(signals, (1 - core) * 128, 128, 0)
    other = exchange(theirs, 1)
    own, perm, table, outer = prep(ids, pltpu.with_memory_space_constraint(signals, pltpu.HBM))

    spec0, xs = dft_first(other, own, perm, table, outer)
    got0 = exchange(spec0, 2)
    spec1 = dft_second(xs, table, outer)
    got1 = exchange(spec1, 2)
    owned = lax.dynamic_index_in_dim(bin_group.reshape(2, 2, 16, 2, 16), half, 3, keepdims=False)
    owned = owned.transpose(1, 0, 2, 3).reshape(2, 512, 1)
    wide, narrow = dft_own(xs, table, outer, owned)
    sib = exchange(narrow, 1)
    sib_got0 = exchange(got0, 1)
    sib_got1 = exchange(got1, 1)

    spec_a, spec_b = (wide, got0, sib, sib_got0), (wide, got1, sib, sib_got1)
    begun = form(0, ids, spec_a, owned, (blocks, w_far))
    parts = form(1, ids, spec_b, owned, (blocks, w_far), (begun,))
    got = lax.all_to_all(parts.reshape(16, 8, 32, 128), ("y", "xlo", "xhi"), 0, 0, tiled=True)
    column = add_first(got)
    final = lax.all_to_all(column, "z", 0, 0, tiled=True)
    return add_last(final)


def solution(mesh):
    fine = Mesh(mesh.devices.reshape(4, 2, 8, 2, 2), ("y", "xlo", "z", "xhi", "core"))
    chan, beam = ("y", "xlo", "z"), ("xhi", "core")
    in_specs = (P(chan, beam), P(None, None, beam, chan), P())
    out_specs = P(chan, None, beam)
    return jax.shard_map(shards, mesh=fine, in_specs=in_specs, out_specs=out_specs, check_vma=False)
```

time: 83.1 us -> 88.1 us (1.060)
  the two profiles are of different devices: /device:TPU:2 before, /device:TPU:8 now
where the time goes in v4:
time: 88.1 us; the launch traced here: 87.7 us
  blocking collectives  40.5 us (46%)
  Pallas kernels  17.3 us (20%)
  waiting for transfers between devices  15.3 us (17%)
  starting transfers between devices  7.24 us (8%)
  local copies, waits for them, and re-layouts  7.14 us (8%)
    all_to_all x1, blocking collectives, shards(): lax.all_to_all(parts.reshape(16, 8, 32, 128), ('y', 'xlo', 'xhi'), 0, 0,...  21.7 us
    all_to_all x1, blocking collectives, shards(): final = lax.all_to_all(column, 'z', 0, 0, tiled=True)  18.8 us
    ppermute x7, waiting for transfers between devices, exchange(): lax.ppermute(value, ('xhi', 'core'), [(i, i ^ flip) for i in range(4)])  15.3 us
    ppermute x7, starting transfers between devices, exchange(): lax.ppermute(value, ('xhi', 'core'), [(i, i ^ flip) for i in range(4)])  7.24 us
    unnamed x12, local copies, waits for them, and re-layouts  4.76 us
    pallas_call x2, Pallas kernels, form(): pl.pallas_call(lambda *refs: form_kernel(part, *refs), in_specs=[pl.Block...  3.8 us
    pallas_call x1, Pallas kernels, dft_own(): pl.pallas_call(own_kernel, in_specs=[VM] * 4, out_specs=[VM, VM], out_sha...  3.78 us
    pallas_call x1, Pallas kernels, prep(): pl.pallas_call(prep_kernel, grid_spec=pltpu.PrefetchScalarGridSpec(num_sc...  3.65 us
  transfers between devices with their start and end apart: 7, of which 3 were waited for; matrix products, arithmetic and copies ran while one was open for 1% of the time, Pallas kernels for 8%

profile of v4, /device:TPU:8, one launch (start us, length us, event | category | flops | bytes accessed | tf_op | source)
XLA Modules:
  0.0 87.7 jit_solution(8150669823840186502)
XLA Ops:
  0.0 1.9 %constant_dynamic-slice_fusion.1 = bf16[128,2048]{1,0:T(8,128)(2,1)} fusion(bf16[256,2048]{1,0:T(8,128)(2,1)} %own_ref.1, s32[]{:T(128)S(6)} %select_n.7), kind=kLoop, calls=%fused_computation.2 | loop fusion | bytes 1048580 | tf_op jit(solution)/shard_map/dynamic_slice | solution.py:288
  1.9 0.0 collective-permute-start
  1.9 0.1 pad_add_fusion.ids_ref.refs_0_
  2.0 3.7 %prep.1 = (bf16[1024,256]{1,0:T(8,128)(2,1)S(1)}, bf16[1024,1024]{1,0:T(8,128)(2,1)S(1)}, bf16[2048,512]{1,0:T(8,128)(2,1)S(1)}, f32[4,256,128]{2,1,0:T(8,128)S(1)}) custom-call(s32[2]{0:T(128)S(1)} %pad_add_fusion.ids_ref.refs_0_, bf16[256,2048]{1,0:T(8,128)(2,1)} %own_ref.1), custom_call_target="tpu_custom_call" | custom-call | tf_op jit(solution)/shard_map/prep/pallas_call | solution.py:74
  5.7 1.3 %copy-done = bf16[1024,1024]{1,0:T(8,128)(2,1)} copy-done((bf16[1024,1024]{1,0:T(8,128)(2,1)}, bf16[1024,1024]{1,0:T(8,128)(2,1)S(1)}, u32[]{:S(2)}) %copy-start) | copy-done | bytes 2097176
  7.0 0.8 copy-done.3
  7.8 0.1 reshape.12
  8.0 0.3 reshape.16.owned_ref.refs_5_
  8.3 0.0 collective-permute-done.other_ref
  8.3 1.6 %copy-done.1 = bf16[1024,1024]{1,0:T(8,128)(2,1)S(1)} copy-done((bf16[1024,1024]{1,0:T(8,128)(2,1)S(1)}, bf16[1024,1024]{1,0:T(8,128)(2,1)}, u32[]{:S(2)}) %copy-start.1) | copy-done | bytes 2097176
  9.9 1.0 %copy-done.4 = bf16[1024,256]{1,0:T(8,128)(2,1)S(1)} copy-done((bf16[1024,256]{1,0:T(8,128)(2,1)S(1)}, bf16[1024,256]{1,0:T(8,128)(2,1)}, u32[]{:S(2)}) %copy-start.4) | copy-done | bytes 524312
  10.9 3.4 %dft_first.1 = (bf16[1024,128]{1,0:T(8,128)(2,1)S(1)}, bf16[1024,512]{1,0:T(8,128)(2,1)S(1)}) custom-call(bf16[128,2048]{1,0:T(8,128)(2,1)} %collective-permute-done.other_ref, bf16[1024,256]{1,0:T(8,128)(2,1)S(1)} %copy-done.4, bf16[1024,1024]{1,0:T(8,128)(2,1)S(1)} %copy-done.1, bf16[2048,512]{1,0:T(8,128)(2,1)S(1)} %get-tuple-element.15.t_ref, ...), custom_call_target="tpu_custom_call" | custom-call | tf_op jit(solution)/shard_map/dft_first/pallas_call | solution.py:158
  14.4 3.8 %dft_own.1 = (f32[2,1024,128]{2,1,0:T(8,128)S(1)}, bf16[2,1024,128]{2,1,0:T(8,128)(2,1)S(1)}) custom-call(bf16[1024,512]{1,0:T(8,128)(2,1)S(1)} %get-tuple-element.17.xs_ref, bf16[2048,512]{1,0:T(8,128)(2,1)S(1)} %get-tuple-element.15.t_ref, f32[4,256,128]{2,1,0:T(8,128)S(1)} %get-tuple-element.16.outer_ref, s32[2,512,1]{2,1,0:T(8,128)S(1)} %reshape.16.owned_ref.refs_5_), custom_call_target="tpu_custom_call" | custom-call | tf_op jit(solution)/shard_map/dft_own/pallas_call | solution.py:182
  18.2 0.0 copy-start.2
  18.2 0.6 collective-permute-start.2
  18.8 3.0 %collective-permute-start.5 = (bf16[1024,128]{1,0:T(8,128)(2,1)S(1)}, bf16[1024,128]{1,0:T(8,128)(2,1)S(1)}, u32[]{:S(2)}, u32[]{:S(2)}) collective-permute-start(bf16[1024,128]{1,0:T(8,128)(2,1)S(1)} %get-tuple-element.20), channel_id=1, source_target_pairs={{0,2},{1,3},{2,0},{3,1},{4,6},{5,7},{6,4},{7,5},{8,10},{9,11},{10,... | collective-permute-start | bytes 786440 | tf_op jit(solution)/shard_map/ppermute | solution.py:283
  21.8 1.9 %dft_second.1 = bf16[1024,128]{1,0:T(8,128)(2,1)S(1)} custom-call(bf16[1024,512]{1,0:T(8,128)(2,1)S(1)} %get-tuple-element.17.xs_ref, bf16[2048,512]{1,0:T(8,128)(2,1)S(1)} %get-tuple-element.15.t_ref, f32[4,256,128]{2,1,0:T(8,128)S(1)} %get-tuple-element.16.outer_ref), custom_call_target="tpu_custom_call" | custom-call | tf_op jit(solution)/shard_map/dft_second/pallas_call | solution.py:170
  23.7 0.6 collective-permute-start.1
  24.3 3.0 %collective-permute-start.4 = (bf16[6,128,256]{2,1,0:T(8,128)(2,1)S(1)}, bf16[6,128,256]{2,1,0:T(8,128)(2,1)S(1)}, u32[]{:S(2)}, u32[]{:S(2)}) collective-permute-start(bf16[6,128,256]{2,1,0:T(8,128)(2,1)S(1)} %bitcast.10), channel_id=1, source_target_pairs={{0,2},{1,3},{2,0},{3,1},{4,6},{5,7},{6,4},{7,5},{8,10},{9,11},{10,... | collective-permute-start | bytes 1179656 | tf_op jit(solution)/shard_map/ppermute | solution.py:283
  27.3 2.1 %collective-permute-done.5.refs_2_ = bf16[1024,128]{1,0:T(8,128)(2,1)S(1)} collective-permute-done((bf16[1024,128]{1,0:T(8,128)(2,1)S(1)}, bf16[1024,128]{1,0:T(8,128)(2,1)S(1)}, u32[]{:S(2)}, u32[]{:S(2)}) %collective-permute-start.5) | collective-permute-done | bytes 262176 | tf_op jit(solution)/shard_map/ppermute | solution.py:283
  29.5 0.0 collective-permute-start.6
  29.5 5.6 %collective-permute-done.1.refs_2_ = bf16[1024,128]{1,0:T(8,128)(2,1)S(1)} collective-permute-done((bf16[1024,128]{1,0:T(8,128)(2,1)S(1)}, bf16[1024,128]{1,0:T(8,128)(2,1)S(1)}, u32[]{:S(2)}, u32[]{:S(2)}) %collective-permute-start.1) | collective-permute-done | bytes 262176 | tf_op jit(solution)/shard_map/ppermute | solution.py:283
  35.1 0.0 collective-permute-start.3
  35.1 7.6 %collective-permute-done.4.refs_7_ = bf16[6,128,256]{2,1,0:T(8,128)(2,1)S(1)} collective-permute-done((bf16[6,128,256]{2,1,0:T(8,128)(2,1)S(1)}, bf16[6,128,256]{2,1,0:T(8,128)(2,1)S(1)}, u32[]{:S(2)}, u32[]{:S(2)}) %collective-permute-start.4) | collective-permute-done | bytes 393248 | tf_op jit(solution)/shard_map/ppermute | solution.py:283
  42.6 0.0 collective-permute-done.2.refs_3_
  42.6 0.0 collective-permute-done.6.refs_4_
  42.6 1.9 %form_a.1.refs_8_ = bf16[4,2,2,8,32,128]{5,4,3,2,1,0:T(8,128)(2,1)S(1)} custom-call(s32[2]{0:T(128)S(1)} %pad_add_fusion.ids_ref.refs_0_, f32[2,1024,128]{2,1,0:T(8,128)S(1)} %get-tuple-element.18.refs_1_, bf16[1024,128]{1,0:T(8,128)(2,1)S(1)} %collective-permute-done.5.refs_2_, bf16[2,1024,128]{2,1,0:T(8,128)(2,1)S(1)} %collective-permute-done.2.refs_3_, ...), custom_call_target="tpu_custom_call" | custom-call | tf_op jit(solution)/shard_map/form_a/pallas_call | solution.py:227
  44.6 1.9 %form_b.1 = bf16[4,2,2,8,32,128]{5,4,3,2,1,0:T(8,128)(2,1)S(1)} custom-call(s32[2]{0:T(128)S(1)} %pad_add_fusion.ids_ref.refs_0_, f32[2,1024,128]{2,1,0:T(8,128)S(1)} %get-tuple-element.18.refs_1_, bf16[1024,128]{1,0:T(8,128)(2,1)S(1)} %collective-permute-done.1.refs_2_, ...), custom_call_target="tpu_custom_call", output_to_operand_aliasing={{}: (8, {})} | custom-call | tf_op jit(solution)/shard_map/form_b/pallas_call | solution.py:227
  46.5 21.7 %all_to_all.10.got_ref = bf16[16,8,32,128]{3,2,1,0:T(8,128)(2,1)S(1)} all-to-all(bf16[16,8,32,128]{3,2,1,0:T(8,128)(2,1)S(1)} %bitcast.9), channel_id=1, replica_groups=mesh['y'=4,'xlo'=2,'z'=8,'xhi'=2,'core'=2] {'y','xlo','xhi'}, dimensions={0} | all-to-all | bytes 2097152 | tf_op jit(solution)/shard_map/all_to_all | solution.py:306
  68.2 0.1 add_first.1
  68.3 18.8 %all_to_all.11.got_ref = f32[8,2,32,128]{3,2,1,0:T(8,128)S(1)} all-to-all(f32[8,2,32,128]{3,2,1,0:T(8,128)S(1)} %add_first.1), channel_id=1, replica_groups=mesh['y'=4,'xlo'=2,'z'=8,'xhi'=2,'core'=2] {'z'}, dimensions={0} | all-to-all | bytes 524288 | tf_op jit(solution)/shard_map/all_to_all | solution.py:308
  87.1 0.6 add_last.1
  (10 shorter events, 0.1 us)
Async XLA Ops:
  0.0 7.8 %copy-start.5 = (s32[2048]{0:T(1024)S(1)}, s32[2048]{0:T(1024)}, u32[]{:S(2)}) copy-start(s32[2048]{0:T(1024)} %param.5) | copy-start | bytes 24580
  1.9 6.4 %collective-permute-start = (bf16[128,2048]{1,0:T(8,128)(2,1)}, bf16[128,2048]{1,0:T(8,128)(2,1)}, u32[]{:S(2)}, u32[]{:S(2)}) collective-permute-start(bf16[128,2048]{1,0:T(8,128)(2,1)} %constant_dynamic-slice_fusion.1), channel_id=1, source_target_pairs={{0,1},{1,0},{2,3},{3,2},{4,5},{5,4},{6,7},{7,6},{8,9},{9,8},{10,11... | collective-permute-start | bytes 1572872 | tf_op jit(solution)/shard_map/ppermute | solution.py:283
  5.7 1.3 %copy-start = (bf16[1024,1024]{1,0:T(8,128)(2,1)}, bf16[1024,1024]{1,0:T(8,128)(2,1)S(1)}, u32[]{:S(2)}) copy-start(bf16[1024,1024]{1,0:T(8,128)(2,1)S(1)} %get-tuple-element.14.perm_ref) | copy-start | bytes 6291460
  7.0 0.8 copy-start.3
  8.3 1.6 %copy-start.1 = (bf16[1024,1024]{1,0:T(8,128)(2,1)S(1)}, bf16[1024,1024]{1,0:T(8,128)(2,1)}, u32[]{:S(2)}) copy-start(bf16[1024,1024]{1,0:T(8,128)(2,1)} %copy-done) | copy-start | bytes 6291460
  9.9 1.0 %copy-start.4 = (bf16[1024,256]{1,0:T(8,128)(2,1)S(1)}, bf16[1024,256]{1,0:T(8,128)(2,1)}, u32[]{:S(2)}) copy-start(bf16[1024,256]{1,0:T(8,128)(2,1)} %copy-done.3) | copy-start | bytes 1572868
  18.2 6.1 %copy-start.2 = (bf16[3,2,128,256]{3,2,1,0:T(8,128)(2,1)S(1)}, bf16[3,2,128,256]{3,2,1,0:T(8,128)(2,1)}, u32[]{:S(2)}) copy-start(bf16[3,2,128,256]{3,2,1,0:T(8,128)(2,1)} %param.4) | copy-start | bytes 1179652
  18.2 24.5 %collective-permute-start.2 = (bf16[2,1024,128]{2,1,0:T(8,128)(2,1)S(1)}, bf16[2,1024,128]{2,1,0:T(8,128)(2,1)S(1)}, u32[]{:S(2)}, u32[]{:S(2)}) collective-permute-start(bf16[2,1024,128]{2,1,0:T(8,128)(2,1)S(1)} %get-tuple-element.19), channel_id=1, source_target_pairs={{0,1},{1,0},{2,3},{3,2},{4,5},{5,4},{6,7},{7,6},{8,9},{9,8},{10,11... | collective-permute-start | bytes 1572872 | tf_op jit(solution)/shard_map/ppermute | solution.py:283
  18.8 10.7 %collective-permute-start.5 = (bf16[1024,128]{1,0:T(8,128)(2,1)S(1)}, bf16[1024,128]{1,0:T(8,128)(2,1)S(1)}, u32[]{:S(2)}, u32[]{:S(2)}) collective-permute-start(bf16[1024,128]{1,0:T(8,128)(2,1)S(1)} %get-tuple-element.20), channel_id=1, source_target_pairs={{0,2},{1,3},{2,0},{3,1},{4,6},{5,7},{6,4},{7,5},{8,10},{9,11},{10,... | collective-permute-start | bytes 786440 | tf_op jit(solution)/shard_map/ppermute | solution.py:283
  23.7 11.4 %collective-permute-start.1 = (bf16[1024,128]{1,0:T(8,128)(2,1)S(1)}, bf16[1024,128]{1,0:T(8,128)(2,1)S(1)}, u32[]{:S(2)}, u32[]{:S(2)}) collective-permute-start(bf16[1024,128]{1,0:T(8,128)(2,1)S(1)} %dft_second.1), channel_id=1, source_target_pairs={{0,2},{1,3},{2,0},{3,1},{4,6},{5,7},{6,4},{7,5},{8,10},{9,11},{10,... | collective-permute-start | bytes 786440 | tf_op jit(solution)/shard_map/ppermute | solution.py:283
  24.3 18.3 %collective-permute-start.4 = (bf16[6,128,256]{2,1,0:T(8,128)(2,1)S(1)}, bf16[6,128,256]{2,1,0:T(8,128)(2,1)S(1)}, u32[]{:S(2)}, u32[]{:S(2)}) collective-permute-start(bf16[6,128,256]{2,1,0:T(8,128)(2,1)S(1)} %bitcast.10), channel_id=1, source_target_pairs={{0,2},{1,3},{2,0},{3,1},{4,6},{5,7},{6,4},{7,5},{8,10},{9,11},{10,... | collective-permute-start | bytes 1179656 | tf_op jit(solution)/shard_map/ppermute | solution.py:283
  29.5 13.2 %collective-permute-start.6 = (bf16[1024,128]{1,0:T(8,128)(2,1)S(1)}, bf16[1024,128]{1,0:T(8,128)(2,1)S(1)}, u32[]{:S(2)}, u32[]{:S(2)}) collective-permute-start(bf16[1024,128]{1,0:T(8,128)(2,1)S(1)} %collective-permute-done.5.refs_2_), channel_id=1, source_target_pairs={{0,1},{1,0},{2,3},{3,2},{4,5},{5,4},{6,7},{7,6},{8,9},{9,8},{10,11... | collective-permute-start | bytes 786440 | tf_op jit(solution)/shard_map/ppermute | solution.py:283
  35.1 9.5 %collective-permute-start.3 = (bf16[1024,128]{1,0:T(8,128)(2,1)S(1)}, bf16[1024,128]{1,0:T(8,128)(2,1)S(1)}, u32[]{:S(2)}, u32[]{:S(2)}) collective-permute-start(bf16[1024,128]{1,0:T(8,128)(2,1)S(1)} %collective-permute-done.1.refs_2_), channel_id=1, source_target_pairs={{0,1},{1,0},{2,3},{3,2},{4,5},{5,4},{6,7},{7,6},{8,9},{9,8},{10,11... | collective-permute-start | bytes 786440 | tf_op jit(solution)/shard_map/ppermute | solution.py:283

commit v5 on v4

--- a/solution.py
+++ b/solution.py
@@ -124,9 +124,10 @@
     lax.fori_loop(0, 16, step, 0, unroll=4)
 
 
-def first_kernel(other_ref, own_ref, perm_ref, t_ref, outer_ref, out_ref, xs_ref, f_ref):
+def first_kernel(ids_ref, other_ref, own_ref, perm_ref, t_ref, outer_ref, out_ref, xs_ref, f_ref):
     xs_ref[:, 0:256] = own_ref[...]
-    for s, rows in enumerate(deinterleave(other_ref[...], perm_ref[...])):
+    other = other_ref[pl.ds(pl.multiple_of(ids_ref[0] * 128, 128), 128), :]
+    for s, rows in enumerate(deinterleave(other, perm_ref[...])):
         xs_ref[s * 128 : (s + 1) * 128, 256:512] = rows
     f_ref[...] = lax.dot_general(
         t_ref[0:512, :], xs_ref[...], (((1,), (1,)), ((), ())), preferred_element_type=F32
@@ -154,16 +155,16 @@
 VM = pl.BlockSpec(memory_space=pltpu.VMEM)
 
 
-def dft_first(other, own, perm, table, outer):
+def dft_first(ids, other, own, perm, table, outer):
     return pl.pallas_call(
         first_kernel,
-        in_specs=[VM] * 5,
+        in_specs=[pl.BlockSpec(memory_space=pltpu.SMEM)] + [VM] * 5,
         out_specs=[VM, VM],
         out_shape=[jax.ShapeDtypeStruct((1024, 128), BF16), jax.ShapeDtypeStruct((1024, 512), BF16)],
         scratch_shapes=[pltpu.VMEM((512, 1024), F32)],
         compiler_params=pltpu.CompilerParams(vmem_limit_bytes=LIMIT),
         name="dft_first",
-    )(other, own, perm, table, outer)
+    )(ids, other, own, perm, table, outer)
 
 
 def dft_second(xs, table, outer):
@@ -220,7 +221,7 @@
         pair = jnp.concatenate([re, im], 3).astype(BF16)
         side = half if b == 0 else 1 - half
         for f2 in range(2):
-            out_ref[2 * f2 + part, :, pl.ds(side, 1)] = pair[f2][:, None]
+            out_ref[2 * f2 + part, :, :, pl.ds(side, 1)] = pair[f2][:, :, None]
 
 
 def form(part, ids, spec, group, weights, begun=()):
@@ -228,7 +229,7 @@
         lambda *refs: form_kernel(part, *refs),
         in_specs=[pl.BlockSpec(memory_space=pltpu.SMEM)] + [VM] * (7 + len(begun)),
         out_specs=VM,
-        out_shape=jax.ShapeDtypeStruct((4, 2, 2, 8, 32, 128), BF16),
+        out_shape=jax.ShapeDtypeStruct((4, 2, 8, 2, 32, 128), BF16),
         input_output_aliases={8: 0} if begun else {},
         scratch_shapes=[pltpu.VMEM((1024, 512), BF16), pltpu.VMEM((768, 512), BF16)],
         compiler_params=pltpu.CompilerParams(vmem_limit_bytes=LIMIT),
@@ -236,43 +237,24 @@
     )(ids, *spec, group, *weights, *begun)
 
 
-def add_first_kernel(got_ref, out_ref):
-    for z in range(8):
-        for side in range(2):
-            total = got_ref[side, z].astype(F32)
-            for src in range(1, 8):
-                total = total + got_ref[2 * src + side, z].astype(F32)
-            out_ref[z, side] = total
-
-
-def add_last_kernel(got_ref, out_ref):
+def add_kernel(got_ref, out_ref):
     for side in range(2):
-        total = got_ref[0, side]
-        for src in range(1, 8):
-            total = total + got_ref[src, side]
+        parts = [got_ref[2 * src + side].astype(F32) for src in range(4)]
+        for src in range(4, 64):
+            parts[src % 4] = parts[src % 4] + got_ref[2 * src + side].astype(F32)
+        total = (parts[0] + parts[1]) + (parts[2] + parts[3])
         for p in range(2):
             out_ref[side * 16 : side * 16 + 16, p, :] = total[p * 16 : p * 16 + 16]
 
 
-def add_first(got):
-    return pl.pallas_call(
-        add_first_kernel,
-        in_specs=[VM],
-        out_specs=VM,
-        out_shape=jax.ShapeDtypeStruct((8, 2, 32, 128), F32),
-        compiler_params=pltpu.CompilerParams(vmem_limit_bytes=LIMIT),
-        name="add_first",
-    )(got)
-
-
-def add_last(got):
-    return pl.pallas_call(
-        add_last_kernel,
+def add(got):
+    return pl.pallas_call(
+        add_kernel,
         in_specs=[VM],
         out_specs=VM,
         out_shape=jax.ShapeDtypeStruct((32, 2, 128), F32),
         compiler_params=pltpu.CompilerParams(vmem_limit_bytes=LIMIT),
-        name="add_last",
+        name="add",
     )(got)
 
 
@@ -285,11 +267,10 @@
     ids = jnp.stack([core, half])
     blocks = weights.reshape(6, 128, 256)
     w_far = exchange(blocks, 2)
-    theirs = lax.dynamic_slice_in_dim(signals, (1 - core) * 128, 128, 0)
-    other = exchange(theirs, 1)
+    other = exchange(signals, 1)
     own, perm, table, outer = prep(ids, pltpu.with_memory_space_constraint(signals, pltpu.HBM))
 
-    spec0, xs = dft_first(other, own, perm, table, outer)
+    spec0, xs = dft_first(ids, other, own, perm, table, outer)
     got0 = exchange(spec0, 2)
     spec1 = dft_second(xs, table, outer)
     got1 = exchange(spec1, 2)
@@ -303,10 +284,8 @@
     spec_a, spec_b = (wide, got0, sib, sib_got0), (wide, got1, sib, sib_got1)
     begun = form(0, ids, spec_a, owned, (blocks, w_far))
     parts = form(1, ids, spec_b, owned, (blocks, w_far), (begun,))
-    got = lax.all_to_all(parts.reshape(16, 8, 32, 128), ("y", "xlo", "xhi"), 0, 0, tiled=True)
-    column = add_first(got)
-    final = lax.all_to_all(column, "z", 0, 0, tiled=True)
-    return add_last(final)
+    got = lax.all_to_all(parts.reshape(128, 32, 128), ("y", "xlo", "z", "xhi"), 0, 0, tiled=True)
+    return add(got)
 
 
 def solution(mesh):

time: 88.1 us -> 91.5 us (1.039)
  the two profiles are of different devices: /device:TPU:8 before, /device:TPU:32 now
where the time goes in v5:
time: 91.5 us; the launch traced here: 91.2 us
  blocking collectives  44.9 us (49%)
  Pallas kernels  17.6 us (19%)
  waiting for transfers between devices  15.3 us (17%)
  starting transfers between devices  7.24 us (8%)
  local copies, waits for them, and re-layouts  5.93 us (6%)
    all_to_all x1, blocking collectives, shards(): lax.all_to_all(parts.reshape(128, 32, 128), ('y', 'xlo', 'z', 'xhi'), 0,...  44.9 us
    ppermute x7, waiting for transfers between devices, exchange(): lax.ppermute(value, ('xhi', 'core'), [(i, i ^ flip) for i in range(4)])  15.3 us
    ppermute x7, starting transfers between devices, exchange(): lax.ppermute(value, ('xhi', 'core'), [(i, i ^ flip) for i in range(4)])  7.24 us
    unnamed x10, local copies, waits for them, and re-layouts  4.77 us
    pallas_call x2, Pallas kernels, form(): pl.pallas_call(lambda *refs: form_kernel(part, *refs), in_specs=[pl.Block...  3.8 us
    pallas_call x1, Pallas kernels, dft_own(): pl.pallas_call(own_kernel, in_specs=[VM] * 4, out_specs=[VM, VM], out_sha...  3.78 us
    pallas_call x1, Pallas kernels, dft_first(): pl.pallas_call(first_kernel, in_specs=[pl.BlockSpec(memory_space=pltpu.SM...  3.66 us
    pallas_call x1, Pallas kernels, prep(): pl.pallas_call(prep_kernel, grid_spec=pltpu.PrefetchScalarGridSpec(num_sc...  3.65 us
  transfers between devices with their start and end apart: 7, of which 3 were waited for; matrix products, arithmetic and copies ran while one was open for 1% of the time, Pallas kernels for 8%

profile of v5, /device:TPU:32, one launch (start us, length us, event | category | flops | bytes accessed | tf_op | source)
XLA Modules:
  0.0 91.2 jit_solution(4663805496234102896)
XLA Ops:
  0.0 0.0 collective-permute-start
  0.0 0.1 pad_add_fusion.ids_ref.refs_0_
  0.1 3.7 %prep.1 = (bf16[1024,256]{1,0:T(8,128)(2,1)S(1)}, bf16[1024,1024]{1,0:T(8,128)(2,1)S(1)}, bf16[2048,512]{1,0:T(8,128)(2,1)S(1)}, f32[4,256,128]{2,1,0:T(8,128)S(1)}) custom-call(s32[2]{0:T(128)S(1)} %pad_add_fusion.ids_ref.refs_0_, bf16[256,2048]{1,0:T(8,128)(2,1)} %own_ref.1), custom_call_target="tpu_custom_call" | custom-call | tf_op jit(solution)/shard_map/prep/pallas_call | solution.py:74
  3.7 0.0 copy-start
  3.7 1.3 %copy-done = bf16[1024,1024]{1,0:T(8,128)(2,1)} copy-done((bf16[1024,1024]{1,0:T(8,128)(2,1)}, bf16[1024,1024]{1,0:T(8,128)(2,1)S(1)}, u32[]{:S(2)}) %copy-start) | copy-done | bytes 2097176
  5.1 0.8 copy-done.3
  5.9 0.8 reshape.12
  6.8 0.3 reshape.16.owned_ref.refs_5_
  7.1 0.0 collective-permute-done.other_ref
  7.1 0.0 copy-start.1
  7.1 1.6 %copy-done.1 = bf16[1024,1024]{1,0:T(8,128)(2,1)S(1)} copy-done((bf16[1024,1024]{1,0:T(8,128)(2,1)S(1)}, bf16[1024,1024]{1,0:T(8,128)(2,1)}, u32[]{:S(2)}) %copy-start.1) | copy-done | bytes 2097176
  8.7 1.0 %copy-done.4 = bf16[1024,256]{1,0:T(8,128)(2,1)S(1)} copy-done((bf16[1024,256]{1,0:T(8,128)(2,1)S(1)}, bf16[1024,256]{1,0:T(8,128)(2,1)}, u32[]{:S(2)}) %copy-start.4) | copy-done | bytes 524312
  9.7 3.7 %dft_first.1 = (bf16[1024,128]{1,0:T(8,128)(2,1)S(1)}, bf16[1024,512]{1,0:T(8,128)(2,1)S(1)}) custom-call(s32[2]{0:T(128)S(1)} %pad_add_fusion.ids_ref.refs_0_, bf16[256,2048]{1,0:T(8,128)(2,1)} %collective-permute-done.other_ref, bf16[1024,256]{1,0:T(8,128)(2,1)S(1)} %copy-done.4, bf16[1024,1024]{1,0:T(8,128)(2,1)S(1)} %copy-done.1, ...), custom_call_target="tpu_custom_call" | custom-call | tf_op jit(solution)/shard_map/dft_first/pallas_call | solution.py:159
  13.4 3.8 %dft_own.1 = (f32[2,1024,128]{2,1,0:T(8,128)S(1)}, bf16[2,1024,128]{2,1,0:T(8,128)(2,1)S(1)}) custom-call(bf16[1024,512]{1,0:T(8,128)(2,1)S(1)} %get-tuple-element.17.xs_ref, bf16[2048,512]{1,0:T(8,128)(2,1)S(1)} %get-tuple-element.15.t_ref, f32[4,256,128]{2,1,0:T(8,128)S(1)} %get-tuple-element.16.outer_ref, s32[2,512,1]{2,1,0:T(8,128)S(1)} %reshape.16.owned_ref.refs_5_), custom_call_target="tpu_custom_call" | custom-call | tf_op jit(solution)/shard_map/dft_own/pallas_call | solution.py:183
  17.2 0.0 copy-start.2
  17.2 0.6 collective-permute-start.2
  17.8 3.0 %collective-permute-start.5 = (bf16[1024,128]{1,0:T(8,128)(2,1)S(1)}, bf16[1024,128]{1,0:T(8,128)(2,1)S(1)}, u32[]{:S(2)}, u32[]{:S(2)}) collective-permute-start(bf16[1024,128]{1,0:T(8,128)(2,1)S(1)} %get-tuple-element.20), channel_id=1, source_target_pairs={{0,2},{1,3},{2,0},{3,1},{4,6},{5,7},{6,4},{7,5},{8,10},{9,11},{10,... | collective-permute-start | bytes 786440 | tf_op jit(solution)/shard_map/ppermute | solution.py:265
  20.8 1.9 %dft_second.1 = bf16[1024,128]{1,0:T(8,128)(2,1)S(1)} custom-call(bf16[1024,512]{1,0:T(8,128)(2,1)S(1)} %get-tuple-element.17.xs_ref, bf16[2048,512]{1,0:T(8,128)(2,1)S(1)} %get-tuple-element.15.t_ref, f32[4,256,128]{2,1,0:T(8,128)S(1)} %get-tuple-element.16.outer_ref), custom_call_target="tpu_custom_call" | custom-call | tf_op jit(solution)/shard_map/dft_second/pallas_call | solution.py:171
  22.7 0.6 collective-permute-start.1
  23.3 3.0 %collective-permute-start.4 = (bf16[6,128,256]{2,1,0:T(8,128)(2,1)S(1)}, bf16[6,128,256]{2,1,0:T(8,128)(2,1)S(1)}, u32[]{:S(2)}, u32[]{:S(2)}) collective-permute-start(bf16[6,128,256]{2,1,0:T(8,128)(2,1)S(1)} %bitcast.10), channel_id=1, source_target_pairs={{0,2},{1,3},{2,0},{3,1},{4,6},{5,7},{6,4},{7,5},{8,10},{9,11},{10,... | collective-permute-start | bytes 1179656 | tf_op jit(solution)/shard_map/ppermute | solution.py:265
  26.3 2.2 %collective-permute-done.5.refs_2_ = bf16[1024,128]{1,0:T(8,128)(2,1)S(1)} collective-permute-done((bf16[1024,128]{1,0:T(8,128)(2,1)S(1)}, bf16[1024,128]{1,0:T(8,128)(2,1)S(1)}, u32[]{:S(2)}, u32[]{:S(2)}) %collective-permute-start.5) | collective-permute-done | bytes 262176 | tf_op jit(solution)/shard_map/ppermute | solution.py:265
  28.5 0.0 collective-permute-start.6
  28.5 5.6 %collective-permute-done.1.refs_2_ = bf16[1024,128]{1,0:T(8,128)(2,1)S(1)} collective-permute-done((bf16[1024,128]{1,0:T(8,128)(2,1)S(1)}, bf16[1024,128]{1,0:T(8,128)(2,1)S(1)}, u32[]{:S(2)}, u32[]{:S(2)}) %collective-permute-start.1) | collective-permute-done | bytes 262176 | tf_op jit(solution)/shard_map/ppermute | solution.py:265
  34.1 0.0 collective-permute-start.3
  34.1 7.6 %collective-permute-done.4.refs_7_ = bf16[6,128,256]{2,1,0:T(8,128)(2,1)S(1)} collective-permute-done((bf16[6,128,256]{2,1,0:T(8,128)(2,1)S(1)}, bf16[6,128,256]{2,1,0:T(8,128)(2,1)S(1)}, u32[]{:S(2)}, u32[]{:S(2)}) %collective-permute-start.4) | collective-permute-done | bytes 393248 | tf_op jit(solution)/shard_map/ppermute | solution.py:265
  41.6 0.0 collective-permute-done.2.refs_3_
  41.6 0.0 collective-permute-done.6.refs_4_
  41.6 1.9 %form_a.1.refs_8_ = bf16[4,2,8,2,32,128]{5,4,3,2,1,0:T(8,128)(2,1)S(1)} custom-call(s32[2]{0:T(128)S(1)} %pad_add_fusion.ids_ref.refs_0_, f32[2,1024,128]{2,1,0:T(8,128)S(1)} %get-tuple-element.18.refs_1_, bf16[1024,128]{1,0:T(8,128)(2,1)S(1)} %collective-permute-done.5.refs_2_, bf16[2,1024,128]{2,1,0:T(8,128)(2,1)S(1)} %collective-permute-done.2.refs_3_, ...), custom_call_target="tpu_custom_call" | custom-call | tf_op jit(solution)/shard_map/form_a/pallas_call | solution.py:228
  43.6 0.0 collective-permute-done.3.refs_4_
  43.6 1.9 %form_b.1 = bf16[4,2,8,2,32,128]{5,4,3,2,1,0:T(8,128)(2,1)S(1)} custom-call(s32[2]{0:T(128)S(1)} %pad_add_fusion.ids_ref.refs_0_, f32[2,1024,128]{2,1,0:T(8,128)S(1)} %get-tuple-element.18.refs_1_, bf16[1024,128]{1,0:T(8,128)(2,1)S(1)} %collective-permute-done.1.refs_2_, ...), custom_call_target="tpu_custom_call", output_to_operand_aliasing={{}: (8, {})} | custom-call | tf_op jit(solution)/shard_map/form_b/pallas_call | solution.py:228
  45.5 44.9 %all_to_all.5.got_ref = bf16[128,32,128]{2,1,0:T(8,128)(2,1)S(1)} all-to-all(bf16[128,32,128]{2,1,0:T(8,128)(2,1)S(1)} %bitcast.9), channel_id=1, replica_groups=mesh['y'=4,'xlo'=2,'z'=8,'xhi'=2,'core'=2] {'y','xlo','z','xhi'}, dimensions={0} | all-to-all | bytes 2097152 | tf_op jit(solution)/shard_map/all_to_all | solution.py:287
  90.4 0.8 add.8
  (5 shorter events, 0.0 us)
Async XLA Ops:
  0.0 7.1 %collective-permute-start = (bf16[256,2048]{1,0:T(8,128)(2,1)}, bf16[256,2048]{1,0:T(8,128)(2,1)}, u32[]{:S(2)}, u32[]{:S(2)}) collective-permute-start(bf16[256,2048]{1,0:T(8,128)(2,1)} %own_ref.1), channel_id=1, source_target_pairs={{0,1},{1,0},{2,3},{3,2},{4,5},{5,4},{6,7},{7,6},{8,9},{9,8},{10,11... | collective-permute-start | bytes 3145736 | tf_op jit(solution)/shard_map/ppermute | solution.py:265
  3.7 1.3 %copy-start = (bf16[1024,1024]{1,0:T(8,128)(2,1)}, bf16[1024,1024]{1,0:T(8,128)(2,1)S(1)}, u32[]{:S(2)}) copy-start(bf16[1024,1024]{1,0:T(8,128)(2,1)S(1)} %get-tuple-element.14.perm_ref) | copy-start | bytes 6291460
  5.1 0.8 copy-start.3
  7.1 1.6 %copy-start.1 = (bf16[1024,1024]{1,0:T(8,128)(2,1)S(1)}, bf16[1024,1024]{1,0:T(8,128)(2,1)}, u32[]{:S(2)}) copy-start(bf16[1024,1024]{1,0:T(8,128)(2,1)} %copy-done) | copy-start | bytes 6291460
  8.7 1.0 %copy-start.4 = (bf16[1024,256]{1,0:T(8,128)(2,1)S(1)}, bf16[1024,256]{1,0:T(8,128)(2,1)}, u32[]{:S(2)}) copy-start(bf16[1024,256]{1,0:T(8,128)(2,1)} %copy-done.3) | copy-start | bytes 1572868
  17.2 6.1 %copy-start.2 = (bf16[3,2,128,256]{3,2,1,0:T(8,128)(2,1)S(1)}, bf16[3,2,128,256]{3,2,1,0:T(8,128)(2,1)}, u32[]{:S(2)}) copy-start(bf16[3,2,128,256]{3,2,1,0:T(8,128)(2,1)} %param.4) | copy-start | bytes 1179652
  17.2 24.5 %collective-permute-start.2 = (bf16[2,1024,128]{2,1,0:T(8,128)(2,1)S(1)}, bf16[2,1024,128]{2,1,0:T(8,128)(2,1)S(1)}, u32[]{:S(2)}, u32[]{:S(2)}) collective-permute-start(bf16[2,1024,128]{2,1,0:T(8,128)(2,1)S(1)} %get-tuple-element.19), channel_id=1, source_target_pairs={{0,1},{1,0},{2,3},{3,2},{4,5},{5,4},{6,7},{7,6},{8,9},{9,8},{10,11... | collective-permute-start | bytes 1572872 | tf_op jit(solution)/shard_map/ppermute | solution.py:265
  17.8 10.7 %collective-permute-start.5 = (bf16[1024,128]{1,0:T(8,128)(2,1)S(1)}, bf16[1024,128]{1,0:T(8,128)(2,1)S(1)}, u32[]{:S(2)}, u32[]{:S(2)}) collective-permute-start(bf16[1024,128]{1,0:T(8,128)(2,1)S(1)} %get-tuple-element.20), channel_id=1, source_target_pairs={{0,2},{1,3},{2,0},{3,1},{4,6},{5,7},{6,4},{7,5},{8,10},{9,11},{10,... | collective-permute-start | bytes 786440 | tf_op jit(solution)/shard_map/ppermute | solution.py:265
  22.7 11.4 %collective-permute-start.1 = (bf16[1024,128]{1,0:T(8,128)(2,1)S(1)}, bf16[1024,128]{1,0:T(8,128)(2,1)S(1)}, u32[]{:S(2)}, u32[]{:S(2)}) collective-permute-start(bf16[1024,128]{1,0:T(8,128)(2,1)S(1)} %dft_second.1), channel_id=1, source_target_pairs={{0,2},{1,3},{2,0},{3,1},{4,6},{5,7},{6,4},{7,5},{8,10},{9,11},{10,... | collective-permute-start | bytes 786440 | tf_op jit(solution)/shard_map/ppermute | solution.py:265
  23.3 18.3 %collective-permute-start.4 = (bf16[6,128,256]{2,1,0:T(8,128)(2,1)S(1)}, bf16[6,128,256]{2,1,0:T(8,128)(2,1)S(1)}, u32[]{:S(2)}, u32[]{:S(2)}) collective-permute-start(bf16[6,128,256]{2,1,0:T(8,128)(2,1)S(1)} %bitcast.10), channel_id=1, source_target_pairs={{0,2},{1,3},{2,0},{3,1},{4,6},{5,7},{6,4},{7,5},{8,10},{9,11},{10,... | collective-permute-start | bytes 1179656 | tf_op jit(solution)/shard_map/ppermute | solution.py:265
  28.5 13.2 %collective-permute-start.6 = (bf16[1024,128]{1,0:T(8,128)(2,1)S(1)}, bf16[1024,128]{1,0:T(8,128)(2,1)S(1)}, u32[]{:S(2)}, u32[]{:S(2)}) collective-permute-start(bf16[1024,128]{1,0:T(8,128)(2,1)S(1)} %collective-permute-done.5.refs_2_), channel_id=1, source_target_pairs={{0,1},{1,0},{2,3},{3,2},{4,5},{5,4},{6,7},{7,6},{8,9},{9,8},{10,11... | collective-permute-start | bytes 786440 | tf_op jit(solution)/shard_map/ppermute | solution.py:265
  34.1 9.5 %collective-permute-start.3 = (bf16[1024,128]{1,0:T(8,128)(2,1)S(1)}, bf16[1024,128]{1,0:T(8,128)(2,1)S(1)}, u32[]{:S(2)}, u32[]{:S(2)}) collective-permute-start(bf16[1024,128]{1,0:T(8,128)(2,1)S(1)} %collective-permute-done.1.refs_2_), channel_id=1, source_target_pairs={{0,1},{1,0},{2,3},{3,2},{4,5},{5,4},{6,7},{7,6},{8,9},{9,8},{10,11... | collective-permute-start | bytes 786440 | tf_op jit(solution)/shard_map/ppermute | solution.py:265

commit v6 on v3

--- a/solution.py
+++ b/solution.py
@@ -13,7 +13,7 @@
 
 STRIDE = 8
 SAMPLES = 8192
-LIMIT = 24 * 1024 * 1024
+LIMIT = 16 * 1024 * 1024
 
 
 def root(numer, denom):
@@ -127,9 +127,10 @@
     lax.fori_loop(0, 16, step, 0, unroll=4)
 
 
-def first_kernel(other_ref, own_ref, perm_ref, t_ref, outer_ref, out_ref, xs_ref, f_ref):
+def first_kernel(ids_ref, other_ref, own_ref, perm_ref, t_ref, outer_ref, out_ref, xs_ref, f_ref):
     xs_ref[:, 0:256] = own_ref[...]
-    for s, rows in enumerate(deinterleave(other_ref[...], perm_ref[...])):
+    other = other_ref[pl.ds(pl.multiple_of(ids_ref[0] * 128, 128), 128), :]
+    for s, rows in enumerate(deinterleave(other, perm_ref[...])):
         xs_ref[s * 128 : (s + 1) * 128, 256:512] = rows
     f_ref[...] = lax.dot_general(
         t_ref[0:512, :], xs_ref[...], (((1,), (1,)), ((), ())), preferred_element_type=F32
@@ -153,16 +154,40 @@
 VM = pl.BlockSpec(memory_space=pltpu.VMEM)
 
 
-def dft_first(other, own, perm, table, outer):
+def dft_first(ids, other, own, perm, table, outer):
     return pl.pallas_call(
         first_kernel,
-        in_specs=[VM] * 5,
+        in_specs=[pl.BlockSpec(memory_space=pltpu.SMEM)] + [VM] * 5,
         out_specs=[VM, VM],
         out_shape=[jax.ShapeDtypeStruct((1024, 128), BF16), jax.ShapeDtypeStruct((1024, 512), BF16)],
         scratch_shapes=[pltpu.VMEM((512, 1024), F32)],
         compiler_params=pltpu.CompilerParams(vmem_limit_bytes=LIMIT),
         name="dft_first",
-    )(other, own, perm, table, outer)
+    )(ids, other, own, perm, table, outer)
+
+
+def last_kernel(ids_ref, xs_ref, t_ref, outer_ref, bins_ref, out_ref, group_ref, f_ref):
+    next_kernel((3,), xs_ref, t_ref, outer_ref, out_ref, f_ref)
+    half, low = ids_ref[1], ids_ref[2]
+    row = iota((512, 128), 0)
+    block = row // 128 * 16 + low * 8 + row // 16 % 8
+    place = block % 4 * 32 + half * 16 + row % 16
+    line = jnp.where(iota((512, 128), 1) == block // 4, 1.0, 0.0).astype(BF16)[:, :16]
+    lines = jnp.dot(line, bins_ref[...].astype(F32).astype(BF16), preferred_element_type=F32)
+    chosen = jnp.where(iota((512, 128), 1) == place, lines, 0.0)
+    group_ref[...] = jnp.broadcast_to(jnp.sum(chosen, axis=1, keepdims=True), (512, 128))
+
+
+def dft_last(ids, xs, table, outer, bins):
+    return pl.pallas_call(
+        last_kernel,
+        in_specs=[pl.BlockSpec(memory_space=pltpu.SMEM)] + [VM] * 4,
+        out_specs=[VM, VM],
+        out_shape=[jax.ShapeDtypeStruct((1024, 128), F32), jax.ShapeDtypeStruct((512, 128), F32)],
+        scratch_shapes=[pltpu.VMEM((1, 512, 1024), F32)],
+        compiler_params=pltpu.CompilerParams(vmem_limit_bytes=LIMIT),
+        name="dft_last",
+    )(ids, xs, table, outer, bins)
 
 
 def dft_next(xs, table, outer, slots, dtype):
@@ -176,7 +201,17 @@
     )(xs, table, outer)
 
 
-def form_kernel(ids_ref, s0_ref, s1_ref, p0_ref, p1_ref, group_ref, w0_ref, w1_ref, w2a_ref, w2b_ref, w3_ref, out_ref, l_ref, w_ref):
+def form_beams(side, l_ref, w_ref, group_ref, out_ref):
+    acc = lax.dot_general(l_ref[...], w_ref[...], (((1,), (1,)), ((), ())), preferred_element_type=F32)
+    acc = acc.reshape(2, 512, 384)
+    group = group_ref[...][None]
+    total = jnp.where(group == 0, acc[:, :, 0:128], jnp.where(group == 1, acc[:, :, 128:256], acc[:, :, 256:384]))
+    re = total[0].reshape(4, 8, 16, 128)
+    im = total[1].reshape(4, 8, 16, 128)
+    out_ref[:, :, pl.ds(side, 1)] = jnp.concatenate([re, im], 2).astype(BF16)[:, :, None]
+
+
+def near_kernel(ids_ref, s0_ref, s1_ref, p0_ref, p1_ref, group_ref, w0_ref, w1_ref, out_ref, l_ref, w_ref):
     core, half = ids_ref[0], ids_ref[1]
     for srcs, place in (((s0_ref, s1_ref), core), ((p0_ref, p1_ref), 1 - core)):
         for xl in range(2):
@@ -187,38 +222,68 @@
             l_ref[0:512, pl.ds(lane0 + 512, 128)] = -si
             l_ref[512:1024, pl.ds(lane0, 128)] = si
             l_ref[512:1024, pl.ds(lane0 + 512, 128)] = sr
-    for g in range(3):
+    for i in range(6):
+        row, col = i // 2 * 128, i % 2 * 512
+        w_ref[row : row + 128, col : col + 256] = w0_ref[i]
+        w_ref[row : row + 128, col + 256 : col + 512] = w1_ref[i]
+    form_beams(half, l_ref, w_ref, group_ref, out_ref)
+
+
+def far_kernel(ids_ref, l_ref, group_ref, w2a_ref, w2b_ref, w3_ref, begun_ref, out_ref, w_ref):
+    for i in range(6):
+        row, col = i // 2 * 128, i % 2 * 512
+        w_ref[row : row + 128, col : col + 256] = w2a_ref[i] if i < 3 else w2b_ref[i - 3]
+        w_ref[row : row + 128, col + 256 : col + 512] = w3_ref[i]
+    form_beams(1 - ids_ref[1], l_ref, w_ref, group_ref, out_ref)
+
+
+PARTS = jax.ShapeDtypeStruct((4, 8, 2, 32, 128), BF16)
+
+
+def form_near(ids, spec, group, weights):
+    return pl.pallas_call(
+        near_kernel,
+        in_specs=[pl.BlockSpec(memory_space=pltpu.SMEM)] + [VM] * 7,
+        out_specs=[VM, VM],
+        out_shape=[PARTS, jax.ShapeDtypeStruct((1024, 1024), BF16)],
+        scratch_shapes=[pltpu.VMEM((384, 1024), BF16)],
+        compiler_params=pltpu.CompilerParams(vmem_limit_bytes=LIMIT),
+        name="form_near",
+    )(ids, *spec, group, *weights)
+
+
+def form_far(ids, lhs, group, weights, begun):
+    return pl.pallas_call(
+        far_kernel,
+        in_specs=[pl.BlockSpec(memory_space=pltpu.SMEM)] + [VM] * 6,
+        out_specs=VM,
+        out_shape=PARTS,
+        input_output_aliases={6: 0},
+        scratch_shapes=[pltpu.VMEM((384, 1024), BF16)],
+        compiler_params=pltpu.CompilerParams(vmem_limit_bytes=LIMIT),
+        name="form_far",
+    )(ids, lhs, group, *weights, begun)
+
+
+def add_kernel(got_ref, out_ref):
+    for side in range(2):
+        parts = [got_ref[2 * src + side].astype(F32) for src in range(4)]
+        for src in range(4, 32):
+            parts[src % 4] = parts[src % 4] + got_ref[2 * src + side].astype(F32)
+        total = (parts[0] + parts[1]) + (parts[2] + parts[3])
         for p in range(2):
-            i = g * 2 + p
-            w2 = w2a_ref[i] if i < 3 else w2b_ref[i - 3]
-            for b, xl, w in ((0, 0, w0_ref[i]), (0, 1, w1_ref[i]), (1, 0, w2), (1, 1, w3_ref[i])):
-                row, col = g * 256 + b * 128, p * 512 + xl * 256
-                w_ref[row : row + 128, col : col + 256] = w
-    total = jnp.zeros((2, 512, 256), F32)
-    groups = group_ref[...]
-    for g in range(3):
-        acc = lax.dot_general(
-            l_ref[...], w_ref[g * 256 : g * 256 + 256, :], (((1,), (1,)), ((), ())), preferred_element_type=F32
-        )
-        total = jnp.where((groups == g)[None], acc.reshape(2, 512, 256), total)
-    for b in range(2):
-        part = total[:, :, b * 128 : b * 128 + 128]
-        re = part[0].reshape(4, 8, 16, 128)
-        im = part[1].reshape(4, 8, 16, 128)
-        both = jnp.concatenate([re, im], 2).astype(BF16)
-        out_ref[:, :, pl.ds(half if b == 0 else 1 - half, 1)] = both[:, :, None]
-
-
-def form(ids, spec, group, weights):
-    return pl.pallas_call(
-        form_kernel,
-        in_specs=[pl.BlockSpec(memory_space=pltpu.SMEM)] + [VM] * 10,
+            out_ref[side * 16 : side * 16 + 16, p, :] = total[p * 16 : p * 16 + 16]
+
+
+def add(got):
+    return pl.pallas_call(
+        add_kernel,
+        in_specs=[VM],
         out_specs=VM,
-        out_shape=jax.ShapeDtypeStruct((4, 8, 2, 32, 128), BF16),
-        scratch_shapes=[pltpu.VMEM((1024, 1024), BF16), pltpu.VMEM((768, 1024), BF16)],
-        compiler_params=pltpu.CompilerParams(vmem_limit_bytes=LIMIT),
-        name="form",
-    )(ids, *spec, group, *weights)
+        out_shape=jax.ShapeDtypeStruct((32, 2, 128), F32),
+        compiler_params=pltpu.CompilerParams(vmem_limit_bytes=LIMIT),
+        name="add",
+    )(got)
 
 
 def shards(signals, weights, bin_group):
@@ -229,32 +294,29 @@
         return lax.ppermute(value, ring, [(i, i ^ flip) for i in range(8)])
 
     ids = jnp.stack([core, half, low])
-    theirs = lax.dynamic_slice_in_dim(signals, (1 - core) * 128, 128, 0)
-    other = exchange(theirs, 1)
     blocks = weights.reshape(6, 128, 256)
     w1 = exchange(blocks, 4)
     w3 = exchange(blocks, 6)
+    other = exchange(signals, 1)
     own, perm, table, outer = prep(ids, pltpu.with_memory_space_constraint(signals, pltpu.HBM))
 
-    spec0, xs = dft_first(other, own, perm, table, outer)
+    spec0, xs = dft_first(ids, other, own, perm, table, outer)
     got0 = exchange(spec0, 2)
     spec1, spec2 = dft_next(xs, table, outer, (1, 2), BF16)
     got1 = exchange(spec1, 4)
     got2 = exchange(spec2, 6)
     w2a = exchange(w1[:3], 6)
     w2b = exchange(w3[3:], 4)
-    (spec3,) = dft_next(xs, table, outer, (3,), F32)
+    spec3, owned = dft_last(ids, xs, table, outer, bin_group.reshape(16, 128))
     same = (spec3 + got0.astype(F32)).astype(BF16)
     same_sib = exchange(same, 1)
     cross = (got1.astype(F32) + got2.astype(F32)).astype(BF16)
     cross_sib = exchange(cross, 1)
 
-    owned = lax.dynamic_index_in_dim(bin_group.reshape(4, 2, 8, 2, 16), low, 1, keepdims=False)
-    owned = lax.dynamic_index_in_dim(owned, half, 2, keepdims=False).reshape(512, 1)
-    parts = form(ids, (same, cross, same_sib, cross_sib), owned, (blocks, w1, w2a, w2b, w3))
+    begun, lhs = form_near(ids, (same, cross, same_sib, cross_sib), owned, (blocks, w1))
+    parts = form_far(ids, lhs, owned, (w2a, w2b, w3), begun)
     got = lax.all_to_all(parts.reshape(64, 32, 128), ("y", "z", "xhi"), 0, 0, tiled=True)
-    summed = jnp.sum(got.reshape(32, 2, 2, 16, 128).astype(F32), axis=0)
-    return summed.transpose(0, 2, 1, 3).reshape(32, 2, 128)
+    return add(got)
 
 
 def solution(mesh):

time: 77.4 us -> 75.6 us (0.977)
  the two profiles are of different devices: /device:TPU:2 before, /device:TPU:1 now
where the time goes in v6:
time: 75.6 us; the launch traced here: 74.1 us
  blocking collectives  28.6 us (38%)
  Pallas kernels  18.2 us (24%)
  waiting for transfers between devices  16.3 us (22%)
  starting transfers between devices  10.6 us (14%)
    all_to_all x1, blocking collectives, shards(): lax.all_to_all(parts.reshape(64, 32, 128), ('y', 'z', 'xhi'), 0, 0, tiled...  28.6 us
    ppermute x10, waiting for transfers between devices, exchange(): return lax.ppermute(value, ring, [(i, i ^ flip) for i in range(8)])  16.3 us
    ppermute x10, starting transfers between devices, exchange(): return lax.ppermute(value, ring, [(i, i ^ flip) for i in range(8)])  10.6 us
    pallas_call x1, Pallas kernels, dft_next(): pl.pallas_call(lambda *refs: next_kernel(slots, *refs), in_specs=[VM] * 3...  3.77 us
    pallas_call x1, Pallas kernels, prep(): pl.pallas_call(prep_kernel, grid_spec=pltpu.PrefetchScalarGridSpec(num_sc...  3.66 us
    pallas_call x1, Pallas kernels, dft_first(): pl.pallas_call(first_kernel, in_specs=[pl.BlockSpec(memory_space=pltpu.SM...  2.98 us
    pallas_call x1, Pallas kernels, dft_last(): pl.pallas_call(last_kernel, in_specs=[pl.BlockSpec(memory_space=pltpu.SME...  2.85 us
    pallas_call x1, Pallas kernels, form_near(): pl.pallas_call(near_kernel, in_specs=[pl.BlockSpec(memory_space=pltpu.SME...  2.4 us
  transfers between devices with their start and end apart: 10, of which 6 were waited for; matrix products, arithmetic and copies ran while one was open for 0% of the time, Pallas kernels for 12%

profile of v6, /device:TPU:1, one launch (start us, length us, event | category | flops | bytes accessed | tf_op | source)
XLA Modules:
  0.0 74.1 jit_solution(12478719204115917277)
XLA Ops:
  0.0 3.2 %collective-permute-start = (bf16[256,2048]{1,0:T(8,128)(2,1)}, bf16[256,2048]{1,0:T(8,128)(2,1)S(1)}, u32[]{:S(2)}, u32[]{:S(2)}) collective-permute-start(bf16[256,2048]{1,0:T(8,128)(2,1)} %own_ref.1), channel_id=1, source_target_pairs={{0,1},{1,0},{2,3},{3,2},{32,33},{33,32},{34,35},{35,34},{4,5},{5,4... | collective-permute-start | bytes 3145736 | tf_op jit(solution)/shard_map/ppermute | solution.py:294
  3.2 0.1 pad_add_fusion.ids_ref
  3.3 3.7 %prep.1 = (bf16[1024,256]{1,0:T(8,128)(2,1)S(1)}, bf16[1024,1024]{1,0:T(8,128)(2,1)S(1)}, bf16[2048,512]{1,0:T(8,128)(2,1)S(1)}, f32[4,256,128]{2,1,0:T(8,128)S(1)}) custom-call(s32[3]{0:T(128)S(1)} %pad_add_fusion.ids_ref, bf16[256,2048]{1,0:T(8,128)(2,1)} %own_ref.1), custom_call_target="tpu_custom_call" | custom-call | tf_op jit(solution)/shard_map/prep/pallas_call | solution.py:78
  6.9 0.0 collective-permute-done.other_ref
  7.0 3.0 %dft_first.1 = (bf16[1024,128]{1,0:T(8,128)(2,1)S(1)}, bf16[1024,512]{1,0:T(8,128)(2,1)S(1)}) custom-call(s32[3]{0:T(128)S(1)} %pad_add_fusion.ids_ref, bf16[256,2048]{1,0:T(8,128)(2,1)S(1)} %collective-permute-done.other_ref, bf16[1024,256]{1,0:T(8,128)(2,1)S(1)} %get-tuple-element.17.own_ref, bf16[1024,1024]{1,0:T(8,128)(2,1)S(1)} %get-tuple-element.18.perm_ref, ...), custom_call_target="tpu_custom_call" | custom-call | tf_op jit(solution)/shard_map/dft_first/pallas_call | solution.py:158
  9.9 0.0 copy-start
  10.0 0.0 copy-start.1
  10.0 3.8 %shard_map.37 = (bf16[1024,128]{1,0:T(8,128)(2,1)S(1)}, bf16[1024,128]{1,0:T(8,128)(2,1)S(1)}) custom-call(bf16[1024,512]{1,0:T(8,128)(2,1)S(1)} %get-tuple-element.21.xs_ref.refs_0_, bf16[2048,512]{1,0:T(8,128)(2,1)S(1)} %get-tuple-element.19.t_ref.refs_1_, f32[4,256,128]{2,1,0:T(8,128)S(1)} %get-tuple-element.20.outer_ref.refs_2_), custom_call_target="tpu_custom_call" | custom-call | tf_op jit(solution)/shard_map/pallas_call | solution.py:194
  13.7 0.1 collective-permute-start.2
  13.8 1.3 %collective-permute-start.3 = (bf16[1024,128]{1,0:T(8,128)(2,1)S(1)}, bf16[1024,128]{1,0:T(8,128)(2,1)S(1)}, u32[]{:S(2)}, u32[]{:S(2)}) collective-permute-start(bf16[1024,128]{1,0:T(8,128)(2,1)S(1)} %get-tuple-element.25), channel_id=1, source_target_pairs={{0,34},{1,35},{2,32},{3,33},{32,2},{33,3},{34,0},{35,1},{4,38},{5,... | collective-permute-start | bytes 786440 | tf_op jit(solution)/shard_map/ppermute | solution.py:294
  15.1 1.9 %collective-permute-start.1 = (bf16[1024,128]{1,0:T(8,128)(2,1)S(1)}, bf16[1024,128]{1,0:T(8,128)(2,1)S(1)}, u32[]{:S(2)}, u32[]{:S(2)}) collective-permute-start(bf16[1024,128]{1,0:T(8,128)(2,1)S(1)} %get-tuple-element.23), channel_id=1, source_target_pairs={{0,2},{1,3},{2,0},{3,1},{32,34},{33,35},{34,32},{35,33},{4,6},{5,7... | collective-permute-start | bytes 786440 | tf_op jit(solution)/shard_map/ppermute | solution.py:294
  17.1 0.1 collective-permute-start.6
  17.2 1.2 %collective-permute-start.8 = (bf16[6,128,256]{2,1,0:T(8,128)(2,1)S(1)}, bf16[6,128,256]{2,1,0:T(8,128)(2,1)S(1)}, u32[]{:S(2)}, u32[]{:S(2)}) collective-permute-start(bf16[6,128,256]{2,1,0:T(8,128)(2,1)S(1)} %bitcast.8), channel_id=1, source_target_pairs={{0,34},{1,35},{2,32},{3,33},{32,2},{33,3},{34,0},{35,1},{4,38},{5,... | collective-permute-start | bytes 1179656 | tf_op jit(solution)/shard_map/ppermute | solution.py:294
  18.4 2.9 %dft_last.1 = (f32[1024,128]{1,0:T(8,128)S(1)}, f32[512,128]{1,0:T(8,128)S(1)}) custom-call(s32[3]{0:T(128)S(1)} %pad_add_fusion.ids_ref, bf16[1024,512]{1,0:T(8,128)(2,1)S(1)} %get-tuple-element.21.xs_ref.refs_0_, bf16[2048,512]{1,0:T(8,128)(2,1)S(1)} %get-tuple-element.19.t_ref.refs_1_, f32[4,256,128]{2,1,0:T(8,128)S(1)} %get-tuple-element.20.outer_ref.refs_2_, ...), custom_call_target="tpu_custom_call" | custom-call | tf_op jit(solution)/shard_map/dft_last/pallas_call | solution.py:182
  21.3 0.4 collective-permute-done.2
  21.7 6.8 %collective-permute-done.3 = bf16[1024,128]{1,0:T(8,128)(2,1)S(1)} collective-permute-done((bf16[1024,128]{1,0:T(8,128)(2,1)S(1)}, bf16[1024,128]{1,0:T(8,128)(2,1)S(1)}, u32[]{:S(2)}, u32[]{:S(2)}) %collective-permute-start.3) | collective-permute-done | bytes 262176 | tf_op jit(solution)/shard_map/ppermute | solution.py:294
  28.5 0.1 add_convert_fusion.s1_ref
  28.6 1.5 %collective-permute-start.5 = (bf16[1024,128]{1,0:T(8,128)(2,1)S(1)}, bf16[1024,128]{1,0:T(8,128)(2,1)S(1)}, u32[]{:S(2)}, u32[]{:S(2)}) collective-permute-start(bf16[1024,128]{1,0:T(8,128)(2,1)S(1)} %add_convert_fusion.s1_ref), channel_id=1, source_target_pairs={{0,1},{1,0},{2,3},{3,2},{32,33},{33,32},{34,35},{35,34},{4,5},{5,4... | collective-permute-start | bytes 786440 | tf_op jit(solution)/shard_map/ppermute | solution.py:294
  30.1 0.0 collective-permute-done.1
  30.1 0.1 add_convert_fusion.1.s0_ref
  30.2 0.1 collective-permute-start.4
  30.3 5.5 %collective-permute-done.6.w1_ref = bf16[6,128,256]{2,1,0:T(8,128)(2,1)S(1)} collective-permute-done((bf16[6,128,256]{2,1,0:T(8,128)(2,1)S(1)}, bf16[6,128,256]{2,1,0:T(8,128)(2,1)S(1)}, u32[]{:S(2)}, u32[]{:S(2)}) %collective-permute-start.6) | collective-permute-done | bytes 393248 | tf_op jit(solution)/shard_map/ppermute | solution.py:294
  35.8 0.9 %collective-permute-start.7 = (bf16[3,128,256]{2,1,0:T(8,128)(2,1)S(1)}, bf16[3,128,256]{2,1,0:T(8,128)(2,1)S(1)}, u32[]{:S(2)}, u32[]{:S(2)}) collective-permute-start(bf16[3,128,256]{2,1,0:T(8,128)(2,1)S(1)} %slice.8), channel_id=1, source_target_pairs={{0,34},{1,35},{2,32},{3,33},{32,2},{33,3},{34,0},{35,1},{4,38},{5,... | collective-permute-start | bytes 589832 | tf_op jit(solution)/shard_map/ppermute | solution.py:294
  36.7 0.4 collective-permute-done.8.w3_ref
  37.1 0.3 collective-permute-start.9
  37.4 0.0 collective-permute-done.5.p1_ref
  37.4 2.4 %form_near.1 = (bf16[4,8,2,32,128]{4,3,2,1,0:T(8,128)(2,1)S(1)}, bf16[1024,1024]{1,0:T(8,128)(2,1)S(1)}) custom-call(s32[3]{0:T(128)S(1)} %pad_add_fusion.ids_ref, bf16[1024,128]{1,0:T(8,128)(2,1)S(1)} %add_convert_fusion.1.s0_ref, bf16[1024,128]{1,0:T(8,128)(2,1)S(1)} %add_convert_fusion.s1_ref, bf16[1024,128]{1,0:T(8,128)(2,1)S(1)} %collective-permute-done.4.p0_ref, ...), custom_call_target="tpu_custom_call" | custom-call | tf_op jit(solution)/shard_map/form_near/pallas_call | solution.py:244
  39.8 2.9 %collective-permute-done.7.w2a_ref = bf16[3,128,256]{2,1,0:T(8,128)(2,1)S(1)} collective-permute-done((bf16[3,128,256]{2,1,0:T(8,128)(2,1)S(1)}, bf16[3,128,256]{2,1,0:T(8,128)(2,1)S(1)}, u32[]{:S(2)}, u32[]{:S(2)}) %collective-permute-start.7) | collective-permute-done | bytes 196640 | tf_op jit(solution)/shard_map/ppermute | solution.py:294
  42.7 0.2 collective-permute-done.9.w2b_ref
  43.0 1.8 %form_far.1 = bf16[4,8,2,32,128]{4,3,2,1,0:T(8,128)(2,1)S(1)} custom-call(s32[3]{0:T(128)S(1)} %pad_add_fusion.ids_ref, bf16[1024,1024]{1,0:T(8,128)(2,1)S(1)} %get-tuple-element.27.l_ref, f32[512,128]{1,0:T(8,128)S(1)} %get-tuple-element.26.group_ref, bf16[3,128,256]{2,1,0:T(8,128)(2,1)S(1)} %collective-permute-done.7.w2a_ref, ...), custom_call_target="tpu_custom_call", output_to_operand_aliasing={{}: (6, {})} | custom-call | tf_op jit(solution)/shard_map/form_far/pallas_call | solution.py:256
  44.8 28.6 %all_to_all.5.got_ref = bf16[64,32,128]{2,1,0:T(8,128)(2,1)S(1)} all-to-all(bf16[64,32,128]{2,1,0:T(8,128)(2,1)S(1)} %bitcast.6), channel_id=1, replica_groups=mesh['y'=4,'xlo'=2,'z'=8,'xhi'=2,'core'=2] {'y','z','xhi'}, dimensions={0} | all-to-all | bytes 1048576 | tf_op jit(solution)/shard_map/all_to_all | solution.py:318
  73.4 0.7 add.15
  (5 shorter events, 0.0 us)
Async XLA Ops:
  0.0 6.9 %collective-permute-start = (bf16[256,2048]{1,0:T(8,128)(2,1)}, bf16[256,2048]{1,0:T(8,128)(2,1)S(1)}, u32[]{:S(2)}, u32[]{:S(2)}) collective-permute-start(bf16[256,2048]{1,0:T(8,128)(2,1)} %own_ref.1), channel_id=1, source_target_pairs={{0,1},{1,0},{2,3},{3,2},{32,33},{33,32},{34,35},{35,34},{4,5},{5,4... | collective-permute-start | bytes 3145736 | tf_op jit(solution)/shard_map/ppermute | solution.py:294
  9.9 7.1 %copy-start = (bf16[3,2,128,256]{3,2,1,0:T(8,128)(2,1)S(1)}, bf16[3,2,128,256]{3,2,1,0:T(8,128)(2,1)}, u32[]{:S(2)}) copy-start(bf16[3,2,128,256]{3,2,1,0:T(8,128)(2,1)} %param.4) | copy-start | bytes 1179652
  10.0 8.5 %copy-start.1 = (s32[2048]{0:T(1024)S(1)}, s32[2048]{0:T(1024)}, u32[]{:S(2)}) copy-start(s32[2048]{0:T(1024)} %param.5) | copy-start | bytes 24580
  13.7 8.0 %collective-permute-start.2 = (bf16[1024,128]{1,0:T(8,128)(2,1)S(1)}, bf16[1024,128]{1,0:T(8,128)(2,1)S(1)}, u32[]{:S(2)}, u32[]{:S(2)}) collective-permute-start(bf16[1024,128]{1,0:T(8,128)(2,1)S(1)} %get-tuple-element.24), channel_id=1, source_target_pairs={{0,32},{1,33},{2,34},{3,35},{32,0},{33,1},{34,2},{35,3},{4,36},{5,... | collective-permute-start | bytes 786440 | tf_op jit(solution)/shard_map/ppermute | solution.py:294
  13.8 14.6 %collective-permute-start.3 = (bf16[1024,128]{1,0:T(8,128)(2,1)S(1)}, bf16[1024,128]{1,0:T(8,128)(2,1)S(1)}, u32[]{:S(2)}, u32[]{:S(2)}) collective-permute-start(bf16[1024,128]{1,0:T(8,128)(2,1)S(1)} %get-tuple-element.25), channel_id=1, source_target_pairs={{0,34},{1,35},{2,32},{3,33},{32,2},{33,3},{34,0},{35,1},{4,38},{5,... | collective-permute-start | bytes 786440 | tf_op jit(solution)/shard_map/ppermute | solution.py:294
  15.1 15.0 %collective-permute-start.1 = (bf16[1024,128]{1,0:T(8,128)(2,1)S(1)}, bf16[1024,128]{1,0:T(8,128)(2,1)S(1)}, u32[]{:S(2)}, u32[]{:S(2)}) collective-permute-start(bf16[1024,128]{1,0:T(8,128)(2,1)S(1)} %get-tuple-element.23), channel_id=1, source_target_pairs={{0,2},{1,3},{2,0},{3,1},{32,34},{33,35},{34,32},{35,33},{4,6},{5,7... | collective-permute-start | bytes 786440 | tf_op jit(solution)/shard_map/ppermute | solution.py:294
  17.1 18.7 %collective-permute-start.6 = (bf16[6,128,256]{2,1,0:T(8,128)(2,1)S(1)}, bf16[6,128,256]{2,1,0:T(8,128)(2,1)S(1)}, u32[]{:S(2)}, u32[]{:S(2)}) collective-permute-start(bf16[6,128,256]{2,1,0:T(8,128)(2,1)S(1)} %bitcast.7), channel_id=1, source_target_pairs={{0,32},{1,33},{2,34},{3,35},{32,0},{33,1},{34,2},{35,3},{4,36},{5,... | collective-permute-start | bytes 1179656 | tf_op jit(solution)/shard_map/ppermute | solution.py:294
  17.2 19.9 %collective-permute-start.8 = (bf16[6,128,256]{2,1,0:T(8,128)(2,1)S(1)}, bf16[6,128,256]{2,1,0:T(8,128)(2,1)S(1)}, u32[]{:S(2)}, u32[]{:S(2)}) collective-permute-start(bf16[6,128,256]{2,1,0:T(8,128)(2,1)S(1)} %bitcast.8), channel_id=1, source_target_pairs={{0,34},{1,35},{2,32},{3,33},{32,2},{33,3},{34,0},{35,1},{4,38},{5,... | collective-permute-start | bytes 1179656 | tf_op jit(solution)/shard_map/ppermute | solution.py:294
  28.6 8.8 %collective-permute-start.5 = (bf16[1024,128]{1,0:T(8,128)(2,1)S(1)}, bf16[1024,128]{1,0:T(8,128)(2,1)S(1)}, u32[]{:S(2)}, u32[]{:S(2)}) collective-permute-start(bf16[1024,128]{1,0:T(8,128)(2,1)S(1)} %add_convert_fusion.s1_ref), channel_id=1, source_target_pairs={{0,1},{1,0},{2,3},{3,2},{32,33},{33,32},{34,35},{35,34},{4,5},{5,4... | collective-permute-start | bytes 786440 | tf_op jit(solution)/shard_map/ppermute | solution.py:294
  30.2 7.2 %collective-permute-start.4 = (bf16[1024,128]{1,0:T(8,128)(2,1)S(1)}, bf16[1024,128]{1,0:T(8,128)(2,1)S(1)}, u32[]{:S(2)}, u32[]{:S(2)}) collective-permute-start(bf16[1024,128]{1,0:T(8,128)(2,1)S(1)} %add_convert_fusion.1.s0_ref), channel_id=1, source_target_pairs={{0,1},{1,0},{2,3},{3,2},{32,33},{33,32},{34,35},{35,34},{4,5},{5,4... | collective-permute-start | bytes 786440 | tf_op jit(solution)/shard_map/ppermute | solution.py:294
  35.8 6.9 %collective-permute-start.7 = (bf16[3,128,256]{2,1,0:T(8,128)(2,1)S(1)}, bf16[3,128,256]{2,1,0:T(8,128)(2,1)S(1)}, u32[]{:S(2)}, u32[]{:S(2)}) collective-permute-start(bf16[3,128,256]{2,1,0:T(8,128)(2,1)S(1)} %slice.8), channel_id=1, source_target_pairs={{0,34},{1,35},{2,32},{3,33},{32,2},{33,3},{34,0},{35,1},{4,38},{5,... | collective-permute-start | bytes 589832 | tf_op jit(solution)/shard_map/ppermute | solution.py:294
  37.1 5.9 %collective-permute-start.9 = (bf16[3,128,256]{2,1,0:T(8,128)(2,1)S(1)}, bf16[3,128,256]{2,1,0:T(8,128)(2,1)S(1)}, u32[]{:S(2)}, u32[]{:S(2)}) collective-permute-start(bf16[3,128,256]{2,1,0:T(8,128)(2,1)S(1)} %slice.9), channel_id=1, source_target_pairs={{0,32},{1,33},{2,34},{3,35},{32,0},{33,1},{34,2},{35,3},{4,36},{5,... | collective-permute-start | bytes 589832 | tf_op jit(solution)/shard_map/ppermute | solution.py:294

commit v7 on v3

v7 whole, which is shorter than its diff:
```python
import math

import jax
import jax.numpy as jnp
from jax import lax
from jax.experimental import pallas as pl
from jax.experimental.pallas import tpu as pltpu
from jax.sharding import Mesh, PartitionSpec as P

F32 = jnp.float32
BF16 = jnp.bfloat16
I32 = jnp.int32

STRIDE = 8
SAMPLES = 8192
LIMIT = 16 * 1024 * 1024
UNROLL = 16


def root(numer, denom):
    angle = 2.0 * math.pi / denom * (numer & (denom - 1)).astype(F32)
    return jnp.cos(angle), -jnp.sin(angle)


def iota(shape, dim):
    return lax.broadcasted_iota(I32, shape, dim)


def deinterleave(x, perm):
    out = []
    rows = jnp.concatenate([x[:, :1024], x[:, 1024:]], 0)
    split = jnp.dot(rows, perm, preferred_element_type=F32).astype(BF16)
    for s in range(STRIDE):
        cols = split[:, s * 128 : (s + 1) * 128]
        out.append(jnp.concatenate([cols[:128], cols[128:]], 1))
    return out


def eighth(q):
    q = q & 7
    half = math.sqrt(0.5)
    odd = (q & 1) != 0
    re = jnp.where(odd, half, jnp.where((q & 2) != 0, 0.0, 1.0))
    re = jnp.where((q > 2) & (q < 6), -re, re)
    im = jnp.where(odd, half, jnp.where((q & 2) != 0, 1.0, 0.0))
    im = jnp.where(q < 4, -im, im)
    return re, im


def owner(ids_ref, slot):
    half, low = ids_ref[1], ids_ref[2]
    return (1 - half if slot in (0, 2) else half), (1 - low if slot in (1, 2) else low)


def block_of(t, low):
    return t // 8 * 16 + low * 8 + t % 8


def make_twiddles(ids_ref, slot, coarse_ref, fine_ref, t_ref, row0):
    half, low = owner(ids_ref, slot)
    first = pl.multiple_of(half * 16, 16)
    fr = fine_ref[0, pl.ds(first, 16), :]
    fi = fine_ref[1, pl.ds(first, 16), :]
    for t in range(16):
        k = block_of(t, low)
        cr = jnp.concatenate([coarse_ref[0, pl.ds(k, 1), :]] * 4, 1)
        ci = jnp.concatenate([coarse_ref[1, pl.ds(k, 1), :]] * 4, 1)
        row = row0 + t * 16
        t_ref[row : row + 16, :] = (cr * fr - ci * fi).astype(BF16)
        t_ref[row + 256 : row + 272, :] = (cr * fi + ci * fr).astype(BF16)


def prep_kernel(ids_ref, own_ref, xs_ref, perm_ref, t_ref, coarse_ref, fine_ref, outer_ref):
    core, half = ids_ref[0], ids_ref[1]
    row, lane = iota((32, 128), 0), iota((32, 128), 1)
    coarse_ref[0], coarse_ref[1] = root(row * lane, 32)
    br, bi = root((row + 1) * lane, 1024)
    for part in range(4):
        u = 2 * core + part if part < 2 else 2 * (1 - core) + part - 2
        er, ei = eighth((row + 1) * u)
        cols = slice(part * 128, part * 128 + 128)
        fine_ref[0, :, cols] = br * er - bi * ei
        fine_ref[1, :, cols] = br * ei + bi * er
    outer_ref[0], outer_ref[1] = root(row * 32, SAMPLES)
    outer_ref[2], outer_ref[3] = root(row + 1, SAMPLES)
    scale = 1.0 / math.sqrt(SAMPLES)
    outer_ref[4] = jnp.where((((row + 1) * half) & 1) != 0, -scale, scale)
    make_twiddles(ids_ref, 0, coarse_ref, fine_ref, t_ref, 0)
    same = jnp.where(iota((1024, 128), 0) // STRIDE == iota((1024, 128), 1), 1.0, 0.0).astype(BF16)
    phase = iota((16, 128), 0) & (STRIDE - 1)
    for s in range(STRIDE):
        keep = jnp.where(phase == s, 1.0, 0.0).astype(BF16)
        perm_ref[:, s * 128 : (s + 1) * 128] = (same.reshape(64, 16, 128) * keep[None]).reshape(1024, 128)
    for s, rows in enumerate(deinterleave(own_ref[...], perm_ref[...])):
        xs_ref[s * 128 : (s + 1) * 128, :] = rows


def prep(ids, signals):
    full = lambda *shape: pl.BlockSpec(shape, lambda i, ids: (0,) * len(shape))
    return pl.pallas_call(
        prep_kernel,
        grid_spec=pltpu.PrefetchScalarGridSpec(
            num_scalar_prefetch=1,
            grid=(1,),
            in_specs=[pl.BlockSpec((128, 2048), lambda i, ids: (ids[0], 0))],
            out_specs=[
                full(1024, 256),
                full(1024, 1024),
                full(512, 512),
                full(2, 32, 128),
                full(2, 32, 512),
                full(5, 32, 128),
            ],
        ),
        out_shape=[
            jax.ShapeDtypeStruct((1024, 256), BF16),
            jax.ShapeDtypeStruct((1024, 1024), BF16),
            jax.ShapeDtypeStruct((512, 512), BF16),
            jax.ShapeDtypeStruct((2, 32, 128), F32),
            jax.ShapeDtypeStruct((2, 32, 512), F32),
            jax.ShapeDtypeStruct((5, 32, 128), F32),
        ],
        compiler_params=pltpu.CompilerParams(vmem_limit_bytes=LIMIT),
        name="prep",
    )(ids, signals)


def times(w, x):
    return w[0] * x[0] - w[1] * x[1], w[0] * x[1] + w[1] * x[0]


def plus(x, y):
    return x[0] + y[0], x[1] + y[1]


def minus(x, y):
    return x[0] - y[0], x[1] - y[1]


def turned(x, y):
    return x[0] + y[1], x[1] - y[0]


def combine(ids_ref, slot, f_ref, outer_ref, out_ref, add_ref=None):
    half, low = owner(ids_ref, slot)
    first = pl.multiple_of(half * 16, 16)
    fine = outer_ref[2, pl.ds(first, 16), :], outer_ref[3, pl.ds(first, 16), :]
    scale = outer_ref[4, pl.ds(first, 16), :]
    eighth_root = math.sqrt(0.5)

    def step(t, carry):
        row0 = pl.multiple_of(t * 16, 16)
        k = block_of(t, low)
        w = times((outer_ref[0, pl.ds(k, 1), :], outer_ref[1, pl.ds(k, 1), :]), fine)
        w2 = times(w, w)
        w4 = times(w2, w2)
        wt = eighth_root * (w[0] + w[1]), eighth_root * (w[1] - w[0])
        term = lambda s: (
            f_ref[pl.ds(row0, 16), s * 128 : (s + 1) * 128],
            f_ref[pl.ds(row0 + 256, 16), s * 128 : (s + 1) * 128],
        )
        sums = []
        for s in range(2):
            near, far = term(s), times(w4, term(s + 4))
            up, down = plus(near, far), minus(near, far)
            near, far = term(s + 2), times(w4, term(s + 6))
            sums.append(
                (plus(up, times(w2, plus(near, far))), turned(down, times(w2, minus(near, far))))
            )
        low_bin = plus(sums[0][0], times(w, sums[1][0]))
        high_bin = plus(sums[0][1], times(wt, sums[1][1]))
        for place, value in enumerate((low_bin[0], high_bin[0], low_bin[1], high_bin[1])):
            rows = pl.ds(row0 + 256 * place, 16)
            value = value * scale
            if add_ref is not None:
                value = value + add_ref[rows, :].astype(F32)
            out_ref[rows, :] = value.astype(out_ref.dtype)
        return carry

    lax.fori_loop(0, 16, step, 0, unroll=UNROLL)


def spectrum(t_ref, row0, xs_ref, f_ref):
    f_ref[...] = lax.dot_general(
        t_ref[row0 : row0 + 512, :], xs_ref[...], (((1,), (1,)), ((), ())), preferred_element_type=F32
    )


def first_kernel(
    ids_ref, other_ref, own_ref, perm_ref, t_ref, coarse_ref, fine_ref, outer_ref, out_ref, xs_ref, rest_ref, f_ref
):
    xs_ref[:, 0:256] = own_ref[...]
    other = other_ref[pl.ds(pl.multiple_of(ids_ref[0] * 128, 128), 128), :]
    for s, rows in enumerate(deinterleave(other, perm_ref[...])):
        xs_ref[s * 128 : (s + 1) * 128, 256:512] = rows
    for slot in (1, 2, 3):
        make_twiddles(ids_ref, slot, coarse_ref, fine_ref, rest_ref, (slot - 1) * 512)
    spectrum(t_ref, 0, xs_ref, f_ref)
    combine(ids_ref, 0, f_ref, outer_ref, out_ref)


def next_kernel(ids_ref, xs_ref, rest_ref, outer_ref, out1_ref, out2_ref, f_ref):
    for index, out_ref in enumerate((out1_ref, out2_ref)):
        spectrum(rest_ref, index * 512, xs_ref, f_ref.at[index])
        combine(ids_ref, 1 + index, f_ref.at[index], outer_ref, out_ref)


def last_kernel(ids_ref, xs_ref, rest_ref, outer_ref, got_ref, bins_ref, out_ref, group_ref, f_ref):
    spectrum(rest_ref, 1024, xs_ref, f_ref)
    half, low = ids_ref[1], ids_ref[2]
    row, lane = iota((512, 128), 0), iota((512, 128), 1)
    line = jnp.where(lane == (row // 128 * 4 + low * 2 + row // 64 % 2), 1.0, 0.0).astype(BF16)[:, :16]
    lines = jnp.dot(line, bins_ref[...].astype(F32).astype(BF16), preferred_element_type=F32)
    place = row // 16 % 4 * 32 + half * 16 + row % 16
    chosen = jnp.where(lane == place, lines, 0.0).astype(BF16)
    group_ref[...] = jnp.dot(chosen, jnp.ones((128, 128), BF16), preferred_element_type=F32)
    combine(ids_ref, 3, f_ref, outer_ref, out_ref, got_ref)


VM = pl.BlockSpec(memory_space=pltpu.VMEM)


SM = pl.BlockSpec(memory_space=pltpu.SMEM)
PIECE = jax.ShapeDtypeStruct((1024, 128), BF16)


def call(kernel, count, out_shape, scratch):
    outs = len(out_shape) if isinstance(out_shape, list) else 0
    return pl.pallas_call(
        kernel,
        in_specs=[SM] + [VM] * count,
        out_specs=[VM] * outs if outs else VM,
        out_shape=out_shape,
        scratch_shapes=scratch,
        compiler_params=pltpu.CompilerParams(vmem_limit_bytes=LIMIT),
    )


def dft_first(*args):
    outs = [PIECE, jax.ShapeDtypeStruct((1024, 512), BF16), jax.ShapeDtypeStruct((1536, 512), BF16)]
    return call(first_kernel, 7, outs, [pltpu.VMEM((512, 1024), F32)])(*args)


def dft_next(*args):
    return call(next_kernel, 3, [PIECE, PIECE], [pltpu.VMEM((2, 512, 1024), F32)])(*args)


def dft_last(*args):
    outs = [PIECE, jax.ShapeDtypeStruct((512, 128), F32)]
    return call(last_kernel, 5, outs, [pltpu.VMEM((512, 1024), F32)])(*args)


def form_kernel(
    ids_ref, s0_ref, s1_ref, p0_ref, p1_ref, group_ref, w0_ref, w1_ref, w2a_ref, w2b_ref, w3_ref, out_ref, l_ref, w_ref
):
    core, half = ids_ref[0], ids_ref[1]
    for srcs, place in (((s0_ref, s1_ref), core), ((p0_ref, p1_ref), 1 - core)):
        for xl in range(2):
            lane0 = pl.multiple_of(xl * 256 + place * 128, 128)
            for r in range(0, 512, 64):
                sr, si = srcs[xl][r : r + 64, :], srcs[xl][512 + r : 576 + r, :]
                l_ref[r : r + 64, pl.ds(lane0, 128)] = sr
                l_ref[r : r + 64, pl.ds(lane0 + 512, 128)] = -si
                l_ref[512 + r : 576 + r, pl.ds(lane0, 128)] = si
                l_ref[512 + r : 576 + r, pl.ds(lane0 + 512, 128)] = sr
    for g in range(3):
        for p in range(2):
            i = g * 2 + p
            w2 = w2a_ref[i] if i < 3 else w2b_ref[i - 3]
            for b, xl, w in ((0, 0, w0_ref[i]), (0, 1, w1_ref[i]), (1, 0, w2), (1, 1, w3_ref[i])):
                row, col = g * 256 + b * 128, p * 512 + xl * 256
                w_ref[row : row + 128, col : col + 256] = w
    total = jnp.zeros((2, 512, 256), F32)
    group = group_ref[...]
    group = jnp.concatenate([group, group], 1)[None]
    for g in range(3):
        acc = lax.dot_general(
            l_ref[...], w_ref[g * 256 : g * 256 + 256, :], (((1,), (1,)), ((), ())), preferred_element_type=F32
        )
        total = jnp.where(group == g, acc.reshape(2, 512, 256), total)
    for b in range(2):
        part = total[:, :, b * 128 : b * 128 + 128]
        re = part[0].reshape(4, 8, 16, 128)
        im = part[1].reshape(4, 8, 16, 128)
        both = jnp.concatenate([re, im], 2).astype(BF16)
        out_ref[:, :, pl.ds(half if b == 0 else 1 - half, 1)] = both[:, :, None]


def form(*args):
    scratch = [pltpu.VMEM((1024, 1024), BF16), pltpu.VMEM((768, 1024), BF16)]
    return call(form_kernel, 10, jax.ShapeDtypeStruct((4, 8, 2, 32, 128), BF16), scratch)(*args)


def add_kernel(got_ref, out_ref):
    for side in range(2):
        parts = [got_ref[2 * src + side].astype(F32) for src in range(4)]
        for src in range(4, 32):
            parts[src % 4] = parts[src % 4] + got_ref[2 * src + side].astype(F32)
        total = (parts[0] + parts[1]) + (parts[2] + parts[3])
        for p in range(2):
            out_ref[side * 16 : side * 16 + 16, p, :] = total[p * 16 : p * 16 + 16]


def add(got):
    return pl.pallas_call(
        add_kernel,
        in_specs=[VM],
        out_specs=VM,
        out_shape=jax.ShapeDtypeStruct((32, 2, 128), F32),
        compiler_params=pltpu.CompilerParams(vmem_limit_bytes=LIMIT),
        name="add",
    )(got)


def shards(signals, weights, bin_group):
    half, core, low = lax.axis_index("xhi"), lax.axis_index("core"), lax.axis_index("xlo")
    ring = ("xlo", "xhi", "core")

    def exchange(value, flip):
        return lax.ppermute(value, ring, [(i, i ^ flip) for i in range(8)])

    ids = jnp.stack([core, half, low])
    blocks = weights.reshape(6, 128, 256)
    w1 = exchange(blocks, 4)
    w3 = exchange(blocks, 6)
    other = exchange(signals, 1)
    own, perm, table, coarse, fine, outer = prep(ids, pltpu.with_memory_space_constraint(signals, pltpu.HBM))

    spec0, xs, rest = dft_first(ids, other, own, perm, table, coarse, fine, outer)
    got0 = exchange(spec0, 2)
    spec1, spec2 = dft_next(ids, xs, rest, outer)
    got1 = exchange(spec1, 4)
    got2 = exchange(spec2, 6)
    w2a = exchange(w1[:3], 6)
    w2b = exchange(w3[3:], 4)
    same, group = dft_last(ids, xs, rest, outer, got0, bin_group.reshape(16, 128))
    same_sib = exchange(same, 1)
    cross = (got1.astype(F32) + got2.astype(F32)).astype(BF16)
    cross_sib = exchange(cross, 1)
    parts = form(ids, same, cross, same_sib, cross_sib, group, blocks, w1, w2a, w2b, w3)
    got = lax.all_to_all(parts.reshape(64, 32, 128), ("y", "z", "xhi"), 0, 0, tiled=True)
    return add(got)


def solution(mesh):
    fine = Mesh(mesh.devices.reshape(4, 2, 8, 2, 2), ("y", "xlo", "z", "xhi", "core"))
    chan, beam = ("y", "xlo", "z"), ("xhi", "core")
    in_specs = (P(chan, beam), P(None, None, beam, chan), P())
    out_specs = P(chan, None, beam)
    return jax.shard_map(shards, mesh=fine, in_specs=in_specs, out_specs=out_specs, check_vma=False)
```

time: 77.4 us -> 78.9 us (1.019)
  the two profiles are of different devices: /device:TPU:2 before, /device:TPU:1 now
where the time goes in v7:
time: 78.9 us; the launch traced here: 77.9 us
  blocking collectives  29.2 us (37%)
  waiting for transfers between devices  22.5 us (29%)
  Pallas kernels  13.3 us (17%)
  starting transfers between devices  12.5 us (16%)
    all_to_all x1, blocking collectives, shards(): lax.all_to_all(parts.reshape(64, 32, 128), ('y', 'z', 'xhi'), 0, 0, tiled...  29.2 us
    ppermute x10, waiting for transfers between devices, exchange(): return lax.ppermute(value, ring, [(i, i ^ flip) for i in range(8)])  22.5 us
    ppermute x10, starting transfers between devices, exchange(): return lax.ppermute(value, ring, [(i, i ^ flip) for i in range(8)])  12.5 us
    pallas_call x1, Pallas kernels, prep(): pl.pallas_call(prep_kernel, grid_spec=pltpu.PrefetchScalarGridSpec(num_sc...  2.89 us
    pallas_call x1, Pallas kernels, form(): call(form_kernel, 10, jax.ShapeDtypeStruct((4, 8, 2, 32, 128), BF16), scr...  2.72 us
    pallas_call x1, Pallas kernels, dft_first(): return call(first_kernel, 7, outs, [pltpu.VMEM((512, 1024), F32)])(*args)  2.53 us
    pallas_call x1, Pallas kernels, dft_next(): call(next_kernel, 3, [PIECE, PIECE], [pltpu.VMEM((2, 512, 1024), F32)])  2.52 us
    pallas_call x1, Pallas kernels, dft_last(): return call(last_kernel, 5, outs, [pltpu.VMEM((512, 1024), F32)])(*args)  1.92 us
  transfers between devices with their start and end apart: 10, of which 5 were waited for; matrix products, arithmetic and copies ran while one was open for 0% of the time, Pallas kernels for 6%

profile of v7, /device:TPU:1, one launch (start us, length us, event | category | flops | bytes accessed | tf_op | source)
XLA Modules:
  0.0 77.9 jit_solution(16436839919905358035)
XLA Ops:
  0.0 3.2 %collective-permute-start = (bf16[256,2048]{1,0:T(8,128)(2,1)}, bf16[256,2048]{1,0:T(8,128)(2,1)S(1)}, u32[]{:S(2)}, u32[]{:S(2)}) collective-permute-start(bf16[256,2048]{1,0:T(8,128)(2,1)} %own_ref.1), channel_id=1, source_target_pairs={{0,1},{1,0},{2,3},{3,2},{32,33},{33,32},{34,35},{35,34},{4,5},{5,4... | collective-permute-start | bytes 3145736 | tf_op jit(solution)/shard_map/ppermute | solution.py:320
  3.2 0.1 pad_add_fusion.ids_ref
  3.3 2.9 %prep.1 = (bf16[1024,256]{1,0:T(8,128)(2,1)S(1)}, bf16[1024,1024]{1,0:T(8,128)(2,1)S(1)}, bf16[512,512]{1,0:T(8,128)(2,1)S(1)}, f32[2,32,128]{2,1,0:T(8,128)S(1)...) custom-call(s32[3]{0:T(128)S(1)} %pad_add_fusion.ids_ref, bf16[256,2048]{1,0:T(8,128)(2,1)} %own_ref.1), custom_call_target="tpu_custom_call" | custom-call | tf_op jit(solution)/shard_map/prep/pallas_call | solution.py:100
  6.2 0.0 collective-permute-done.other_ref
  6.2 2.5 %shard_map.37 = (bf16[1024,128]{1,0:T(8,128)(2,1)S(1)}, bf16[1024,512]{1,0:T(8,128)(2,1)S(1)}, bf16[1536,512]{1,0:T(8,128)(2,1)S(1)}) custom-call(s32[3]{0:T(128)S(1)} %pad_add_fusion.ids_ref, bf16[256,2048]{1,0:T(8,128)(2,1)S(1)} %collective-permute-done.other_ref, bf16[1024,256]{1,0:T(8,128)(2,1)S(1)} %get-tuple-element.18.own_ref, ...), custom_call_target="tpu_custom_call" | custom-call | tf_op jit(solution)/shard_map/pallas_call | solution.py:241
  8.7 0.0 copy-start
  8.7 0.0 copy-start.1
  8.7 2.5 %shard_map.39 = (bf16[1024,128]{1,0:T(8,128)(2,1)S(1)}, bf16[1024,128]{1,0:T(8,128)(2,1)S(1)}) custom-call(s32[3]{0:T(128)S(1)} %pad_add_fusion.ids_ref, bf16[1024,512]{1,0:T(8,128)(2,1)S(1)} %get-tuple-element.24.xs_ref, bf16[1536,512]{1,0:T(8,128)(2,1)S(1)} %get-tuple-element.25.rest_ref, f32[5,32,128]{2,1,0:T(8,128)S(1)} %get-tuple-element.23.outer_ref), custom_call_target="tpu_custom_call" | custom-call | tf_op jit(solution)/shard_map/pallas_call | solution.py:245
  11.3 0.1 collective-permute-start.2
  11.4 1.3 %collective-permute-start.3 = (bf16[1024,128]{1,0:T(8,128)(2,1)S(1)}, bf16[1024,128]{1,0:T(8,128)(2,1)S(1)}, u32[]{:S(2)}, u32[]{:S(2)}) collective-permute-start(bf16[1024,128]{1,0:T(8,128)(2,1)S(1)} %get-tuple-element.29), channel_id=1, source_target_pairs={{0,34},{1,35},{2,32},{3,33},{32,2},{33,3},{34,0},{35,1},{4,38},{5,... | collective-permute-start | bytes 786440 | tf_op jit(solution)/shard_map/ppermute | solution.py:320
  12.7 0.0 copy-done
  12.7 0.3 collective-permute-start.6
  13.0 1.9 %collective-permute-start.8 = (bf16[6,128,256]{2,1,0:T(8,128)(2,1)S(1)}, bf16[6,128,256]{2,1,0:T(8,128)(2,1)S(1)}, u32[]{:S(2)}, u32[]{:S(2)}) collective-permute-start(bf16[6,128,256]{2,1,0:T(8,128)(2,1)S(1)} %bitcast.8), channel_id=1, source_target_pairs={{0,34},{1,35},{2,32},{3,33},{32,2},{33,3},{34,0},{35,1},{4,38},{5,... | collective-permute-start | bytes 1179656 | tf_op jit(solution)/shard_map/ppermute | solution.py:320
  14.9 1.0 %collective-permute-start.1 = (bf16[1024,128]{1,0:T(8,128)(2,1)S(1)}, bf16[1024,128]{1,0:T(8,128)(2,1)S(1)}, u32[]{:S(2)}, u32[]{:S(2)}) collective-permute-start(bf16[1024,128]{1,0:T(8,128)(2,1)S(1)} %get-tuple-element.26), channel_id=1, source_target_pairs={{0,2},{1,3},{2,0},{3,1},{32,34},{33,35},{34,32},{35,33},{4,6},{5,7... | collective-permute-start | bytes 786440 | tf_op jit(solution)/shard_map/ppermute | solution.py:320
  15.9 3.3 %collective-permute-done.2 = bf16[1024,128]{1,0:T(8,128)(2,1)S(1)} collective-permute-done((bf16[1024,128]{1,0:T(8,128)(2,1)S(1)}, bf16[1024,128]{1,0:T(8,128)(2,1)S(1)}, u32[]{:S(2)}, u32[]{:S(2)}) %collective-permute-start.2) | collective-permute-done | bytes 262176 | tf_op jit(solution)/shard_map/ppermute | solution.py:320
  19.2 1.3 %collective-permute-done.3 = bf16[1024,128]{1,0:T(8,128)(2,1)S(1)} collective-permute-done((bf16[1024,128]{1,0:T(8,128)(2,1)S(1)}, bf16[1024,128]{1,0:T(8,128)(2,1)S(1)}, u32[]{:S(2)}, u32[]{:S(2)}) %collective-permute-start.3) | collective-permute-done | bytes 262176 | tf_op jit(solution)/shard_map/ppermute | solution.py:320
  20.5 0.1 add_convert_fusion.s1_ref
  20.6 1.4 %collective-permute-start.5 = (bf16[1024,128]{1,0:T(8,128)(2,1)S(1)}, bf16[1024,128]{1,0:T(8,128)(2,1)S(1)}, u32[]{:S(2)}, u32[]{:S(2)}) collective-permute-start(bf16[1024,128]{1,0:T(8,128)(2,1)S(1)} %add_convert_fusion.s1_ref), channel_id=1, source_target_pairs={{0,1},{1,0},{2,3},{3,2},{32,33},{33,32},{34,35},{35,34},{4,5},{5,4... | collective-permute-start | bytes 786440 | tf_op jit(solution)/shard_map/ppermute | solution.py:320
  22.0 11.8 %collective-permute-done.1.got_ref = bf16[1024,128]{1,0:T(8,128)(2,1)S(1)} collective-permute-done((bf16[1024,128]{1,0:T(8,128)(2,1)S(1)}, bf16[1024,128]{1,0:T(8,128)(2,1)S(1)}, u32[]{:S(2)}, u32[]{:S(2)}) %collective-permute-start.1) | collective-permute-done | bytes 262176 | tf_op jit(solution)/shard_map/ppermute | solution.py:320
  33.8 1.9 %shard_map.38 = (bf16[1024,128]{1,0:T(8,128)(2,1)S(1)}, f32[512,128]{1,0:T(8,128)S(1)}) custom-call(s32[3]{0:T(128)S(1)} %pad_add_fusion.ids_ref, bf16[1024,512]{1,0:T(8,128)(2,1)S(1)} %get-tuple-element.24.xs_ref, bf16[1536,512]{1,0:T(8,128)(2,1)S(1)} %get-tuple-element.25.rest_ref, f32[5,32,128]{2,1,0:T(8,128)S(1)} %get-tuple-element.23.outer_ref, ...), custom_call_target="tpu_custom_call" | custom-call | tf_op jit(solution)/shard_map/pallas_call | solution.py:250
  35.7 1.0 %collective-permute-start.4 = (bf16[1024,128]{1,0:T(8,128)(2,1)S(1)}, bf16[1024,128]{1,0:T(8,128)(2,1)S(1)}, u32[]{:S(2)}, u32[]{:S(2)}) collective-permute-start(bf16[1024,128]{1,0:T(8,128)(2,1)S(1)} %get-tuple-element.27.s0_ref), channel_id=1, source_target_pairs={{0,1},{1,0},{2,3},{3,2},{32,33},{33,32},{34,35},{35,34},{4,5},{5,4... | collective-permute-start | bytes 786440 | tf_op jit(solution)/shard_map/ppermute | solution.py:320
  36.7 0.0 collective-permute-done.6.w1_ref
  36.7 2.0 %collective-permute-start.7 = (bf16[3,128,256]{2,1,0:T(8,128)(2,1)S(1)}, bf16[3,128,256]{2,1,0:T(8,128)(2,1)S(1)}, u32[]{:S(2)}, u32[]{:S(2)}) collective-permute-start(bf16[3,128,256]{2,1,0:T(8,128)(2,1)S(1)} %slice.8), channel_id=1, source_target_pairs={{0,34},{1,35},{2,32},{3,33},{32,2},{33,3},{34,0},{35,1},{4,38},{5,... | collective-permute-start | bytes 589832 | tf_op jit(solution)/shard_map/ppermute | solution.py:320
  38.7 0.0 collective-permute-done.8.w3_ref
  38.8 0.3 collective-permute-start.9
  39.0 5.4 %collective-permute-done.7.w2a_ref = bf16[3,128,256]{2,1,0:T(8,128)(2,1)S(1)} collective-permute-done((bf16[3,128,256]{2,1,0:T(8,128)(2,1)S(1)}, bf16[3,128,256]{2,1,0:T(8,128)(2,1)S(1)}, u32[]{:S(2)}, u32[]{:S(2)}) %collective-permute-start.7) | collective-permute-done | bytes 196640 | tf_op jit(solution)/shard_map/ppermute | solution.py:320
  44.5 0.7 collective-permute-done.9.w2b_ref
  45.2 0.0 collective-permute-done.5.p1_ref
  45.2 0.0 collective-permute-done.4.p0_ref
  45.2 2.7 %shard_map.40 = bf16[4,8,2,32,128]{4,3,2,1,0:T(8,128)(2,1)S(1)} custom-call(s32[3]{0:T(128)S(1)} %pad_add_fusion.ids_ref, bf16[1024,128]{1,0:T(8,128)(2,1)S(1)} %get-tuple-element.27.s0_ref, bf16[1024,128]{1,0:T(8,128)(2,1)S(1)} %add_convert_fusion.s1_ref, bf16[1024,128]{1,0:T(8,128)(2,1)S(1)} %collective-permute-done.4.p0_ref, ...), custom_call_target="tpu_custom_call" | custom-call | tf_op jit(solution)/shard_map/pallas_call | solution.py:291
  47.9 29.2 %all_to_all.5.got_ref = bf16[64,32,128]{2,1,0:T(8,128)(2,1)S(1)} all-to-all(bf16[64,32,128]{2,1,0:T(8,128)(2,1)S(1)} %bitcast.6), channel_id=1, replica_groups=mesh['y'=4,'xlo'=2,'z'=8,'xhi'=2,'core'=2] {'y','z','xhi'}, dimensions={0} | all-to-all | bytes 1048576 | tf_op jit(solution)/shard_map/all_to_all | solution.py:341
  77.2 0.7 add.10
  (3 shorter events, 0.0 us)
Async XLA Ops:
  0.0 6.2 %collective-permute-start = (bf16[256,2048]{1,0:T(8,128)(2,1)}, bf16[256,2048]{1,0:T(8,128)(2,1)S(1)}, u32[]{:S(2)}, u32[]{:S(2)}) collective-permute-start(bf16[256,2048]{1,0:T(8,128)(2,1)} %own_ref.1), channel_id=1, source_target_pairs={{0,1},{1,0},{2,3},{3,2},{32,33},{33,32},{34,35},{35,34},{4,5},{5,4... | collective-permute-start | bytes 3145736 | tf_op jit(solution)/shard_map/ppermute | solution.py:320
  8.7 4.0 %copy-start = (bf16[3,2,128,256]{3,2,1,0:T(8,128)(2,1)S(1)}, bf16[3,2,128,256]{3,2,1,0:T(8,128)(2,1)}, u32[]{:S(2)}) copy-start(bf16[3,2,128,256]{3,2,1,0:T(8,128)(2,1)} %param.4) | copy-start | bytes 1179652
  8.7 25.1 %copy-start.1 = (s32[2048]{0:T(1024)S(1)}, s32[2048]{0:T(1024)}, u32[]{:S(2)}) copy-start(s32[2048]{0:T(1024)} %param.5) | copy-start | bytes 24580
  11.3 8.0 %collective-permute-start.2 = (bf16[1024,128]{1,0:T(8,128)(2,1)S(1)}, bf16[1024,128]{1,0:T(8,128)(2,1)S(1)}, u32[]{:S(2)}, u32[]{:S(2)}) collective-permute-start(bf16[1024,128]{1,0:T(8,128)(2,1)S(1)} %get-tuple-element.28), channel_id=1, source_target_pairs={{0,32},{1,33},{2,34},{3,35},{32,0},{33,1},{34,2},{35,3},{4,36},{5,... | collective-permute-start | bytes 786440 | tf_op jit(solution)/shard_map/ppermute | solution.py:320
  11.4 9.2 %collective-permute-start.3 = (bf16[1024,128]{1,0:T(8,128)(2,1)S(1)}, bf16[1024,128]{1,0:T(8,128)(2,1)S(1)}, u32[]{:S(2)}, u32[]{:S(2)}) collective-permute-start(bf16[1024,128]{1,0:T(8,128)(2,1)S(1)} %get-tuple-element.29), channel_id=1, source_target_pairs={{0,34},{1,35},{2,32},{3,33},{32,2},{33,3},{34,0},{35,1},{4,38},{5,... | collective-permute-start | bytes 786440 | tf_op jit(solution)/shard_map/ppermute | solution.py:320
  12.7 24.0 %collective-permute-start.6 = (bf16[6,128,256]{2,1,0:T(8,128)(2,1)S(1)}, bf16[6,128,256]{2,1,0:T(8,128)(2,1)S(1)}, u32[]{:S(2)}, u32[]{:S(2)}) collective-permute-start(bf16[6,128,256]{2,1,0:T(8,128)(2,1)S(1)} %bitcast.7), channel_id=1, source_target_pairs={{0,32},{1,33},{2,34},{3,35},{32,0},{33,1},{34,2},{35,3},{4,36},{5,... | collective-permute-start | bytes 1179656 | tf_op jit(solution)/shard_map/ppermute | solution.py:320
  13.0 25.8 %collective-permute-start.8 = (bf16[6,128,256]{2,1,0:T(8,128)(2,1)S(1)}, bf16[6,128,256]{2,1,0:T(8,128)(2,1)S(1)}, u32[]{:S(2)}, u32[]{:S(2)}) collective-permute-start(bf16[6,128,256]{2,1,0:T(8,128)(2,1)S(1)} %bitcast.8), channel_id=1, source_target_pairs={{0,34},{1,35},{2,32},{3,33},{32,2},{33,3},{34,0},{35,1},{4,38},{5,... | collective-permute-start | bytes 1179656 | tf_op jit(solution)/shard_map/ppermute | solution.py:320
  14.9 18.9 %collective-permute-start.1 = (bf16[1024,128]{1,0:T(8,128)(2,1)S(1)}, bf16[1024,128]{1,0:T(8,128)(2,1)S(1)}, u32[]{:S(2)}, u32[]{:S(2)}) collective-permute-start(bf16[1024,128]{1,0:T(8,128)(2,1)S(1)} %get-tuple-element.26), channel_id=1, source_target_pairs={{0,2},{1,3},{2,0},{3,1},{32,34},{33,35},{34,32},{35,33},{4,6},{5,7... | collective-permute-start | bytes 786440 | tf_op jit(solution)/shard_map/ppermute | solution.py:320
  20.6 24.6 %collective-permute-start.5 = (bf16[1024,128]{1,0:T(8,128)(2,1)S(1)}, bf16[1024,128]{1,0:T(8,128)(2,1)S(1)}, u32[]{:S(2)}, u32[]{:S(2)}) collective-permute-start(bf16[1024,128]{1,0:T(8,128)(2,1)S(1)} %add_convert_fusion.s1_ref), channel_id=1, source_target_pairs={{0,1},{1,0},{2,3},{3,2},{32,33},{33,32},{34,35},{35,34},{4,5},{5,4... | collective-permute-start | bytes 786440 | tf_op jit(solution)/shard_map/ppermute | solution.py:320
  35.7 9.5 %collective-permute-start.4 = (bf16[1024,128]{1,0:T(8,128)(2,1)S(1)}, bf16[1024,128]{1,0:T(8,128)(2,1)S(1)}, u32[]{:S(2)}, u32[]{:S(2)}) collective-permute-start(bf16[1024,128]{1,0:T(8,128)(2,1)S(1)} %get-tuple-element.27.s0_ref), channel_id=1, source_target_pairs={{0,1},{1,0},{2,3},{3,2},{32,33},{33,32},{34,35},{35,34},{4,5},{5,4... | collective-permute-start | bytes 786440 | tf_op jit(solution)/shard_map/ppermute | solution.py:320
  36.7 7.7 %collective-permute-start.7 = (bf16[3,128,256]{2,1,0:T(8,128)(2,1)S(1)}, bf16[3,128,256]{2,1,0:T(8,128)(2,1)S(1)}, u32[]{:S(2)}, u32[]{:S(2)}) collective-permute-start(bf16[3,128,256]{2,1,0:T(8,128)(2,1)S(1)} %slice.8), channel_id=1, source_target_pairs={{0,34},{1,35},{2,32},{3,33},{32,2},{33,3},{34,0},{35,1},{4,38},{5,... | collective-permute-start | bytes 589832 | tf_op jit(solution)/shard_map/ppermute | solution.py:320
  38.8 6.4 %collective-permute-start.9 = (bf16[3,128,256]{2,1,0:T(8,128)(2,1)S(1)}, bf16[3,128,256]{2,1,0:T(8,128)(2,1)S(1)}, u32[]{:S(2)}, u32[]{:S(2)}) collective-permute-start(bf16[3,128,256]{2,1,0:T(8,128)(2,1)S(1)} %slice.9), channel_id=1, source_target_pairs={{0,32},{1,33},{2,34},{3,35},{32,0},{33,1},{34,2},{35,3},{4,36},{5,... | collective-permute-start | bytes 589832 | tf_op jit(solution)/shard_map/ppermute | solution.py:320

commit v8 on v7

--- a/solution.py
+++ b/solution.py
@@ -141,7 +141,7 @@
     return x[0] + y[1], x[1] - y[0]
 
 
-def combine(ids_ref, slot, f_ref, outer_ref, out_ref, add_ref=None):
+def combine(ids_ref, slot, f_ref, outer_ref, out_ref):
     half, low = owner(ids_ref, slot)
     first = pl.multiple_of(half * 16, 16)
     fine = outer_ref[2, pl.ds(first, 16), :], outer_ref[3, pl.ds(first, 16), :]
@@ -171,10 +171,7 @@
         high_bin = plus(sums[0][1], times(wt, sums[1][1]))
         for place, value in enumerate((low_bin[0], high_bin[0], low_bin[1], high_bin[1])):
             rows = pl.ds(row0 + 256 * place, 16)
-            value = value * scale
-            if add_ref is not None:
-                value = value + add_ref[rows, :].astype(F32)
-            out_ref[rows, :] = value.astype(out_ref.dtype)
+            out_ref[rows, :] = (value * scale).astype(out_ref.dtype)
         return carry
 
     lax.fori_loop(0, 16, step, 0, unroll=UNROLL)
@@ -205,7 +202,7 @@
         combine(ids_ref, 1 + index, f_ref.at[index], outer_ref, out_ref)
 
 
-def last_kernel(ids_ref, xs_ref, rest_ref, outer_ref, got_ref, bins_ref, out_ref, group_ref, f_ref):
+def last_kernel(ids_ref, xs_ref, rest_ref, outer_ref, bins_ref, out_ref, group_ref, f_ref):
     spectrum(rest_ref, 1024, xs_ref, f_ref)
     half, low = ids_ref[1], ids_ref[2]
     row, lane = iota((512, 128), 0), iota((512, 128), 1)
@@ -214,7 +211,7 @@
     place = row // 16 % 4 * 32 + half * 16 + row % 16
     chosen = jnp.where(lane == place, lines, 0.0).astype(BF16)
     group_ref[...] = jnp.dot(chosen, jnp.ones((128, 128), BF16), preferred_element_type=F32)
-    combine(ids_ref, 3, f_ref, outer_ref, out_ref, got_ref)
+    combine(ids_ref, 3, f_ref, outer_ref, out_ref)
 
 
 VM = pl.BlockSpec(memory_space=pltpu.VMEM)
@@ -224,7 +221,7 @@
 PIECE = jax.ShapeDtypeStruct((1024, 128), BF16)
 
 
-def call(kernel, count, out_shape, scratch):
+def call(kernel, count, out_shape, scratch, alias={}):
     outs = len(out_shape) if isinstance(out_shape, list) else 0
     return pl.pallas_call(
         kernel,
@@ -232,6 +229,7 @@
         out_specs=[VM] * outs if outs else VM,
         out_shape=out_shape,
         scratch_shapes=scratch,
+        input_output_aliases=alias,
         compiler_params=pltpu.CompilerParams(vmem_limit_bytes=LIMIT),
     )
 
@@ -246,13 +244,21 @@
 
 
 def dft_last(*args):
-    outs = [PIECE, jax.ShapeDtypeStruct((512, 128), F32)]
-    return call(last_kernel, 5, outs, [pltpu.VMEM((512, 1024), F32)])(*args)
-
-
-def form_kernel(
-    ids_ref, s0_ref, s1_ref, p0_ref, p1_ref, group_ref, w0_ref, w1_ref, w2a_ref, w2b_ref, w3_ref, out_ref, l_ref, w_ref
-):
+    outs = [jax.ShapeDtypeStruct((1024, 128), F32), jax.ShapeDtypeStruct((512, 128), F32)]
+    return call(last_kernel, 4, outs, [pltpu.VMEM((512, 1024), F32)])(*args)
+
+
+def form_beams(side, l_ref, w_ref, group_ref, out_ref):
+    acc = lax.dot_general(l_ref[...], w_ref[...], (((1,), (1,)), ((), ())), preferred_element_type=F32)
+    acc = acc.reshape(2, 512, 384)
+    group = group_ref[...][None]
+    total = jnp.where(group == 0, acc[:, :, 0:128], jnp.where(group == 1, acc[:, :, 128:256], acc[:, :, 256:384]))
+    re = total[0].reshape(4, 8, 16, 128)
+    im = total[1].reshape(4, 8, 16, 128)
+    out_ref[:, :, pl.ds(side, 1)] = jnp.concatenate([re, im], 2).astype(BF16)[:, :, None]
+
+
+def near_kernel(ids_ref, s0_ref, s1_ref, p0_ref, p1_ref, group_ref, w0_ref, w1_ref, out_ref, l_ref, w_ref):
     core, half = ids_ref[0], ids_ref[1]
     for srcs, place in (((s0_ref, s1_ref), core), ((p0_ref, p1_ref), 1 - core)):
         for xl in range(2):
@@ -263,32 +269,31 @@
                 l_ref[r : r + 64, pl.ds(lane0 + 512, 128)] = -si
                 l_ref[512 + r : 576 + r, pl.ds(lane0, 128)] = si
                 l_ref[512 + r : 576 + r, pl.ds(lane0 + 512, 128)] = sr
-    for g in range(3):
-        for p in range(2):
-            i = g * 2 + p
-            w2 = w2a_ref[i] if i < 3 else w2b_ref[i - 3]
-            for b, xl, w in ((0, 0, w0_ref[i]), (0, 1, w1_ref[i]), (1, 0, w2), (1, 1, w3_ref[i])):
-                row, col = g * 256 + b * 128, p * 512 + xl * 256
-                w_ref[row : row + 128, col : col + 256] = w
-    total = jnp.zeros((2, 512, 256), F32)
-    group = group_ref[...]
-    group = jnp.concatenate([group, group], 1)[None]
-    for g in range(3):
-        acc = lax.dot_general(
-            l_ref[...], w_ref[g * 256 : g * 256 + 256, :], (((1,), (1,)), ((), ())), preferred_element_type=F32
-        )
-        total = jnp.where(group == g, acc.reshape(2, 512, 256), total)
-    for b in range(2):
-        part = total[:, :, b * 128 : b * 128 + 128]
-        re = part[0].reshape(4, 8, 16, 128)
-        im = part[1].reshape(4, 8, 16, 128)
-        both = jnp.concatenate([re, im], 2).astype(BF16)
-        out_ref[:, :, pl.ds(half if b == 0 else 1 - half, 1)] = both[:, :, None]
-
-
-def form(*args):
-    scratch = [pltpu.VMEM((1024, 1024), BF16), pltpu.VMEM((768, 1024), BF16)]
-    return call(form_kernel, 10, jax.ShapeDtypeStruct((4, 8, 2, 32, 128), BF16), scratch)(*args)
+    for i in range(6):
+        row, col = i // 2 * 128, i % 2 * 512
+        w_ref[row : row + 128, col : col + 256] = w0_ref[i]
+        w_ref[row : row + 128, col + 256 : col + 512] = w1_ref[i]
+    form_beams(half, l_ref, w_ref, group_ref, out_ref)
+
+
+def far_kernel(ids_ref, l_ref, group_ref, w2a_ref, w2b_ref, w3_ref, begun_ref, out_ref, w_ref):
+    for i in range(6):
+        row, col = i // 2 * 128, i % 2 * 512
+        w_ref[row : row + 128, col : col + 256] = w2a_ref[i] if i < 3 else w2b_ref[i - 3]
+        w_ref[row : row + 128, col + 256 : col + 512] = w3_ref[i]
+    form_beams(1 - ids_ref[1], l_ref, w_ref, group_ref, out_ref)
+
+
+PARTS = jax.ShapeDtypeStruct((4, 8, 2, 32, 128), BF16)
+
+
+def form_near(*args):
+    outs = [PARTS, jax.ShapeDtypeStruct((1024, 1024), BF16)]
+    return call(near_kernel, 7, outs, [pltpu.VMEM((384, 1024), BF16)])(*args)
+
+
+def form_far(*args):
+    return call(far_kernel, 6, PARTS, [pltpu.VMEM((384, 1024), BF16)], {6: 0})(*args)
 
 
 def add_kernel(got_ref, out_ref):
@@ -331,13 +336,15 @@
     spec1, spec2 = dft_next(ids, xs, rest, outer)
     got1 = exchange(spec1, 4)
     got2 = exchange(spec2, 6)
+    mine, group = dft_last(ids, xs, rest, outer, bin_group.reshape(16, 128))
     w2a = exchange(w1[:3], 6)
     w2b = exchange(w3[3:], 4)
-    same, group = dft_last(ids, xs, rest, outer, got0, bin_group.reshape(16, 128))
+    same = (mine + got0.astype(F32)).astype(BF16)
     same_sib = exchange(same, 1)
     cross = (got1.astype(F32) + got2.astype(F32)).astype(BF16)
     cross_sib = exchange(cross, 1)
-    parts = form(ids, same, cross, same_sib, cross_sib, group, blocks, w1, w2a, w2b, w3)
+    begun, lhs = form_near(ids, same, cross, same_sib, cross_sib, group, blocks, w1)
+    parts = form_far(ids, lhs, group, w2a, w2b, w3, begun)
     got = lax.all_to_all(parts.reshape(64, 32, 128), ("y", "z", "xhi"), 0, 0, tiled=True)
     return add(got)
 

time: 78.9 us -> 73.2 us (0.928)
  the two profiles are of different devices: /device:TPU:1 before, /device:TPU:2 now
where the time goes in v8:
time: 73.2 us; the launch traced here: 73 us
  blocking collectives  31 us (42%)
  waiting for transfers between devices  16.7 us (23%)
  Pallas kernels  14.5 us (20%)
  starting transfers between devices  10.5 us (14%)
    all_to_all x1, blocking collectives, shards(): lax.all_to_all(parts.reshape(64, 32, 128), ('y', 'z', 'xhi'), 0, 0, tiled...  31 us
    ppermute x10, waiting for transfers between devices, exchange(): return lax.ppermute(value, ring, [(i, i ^ flip) for i in range(8)])  16.7 us
    ppermute x10, starting transfers between devices, exchange(): return lax.ppermute(value, ring, [(i, i ^ flip) for i in range(8)])  10.5 us
    pallas_call x1, Pallas kernels, prep(): pl.pallas_call(prep_kernel, grid_spec=pltpu.PrefetchScalarGridSpec(num_sc...  2.89 us
    pallas_call x1, Pallas kernels, dft_first(): return call(first_kernel, 7, outs, [pltpu.VMEM((512, 1024), F32)])(*args)  2.53 us
    pallas_call x1, Pallas kernels, dft_next(): call(next_kernel, 3, [PIECE, PIECE], [pltpu.VMEM((2, 512, 1024), F32)])  2.52 us
    pallas_call x1, Pallas kernels, form_near(): return call(near_kernel, 7, outs, [pltpu.VMEM((384, 1024), BF16)])(*args)  2.14 us
    pallas_call x1, Pallas kernels, dft_last(): return call(last_kernel, 4, outs, [pltpu.VMEM((512, 1024), F32)])(*args)  1.87 us
  transfers between devices with their start and end apart: 10, of which 6 were waited for; matrix products, arithmetic and copies ran while one was open for 0% of the time, Pallas kernels for 9%

profile of v8, /device:TPU:2, one launch (start us, length us, event | category | flops | bytes accessed | tf_op | source)
XLA Modules:
  0.0 73.0 jit_solution(15278389835231449493)
XLA Ops:
  0.0 0.0 collective-permute-start
  0.0 0.1 pad_add_fusion.ids_ref
  0.1 2.9 %prep.1 = (bf16[1024,256]{1,0:T(8,128)(2,1)S(1)}, bf16[1024,1024]{1,0:T(8,128)(2,1)S(1)}, bf16[512,512]{1,0:T(8,128)(2,1)S(1)}, f32[2,32,128]{2,1,0:T(8,128)S(1)...) custom-call(s32[3]{0:T(128)S(1)} %pad_add_fusion.ids_ref, bf16[256,2048]{1,0:T(8,128)(2,1)} %own_ref.1), custom_call_target="tpu_custom_call" | custom-call | tf_op jit(solution)/shard_map/prep/pallas_call | solution.py:100
  3.0 0.0 collective-permute-done.other_ref
  3.0 2.5 %shard_map.37 = (bf16[1024,128]{1,0:T(8,128)(2,1)S(1)}, bf16[1024,512]{1,0:T(8,128)(2,1)S(1)}, bf16[1536,512]{1,0:T(8,128)(2,1)S(1)}) custom-call(s32[3]{0:T(128)S(1)} %pad_add_fusion.ids_ref, bf16[256,2048]{1,0:T(8,128)(2,1)S(1)} %collective-permute-done.other_ref, bf16[1024,256]{1,0:T(8,128)(2,1)S(1)} %get-tuple-element.20.own_ref, ...), custom_call_target="tpu_custom_call" | custom-call | tf_op jit(solution)/shard_map/pallas_call | solution.py:239
  5.5 0.0 copy-start
  5.5 0.0 copy-start.1
  5.5 2.5 %shard_map.39 = (bf16[1024,128]{1,0:T(8,128)(2,1)S(1)}, bf16[1024,128]{1,0:T(8,128)(2,1)S(1)}) custom-call(s32[3]{0:T(128)S(1)} %pad_add_fusion.ids_ref, bf16[1024,512]{1,0:T(8,128)(2,1)S(1)} %get-tuple-element.26.xs_ref, bf16[1536,512]{1,0:T(8,128)(2,1)S(1)} %get-tuple-element.27.rest_ref, f32[5,32,128]{2,1,0:T(8,128)S(1)} %get-tuple-element.25.outer_ref), custom_call_target="tpu_custom_call" | custom-call | tf_op jit(solution)/shard_map/pallas_call | solution.py:243
  8.1 2.3 %collective-permute-start.2 = (bf16[1024,128]{1,0:T(8,128)(2,1)S(1)}, bf16[1024,128]{1,0:T(8,128)(2,1)S(1)}, u32[]{:S(2)}, u32[]{:S(2)}) collective-permute-start(bf16[1024,128]{1,0:T(8,128)(2,1)S(1)} %get-tuple-element.30), channel_id=1, source_target_pairs={{0,32},{1,33},{2,34},{3,35},{32,0},{33,1},{34,2},{35,3},{4,36},{5,... | collective-permute-start | bytes 786440 | tf_op jit(solution)/shard_map/ppermute | solution.py:325
  10.4 0.4 collective-permute-start.3
  10.8 1.7 %collective-permute-start.1 = (bf16[1024,128]{1,0:T(8,128)(2,1)S(1)}, bf16[1024,128]{1,0:T(8,128)(2,1)S(1)}, u32[]{:S(2)}, u32[]{:S(2)}) collective-permute-start(bf16[1024,128]{1,0:T(8,128)(2,1)S(1)} %get-tuple-element.29), channel_id=1, source_target_pairs={{0,2},{1,3},{2,0},{3,1},{32,34},{33,35},{34,32},{35,33},{4,6},{5,7... | collective-permute-start | bytes 786440 | tf_op jit(solution)/shard_map/ppermute | solution.py:325
  12.6 1.9 %collective-permute-start.6 = (bf16[6,128,256]{2,1,0:T(8,128)(2,1)S(1)}, bf16[6,128,256]{2,1,0:T(8,128)(2,1)S(1)}, u32[]{:S(2)}, u32[]{:S(2)}) collective-permute-start(bf16[6,128,256]{2,1,0:T(8,128)(2,1)S(1)} %bitcast.7), channel_id=1, source_target_pairs={{0,32},{1,33},{2,34},{3,35},{32,0},{33,1},{34,2},{35,3},{4,36},{5,... | collective-permute-start | bytes 1179656 | tf_op jit(solution)/shard_map/ppermute | solution.py:325
  14.5 0.4 collective-permute-start.8
  14.9 1.9 %shard_map.38 = (f32[1024,128]{1,0:T(8,128)S(1)}, f32[512,128]{1,0:T(8,128)S(1)}) custom-call(s32[3]{0:T(128)S(1)} %pad_add_fusion.ids_ref, bf16[1024,512]{1,0:T(8,128)(2,1)S(1)} %get-tuple-element.26.xs_ref, bf16[1536,512]{1,0:T(8,128)(2,1)S(1)} %get-tuple-element.27.rest_ref, f32[5,32,128]{2,1,0:T(8,128)S(1)} %get-tuple-element.25.outer_ref, ...), custom_call_target="tpu_custom_call" | custom-call | tf_op jit(solution)/shard_map/pallas_call | solution.py:248
  16.8 0.7 %collective-permute-done.2 = bf16[1024,128]{1,0:T(8,128)(2,1)S(1)} collective-permute-done((bf16[1024,128]{1,0:T(8,128)(2,1)S(1)}, bf16[1024,128]{1,0:T(8,128)(2,1)S(1)}, u32[]{:S(2)}, u32[]{:S(2)}) %collective-permute-start.2) | collective-permute-done | bytes 262176 | tf_op jit(solution)/shard_map/ppermute | solution.py:325
  17.6 7.6 %collective-permute-done.3 = bf16[1024,128]{1,0:T(8,128)(2,1)S(1)} collective-permute-done((bf16[1024,128]{1,0:T(8,128)(2,1)S(1)}, bf16[1024,128]{1,0:T(8,128)(2,1)S(1)}, u32[]{:S(2)}, u32[]{:S(2)}) %collective-permute-start.3) | collective-permute-done | bytes 262176 | tf_op jit(solution)/shard_map/ppermute | solution.py:325
  25.2 0.1 add_convert_fusion.s1_ref
  25.3 0.1 collective-permute-start.5
  25.4 0.0 collective-permute-done.1
  25.4 0.1 add_convert_fusion.1.s0_ref
  25.5 0.6 collective-permute-start.4
  26.0 5.4 %collective-permute-done.6.w1_ref = bf16[6,128,256]{2,1,0:T(8,128)(2,1)S(1)} collective-permute-done((bf16[6,128,256]{2,1,0:T(8,128)(2,1)S(1)}, bf16[6,128,256]{2,1,0:T(8,128)(2,1)S(1)}, u32[]{:S(2)}, u32[]{:S(2)}) %collective-permute-start.6) | collective-permute-done | bytes 393248 | tf_op jit(solution)/shard_map/ppermute | solution.py:325
  31.5 1.1 %collective-permute-start.7 = (bf16[3,128,256]{2,1,0:T(8,128)(2,1)S(1)}, bf16[3,128,256]{2,1,0:T(8,128)(2,1)S(1)}, u32[]{:S(2)}, u32[]{:S(2)}) collective-permute-start(bf16[3,128,256]{2,1,0:T(8,128)(2,1)S(1)} %slice.8), channel_id=1, source_target_pairs={{0,34},{1,35},{2,32},{3,33},{32,2},{33,3},{34,0},{35,1},{4,38},{5,... | collective-permute-start | bytes 589832 | tf_op jit(solution)/shard_map/ppermute | solution.py:325
  32.6 0.3 collective-permute-done.8.w3_ref
  32.9 1.9 %collective-permute-start.9 = (bf16[3,128,256]{2,1,0:T(8,128)(2,1)S(1)}, bf16[3,128,256]{2,1,0:T(8,128)(2,1)S(1)}, u32[]{:S(2)}, u32[]{:S(2)}) collective-permute-start(bf16[3,128,256]{2,1,0:T(8,128)(2,1)S(1)} %slice.9), channel_id=1, source_target_pairs={{0,32},{1,33},{2,34},{3,35},{32,0},{33,1},{34,2},{35,3},{4,36},{5,... | collective-permute-start | bytes 589832 | tf_op jit(solution)/shard_map/ppermute | solution.py:325
  34.8 0.0 collective-permute-done.5.p1_ref
  34.8 2.1 %shard_map.40 = (bf16[4,8,2,32,128]{4,3,2,1,0:T(8,128)(2,1)S(1)}, bf16[1024,1024]{1,0:T(8,128)(2,1)S(1)}) custom-call(s32[3]{0:T(128)S(1)} %pad_add_fusion.ids_ref, bf16[1024,128]{1,0:T(8,128)(2,1)S(1)} %add_convert_fusion.1.s0_ref, bf16[1024,128]{1,0:T(8,128)(2,1)S(1)} %add_convert_fusion.s1_ref, bf16[1024,128]{1,0:T(8,128)(2,1)S(1)} %collective-permute-done.4.p0_ref, ...), custom_call_target="tpu_custom_call" | custom-call | tf_op jit(solution)/shard_map/pallas_call | solution.py:292
  36.9 1.4 %collective-permute-done.7.w2a_ref = bf16[3,128,256]{2,1,0:T(8,128)(2,1)S(1)} collective-permute-done((bf16[3,128,256]{2,1,0:T(8,128)(2,1)S(1)}, bf16[3,128,256]{2,1,0:T(8,128)(2,1)S(1)}, u32[]{:S(2)}, u32[]{:S(2)}) %collective-permute-start.7) | collective-permute-done | bytes 196640 | tf_op jit(solution)/shard_map/ppermute | solution.py:325
  38.3 1.2 %collective-permute-done.9.w2b_ref = bf16[3,128,256]{2,1,0:T(8,128)(2,1)S(1)} collective-permute-done((bf16[3,128,256]{2,1,0:T(8,128)(2,1)S(1)}, bf16[3,128,256]{2,1,0:T(8,128)(2,1)S(1)}, u32[]{:S(2)}, u32[]{:S(2)}) %collective-permute-start.9) | collective-permute-done | bytes 196640 | tf_op jit(solution)/shard_map/ppermute | solution.py:325
  39.5 1.8 %shard_map.41 = bf16[4,8,2,32,128]{4,3,2,1,0:T(8,128)(2,1)S(1)} custom-call(s32[3]{0:T(128)S(1)} %pad_add_fusion.ids_ref, bf16[1024,1024]{1,0:T(8,128)(2,1)S(1)} %get-tuple-element.33.l_ref, f32[512,128]{1,0:T(8,128)S(1)} %get-tuple-element.32.group_ref, bf16[3,128,256]{2,1,0:T(8,128)(2,1)S(1)} %collective-permute-done.7.w2a_ref, ...), custom_call_target="tpu_custom_call", output_to_operand_aliasing={{}: (6, {})} | custom-call | tf_op jit(solution)/shard_map/pallas_call | solution.py:296
  41.3 31.0 %all_to_all.5.got_ref = bf16[64,32,128]{2,1,0:T(8,128)(2,1)S(1)} all-to-all(bf16[64,32,128]{2,1,0:T(8,128)(2,1)S(1)} %bitcast.6), channel_id=1, replica_groups=mesh['y'=4,'xlo'=2,'z'=8,'xhi'=2,'core'=2] {'y','z','xhi'}, dimensions={0} | all-to-all | bytes 1048576 | tf_op jit(solution)/shard_map/all_to_all | solution.py:348
  72.3 0.7 add.15
  (5 shorter events, 0.0 us)
Async XLA Ops:
  0.0 3.0 %collective-permute-start = (bf16[256,2048]{1,0:T(8,128)(2,1)}, bf16[256,2048]{1,0:T(8,128)(2,1)S(1)}, u32[]{:S(2)}, u32[]{:S(2)}) collective-permute-start(bf16[256,2048]{1,0:T(8,128)(2,1)} %own_ref.1), channel_id=1, source_target_pairs={{0,1},{1,0},{2,3},{3,2},{32,33},{33,32},{34,35},{35,34},{4,5},{5,4... | collective-permute-start | bytes 3145736 | tf_op jit(solution)/shard_map/ppermute | solution.py:325
  5.5 7.1 %copy-start = (bf16[3,2,128,256]{3,2,1,0:T(8,128)(2,1)S(1)}, bf16[3,2,128,256]{3,2,1,0:T(8,128)(2,1)}, u32[]{:S(2)}) copy-start(bf16[3,2,128,256]{3,2,1,0:T(8,128)(2,1)} %param.4) | copy-start | bytes 1179652
  5.5 9.4 %copy-start.1 = (s32[2048]{0:T(1024)S(1)}, s32[2048]{0:T(1024)}, u32[]{:S(2)}) copy-start(s32[2048]{0:T(1024)} %param.5) | copy-start | bytes 24580
  8.1 9.5 %collective-permute-start.2 = (bf16[1024,128]{1,0:T(8,128)(2,1)S(1)}, bf16[1024,128]{1,0:T(8,128)(2,1)S(1)}, u32[]{:S(2)}, u32[]{:S(2)}) collective-permute-start(bf16[1024,128]{1,0:T(8,128)(2,1)S(1)} %get-tuple-element.30), channel_id=1, source_target_pairs={{0,32},{1,33},{2,34},{3,35},{32,0},{33,1},{34,2},{35,3},{4,36},{5,... | collective-permute-start | bytes 786440 | tf_op jit(solution)/shard_map/ppermute | solution.py:325
  10.4 14.8 %collective-permute-start.3 = (bf16[1024,128]{1,0:T(8,128)(2,1)S(1)}, bf16[1024,128]{1,0:T(8,128)(2,1)S(1)}, u32[]{:S(2)}, u32[]{:S(2)}) collective-permute-start(bf16[1024,128]{1,0:T(8,128)(2,1)S(1)} %get-tuple-element.31), channel_id=1, source_target_pairs={{0,34},{1,35},{2,32},{3,33},{32,2},{33,3},{34,0},{35,1},{4,38},{5,... | collective-permute-start | bytes 786440 | tf_op jit(solution)/shard_map/ppermute | solution.py:325
  10.8 14.5 %collective-permute-start.1 = (bf16[1024,128]{1,0:T(8,128)(2,1)S(1)}, bf16[1024,128]{1,0:T(8,128)(2,1)S(1)}, u32[]{:S(2)}, u32[]{:S(2)}) collective-permute-start(bf16[1024,128]{1,0:T(8,128)(2,1)S(1)} %get-tuple-element.29), channel_id=1, source_target_pairs={{0,2},{1,3},{2,0},{3,1},{32,34},{33,35},{34,32},{35,33},{4,6},{5,7... | collective-permute-start | bytes 786440 | tf_op jit(solution)/shard_map/ppermute | solution.py:325
  12.6 18.9 %collective-permute-start.6 = (bf16[6,128,256]{2,1,0:T(8,128)(2,1)S(1)}, bf16[6,128,256]{2,1,0:T(8,128)(2,1)S(1)}, u32[]{:S(2)}, u32[]{:S(2)}) collective-permute-start(bf16[6,128,256]{2,1,0:T(8,128)(2,1)S(1)} %bitcast.7), channel_id=1, source_target_pairs={{0,32},{1,33},{2,34},{3,35},{32,0},{33,1},{34,2},{35,3},{4,36},{5,... | collective-permute-start | bytes 1179656 | tf_op jit(solution)/shard_map/ppermute | solution.py:325
  14.5 18.4 %collective-permute-start.8 = (bf16[6,128,256]{2,1,0:T(8,128)(2,1)S(1)}, bf16[6,128,256]{2,1,0:T(8,128)(2,1)S(1)}, u32[]{:S(2)}, u32[]{:S(2)}) collective-permute-start(bf16[6,128,256]{2,1,0:T(8,128)(2,1)S(1)} %bitcast.8), channel_id=1, source_target_pairs={{0,34},{1,35},{2,32},{3,33},{32,2},{33,3},{34,0},{35,1},{4,38},{5,... | collective-permute-start | bytes 1179656 | tf_op jit(solution)/shard_map/ppermute | solution.py:325
  25.3 9.5 %collective-permute-start.5 = (bf16[1024,128]{1,0:T(8,128)(2,1)S(1)}, bf16[1024,128]{1,0:T(8,128)(2,1)S(1)}, u32[]{:S(2)}, u32[]{:S(2)}) collective-permute-start(bf16[1024,128]{1,0:T(8,128)(2,1)S(1)} %add_convert_fusion.s1_ref), channel_id=1, source_target_pairs={{0,1},{1,0},{2,3},{3,2},{32,33},{33,32},{34,35},{35,34},{4,5},{5,4... | collective-permute-start | bytes 786440 | tf_op jit(solution)/shard_map/ppermute | solution.py:325
  25.5 9.3 %collective-permute-start.4 = (bf16[1024,128]{1,0:T(8,128)(2,1)S(1)}, bf16[1024,128]{1,0:T(8,128)(2,1)S(1)}, u32[]{:S(2)}, u32[]{:S(2)}) collective-permute-start(bf16[1024,128]{1,0:T(8,128)(2,1)S(1)} %add_convert_fusion.1.s0_ref), channel_id=1, source_target_pairs={{0,1},{1,0},{2,3},{3,2},{32,33},{33,32},{34,35},{35,34},{4,5},{5,4... | collective-permute-start | bytes 786440 | tf_op jit(solution)/shard_map/ppermute | solution.py:325
  31.5 6.8 %collective-permute-start.7 = (bf16[3,128,256]{2,1,0:T(8,128)(2,1)S(1)}, bf16[3,128,256]{2,1,0:T(8,128)(2,1)S(1)}, u32[]{:S(2)}, u32[]{:S(2)}) collective-permute-start(bf16[3,128,256]{2,1,0:T(8,128)(2,1)S(1)} %slice.8), channel_id=1, source_target_pairs={{0,34},{1,35},{2,32},{3,33},{32,2},{33,3},{34,0},{35,1},{4,38},{5,... | collective-permute-start | bytes 589832 | tf_op jit(solution)/shard_map/ppermute | solution.py:325
  32.9 6.6 %collective-permute-start.9 = (bf16[3,128,256]{2,1,0:T(8,128)(2,1)S(1)}, bf16[3,128,256]{2,1,0:T(8,128)(2,1)S(1)}, u32[]{:S(2)}, u32[]{:S(2)}) collective-permute-start(bf16[3,128,256]{2,1,0:T(8,128)(2,1)S(1)} %slice.9), channel_id=1, source_target_pairs={{0,32},{1,33},{2,34},{3,35},{32,0},{33,1},{34,2},{35,3},{4,36},{5,... | collective-permute-start | bytes 589832 | tf_op jit(solution)/shard_map/ppermute | solution.py:325

commit v9 on v8

--- a/solution.py
+++ b/solution.py
@@ -248,59 +248,92 @@
     return call(last_kernel, 4, outs, [pltpu.VMEM((512, 1024), F32)])(*args)
 
 
-def form_beams(side, l_ref, w_ref, group_ref, out_ref):
-    acc = lax.dot_general(l_ref[...], w_ref[...], (((1,), (1,)), ((), ())), preferred_element_type=F32)
+def product(lhs, weights):
+    return lax.dot_general(lhs, weights, (((1,), (1,)), ((), ())), preferred_element_type=F32)
+
+
+def store_beams(side, acc, group_ref, out_ref):
     acc = acc.reshape(2, 512, 384)
     group = group_ref[...][None]
     total = jnp.where(group == 0, acc[:, :, 0:128], jnp.where(group == 1, acc[:, :, 128:256], acc[:, :, 256:384]))
     re = total[0].reshape(4, 8, 16, 128)
     im = total[1].reshape(4, 8, 16, 128)
-    out_ref[:, :, pl.ds(side, 1)] = jnp.concatenate([re, im], 2).astype(BF16)[:, :, None]
-
-
-def near_kernel(ids_ref, s0_ref, s1_ref, p0_ref, p1_ref, group_ref, w0_ref, w1_ref, out_ref, l_ref, w_ref):
-    core, half = ids_ref[0], ids_ref[1]
-    for srcs, place in (((s0_ref, s1_ref), core), ((p0_ref, p1_ref), 1 - core)):
-        for xl in range(2):
-            lane0 = pl.multiple_of(xl * 256 + place * 128, 128)
-            for r in range(0, 512, 64):
-                sr, si = srcs[xl][r : r + 64, :], srcs[xl][512 + r : 576 + r, :]
-                l_ref[r : r + 64, pl.ds(lane0, 128)] = sr
-                l_ref[r : r + 64, pl.ds(lane0 + 512, 128)] = -si
-                l_ref[512 + r : 576 + r, pl.ds(lane0, 128)] = si
-                l_ref[512 + r : 576 + r, pl.ds(lane0 + 512, 128)] = sr
-    for i in range(6):
-        row, col = i // 2 * 128, i % 2 * 512
-        w_ref[row : row + 128, col : col + 256] = w0_ref[i]
-        w_ref[row : row + 128, col + 256 : col + 512] = w1_ref[i]
-    form_beams(half, l_ref, w_ref, group_ref, out_ref)
-
-
-def far_kernel(ids_ref, l_ref, group_ref, w2a_ref, w2b_ref, w3_ref, begun_ref, out_ref, w_ref):
-    for i in range(6):
-        row, col = i // 2 * 128, i % 2 * 512
-        w_ref[row : row + 128, col : col + 256] = w2a_ref[i] if i < 3 else w2b_ref[i - 3]
-        w_ref[row : row + 128, col + 256 : col + 512] = w3_ref[i]
-    form_beams(1 - ids_ref[1], l_ref, w_ref, group_ref, out_ref)
-
-
-PARTS = jax.ShapeDtypeStruct((4, 8, 2, 32, 128), BF16)
-
-
-def form_near(*args):
-    outs = [PARTS, jax.ShapeDtypeStruct((1024, 1024), BF16)]
-    return call(near_kernel, 7, outs, [pltpu.VMEM((384, 1024), BF16)])(*args)
+    both = jnp.concatenate([re, im], 2).astype(BF16)
+    for y in range(4):
+        out_ref[:, pl.ds(side, 1), y] = both[y][:, None]
+
+
+def place_rows(l_ref, xl, src):
+    for r in range(0, 512, 64):
+        sr, si = src[r : r + 64, :], src[512 + r : 576 + r, :]
+        c0, c1 = slice(xl * 256, xl * 256 + 128), slice(xl * 256 + 128, xl * 256 + 256)
+        l_ref[r : r + 64, c0] = sr
+        l_ref[r : r + 64, c1] = -si
+        l_ref[512 + r : 576 + r, c0] = si
+        l_ref[512 + r : 576 + r, c1] = sr
+
+
+def place_weights(core, w_ref, col, blocks):
+    for which in range(2):
+        lane0 = pl.multiple_of((core if which == 0 else 1 - core) * 128, 128)
+        for i in range(6):
+            row, at = i // 2 * 128, col + i % 2 * 128
+            w_ref[which, row : row + 128, at : at + 128] = blocks[i][:, pl.ds(lane0, 128)]
+
+
+def pack_kernel(ids_ref, w0_ref, w1_ref, w3_ref, near_ref, side_ref):
+    place_weights(ids_ref[0], near_ref, 0, [w0_ref.at[i] for i in range(6)])
+    place_weights(ids_ref[0], near_ref, 256, [w1_ref.at[i] for i in range(6)])
+    place_weights(ids_ref[0], side_ref, 0, [w3_ref.at[i] for i in range(6)])
+
+
+def own_kernel(ids_ref, same_ref, cross_ref, near_ref, l_ref, acc_ref):
+    place_rows(l_ref, 0, same_ref)
+    place_rows(l_ref, 1, cross_ref)
+    acc_ref[...] = product(l_ref[...], near_ref[0])
+
+
+def sib_kernel(ids_ref, same_ref, cross_ref, near_ref, side_ref, own_ref, acc_ref, group_ref, out_ref, l_ref, far_ref):
+    place_rows(l_ref, 0, same_ref)
+    place_rows(l_ref, 1, cross_ref)
+    store_beams(ids_ref[1], acc_ref[...] + product(l_ref[...], near_ref[1]), group_ref, out_ref)
+    far_ref[...] = product(own_ref[:, 256:512], side_ref[0]) + product(l_ref[:, 256:512], side_ref[1])
+
+
+def far_kernel(ids_ref, own_ref, sib_ref, acc_ref, group_ref, w2a_ref, w2b_ref, begun_ref, out_ref, w_ref):
+    place_weights(ids_ref[0], w_ref, 0, [w2a_ref.at[i] for i in range(3)] + [w2b_ref.at[i] for i in range(3)])
+    acc = acc_ref[...] + product(own_ref[:, 0:256], w_ref[0]) + product(sib_ref[:, 0:256], w_ref[1])
+    store_beams(1 - ids_ref[1], acc, group_ref, out_ref)
+
+
+PARTS = jax.ShapeDtypeStruct((8, 2, 4, 32, 128), BF16)
+ROWS = jax.ShapeDtypeStruct((1024, 512), BF16)
+SUMS = jax.ShapeDtypeStruct((1024, 384), F32)
+
+
+def pack(*args):
+    outs = [jax.ShapeDtypeStruct((2, 384, 512), BF16), jax.ShapeDtypeStruct((2, 384, 256), BF16)]
+    return call(pack_kernel, 3, outs, [])(*args)
+
+
+def form_own(*args):
+    return call(own_kernel, 3, [ROWS, SUMS], [])(*args)
+
+
+def form_sib(*args):
+    return call(sib_kernel, 7, [PARTS, ROWS, SUMS], [])(*args)
 
 
 def form_far(*args):
-    return call(far_kernel, 6, PARTS, [pltpu.VMEM((384, 1024), BF16)], {6: 0})(*args)
+    return call(far_kernel, 7, PARTS, [pltpu.VMEM((2, 384, 256), BF16)], {7: 0})(*args)
 
 
 def add_kernel(got_ref, out_ref):
     for side in range(2):
-        parts = [got_ref[2 * src + side].astype(F32) for src in range(4)]
-        for src in range(4, 32):
-            parts[src % 4] = parts[src % 4] + got_ref[2 * src + side].astype(F32)
+        sources = [(z * 2 + side) * 4 + y for z in range(8) for y in range(4)]
+        parts = [got_ref[src].astype(F32) for src in sources[:4]]
+        for place, src in enumerate(sources[4:]):
+            parts[place % 4] = parts[place % 4] + got_ref[src].astype(F32)
         total = (parts[0] + parts[1]) + (parts[2] + parts[3])
         for p in range(2):
             out_ref[side * 16 : side * 16 + 16, p, :] = total[p * 16 : p * 16 + 16]
@@ -337,15 +370,17 @@
     got1 = exchange(spec1, 4)
     got2 = exchange(spec2, 6)
     mine, group = dft_last(ids, xs, rest, outer, bin_group.reshape(16, 128))
+    same = (mine + got0.astype(F32)).astype(BF16)
+    same_sib = exchange(same, 1)
     w2a = exchange(w1[:3], 6)
     w2b = exchange(w3[3:], 4)
-    same = (mine + got0.astype(F32)).astype(BF16)
-    same_sib = exchange(same, 1)
+    near, side = pack(ids, blocks, w1, w3)
     cross = (got1.astype(F32) + got2.astype(F32)).astype(BF16)
     cross_sib = exchange(cross, 1)
-    begun, lhs = form_near(ids, same, cross, same_sib, cross_sib, group, blocks, w1)
-    parts = form_far(ids, lhs, group, w2a, w2b, w3, begun)
-    got = lax.all_to_all(parts.reshape(64, 32, 128), ("y", "z", "xhi"), 0, 0, tiled=True)
+    lhs, acc = form_own(ids, same, cross, near)
+    begun, lhs_sib, acc_far = form_sib(ids, same_sib, cross_sib, near, side, lhs, acc, group)
+    parts = form_far(ids, lhs, lhs_sib, acc_far, group, w2a, w2b, begun)
+    got = lax.all_to_all(parts.reshape(64, 32, 128), ("z", "xhi", "y"), 0, 0, tiled=True)
     return add(got)
 
 

time: 73.2 us -> 72.7 us (level)
  the two profiles are of different devices: /device:TPU:2 before, /device:TPU:24 now
where the time goes in v9:
time: 72.7 us; the launch traced here: 72.5 us
  blocking collectives  30.2 us (42%)
  Pallas kernels  15.7 us (22%)
  waiting for transfers between devices  14.5 us (20%)
  starting transfers between devices  11.8 us (16%)
    all_to_all x1, blocking collectives, shards(): lax.all_to_all(parts.reshape(64, 32, 128), ('z', 'xhi', 'y'), 0, 0, tiled...  30.2 us
    ppermute x10, waiting for transfers between devices, exchange(): return lax.ppermute(value, ring, [(i, i ^ flip) for i in range(8)])  14.5 us
    ppermute x10, starting transfers between devices, exchange(): return lax.ppermute(value, ring, [(i, i ^ flip) for i in range(8)])  11.8 us
    pallas_call x1, Pallas kernels, prep(): pl.pallas_call(prep_kernel, grid_spec=pltpu.PrefetchScalarGridSpec(num_sc...  2.89 us
    pallas_call x1, Pallas kernels, dft_first(): return call(first_kernel, 7, outs, [pltpu.VMEM((512, 1024), F32)])(*args)  2.53 us
    pallas_call x1, Pallas kernels, dft_next(): call(next_kernel, 3, [PIECE, PIECE], [pltpu.VMEM((2, 512, 1024), F32)])  2.52 us
    pallas_call x1, Pallas kernels, dft_last(): return call(last_kernel, 4, outs, [pltpu.VMEM((512, 1024), F32)])(*args)  1.86 us
    pallas_call x1, Pallas kernels, form_sib(): return call(sib_kernel, 7, [PARTS, ROWS, SUMS], [])(*args)  1.84 us
  transfers between devices with their start and end apart: 10, of which 4 were waited for; matrix products, arithmetic and copies ran while one was open for 0% of the time, Pallas kernels for 12%

profile of v9, /device:TPU:24, one launch (start us, length us, event | category | flops | bytes accessed | tf_op | source)
XLA Modules:
  0.0 72.5 jit_solution(968477033697600118)
XLA Ops:
  0.0 0.0 collective-permute-start
  0.0 0.1 pad_add_fusion.ids_ref
  0.1 2.9 %prep.1 = (bf16[1024,256]{1,0:T(8,128)(2,1)S(1)}, bf16[1024,1024]{1,0:T(8,128)(2,1)S(1)}, bf16[512,512]{1,0:T(8,128)(2,1)S(1)}, f32[2,32,128]{2,1,0:T(8,128)S(1)...) custom-call(s32[3]{0:T(128)S(1)} %pad_add_fusion.ids_ref, bf16[256,2048]{1,0:T(8,128)(2,1)} %own_ref.1), custom_call_target="tpu_custom_call" | custom-call | tf_op jit(solution)/shard_map/prep/pallas_call | solution.py:100
  3.0 0.0 collective-permute-done.other_ref
  3.0 2.5 %shard_map.37 = (bf16[1024,128]{1,0:T(8,128)(2,1)S(1)}, bf16[1024,512]{1,0:T(8,128)(2,1)S(1)}, bf16[1536,512]{1,0:T(8,128)(2,1)S(1)}) custom-call(s32[3]{0:T(128)S(1)} %pad_add_fusion.ids_ref, bf16[256,2048]{1,0:T(8,128)(2,1)S(1)} %collective-permute-done.other_ref, bf16[1024,256]{1,0:T(8,128)(2,1)S(1)} %get-tuple-element.25.own_ref, ...), custom_call_target="tpu_custom_call" | custom-call | tf_op jit(solution)/shard_map/pallas_call | solution.py:239
  5.5 0.0 copy-start
  5.5 0.0 copy-start.1
  5.5 2.5 %shard_map.39 = (bf16[1024,128]{1,0:T(8,128)(2,1)S(1)}, bf16[1024,128]{1,0:T(8,128)(2,1)S(1)}) custom-call(s32[3]{0:T(128)S(1)} %pad_add_fusion.ids_ref, bf16[1024,512]{1,0:T(8,128)(2,1)S(1)} %get-tuple-element.31.xs_ref, bf16[1536,512]{1,0:T(8,128)(2,1)S(1)} %get-tuple-element.32.rest_ref, f32[5,32,128]{2,1,0:T(8,128)S(1)} %get-tuple-element.30.outer_ref), custom_call_target="tpu_custom_call" | custom-call | tf_op jit(solution)/shard_map/pallas_call | solution.py:243
  8.1 1.6 %collective-permute-start.2 = (bf16[1024,128]{1,0:T(8,128)(2,1)S(1)}, bf16[1024,128]{1,0:T(8,128)(2,1)S(1)}, u32[]{:S(2)}, u32[]{:S(2)}) collective-permute-start(bf16[1024,128]{1,0:T(8,128)(2,1)S(1)} %get-tuple-element.35), channel_id=1, source_target_pairs={{0,32},{1,33},{2,34},{3,35},{32,0},{33,1},{34,2},{35,3},{4,36},{5,... | collective-permute-start | bytes 786440 | tf_op jit(solution)/shard_map/ppermute | solution.py:358
  9.7 2.1 %collective-permute-start.3 = (bf16[1024,128]{1,0:T(8,128)(2,1)S(1)}, bf16[1024,128]{1,0:T(8,128)(2,1)S(1)}, u32[]{:S(2)}, u32[]{:S(2)}) collective-permute-start(bf16[1024,128]{1,0:T(8,128)(2,1)S(1)} %get-tuple-element.36), channel_id=1, source_target_pairs={{0,34},{1,35},{2,32},{3,33},{32,2},{33,3},{34,0},{35,1},{4,38},{5,... | collective-permute-start | bytes 786440 | tf_op jit(solution)/shard_map/ppermute | solution.py:358
  11.7 0.6 collective-permute-start.1
  12.4 1.4 %collective-permute-start.4 = (bf16[6,128,256]{2,1,0:T(8,128)(2,1)S(1)}, bf16[6,128,256]{2,1,0:T(8,128)(2,1)S(1)}, u32[]{:S(2)}, u32[]{:S(2)}) collective-permute-start(bf16[6,128,256]{2,1,0:T(8,128)(2,1)S(1)} %bitcast.7), channel_id=1, source_target_pairs={{0,32},{1,33},{2,34},{3,35},{32,0},{33,1},{34,2},{35,3},{4,36},{5,... | collective-permute-start | bytes 1179656 | tf_op jit(solution)/shard_map/ppermute | solution.py:358
  13.8 2.1 %collective-permute-start.5 = (bf16[6,128,256]{2,1,0:T(8,128)(2,1)S(1)}, bf16[6,128,256]{2,1,0:T(8,128)(2,1)S(1)}, u32[]{:S(2)}, u32[]{:S(2)}) collective-permute-start(bf16[6,128,256]{2,1,0:T(8,128)(2,1)S(1)} %bitcast.8), channel_id=1, source_target_pairs={{0,34},{1,35},{2,32},{3,33},{32,2},{33,3},{34,0},{35,1},{4,38},{5,... | collective-permute-start | bytes 1179656 | tf_op jit(solution)/shard_map/ppermute | solution.py:358
  15.8 1.9 %shard_map.38 = (f32[1024,128]{1,0:T(8,128)S(1)}, f32[512,128]{1,0:T(8,128)S(1)}) custom-call(s32[3]{0:T(128)S(1)} %pad_add_fusion.ids_ref, bf16[1024,512]{1,0:T(8,128)(2,1)S(1)} %get-tuple-element.31.xs_ref, bf16[1536,512]{1,0:T(8,128)(2,1)S(1)} %get-tuple-element.32.rest_ref, f32[5,32,128]{2,1,0:T(8,128)S(1)} %get-tuple-element.30.outer_ref, ...), custom_call_target="tpu_custom_call" | custom-call | tf_op jit(solution)/shard_map/pallas_call | solution.py:248
  17.7 7.9 %collective-permute-done.3 = bf16[1024,128]{1,0:T(8,128)(2,1)S(1)} collective-permute-done((bf16[1024,128]{1,0:T(8,128)(2,1)S(1)}, bf16[1024,128]{1,0:T(8,128)(2,1)S(1)}, u32[]{:S(2)}, u32[]{:S(2)}) %collective-permute-start.3) | collective-permute-done | bytes 262176 | tf_op jit(solution)/shard_map/ppermute | solution.py:358
  25.7 0.1 add_convert_fusion.cross_ref
  25.7 0.1 collective-permute-start.7
  25.8 0.0 collective-permute-done.1
  25.9 0.1 add_convert_fusion.1.same_ref
  25.9 0.6 collective-permute-start.6
  26.5 4.5 %collective-permute-done.4.w1_ref = bf16[6,128,256]{2,1,0:T(8,128)(2,1)S(1)} collective-permute-done((bf16[6,128,256]{2,1,0:T(8,128)(2,1)S(1)}, bf16[6,128,256]{2,1,0:T(8,128)(2,1)S(1)}, u32[]{:S(2)}, u32[]{:S(2)}) %collective-permute-start.4) | collective-permute-done | bytes 393248 | tf_op jit(solution)/shard_map/ppermute | solution.py:358
  31.0 2.9 %collective-permute-start.8 = (bf16[3,128,256]{2,1,0:T(8,128)(2,1)S(1)}, bf16[3,128,256]{2,1,0:T(8,128)(2,1)S(1)}, u32[]{:S(2)}, u32[]{:S(2)}) collective-permute-start(bf16[3,128,256]{2,1,0:T(8,128)(2,1)S(1)} %slice.8), channel_id=1, source_target_pairs={{0,34},{1,35},{2,32},{3,33},{32,2},{33,3},{34,0},{35,1},{4,38},{5,... | collective-permute-start | bytes 589832 | tf_op jit(solution)/shard_map/ppermute | solution.py:358
  33.9 0.5 collective-permute-start.9
  34.3 0.7 %shard_map.40 = (bf16[2,384,512]{2,1,0:T(8,128)(2,1)S(1)}, bf16[2,384,256]{2,1,0:T(8,128)(2,1)S(1)}) custom-call(s32[3]{0:T(128)S(1)} %pad_add_fusion.ids_ref, bf16[6,128,256]{2,1,0:T(8,128)(2,1)S(1)} %bitcast.9, bf16[6,128,256]{2,1,0:T(8,128)(2,1)S(1)} %collective-permute-done.4.w1_ref, bf16[6,128,256]{2,1,0:T(8,128)(2,1)S(1)} %collective-permute-done.5.w3_ref), custom_call_target="tpu_custom_call" | custom-call | tf_op jit(solution)/shard_map/pallas_call | solution.py:316
  35.1 1.3 %shard_map.41 = (bf16[1024,512]{1,0:T(8,128)(2,1)S(1)}, f32[1024,384]{1,0:T(8,128)S(1)}) custom-call(s32[3]{0:T(128)S(1)} %pad_add_fusion.ids_ref, bf16[1024,128]{1,0:T(8,128)(2,1)S(1)} %add_convert_fusion.1.same_ref, bf16[1024,128]{1,0:T(8,128)(2,1)S(1)} %add_convert_fusion.cross_ref, bf16[2,384,512]{2,1,0:T(8,128)(2,1)S(1)} %get-tuple-element.37.near_ref), custom_call_target="tpu_custom_call" | custom-call | tf_op jit(solution)/shard_map/pallas_call | solution.py:320
  36.4 0.0 collective-permute-done.7.cross_ref
  36.4 1.8 %shard_map.42 = (bf16[8,2,4,32,128]{4,3,2,1,0:T(8,128)(2,1)S(1)}, bf16[1024,512]{1,0:T(8,128)(2,1)S(1)}, f32[1024,384]{1,0:T(8,128)S(1)}) custom-call(s32[3]{0:T(128)S(1)} %pad_add_fusion.ids_ref, bf16[1024,128]{1,0:T(8,128)(2,1)S(1)} %collective-permute-done.6.same_ref, bf16[1024,128]{1,0:T(8,128)(2,1)S(1)} %collective-permute-done.7.cross_ref, ...), custom_call_target="tpu_custom_call" | custom-call | tf_op jit(solution)/shard_map/pallas_call | solution.py:324
  38.2 0.5 collective-permute-done.8.w2a_ref
  38.7 1.6 %collective-permute-done.9.w2b_ref = bf16[3,128,256]{2,1,0:T(8,128)(2,1)S(1)} collective-permute-done((bf16[3,128,256]{2,1,0:T(8,128)(2,1)S(1)}, bf16[3,128,256]{2,1,0:T(8,128)(2,1)S(1)}, u32[]{:S(2)}, u32[]{:S(2)}) %collective-permute-start.9) | collective-permute-done | bytes 196640 | tf_op jit(solution)/shard_map/ppermute | solution.py:358
  40.3 1.3 %shard_map.43 = bf16[8,2,4,32,128]{4,3,2,1,0:T(8,128)(2,1)S(1)} custom-call(s32[3]{0:T(128)S(1)} %pad_add_fusion.ids_ref, bf16[1024,512]{1,0:T(8,128)(2,1)S(1)} %get-tuple-element.38.own_ref, bf16[1024,512]{1,0:T(8,128)(2,1)S(1)} %get-tuple-element.42.sib_ref, f32[1024,384]{1,0:T(8,128)S(1)} %get-tuple-element.43.acc_ref, ...), custom_call_target="tpu_custom_call", output_to_operand_aliasing={{}: (7, {})} | custom-call | tf_op jit(solution)/shard_map/pallas_call | solution.py:328
  41.6 30.2 %all_to_all.5.got_ref = bf16[64,32,128]{2,1,0:T(8,128)(2,1)S(1)} all-to-all(bf16[64,32,128]{2,1,0:T(8,128)(2,1)S(1)} %bitcast.6), channel_id=1, replica_groups=mesh['y'=4,'xlo'=2,'z'=8,'xhi'=2,'core'=2] {'z','xhi','y'}, dimensions={0} | all-to-all | bytes 1048576 | tf_op jit(solution)/shard_map/all_to_all | solution.py:383
  71.8 0.7 add.15
  (7 shorter events, 0.0 us)
Async XLA Ops:
  0.0 3.0 %collective-permute-start = (bf16[256,2048]{1,0:T(8,128)(2,1)}, bf16[256,2048]{1,0:T(8,128)(2,1)S(1)}, u32[]{:S(2)}, u32[]{:S(2)}) collective-permute-start(bf16[256,2048]{1,0:T(8,128)(2,1)} %own_ref.1), channel_id=1, source_target_pairs={{0,1},{1,0},{2,3},{3,2},{32,33},{33,32},{34,35},{35,34},{4,5},{5,4... | collective-permute-start | bytes 3145736 | tf_op jit(solution)/shard_map/ppermute | solution.py:358
  5.5 6.9 %copy-start = (bf16[3,2,128,256]{3,2,1,0:T(8,128)(2,1)S(1)}, bf16[3,2,128,256]{3,2,1,0:T(8,128)(2,1)}, u32[]{:S(2)}) copy-start(bf16[3,2,128,256]{3,2,1,0:T(8,128)(2,1)} %param.4) | copy-start | bytes 1179652
  5.5 10.3 %copy-start.1 = (s32[2048]{0:T(1024)S(1)}, s32[2048]{0:T(1024)}, u32[]{:S(2)}) copy-start(s32[2048]{0:T(1024)} %param.5) | copy-start | bytes 24580
  8.1 9.6 %collective-permute-start.2 = (bf16[1024,128]{1,0:T(8,128)(2,1)S(1)}, bf16[1024,128]{1,0:T(8,128)(2,1)S(1)}, u32[]{:S(2)}, u32[]{:S(2)}) collective-permute-start(bf16[1024,128]{1,0:T(8,128)(2,1)S(1)} %get-tuple-element.35), channel_id=1, source_target_pairs={{0,32},{1,33},{2,34},{3,35},{32,0},{33,1},{34,2},{35,3},{4,36},{5,... | collective-permute-start | bytes 786440 | tf_op jit(solution)/shard_map/ppermute | solution.py:358
  9.7 16.0 %collective-permute-start.3 = (bf16[1024,128]{1,0:T(8,128)(2,1)S(1)}, bf16[1024,128]{1,0:T(8,128)(2,1)S(1)}, u32[]{:S(2)}, u32[]{:S(2)}) collective-permute-start(bf16[1024,128]{1,0:T(8,128)(2,1)S(1)} %get-tuple-element.36), channel_id=1, source_target_pairs={{0,34},{1,35},{2,32},{3,33},{32,2},{33,3},{34,0},{35,1},{4,38},{5,... | collective-permute-start | bytes 786440 | tf_op jit(solution)/shard_map/ppermute | solution.py:358
  11.7 14.1 %collective-permute-start.1 = (bf16[1024,128]{1,0:T(8,128)(2,1)S(1)}, bf16[1024,128]{1,0:T(8,128)(2,1)S(1)}, u32[]{:S(2)}, u32[]{:S(2)}) collective-permute-start(bf16[1024,128]{1,0:T(8,128)(2,1)S(1)} %get-tuple-element.34), channel_id=1, source_target_pairs={{0,2},{1,3},{2,0},{3,1},{32,34},{33,35},{34,32},{35,33},{4,6},{5,7... | collective-permute-start | bytes 786440 | tf_op jit(solution)/shard_map/ppermute | solution.py:358
  12.4 18.6 %collective-permute-start.4 = (bf16[6,128,256]{2,1,0:T(8,128)(2,1)S(1)}, bf16[6,128,256]{2,1,0:T(8,128)(2,1)S(1)}, u32[]{:S(2)}, u32[]{:S(2)}) collective-permute-start(bf16[6,128,256]{2,1,0:T(8,128)(2,1)S(1)} %bitcast.7), channel_id=1, source_target_pairs={{0,32},{1,33},{2,34},{3,35},{32,0},{33,1},{34,2},{35,3},{4,36},{5,... | collective-permute-start | bytes 1179656 | tf_op jit(solution)/shard_map/ppermute | solution.py:358
  13.8 20.1 %collective-permute-start.5 = (bf16[6,128,256]{2,1,0:T(8,128)(2,1)S(1)}, bf16[6,128,256]{2,1,0:T(8,128)(2,1)S(1)}, u32[]{:S(2)}, u32[]{:S(2)}) collective-permute-start(bf16[6,128,256]{2,1,0:T(8,128)(2,1)S(1)} %bitcast.8), channel_id=1, source_target_pairs={{0,34},{1,35},{2,32},{3,33},{32,2},{33,3},{34,0},{35,1},{4,38},{5,... | collective-permute-start | bytes 1179656 | tf_op jit(solution)/shard_map/ppermute | solution.py:358
  25.7 10.6 %collective-permute-start.7 = (bf16[1024,128]{1,0:T(8,128)(2,1)S(1)}, bf16[1024,128]{1,0:T(8,128)(2,1)S(1)}, u32[]{:S(2)}, u32[]{:S(2)}) collective-permute-start(bf16[1024,128]{1,0:T(8,128)(2,1)S(1)} %add_convert_fusion.cross_ref), channel_id=1, source_target_pairs={{0,1},{1,0},{2,3},{3,2},{32,33},{33,32},{34,35},{35,34},{4,5},{5,4... | collective-permute-start | bytes 786440 | tf_op jit(solution)/shard_map/ppermute | solution.py:358
  25.9 10.5 %collective-permute-start.6 = (bf16[1024,128]{1,0:T(8,128)(2,1)S(1)}, bf16[1024,128]{1,0:T(8,128)(2,1)S(1)}, u32[]{:S(2)}, u32[]{:S(2)}) collective-permute-start(bf16[1024,128]{1,0:T(8,128)(2,1)S(1)} %add_convert_fusion.1.same_ref), channel_id=1, source_target_pairs={{0,1},{1,0},{2,3},{3,2},{32,33},{33,32},{34,35},{35,34},{4,5},{5,4... | collective-permute-start | bytes 786440 | tf_op jit(solution)/shard_map/ppermute | solution.py:358
  31.0 7.7 %collective-permute-start.8 = (bf16[3,128,256]{2,1,0:T(8,128)(2,1)S(1)}, bf16[3,128,256]{2,1,0:T(8,128)(2,1)S(1)}, u32[]{:S(2)}, u32[]{:S(2)}) collective-permute-start(bf16[3,128,256]{2,1,0:T(8,128)(2,1)S(1)} %slice.8), channel_id=1, source_target_pairs={{0,34},{1,35},{2,32},{3,33},{32,2},{33,3},{34,0},{35,1},{4,38},{5,... | collective-permute-start | bytes 589832 | tf_op jit(solution)/shard_map/ppermute | solution.py:358
  33.9 6.4 %collective-permute-start.9 = (bf16[3,128,256]{2,1,0:T(8,128)(2,1)S(1)}, bf16[3,128,256]{2,1,0:T(8,128)(2,1)S(1)}, u32[]{:S(2)}, u32[]{:S(2)}) collective-permute-start(bf16[3,128,256]{2,1,0:T(8,128)(2,1)S(1)} %slice.9), channel_id=1, source_target_pairs={{0,32},{1,33},{2,34},{3,35},{32,0},{33,1},{34,2},{35,3},{4,36},{5,... | collective-permute-start | bytes 589832 | tf_op jit(solution)/shard_map/ppermute | solution.py:358

commit v10 on v9

--- a/solution.py
+++ b/solution.py
@@ -281,23 +281,34 @@
             w_ref[which, row : row + 128, at : at + 128] = blocks[i][:, pl.ds(lane0, 128)]
 
 
-def pack_kernel(ids_ref, w0_ref, w1_ref, w3_ref, near_ref, side_ref):
-    place_weights(ids_ref[0], near_ref, 0, [w0_ref.at[i] for i in range(6)])
-    place_weights(ids_ref[0], near_ref, 256, [w1_ref.at[i] for i in range(6)])
-    place_weights(ids_ref[0], side_ref, 0, [w3_ref.at[i] for i in range(6)])
-
-
-def own_kernel(ids_ref, same_ref, cross_ref, near_ref, l_ref, acc_ref):
+def pack_near_kernel(ids_ref, w0_ref, w1_ref, p0_ref, p1_ref):
+    place_weights(ids_ref[0], p0_ref, 0, [w0_ref.at[i] for i in range(6)])
+    place_weights(ids_ref[0], p1_ref, 0, [w1_ref.at[i] for i in range(6)])
+
+
+def pack_side_kernel(ids_ref, w3_ref, p3_ref):
+    place_weights(ids_ref[0], p3_ref, 0, [w3_ref.at[i] for i in range(6)])
+
+
+def half_sums(which, l_ref, p0_ref, p1_ref, p3_ref):
+    both = product(l_ref[:, 256:512], jnp.concatenate([p1_ref[which], p3_ref[which]], 0))
+    return product(l_ref[:, 0:256], p0_ref[which]) + both[:, 0:384], both[:, 384:768]
+
+
+def own_kernel(ids_ref, same_ref, cross_ref, p0_ref, p1_ref, p3_ref, l_ref, near_ref, far_ref):
     place_rows(l_ref, 0, same_ref)
     place_rows(l_ref, 1, cross_ref)
-    acc_ref[...] = product(l_ref[...], near_ref[0])
-
-
-def sib_kernel(ids_ref, same_ref, cross_ref, near_ref, side_ref, own_ref, acc_ref, group_ref, out_ref, l_ref, far_ref):
+    near_ref[...], far_ref[...] = half_sums(0, l_ref, p0_ref, p1_ref, p3_ref)
+
+
+def sib_kernel(
+    ids_ref, same_ref, cross_ref, p0_ref, p1_ref, p3_ref, near_ref, begun_ref, group_ref, out_ref, l_ref, far_ref
+):
     place_rows(l_ref, 0, same_ref)
     place_rows(l_ref, 1, cross_ref)
-    store_beams(ids_ref[1], acc_ref[...] + product(l_ref[...], near_ref[1]), group_ref, out_ref)
-    far_ref[...] = product(own_ref[:, 256:512], side_ref[0]) + product(l_ref[:, 256:512], side_ref[1])
+    near, far = half_sums(1, l_ref, p0_ref, p1_ref, p3_ref)
+    store_beams(ids_ref[1], near_ref[...] + near, group_ref, out_ref)
+    far_ref[...] = begun_ref[...] + far
 
 
 def far_kernel(ids_ref, own_ref, sib_ref, acc_ref, group_ref, w2a_ref, w2b_ref, begun_ref, out_ref, w_ref):
@@ -311,17 +322,23 @@
 SUMS = jax.ShapeDtypeStruct((1024, 384), F32)
 
 
-def pack(*args):
-    outs = [jax.ShapeDtypeStruct((2, 384, 512), BF16), jax.ShapeDtypeStruct((2, 384, 256), BF16)]
-    return call(pack_kernel, 3, outs, [])(*args)
+PACKED = jax.ShapeDtypeStruct((2, 384, 256), BF16)
+
+
+def pack_near(*args):
+    return call(pack_near_kernel, 2, [PACKED, PACKED], [])(*args)
+
+
+def pack_side(*args):
+    return call(pack_side_kernel, 1, PACKED, [])(*args)
 
 
 def form_own(*args):
-    return call(own_kernel, 3, [ROWS, SUMS], [])(*args)
+    return call(own_kernel, 5, [ROWS, SUMS, SUMS], [])(*args)
 
 
 def form_sib(*args):
-    return call(sib_kernel, 7, [PARTS, ROWS, SUMS], [])(*args)
+    return call(sib_kernel, 8, [PARTS, ROWS, SUMS], [])(*args)
 
 
 def form_far(*args):
@@ -372,13 +389,14 @@
     mine, group = dft_last(ids, xs, rest, outer, bin_group.reshape(16, 128))
     same = (mine + got0.astype(F32)).astype(BF16)
     same_sib = exchange(same, 1)
+    p0, p1 = pack_near(ids, blocks, w1)
     w2a = exchange(w1[:3], 6)
     w2b = exchange(w3[3:], 4)
-    near, side = pack(ids, blocks, w1, w3)
+    p3 = pack_side(ids, w3)
     cross = (got1.astype(F32) + got2.astype(F32)).astype(BF16)
     cross_sib = exchange(cross, 1)
-    lhs, acc = form_own(ids, same, cross, near)
-    begun, lhs_sib, acc_far = form_sib(ids, same_sib, cross_sib, near, side, lhs, acc, group)
+    lhs, near, far = form_own(ids, same, cross, p0, p1, p3)
+    begun, lhs_sib, acc_far = form_sib(ids, same_sib, cross_sib, p0, p1, p3, near, far, group)
     parts = form_far(ids, lhs, lhs_sib, acc_far, group, w2a, w2b, begun)
     got = lax.all_to_all(parts.reshape(64, 32, 128), ("z", "xhi", "y"), 0, 0, tiled=True)
     return add(got)

time: 72.7 us -> 73.8 us (1.015)
  the two profiles are of different devices: /device:TPU:24 before, /device:TPU:2 now
where the time goes in v10:
time: 73.8 us; the launch traced here: 73.6 us
  blocking collectives  30.6 us (41%)
  Pallas kernels  16 us (22%)
  waiting for transfers between devices  15.7 us (21%)
  starting transfers between devices  11 us (15%)
    all_to_all x1, blocking collectives, shards(): lax.all_to_all(parts.reshape(64, 32, 128), ('z', 'xhi', 'y'), 0, 0, tiled...  30.6 us
    ppermute x10, waiting for transfers between devices, exchange(): return lax.ppermute(value, ring, [(i, i ^ flip) for i in range(8)])  15.7 us
    ppermute x10, starting transfers between devices, exchange(): return lax.ppermute(value, ring, [(i, i ^ flip) for i in range(8)])  11 us
    pallas_call x1, Pallas kernels, prep(): pl.pallas_call(prep_kernel, grid_spec=pltpu.PrefetchScalarGridSpec(num_sc...  2.89 us
    pallas_call x1, Pallas kernels, dft_first(): return call(first_kernel, 7, outs, [pltpu.VMEM((512, 1024), F32)])(*args)  2.53 us
    pallas_call x1, Pallas kernels, dft_next(): call(next_kernel, 3, [PIECE, PIECE], [pltpu.VMEM((2, 512, 1024), F32)])  2.52 us
    pallas_call x1, Pallas kernels, dft_last(): return call(last_kernel, 4, outs, [pltpu.VMEM((512, 1024), F32)])(*args)  1.87 us
  transfers between devices with their start and end apart: 10, of which 4 were waited for; matrix products, arithmetic and copies ran while one was open for 0% of the time, Pallas kernels for 12%

profile of v10, /device:TPU:2, one launch (start us, length us, event | category | flops | bytes accessed | tf_op | source)
XLA Modules:
  0.0 73.6 jit_solution(7505339261439411598)
XLA Ops:
  0.0 0.0 collective-permute-start
  0.0 0.1 pad_add_fusion.ids_ref
  0.1 2.9 %prep.1 = (bf16[1024,256]{1,0:T(8,128)(2,1)S(1)}, bf16[1024,1024]{1,0:T(8,128)(2,1)S(1)}, bf16[512,512]{1,0:T(8,128)(2,1)S(1)}, f32[2,32,128]{2,1,0:T(8,128)S(1)...) custom-call(s32[3]{0:T(128)S(1)} %pad_add_fusion.ids_ref, bf16[256,2048]{1,0:T(8,128)(2,1)} %own_ref.1), custom_call_target="tpu_custom_call" | custom-call | tf_op jit(solution)/shard_map/prep/pallas_call | solution.py:100
  3.0 0.0 collective-permute-done.other_ref
  3.0 2.5 %shard_map.37 = (bf16[1024,128]{1,0:T(8,128)(2,1)S(1)}, bf16[1024,512]{1,0:T(8,128)(2,1)S(1)}, bf16[1536,512]{1,0:T(8,128)(2,1)S(1)}) custom-call(s32[3]{0:T(128)S(1)} %pad_add_fusion.ids_ref, bf16[256,2048]{1,0:T(8,128)(2,1)S(1)} %collective-permute-done.other_ref, bf16[1024,256]{1,0:T(8,128)(2,1)S(1)} %get-tuple-element.26.own_ref, ...), custom_call_target="tpu_custom_call" | custom-call | tf_op jit(solution)/shard_map/pallas_call | solution.py:239
  5.5 0.0 copy-start
  5.5 0.0 copy-start.1
  5.5 2.5 %shard_map.39 = (bf16[1024,128]{1,0:T(8,128)(2,1)S(1)}, bf16[1024,128]{1,0:T(8,128)(2,1)S(1)}) custom-call(s32[3]{0:T(128)S(1)} %pad_add_fusion.ids_ref, bf16[1024,512]{1,0:T(8,128)(2,1)S(1)} %get-tuple-element.32.xs_ref, bf16[1536,512]{1,0:T(8,128)(2,1)S(1)} %get-tuple-element.33.rest_ref, f32[5,32,128]{2,1,0:T(8,128)S(1)} %get-tuple-element.31.outer_ref), custom_call_target="tpu_custom_call" | custom-call | tf_op jit(solution)/shard_map/pallas_call | solution.py:243
  8.1 2.3 %collective-permute-start.2 = (bf16[1024,128]{1,0:T(8,128)(2,1)S(1)}, bf16[1024,128]{1,0:T(8,128)(2,1)S(1)}, u32[]{:S(2)}, u32[]{:S(2)}) collective-permute-start(bf16[1024,128]{1,0:T(8,128)(2,1)S(1)} %get-tuple-element.36), channel_id=1, source_target_pairs={{0,32},{1,33},{2,34},{3,35},{32,0},{33,1},{34,2},{35,3},{4,36},{5,... | collective-permute-start | bytes 786440 | tf_op jit(solution)/shard_map/ppermute | solution.py:375
  10.4 0.4 collective-permute-start.3
  10.8 1.7 %collective-permute-start.1 = (bf16[1024,128]{1,0:T(8,128)(2,1)S(1)}, bf16[1024,128]{1,0:T(8,128)(2,1)S(1)}, u32[]{:S(2)}, u32[]{:S(2)}) collective-permute-start(bf16[1024,128]{1,0:T(8,128)(2,1)S(1)} %get-tuple-element.35), channel_id=1, source_target_pairs={{0,2},{1,3},{2,0},{3,1},{32,34},{33,35},{34,32},{35,33},{4,6},{5,7... | collective-permute-start | bytes 786440 | tf_op jit(solution)/shard_map/ppermute | solution.py:375
  12.6 1.2 %collective-permute-start.5 = (bf16[6,128,256]{2,1,0:T(8,128)(2,1)S(1)}, bf16[6,128,256]{2,1,0:T(8,128)(2,1)S(1)}, u32[]{:S(2)}, u32[]{:S(2)}) collective-permute-start(bf16[6,128,256]{2,1,0:T(8,128)(2,1)S(1)} %bitcast.7), channel_id=1, source_target_pairs={{0,34},{1,35},{2,32},{3,33},{32,2},{33,3},{34,0},{35,1},{4,38},{5,... | collective-permute-start | bytes 1179656 | tf_op jit(solution)/shard_map/ppermute | solution.py:375
  13.7 1.8 %collective-permute-start.4 = (bf16[6,128,256]{2,1,0:T(8,128)(2,1)S(1)}, bf16[6,128,256]{2,1,0:T(8,128)(2,1)S(1)}, u32[]{:S(2)}, u32[]{:S(2)}) collective-permute-start(bf16[6,128,256]{2,1,0:T(8,128)(2,1)S(1)} %bitcast.8), channel_id=1, source_target_pairs={{0,32},{1,33},{2,34},{3,35},{32,0},{33,1},{34,2},{35,3},{4,36},{5,... | collective-permute-start | bytes 1179656 | tf_op jit(solution)/shard_map/ppermute | solution.py:375
  15.6 1.9 %shard_map.38 = (f32[1024,128]{1,0:T(8,128)S(1)}, f32[512,128]{1,0:T(8,128)S(1)}) custom-call(s32[3]{0:T(128)S(1)} %pad_add_fusion.ids_ref, bf16[1024,512]{1,0:T(8,128)(2,1)S(1)} %get-tuple-element.32.xs_ref, bf16[1536,512]{1,0:T(8,128)(2,1)S(1)} %get-tuple-element.33.rest_ref, f32[5,32,128]{2,1,0:T(8,128)S(1)} %get-tuple-element.31.outer_ref, ...), custom_call_target="tpu_custom_call" | custom-call | tf_op jit(solution)/shard_map/pallas_call | solution.py:248
  17.4 0.1 collective-permute-done.2
  17.6 7.6 %collective-permute-done.3 = bf16[1024,128]{1,0:T(8,128)(2,1)S(1)} collective-permute-done((bf16[1024,128]{1,0:T(8,128)(2,1)S(1)}, bf16[1024,128]{1,0:T(8,128)(2,1)S(1)}, u32[]{:S(2)}, u32[]{:S(2)}) %collective-permute-start.3) | collective-permute-done | bytes 262176 | tf_op jit(solution)/shard_map/ppermute | solution.py:375
  25.2 0.1 add_convert_fusion.cross_ref
  25.3 0.1 collective-permute-start.7
  25.4 0.0 collective-permute-done.1
  25.4 0.1 add_convert_fusion.1.same_ref
  25.5 0.6 collective-permute-start.6
  26.0 6.9 %collective-permute-done.5.w3_ref = bf16[6,128,256]{2,1,0:T(8,128)(2,1)S(1)} collective-permute-done((bf16[6,128,256]{2,1,0:T(8,128)(2,1)S(1)}, bf16[6,128,256]{2,1,0:T(8,128)(2,1)S(1)}, u32[]{:S(2)}, u32[]{:S(2)}) %collective-permute-start.5) | collective-permute-done | bytes 393248 | tf_op jit(solution)/shard_map/ppermute | solution.py:375
  32.9 1.7 %collective-permute-start.9 = (bf16[3,128,256]{2,1,0:T(8,128)(2,1)S(1)}, bf16[3,128,256]{2,1,0:T(8,128)(2,1)S(1)}, u32[]{:S(2)}, u32[]{:S(2)}) collective-permute-start(bf16[3,128,256]{2,1,0:T(8,128)(2,1)S(1)} %slice.9), channel_id=1, source_target_pairs={{0,32},{1,33},{2,34},{3,35},{32,0},{33,1},{34,2},{35,3},{4,36},{5,... | collective-permute-start | bytes 589832 | tf_op jit(solution)/shard_map/ppermute | solution.py:375
  34.6 1.2 %collective-permute-start.8 = (bf16[3,128,256]{2,1,0:T(8,128)(2,1)S(1)}, bf16[3,128,256]{2,1,0:T(8,128)(2,1)S(1)}, u32[]{:S(2)}, u32[]{:S(2)}) collective-permute-start(bf16[3,128,256]{2,1,0:T(8,128)(2,1)S(1)} %slice.8), channel_id=1, source_target_pairs={{0,34},{1,35},{2,32},{3,33},{32,2},{33,3},{34,0},{35,1},{4,38},{5,... | collective-permute-start | bytes 589832 | tf_op jit(solution)/shard_map/ppermute | solution.py:375
  35.8 0.6 shard_map.41.p3_ref
  36.4 0.7 shard_map.40
  37.1 1.4 %shard_map.42 = (bf16[1024,512]{1,0:T(8,128)(2,1)S(1)}, f32[1024,384]{1,0:T(8,128)S(1)}, f32[1024,384]{1,0:T(8,128)S(1)}) custom-call(s32[3]{0:T(128)S(1)} %pad_add_fusion.ids_ref, bf16[1024,128]{1,0:T(8,128)(2,1)S(1)} %add_convert_fusion.1.same_ref, bf16[1024,128]{1,0:T(8,128)(2,1)S(1)} %add_convert_fusion.cross_ref, ...), custom_call_target="tpu_custom_call" | custom-call | tf_op jit(solution)/shard_map/pallas_call | solution.py:337
  38.5 1.4 %shard_map.43 = (bf16[8,2,4,32,128]{4,3,2,1,0:T(8,128)(2,1)S(1)}, bf16[1024,512]{1,0:T(8,128)(2,1)S(1)}, f32[1024,384]{1,0:T(8,128)S(1)}) custom-call(s32[3]{0:T(128)S(1)} %pad_add_fusion.ids_ref, bf16[1024,128]{1,0:T(8,128)(2,1)S(1)} %collective-permute-done.6.same_ref, bf16[1024,128]{1,0:T(8,128)(2,1)S(1)} %collective-permute-done.7.cross_ref, ...), custom_call_target="tpu_custom_call" | custom-call | tf_op jit(solution)/shard_map/pallas_call | solution.py:341
  40.0 1.0 %collective-permute-done.8.w2a_ref = bf16[3,128,256]{2,1,0:T(8,128)(2,1)S(1)} collective-permute-done((bf16[3,128,256]{2,1,0:T(8,128)(2,1)S(1)}, bf16[3,128,256]{2,1,0:T(8,128)(2,1)S(1)}, u32[]{:S(2)}, u32[]{:S(2)}) %collective-permute-start.8) | collective-permute-done | bytes 196640 | tf_op jit(solution)/shard_map/ppermute | solution.py:375
  41.0 1.3 %shard_map.44 = bf16[8,2,4,32,128]{4,3,2,1,0:T(8,128)(2,1)S(1)} custom-call(s32[3]{0:T(128)S(1)} %pad_add_fusion.ids_ref, bf16[1024,512]{1,0:T(8,128)(2,1)S(1)} %get-tuple-element.40.own_ref, bf16[1024,512]{1,0:T(8,128)(2,1)S(1)} %get-tuple-element.44.sib_ref, f32[1024,384]{1,0:T(8,128)S(1)} %get-tuple-element.45.acc_ref, ...), custom_call_target="tpu_custom_call", output_to_operand_aliasing={{}: (7, {})} | custom-call | tf_op jit(solution)/shard_map/pallas_call | solution.py:345
  42.3 30.6 %all_to_all.5.got_ref = bf16[64,32,128]{2,1,0:T(8,128)(2,1)S(1)} all-to-all(bf16[64,32,128]{2,1,0:T(8,128)(2,1)S(1)} %bitcast.6), channel_id=1, replica_groups=mesh['y'=4,'xlo'=2,'z'=8,'xhi'=2,'core'=2] {'z','xhi','y'}, dimensions={0} | all-to-all | bytes 1048576 | tf_op jit(solution)/shard_map/all_to_all | solution.py:401
  72.9 0.7 add.15
  (8 shorter events, 0.0 us)
Async XLA Ops:
  0.0 3.0 %collective-permute-start = (bf16[256,2048]{1,0:T(8,128)(2,1)}, bf16[256,2048]{1,0:T(8,128)(2,1)S(1)}, u32[]{:S(2)}, u32[]{:S(2)}) collective-permute-start(bf16[256,2048]{1,0:T(8,128)(2,1)} %own_ref.1), channel_id=1, source_target_pairs={{0,1},{1,0},{2,3},{3,2},{32,33},{33,32},{34,35},{35,34},{4,5},{5,4... | collective-permute-start | bytes 3145736 | tf_op jit(solution)/shard_map/ppermute | solution.py:375
  5.5 7.1 %copy-start = (bf16[3,2,128,256]{3,2,1,0:T(8,128)(2,1)S(1)}, bf16[3,2,128,256]{3,2,1,0:T(8,128)(2,1)}, u32[]{:S(2)}) copy-start(bf16[3,2,128,256]{3,2,1,0:T(8,128)(2,1)} %param.4) | copy-start | bytes 1179652
  5.5 10.0 %copy-start.1 = (s32[2048]{0:T(1024)S(1)}, s32[2048]{0:T(1024)}, u32[]{:S(2)}) copy-start(s32[2048]{0:T(1024)} %param.5) | copy-start | bytes 24580
  8.1 9.5 %collective-permute-start.2 = (bf16[1024,128]{1,0:T(8,128)(2,1)S(1)}, bf16[1024,128]{1,0:T(8,128)(2,1)S(1)}, u32[]{:S(2)}, u32[]{:S(2)}) collective-permute-start(bf16[1024,128]{1,0:T(8,128)(2,1)S(1)} %get-tuple-element.36), channel_id=1, source_target_pairs={{0,32},{1,33},{2,34},{3,35},{32,0},{33,1},{34,2},{35,3},{4,36},{5,... | collective-permute-start | bytes 786440 | tf_op jit(solution)/shard_map/ppermute | solution.py:375
  10.4 14.8 %collective-permute-start.3 = (bf16[1024,128]{1,0:T(8,128)(2,1)S(1)}, bf16[1024,128]{1,0:T(8,128)(2,1)S(1)}, u32[]{:S(2)}, u32[]{:S(2)}) collective-permute-start(bf16[1024,128]{1,0:T(8,128)(2,1)S(1)} %get-tuple-element.37), channel_id=1, source_target_pairs={{0,34},{1,35},{2,32},{3,33},{32,2},{33,3},{34,0},{35,1},{4,38},{5,... | collective-permute-start | bytes 786440 | tf_op jit(solution)/shard_map/ppermute | solution.py:375
  10.8 14.5 %collective-permute-start.1 = (bf16[1024,128]{1,0:T(8,128)(2,1)S(1)}, bf16[1024,128]{1,0:T(8,128)(2,1)S(1)}, u32[]{:S(2)}, u32[]{:S(2)}) collective-permute-start(bf16[1024,128]{1,0:T(8,128)(2,1)S(1)} %get-tuple-element.35), channel_id=1, source_target_pairs={{0,2},{1,3},{2,0},{3,1},{32,34},{33,35},{34,32},{35,33},{4,6},{5,7... | collective-permute-start | bytes 786440 | tf_op jit(solution)/shard_map/ppermute | solution.py:375
  12.6 20.3 %collective-permute-start.5 = (bf16[6,128,256]{2,1,0:T(8,128)(2,1)S(1)}, bf16[6,128,256]{2,1,0:T(8,128)(2,1)S(1)}, u32[]{:S(2)}, u32[]{:S(2)}) collective-permute-start(bf16[6,128,256]{2,1,0:T(8,128)(2,1)S(1)} %bitcast.7), channel_id=1, source_target_pairs={{0,34},{1,35},{2,32},{3,33},{32,2},{33,3},{34,0},{35,1},{4,38},{5,... | collective-permute-start | bytes 1179656 | tf_op jit(solution)/shard_map/ppermute | solution.py:375
  13.7 20.8 %collective-permute-start.4 = (bf16[6,128,256]{2,1,0:T(8,128)(2,1)S(1)}, bf16[6,128,256]{2,1,0:T(8,128)(2,1)S(1)}, u32[]{:S(2)}, u32[]{:S(2)}) collective-permute-start(bf16[6,128,256]{2,1,0:T(8,128)(2,1)S(1)} %bitcast.8), channel_id=1, source_target_pairs={{0,32},{1,33},{2,34},{3,35},{32,0},{33,1},{34,2},{35,3},{4,36},{5,... | collective-permute-start | bytes 1179656 | tf_op jit(solution)/shard_map/ppermute | solution.py:375
  25.3 13.2 %collective-permute-start.7 = (bf16[1024,128]{1,0:T(8,128)(2,1)S(1)}, bf16[1024,128]{1,0:T(8,128)(2,1)S(1)}, u32[]{:S(2)}, u32[]{:S(2)}) collective-permute-start(bf16[1024,128]{1,0:T(8,128)(2,1)S(1)} %add_convert_fusion.cross_ref), channel_id=1, source_target_pairs={{0,1},{1,0},{2,3},{3,2},{32,33},{33,32},{34,35},{35,34},{4,5},{5,4... | collective-permute-start | bytes 786440 | tf_op jit(solution)/shard_map/ppermute | solution.py:375
  25.5 13.1 %collective-permute-start.6 = (bf16[1024,128]{1,0:T(8,128)(2,1)S(1)}, bf16[1024,128]{1,0:T(8,128)(2,1)S(1)}, u32[]{:S(2)}, u32[]{:S(2)}) collective-permute-start(bf16[1024,128]{1,0:T(8,128)(2,1)S(1)} %add_convert_fusion.1.same_ref), channel_id=1, source_target_pairs={{0,1},{1,0},{2,3},{3,2},{32,33},{33,32},{34,35},{35,34},{4,5},{5,4... | collective-permute-start | bytes 786440 | tf_op jit(solution)/shard_map/ppermute | solution.py:375
  32.9 7.1 %collective-permute-start.9 = (bf16[3,128,256]{2,1,0:T(8,128)(2,1)S(1)}, bf16[3,128,256]{2,1,0:T(8,128)(2,1)S(1)}, u32[]{:S(2)}, u32[]{:S(2)}) collective-permute-start(bf16[3,128,256]{2,1,0:T(8,128)(2,1)S(1)} %slice.9), channel_id=1, source_target_pairs={{0,32},{1,33},{2,34},{3,35},{32,0},{33,1},{34,2},{35,3},{4,36},{5,... | collective-permute-start | bytes 589832 | tf_op jit(solution)/shard_map/ppermute | solution.py:375
  34.6 6.4 %collective-permute-start.8 = (bf16[3,128,256]{2,1,0:T(8,128)(2,1)S(1)}, bf16[3,128,256]{2,1,0:T(8,128)(2,1)S(1)}, u32[]{:S(2)}, u32[]{:S(2)}) collective-permute-start(bf16[3,128,256]{2,1,0:T(8,128)(2,1)S(1)} %slice.8), channel_id=1, source_target_pairs={{0,34},{1,35},{2,32},{3,33},{32,2},{33,3},{34,0},{35,1},{4,38},{5,... | collective-permute-start | bytes 589832 | tf_op jit(solution)/shard_map/ppermute | solution.py:375

commit v11 on v10

--- a/solution.py
+++ b/solution.py
@@ -259,8 +259,7 @@
     re = total[0].reshape(4, 8, 16, 128)
     im = total[1].reshape(4, 8, 16, 128)
     both = jnp.concatenate([re, im], 2).astype(BF16)
-    for y in range(4):
-        out_ref[:, pl.ds(side, 1), y] = both[y][:, None]
+    out_ref[:, pl.ds(side, 1)] = both[:, None]
 
 
 def place_rows(l_ref, xl, src):
@@ -317,7 +316,7 @@
     store_beams(1 - ids_ref[1], acc, group_ref, out_ref)
 
 
-PARTS = jax.ShapeDtypeStruct((8, 2, 4, 32, 128), BF16)
+PARTS = jax.ShapeDtypeStruct((4, 2, 8, 32, 128), BF16)
 ROWS = jax.ShapeDtypeStruct((1024, 512), BF16)
 SUMS = jax.ShapeDtypeStruct((1024, 384), F32)
 
@@ -345,26 +344,26 @@
     return call(far_kernel, 7, PARTS, [pltpu.VMEM((2, 384, 256), BF16)], {7: 0})(*args)
 
 
-def add_kernel(got_ref, out_ref):
+def add_first_kernel(ids_ref, got_ref, out_ref):
     for side in range(2):
-        sources = [(z * 2 + side) * 4 + y for z in range(8) for y in range(4)]
-        parts = [got_ref[src].astype(F32) for src in sources[:4]]
-        for place, src in enumerate(sources[4:]):
-            parts[place % 4] = parts[place % 4] + got_ref[src].astype(F32)
-        total = (parts[0] + parts[1]) + (parts[2] + parts[3])
+        parts = [got_ref[y, side].astype(F32) for y in range(4)]
+        out_ref[:, side] = (parts[0] + parts[1]) + (parts[2] + parts[3])
+
+
+def add_last_kernel(ids_ref, got_ref, out_ref):
+    for side in range(2):
+        parts = [got_ref[z, side] for z in range(8)]
+        total = ((parts[0] + parts[1]) + (parts[2] + parts[3])) + ((parts[4] + parts[5]) + (parts[6] + parts[7]))
         for p in range(2):
             out_ref[side * 16 : side * 16 + 16, p, :] = total[p * 16 : p * 16 + 16]
 
 
-def add(got):
-    return pl.pallas_call(
-        add_kernel,
-        in_specs=[VM],
-        out_specs=VM,
-        out_shape=jax.ShapeDtypeStruct((32, 2, 128), F32),
-        compiler_params=pltpu.CompilerParams(vmem_limit_bytes=LIMIT),
-        name="add",
-    )(got)
+def add_first(*args):
+    return call(add_first_kernel, 1, jax.ShapeDtypeStruct((8, 2, 32, 128), F32), [])(*args)
+
+
+def add_last(*args):
+    return call(add_last_kernel, 1, jax.ShapeDtypeStruct((32, 2, 128), F32), [])(*args)
 
 
 def shards(signals, weights, bin_group):
@@ -398,8 +397,9 @@
     lhs, near, far = form_own(ids, same, cross, p0, p1, p3)
     begun, lhs_sib, acc_far = form_sib(ids, same_sib, cross_sib, p0, p1, p3, near, far, group)
     parts = form_far(ids, lhs, lhs_sib, acc_far, group, w2a, w2b, begun)
-    got = lax.all_to_all(parts.reshape(64, 32, 128), ("z", "xhi", "y"), 0, 0, tiled=True)
-    return add(got)
+    got = lax.all_to_all(parts.reshape(8, 8, 32, 128), ("y", "xhi"), 0, 0, tiled=True)
+    column = add_first(ids, got.reshape(4, 2, 8, 32, 128))
+    return add_last(ids, lax.all_to_all(column, "z", 0, 0, tiled=True))
 
 
 def solution(mesh):

time: 73.8 us -> 78.6 us (1.065)
  blocking collectives: 30.6 us -> 34.3 us
  Pallas kernels: 16 us -> 17.1 us
    all_to_all x1 -> x2, blocking collectives: 30.6 us -> 34.3 us  [the longest x1 18.7 us: shards(): return add_last(ids, lax.all_to_all(column, 'z', 0, 0, tiled=True))]
    pallas_call x1 -> x2, Pallas kernels: 0.7 us -> 1.79 us  [the longest x1 1.19 us: add_last(): call(add_last_kernel, 1, jax.ShapeDtypeStruct((32, 2, 128), F32), [])(*args)]
  transfers between devices with their start and end apart: 10 -> 10, of which waited for: 4 -> 4; matrix products, arithmetic and copies ran while one was open for 0% -> 0% of each run, Pallas kernels for 12% -> 11%
where the time goes in v11:
time: 78.6 us; the launch traced here: 78.4 us
  blocking collectives  34.3 us (44%)
  Pallas kernels  17.1 us (22%)
  waiting for transfers between devices  15.7 us (20%)
  starting transfers between devices  11 us (14%)
    all_to_all x1, blocking collectives, shards(): return add_last(ids, lax.all_to_all(column, 'z', 0, 0, tiled=True))  18.7 us
    ppermute x10, waiting for transfers between devices, exchange(): return lax.ppermute(value, ring, [(i, i ^ flip) for i in range(8)])  15.7 us
    all_to_all x1, blocking collectives, shards(): lax.all_to_all(parts.reshape(8, 8, 32, 128), ('y', 'xhi'), 0, 0, tiled=True)  15.6 us
    ppermute x10, starting transfers between devices, exchange(): return lax.ppermute(value, ring, [(i, i ^ flip) for i in range(8)])  11 us
    pallas_call x1, Pallas kernels, prep(): pl.pallas_call(prep_kernel, grid_spec=pltpu.PrefetchScalarGridSpec(num_sc...  2.89 us
    pallas_call x1, Pallas kernels, dft_first(): return call(first_kernel, 7, outs, [pltpu.VMEM((512, 1024), F32)])(*args)  2.53 us
    pallas_call x1, Pallas kernels, dft_next(): call(next_kernel, 3, [PIECE, PIECE], [pltpu.VMEM((2, 512, 1024), F32)])  2.52 us
    pallas_call x1, Pallas kernels, dft_last(): return call(last_kernel, 4, outs, [pltpu.VMEM((512, 1024), F32)])(*args)  1.87 us
  transfers between devices with their start and end apart: 10, of which 4 were waited for; matrix products, arithmetic and copies ran while one was open for 0% of the time, Pallas kernels for 11%

profile of v11, /device:TPU:2, one launch (start us, length us, event | category | flops | bytes accessed | tf_op | source)
XLA Modules:
  0.0 78.4 jit_solution(2774412403519406947)
XLA Ops:
  0.0 0.0 collective-permute-start
  0.0 0.1 pad_add_fusion.ids_ref
  0.1 2.9 %prep.1 = (bf16[1024,256]{1,0:T(8,128)(2,1)S(1)}, bf16[1024,1024]{1,0:T(8,128)(2,1)S(1)}, bf16[512,512]{1,0:T(8,128)(2,1)S(1)}, f32[2,32,128]{2,1,0:T(8,128)S(1)...) custom-call(s32[3]{0:T(128)S(1)} %pad_add_fusion.ids_ref, bf16[256,2048]{1,0:T(8,128)(2,1)} %own_ref.1), custom_call_target="tpu_custom_call" | custom-call | tf_op jit(solution)/shard_map/prep/pallas_call | solution.py:100
  3.0 2.5 %shard_map.37 = (bf16[1024,128]{1,0:T(8,128)(2,1)S(1)}, bf16[1024,512]{1,0:T(8,128)(2,1)S(1)}, bf16[1536,512]{1,0:T(8,128)(2,1)S(1)}) custom-call(s32[3]{0:T(128)S(1)} %pad_add_fusion.ids_ref, bf16[256,2048]{1,0:T(8,128)(2,1)S(1)} %collective-permute-done.other_ref, bf16[1024,256]{1,0:T(8,128)(2,1)S(1)} %get-tuple-element.26.own_ref, ...), custom_call_target="tpu_custom_call" | custom-call | tf_op jit(solution)/shard_map/pallas_call | solution.py:239
  5.5 0.0 copy-start
  5.5 0.0 copy-start.1
  5.5 2.5 %shard_map.39 = (bf16[1024,128]{1,0:T(8,128)(2,1)S(1)}, bf16[1024,128]{1,0:T(8,128)(2,1)S(1)}) custom-call(s32[3]{0:T(128)S(1)} %pad_add_fusion.ids_ref, bf16[1024,512]{1,0:T(8,128)(2,1)S(1)} %get-tuple-element.32.xs_ref, bf16[1536,512]{1,0:T(8,128)(2,1)S(1)} %get-tuple-element.33.rest_ref, f32[5,32,128]{2,1,0:T(8,128)S(1)} %get-tuple-element.31.outer_ref), custom_call_target="tpu_custom_call" | custom-call | tf_op jit(solution)/shard_map/pallas_call | solution.py:243
  8.1 2.3 %collective-permute-start.2 = (bf16[1024,128]{1,0:T(8,128)(2,1)S(1)}, bf16[1024,128]{1,0:T(8,128)(2,1)S(1)}, u32[]{:S(2)}, u32[]{:S(2)}) collective-permute-start(bf16[1024,128]{1,0:T(8,128)(2,1)S(1)} %get-tuple-element.36), channel_id=1, source_target_pairs={{0,32},{1,33},{2,34},{3,35},{32,0},{33,1},{34,2},{35,3},{4,36},{5,... | collective-permute-start | bytes 786440 | tf_op jit(solution)/shard_map/ppermute | solution.py:374
  10.4 0.4 collective-permute-start.3
  10.8 1.7 %collective-permute-start.1 = (bf16[1024,128]{1,0:T(8,128)(2,1)S(1)}, bf16[1024,128]{1,0:T(8,128)(2,1)S(1)}, u32[]{:S(2)}, u32[]{:S(2)}) collective-permute-start(bf16[1024,128]{1,0:T(8,128)(2,1)S(1)} %get-tuple-element.35), channel_id=1, source_target_pairs={{0,2},{1,3},{2,0},{3,1},{32,34},{33,35},{34,32},{35,33},{4,6},{5,7... | collective-permute-start | bytes 786440 | tf_op jit(solution)/shard_map/ppermute | solution.py:374
  12.6 1.2 %collective-permute-start.5 = (bf16[6,128,256]{2,1,0:T(8,128)(2,1)S(1)}, bf16[6,128,256]{2,1,0:T(8,128)(2,1)S(1)}, u32[]{:S(2)}, u32[]{:S(2)}) collective-permute-start(bf16[6,128,256]{2,1,0:T(8,128)(2,1)S(1)} %bitcast.9), channel_id=1, source_target_pairs={{0,34},{1,35},{2,32},{3,33},{32,2},{33,3},{34,0},{35,1},{4,38},{5,... | collective-permute-start | bytes 1179656 | tf_op jit(solution)/shard_map/ppermute | solution.py:374
  13.7 1.8 %collective-permute-start.4 = (bf16[6,128,256]{2,1,0:T(8,128)(2,1)S(1)}, bf16[6,128,256]{2,1,0:T(8,128)(2,1)S(1)}, u32[]{:S(2)}, u32[]{:S(2)}) collective-permute-start(bf16[6,128,256]{2,1,0:T(8,128)(2,1)S(1)} %bitcast.10), channel_id=1, source_target_pairs={{0,32},{1,33},{2,34},{3,35},{32,0},{33,1},{34,2},{35,3},{4,36},{5,... | collective-permute-start | bytes 1179656 | tf_op jit(solution)/shard_map/ppermute | solution.py:374
  15.6 1.9 %shard_map.38 = (f32[1024,128]{1,0:T(8,128)S(1)}, f32[512,128]{1,0:T(8,128)S(1)}) custom-call(s32[3]{0:T(128)S(1)} %pad_add_fusion.ids_ref, bf16[1024,512]{1,0:T(8,128)(2,1)S(1)} %get-tuple-element.32.xs_ref, bf16[1536,512]{1,0:T(8,128)(2,1)S(1)} %get-tuple-element.33.rest_ref, f32[5,32,128]{2,1,0:T(8,128)S(1)} %get-tuple-element.31.outer_ref, ...), custom_call_target="tpu_custom_call" | custom-call | tf_op jit(solution)/shard_map/pallas_call | solution.py:248
  17.4 0.1 collective-permute-done.2
  17.6 7.6 %collective-permute-done.3 = bf16[1024,128]{1,0:T(8,128)(2,1)S(1)} collective-permute-done((bf16[1024,128]{1,0:T(8,128)(2,1)S(1)}, bf16[1024,128]{1,0:T(8,128)(2,1)S(1)}, u32[]{:S(2)}, u32[]{:S(2)}) %collective-permute-start.3) | collective-permute-done | bytes 262176 | tf_op jit(solution)/shard_map/ppermute | solution.py:374
  25.2 0.1 add_convert_fusion.cross_ref
  25.3 0.1 collective-permute-start.7
  25.4 0.1 add_convert_fusion.1.same_ref
  25.5 0.6 collective-permute-start.6
  26.0 6.9 %collective-permute-done.5.w3_ref = bf16[6,128,256]{2,1,0:T(8,128)(2,1)S(1)} collective-permute-done((bf16[6,128,256]{2,1,0:T(8,128)(2,1)S(1)}, bf16[6,128,256]{2,1,0:T(8,128)(2,1)S(1)}, u32[]{:S(2)}, u32[]{:S(2)}) %collective-permute-start.5) | collective-permute-done | bytes 393248 | tf_op jit(solution)/shard_map/ppermute | solution.py:374
  32.9 1.7 %collective-permute-start.9 = (bf16[3,128,256]{2,1,0:T(8,128)(2,1)S(1)}, bf16[3,128,256]{2,1,0:T(8,128)(2,1)S(1)}, u32[]{:S(2)}, u32[]{:S(2)}) collective-permute-start(bf16[3,128,256]{2,1,0:T(8,128)(2,1)S(1)} %slice.9), channel_id=1, source_target_pairs={{0,32},{1,33},{2,34},{3,35},{32,0},{33,1},{34,2},{35,3},{4,36},{5,... | collective-permute-start | bytes 589832 | tf_op jit(solution)/shard_map/ppermute | solution.py:374
  34.6 1.2 %collective-permute-start.8 = (bf16[3,128,256]{2,1,0:T(8,128)(2,1)S(1)}, bf16[3,128,256]{2,1,0:T(8,128)(2,1)S(1)}, u32[]{:S(2)}, u32[]{:S(2)}) collective-permute-start(bf16[3,128,256]{2,1,0:T(8,128)(2,1)S(1)} %slice.8), channel_id=1, source_target_pairs={{0,34},{1,35},{2,32},{3,33},{32,2},{33,3},{34,0},{35,1},{4,38},{5,... | collective-permute-start | bytes 589832 | tf_op jit(solution)/shard_map/ppermute | solution.py:374
  35.8 0.6 shard_map.41.p3_ref
  36.4 0.7 shard_map.40
  37.1 1.4 %shard_map.42 = (bf16[1024,512]{1,0:T(8,128)(2,1)S(1)}, f32[1024,384]{1,0:T(8,128)S(1)}, f32[1024,384]{1,0:T(8,128)S(1)}) custom-call(s32[3]{0:T(128)S(1)} %pad_add_fusion.ids_ref, bf16[1024,128]{1,0:T(8,128)(2,1)S(1)} %add_convert_fusion.1.same_ref, bf16[1024,128]{1,0:T(8,128)(2,1)S(1)} %add_convert_fusion.cross_ref, ...), custom_call_target="tpu_custom_call" | custom-call | tf_op jit(solution)/shard_map/pallas_call | solution.py:336
  38.5 1.4 %shard_map.43 = (bf16[4,2,8,32,128]{4,3,2,1,0:T(8,128)(2,1)S(1)}, bf16[1024,512]{1,0:T(8,128)(2,1)S(1)}, f32[1024,384]{1,0:T(8,128)S(1)}) custom-call(s32[3]{0:T(128)S(1)} %pad_add_fusion.ids_ref, bf16[1024,128]{1,0:T(8,128)(2,1)S(1)} %collective-permute-done.6.same_ref, bf16[1024,128]{1,0:T(8,128)(2,1)S(1)} %collective-permute-done.7.cross_ref, ...), custom_call_target="tpu_custom_call" | custom-call | tf_op jit(solution)/shard_map/pallas_call | solution.py:340
  40.0 1.0 %collective-permute-done.8.w2a_ref = bf16[3,128,256]{2,1,0:T(8,128)(2,1)S(1)} collective-permute-done((bf16[3,128,256]{2,1,0:T(8,128)(2,1)S(1)}, bf16[3,128,256]{2,1,0:T(8,128)(2,1)S(1)}, u32[]{:S(2)}, u32[]{:S(2)}) %collective-permute-start.8) | collective-permute-done | bytes 196640 | tf_op jit(solution)/shard_map/ppermute | solution.py:374
  41.0 1.3 %shard_map.44 = bf16[4,2,8,32,128]{4,3,2,1,0:T(8,128)(2,1)S(1)} custom-call(s32[3]{0:T(128)S(1)} %pad_add_fusion.ids_ref, bf16[1024,512]{1,0:T(8,128)(2,1)S(1)} %get-tuple-element.40.own_ref, bf16[1024,512]{1,0:T(8,128)(2,1)S(1)} %get-tuple-element.44.sib_ref, f32[1024,384]{1,0:T(8,128)S(1)} %get-tuple-element.45.acc_ref, ...), custom_call_target="tpu_custom_call", output_to_operand_aliasing={{}: (7, {})} | custom-call | tf_op jit(solution)/shard_map/pallas_call | solution.py:344
  42.3 15.6 %all_to_all.10 = bf16[8,8,32,128]{3,2,1,0:T(8,128)(2,1)S(1)} all-to-all(bf16[8,8,32,128]{3,2,1,0:T(8,128)(2,1)S(1)} %bitcast.8), channel_id=1, replica_groups=mesh['y'=4,'xlo'=2,'z'=8,'xhi'=2,'core'=2] {'y','xhi'}, dimensions={0} | all-to-all | bytes 1048576 | tf_op jit(solution)/shard_map/all_to_all | solution.py:400
  57.9 0.6 shard_map.45
  58.5 18.7 %all_to_all.11.got_ref = f32[8,2,32,128]{3,2,1,0:T(8,128)S(1)} all-to-all(f32[8,2,32,128]{3,2,1,0:T(8,128)S(1)} %shard_map.45), channel_id=1, replica_groups=mesh['y'=4,'xlo'=2,'z'=8,'xhi'=2,'core'=2] {'z'}, dimensions={0} | all-to-all | bytes 524288 | tf_op jit(solution)/shard_map/all_to_all | solution.py:402
  77.3 1.2 %shard_map.46 = f32[32,2,128]{2,1,0:T(2,128)} custom-call(s32[3]{0:T(128)S(1)} %pad_add_fusion.ids_ref, f32[8,2,32,128]{3,2,1,0:T(8,128)S(1)} %all_to_all.11.got_ref), custom_call_target="tpu_custom_call" | custom-call | tf_op jit(solution)/shard_map/pallas_call | solution.py:366
  (10 shorter events, 0.0 us)
Async XLA Ops:
  0.0 3.0 %collective-permute-start = (bf16[256,2048]{1,0:T(8,128)(2,1)}, bf16[256,2048]{1,0:T(8,128)(2,1)S(1)}, u32[]{:S(2)}, u32[]{:S(2)}) collective-permute-start(bf16[256,2048]{1,0:T(8,128)(2,1)} %own_ref.1), channel_id=1, source_target_pairs={{0,1},{1,0},{2,3},{3,2},{32,33},{33,32},{34,35},{35,34},{4,5},{5,4... | collective-permute-start | bytes 3145736 | tf_op jit(solution)/shard_map/ppermute | solution.py:374
  5.5 7.1 %copy-start = (bf16[3,2,128,256]{3,2,1,0:T(8,128)(2,1)S(1)}, bf16[3,2,128,256]{3,2,1,0:T(8,128)(2,1)}, u32[]{:S(2)}) copy-start(bf16[3,2,128,256]{3,2,1,0:T(8,128)(2,1)} %param.4) | copy-start | bytes 1179652
  5.5 10.0 %copy-start.1 = (s32[2048]{0:T(1024)S(1)}, s32[2048]{0:T(1024)}, u32[]{:S(2)}) copy-start(s32[2048]{0:T(1024)} %param.5) | copy-start | bytes 24580
  8.1 9.5 %collective-permute-start.2 = (bf16[1024,128]{1,0:T(8,128)(2,1)S(1)}, bf16[1024,128]{1,0:T(8,128)(2,1)S(1)}, u32[]{:S(2)}, u32[]{:S(2)}) collective-permute-start(bf16[1024,128]{1,0:T(8,128)(2,1)S(1)} %get-tuple-element.36), channel_id=1, source_target_pairs={{0,32},{1,33},{2,34},{3,35},{32,0},{33,1},{34,2},{35,3},{4,36},{5,... | collective-permute-start | bytes 786440 | tf_op jit(solution)/shard_map/ppermute | solution.py:374
  10.4 14.8 %collective-permute-start.3 = (bf16[1024,128]{1,0:T(8,128)(2,1)S(1)}, bf16[1024,128]{1,0:T(8,128)(2,1)S(1)}, u32[]{:S(2)}, u32[]{:S(2)}) collective-permute-start(bf16[1024,128]{1,0:T(8,128)(2,1)S(1)} %get-tuple-element.37), channel_id=1, source_target_pairs={{0,34},{1,35},{2,32},{3,33},{32,2},{33,3},{34,0},{35,1},{4,38},{5,... | collective-permute-start | bytes 786440 | tf_op jit(solution)/shard_map/ppermute | solution.py:374
  10.8 14.5 %collective-permute-start.1 = (bf16[1024,128]{1,0:T(8,128)(2,1)S(1)}, bf16[1024,128]{1,0:T(8,128)(2,1)S(1)}, u32[]{:S(2)}, u32[]{:S(2)}) collective-permute-start(bf16[1024,128]{1,0:T(8,128)(2,1)S(1)} %get-tuple-element.35), channel_id=1, source_target_pairs={{0,2},{1,3},{2,0},{3,1},{32,34},{33,35},{34,32},{35,33},{4,6},{5,7... | collective-permute-start | bytes 786440 | tf_op jit(solution)/shard_map/ppermute | solution.py:374
  12.6 20.3 %collective-permute-start.5 = (bf16[6,128,256]{2,1,0:T(8,128)(2,1)S(1)}, bf16[6,128,256]{2,1,0:T(8,128)(2,1)S(1)}, u32[]{:S(2)}, u32[]{:S(2)}) collective-permute-start(bf16[6,128,256]{2,1,0:T(8,128)(2,1)S(1)} %bitcast.9), channel_id=1, source_target_pairs={{0,34},{1,35},{2,32},{3,33},{32,2},{33,3},{34,0},{35,1},{4,38},{5,... | collective-permute-start | bytes 1179656 | tf_op jit(solution)/shard_map/ppermute | solution.py:374
  13.7 20.8 %collective-permute-start.4 = (bf16[6,128,256]{2,1,0:T(8,128)(2,1)S(1)}, bf16[6,128,256]{2,1,0:T(8,128)(2,1)S(1)}, u32[]{:S(2)}, u32[]{:S(2)}) collective-permute-start(bf16[6,128,256]{2,1,0:T(8,128)(2,1)S(1)} %bitcast.10), channel_id=1, source_target_pairs={{0,32},{1,33},{2,34},{3,35},{32,0},{33,1},{34,2},{35,3},{4,36},{5,... | collective-permute-start | bytes 1179656 | tf_op jit(solution)/shard_map/ppermute | solution.py:374
  25.3 13.2 %collective-permute-start.7 = (bf16[1024,128]{1,0:T(8,128)(2,1)S(1)}, bf16[1024,128]{1,0:T(8,128)(2,1)S(1)}, u32[]{:S(2)}, u32[]{:S(2)}) collective-permute-start(bf16[1024,128]{1,0:T(8,128)(2,1)S(1)} %add_convert_fusion.cross_ref), channel_id=1, source_target_pairs={{0,1},{1,0},{2,3},{3,2},{32,33},{33,32},{34,35},{35,34},{4,5},{5,4... | collective-permute-start | bytes 786440 | tf_op jit(solution)/shard_map/ppermute | solution.py:374
  25.5 13.1 %collective-permute-start.6 = (bf16[1024,128]{1,0:T(8,128)(2,1)S(1)}, bf16[1024,128]{1,0:T(8,128)(2,1)S(1)}, u32[]{:S(2)}, u32[]{:S(2)}) collective-permute-start(bf16[1024,128]{1,0:T(8,128)(2,1)S(1)} %add_convert_fusion.1.same_ref), channel_id=1, source_target_pairs={{0,1},{1,0},{2,3},{3,2},{32,33},{33,32},{34,35},{35,34},{4,5},{5,4... | collective-permute-start | bytes 786440 | tf_op jit(solution)/shard_map/ppermute | solution.py:374
  32.9 7.1 %collective-permute-start.9 = (bf16[3,128,256]{2,1,0:T(8,128)(2,1)S(1)}, bf16[3,128,256]{2,1,0:T(8,128)(2,1)S(1)}, u32[]{:S(2)}, u32[]{:S(2)}) collective-permute-start(bf16[3,128,256]{2,1,0:T(8,128)(2,1)S(1)} %slice.9), channel_id=1, source_target_pairs={{0,32},{1,33},{2,34},{3,35},{32,0},{33,1},{34,2},{35,3},{4,36},{5,... | collective-permute-start | bytes 589832 | tf_op jit(solution)/shard_map/ppermute | solution.py:374
  34.6 6.4 %collective-permute-start.8 = (bf16[3,128,256]{2,1,0:T(8,128)(2,1)S(1)}, bf16[3,128,256]{2,1,0:T(8,128)(2,1)S(1)}, u32[]{:S(2)}, u32[]{:S(2)}) collective-permute-start(bf16[3,128,256]{2,1,0:T(8,128)(2,1)S(1)} %slice.8), channel_id=1, source_target_pairs={{0,34},{1,35},{2,32},{3,33},{32,2},{33,3},{34,0},{35,1},{4,38},{5,... | collective-permute-start | bytes 589832 | tf_op jit(solution)/shard_map/ppermute | solution.py:374

commit v12 on v10

--- a/solution.py
+++ b/solution.py
@@ -263,14 +263,13 @@
         out_ref[:, pl.ds(side, 1), y] = both[y][:, None]
 
 
-def place_rows(l_ref, xl, src):
+def place_rows(l_ref, src):
     for r in range(0, 512, 64):
         sr, si = src[r : r + 64, :], src[512 + r : 576 + r, :]
-        c0, c1 = slice(xl * 256, xl * 256 + 128), slice(xl * 256 + 128, xl * 256 + 256)
-        l_ref[r : r + 64, c0] = sr
-        l_ref[r : r + 64, c1] = -si
-        l_ref[512 + r : 576 + r, c0] = si
-        l_ref[512 + r : 576 + r, c1] = sr
+        l_ref[r : r + 64, 0:128] = sr
+        l_ref[r : r + 64, 128:256] = -si
+        l_ref[512 + r : 576 + r, 0:128] = si
+        l_ref[512 + r : 576 + r, 128:256] = sr
 
 
 def place_weights(core, w_ref, col, blocks):
@@ -290,35 +289,37 @@
     place_weights(ids_ref[0], p3_ref, 0, [w3_ref.at[i] for i in range(6)])
 
 
-def half_sums(which, l_ref, p0_ref, p1_ref, p3_ref):
-    both = product(l_ref[:, 256:512], jnp.concatenate([p1_ref[which], p3_ref[which]], 0))
-    return product(l_ref[:, 0:256], p0_ref[which]) + both[:, 0:384], both[:, 384:768]
-
-
-def own_kernel(ids_ref, same_ref, cross_ref, p0_ref, p1_ref, p3_ref, l_ref, near_ref, far_ref):
-    place_rows(l_ref, 0, same_ref)
-    place_rows(l_ref, 1, cross_ref)
-    near_ref[...], far_ref[...] = half_sums(0, l_ref, p0_ref, p1_ref, p3_ref)
-
-
-def sib_kernel(
-    ids_ref, same_ref, cross_ref, p0_ref, p1_ref, p3_ref, near_ref, begun_ref, group_ref, out_ref, l_ref, far_ref
-):
-    place_rows(l_ref, 0, same_ref)
-    place_rows(l_ref, 1, cross_ref)
-    near, far = half_sums(1, l_ref, p0_ref, p1_ref, p3_ref)
+def early_kernel(ids_ref, own_ref, sib_ref, p0_ref, l_ref, near_ref):
+    place_rows(l_ref.at[0], own_ref)
+    place_rows(l_ref.at[1], sib_ref)
+    near_ref[...] = product(l_ref[0], p0_ref[0]) + product(l_ref[1], p0_ref[1])
+
+
+def cross_sums(which, l_ref, p1_ref, p3_ref):
+    both = product(l_ref[...], jnp.concatenate([p1_ref[which], p3_ref[which]], 0))
+    return both[:, 0:384], both[:, 384:768]
+
+
+def own_kernel(ids_ref, cross_ref, p1_ref, p3_ref, begun_ref, near_ref, far_ref, l_ref):
+    place_rows(l_ref, cross_ref)
+    near, far_ref[...] = cross_sums(0, l_ref, p1_ref, p3_ref)
+    near_ref[...] = begun_ref[...] + near
+
+
+def sib_kernel(ids_ref, cross_ref, p1_ref, p3_ref, near_ref, begun_ref, group_ref, out_ref, far_ref, l_ref):
+    place_rows(l_ref, cross_ref)
+    near, far = cross_sums(1, l_ref, p1_ref, p3_ref)
     store_beams(ids_ref[1], near_ref[...] + near, group_ref, out_ref)
     far_ref[...] = begun_ref[...] + far
 
 
-def far_kernel(ids_ref, own_ref, sib_ref, acc_ref, group_ref, w2a_ref, w2b_ref, begun_ref, out_ref, w_ref):
+def far_kernel(ids_ref, l_ref, acc_ref, group_ref, w2a_ref, w2b_ref, begun_ref, out_ref, w_ref):
     place_weights(ids_ref[0], w_ref, 0, [w2a_ref.at[i] for i in range(3)] + [w2b_ref.at[i] for i in range(3)])
-    acc = acc_ref[...] + product(own_ref[:, 0:256], w_ref[0]) + product(sib_ref[:, 0:256], w_ref[1])
+    acc = acc_ref[...] + product(l_ref[0], w_ref[0]) + product(l_ref[1], w_ref[1])
     store_beams(1 - ids_ref[1], acc, group_ref, out_ref)
 
 
 PARTS = jax.ShapeDtypeStruct((8, 2, 4, 32, 128), BF16)
-ROWS = jax.ShapeDtypeStruct((1024, 512), BF16)
 SUMS = jax.ShapeDtypeStruct((1024, 384), F32)
 
 
@@ -333,16 +334,23 @@
     return call(pack_side_kernel, 1, PACKED, [])(*args)
 
 
+LHS = pltpu.VMEM((1024, 256), BF16)
+
+
+def form_early(*args):
+    return call(early_kernel, 3, [jax.ShapeDtypeStruct((2, 1024, 256), BF16), SUMS], [])(*args)
+
+
 def form_own(*args):
-    return call(own_kernel, 5, [ROWS, SUMS, SUMS], [])(*args)
+    return call(own_kernel, 4, [SUMS, SUMS], [LHS])(*args)
 
 
 def form_sib(*args):
-    return call(sib_kernel, 8, [PARTS, ROWS, SUMS], [])(*args)
+    return call(sib_kernel, 6, [PARTS, SUMS], [LHS])(*args)
 
 
 def form_far(*args):
-    return call(far_kernel, 7, PARTS, [pltpu.VMEM((2, 384, 256), BF16)], {7: 0})(*args)
+    return call(far_kernel, 6, PARTS, [pltpu.VMEM((2, 384, 256), BF16)], {6: 0})(*args)
 
 
 def add_kernel(got_ref, out_ref):
@@ -393,11 +401,12 @@
     w2a = exchange(w1[:3], 6)
     w2b = exchange(w3[3:], 4)
     p3 = pack_side(ids, w3)
+    lhs, near = form_early(ids, same, same_sib, p0)
     cross = (got1.astype(F32) + got2.astype(F32)).astype(BF16)
     cross_sib = exchange(cross, 1)
-    lhs, near, far = form_own(ids, same, cross, p0, p1, p3)
-    begun, lhs_sib, acc_far = form_sib(ids, same_sib, cross_sib, p0, p1, p3, near, far, group)
-    parts = form_far(ids, lhs, lhs_sib, acc_far, group, w2a, w2b, begun)
+    near, far = form_own(ids, cross, p1, p3, near)
+    begun, far = form_sib(ids, cross_sib, p1, p3, near, far, group)
+    parts = form_far(ids, lhs, far, group, w2a, w2b, begun)
     got = lax.all_to_all(parts.reshape(64, 32, 128), ("z", "xhi", "y"), 0, 0, tiled=True)
     return add(got)
 

time: 73.8 us -> 71.3 us (0.966)
  the two profiles are of different devices: /device:TPU:2 before, /device:TPU:24 now
where the time goes in v12:
time: 71.3 us; the launch traced here: 71.2 us
  blocking collectives  31.4 us (44%)
  Pallas kernels  16.7 us (23%)
  waiting for transfers between devices  11.7 us (16%)
  starting transfers between devices  11 us (15%)
    all_to_all x1, blocking collectives, shards(): lax.all_to_all(parts.reshape(64, 32, 128), ('z', 'xhi', 'y'), 0, 0, tiled...  31.4 us
    ppermute x10, waiting for transfers between devices, exchange(): return lax.ppermute(value, ring, [(i, i ^ flip) for i in range(8)])  11.7 us
    ppermute x10, starting transfers between devices, exchange(): return lax.ppermute(value, ring, [(i, i ^ flip) for i in range(8)])  11 us
    pallas_call x1, Pallas kernels, prep(): pl.pallas_call(prep_kernel, grid_spec=pltpu.PrefetchScalarGridSpec(num_sc...  2.89 us
    pallas_call x1, Pallas kernels, dft_first(): return call(first_kernel, 7, outs, [pltpu.VMEM((512, 1024), F32)])(*args)  2.53 us
    pallas_call x1, Pallas kernels, dft_next(): call(next_kernel, 3, [PIECE, PIECE], [pltpu.VMEM((2, 512, 1024), F32)])  2.52 us
    pallas_call x1, Pallas kernels, dft_last(): return call(last_kernel, 4, outs, [pltpu.VMEM((512, 1024), F32)])(*args)  1.87 us
  transfers between devices with their start and end apart: 10, of which 4 were waited for; matrix products, arithmetic and copies ran while one was open for 0% of the time, Pallas kernels for 17%

profile of v12, /device:TPU:24, one launch (start us, length us, event | category | flops | bytes accessed | tf_op | source)
XLA Modules:
  0.0 71.2 jit_solution(299698437348285227)
XLA Ops:
  0.0 0.0 collective-permute-start
  0.0 0.1 pad_add_fusion.ids_ref
  0.1 2.9 %prep.1 = (bf16[1024,256]{1,0:T(8,128)(2,1)S(1)}, bf16[1024,1024]{1,0:T(8,128)(2,1)S(1)}, bf16[512,512]{1,0:T(8,128)(2,1)S(1)}, f32[2,32,128]{2,1,0:T(8,128)S(1)...) custom-call(s32[3]{0:T(128)S(1)} %pad_add_fusion.ids_ref, bf16[256,2048]{1,0:T(8,128)(2,1)} %own_ref.1), custom_call_target="tpu_custom_call" | custom-call | tf_op jit(solution)/shard_map/prep/pallas_call | solution.py:100
  3.0 0.0 collective-permute-done.other_ref
  3.0 2.5 %shard_map.37 = (bf16[1024,128]{1,0:T(8,128)(2,1)S(1)}, bf16[1024,512]{1,0:T(8,128)(2,1)S(1)}, bf16[1536,512]{1,0:T(8,128)(2,1)S(1)}) custom-call(s32[3]{0:T(128)S(1)} %pad_add_fusion.ids_ref, bf16[256,2048]{1,0:T(8,128)(2,1)S(1)} %collective-permute-done.other_ref, bf16[1024,256]{1,0:T(8,128)(2,1)S(1)} %get-tuple-element.26.own_ref, ...), custom_call_target="tpu_custom_call" | custom-call | tf_op jit(solution)/shard_map/pallas_call | solution.py:239
  5.5 0.0 copy-start
  5.5 0.0 copy-start.1
  5.5 3.1 %collective-permute-start.1 = (bf16[1024,128]{1,0:T(8,128)(2,1)S(1)}, bf16[1024,128]{1,0:T(8,128)(2,1)S(1)}, u32[]{:S(2)}, u32[]{:S(2)}) collective-permute-start(bf16[1024,128]{1,0:T(8,128)(2,1)S(1)} %get-tuple-element.35), channel_id=1, source_target_pairs={{0,2},{1,3},{2,0},{3,1},{32,34},{33,35},{34,32},{35,33},{4,6},{5,7... | collective-permute-start | bytes 786440 | tf_op jit(solution)/shard_map/ppermute | solution.py:383
  8.7 2.5 %shard_map.41 = (bf16[1024,128]{1,0:T(8,128)(2,1)S(1)}, bf16[1024,128]{1,0:T(8,128)(2,1)S(1)}) custom-call(s32[3]{0:T(128)S(1)} %pad_add_fusion.ids_ref, bf16[1024,512]{1,0:T(8,128)(2,1)S(1)} %get-tuple-element.32.xs_ref, bf16[1536,512]{1,0:T(8,128)(2,1)S(1)} %get-tuple-element.33.rest_ref, f32[5,32,128]{2,1,0:T(8,128)S(1)} %get-tuple-element.31.outer_ref), custom_call_target="tpu_custom_call" | custom-call | tf_op jit(solution)/shard_map/pallas_call | solution.py:243
  11.2 1.2 %collective-permute-start.5 = (bf16[1024,128]{1,0:T(8,128)(2,1)S(1)}, bf16[1024,128]{1,0:T(8,128)(2,1)S(1)}, u32[]{:S(2)}, u32[]{:S(2)}) collective-permute-start(bf16[1024,128]{1,0:T(8,128)(2,1)S(1)} %get-tuple-element.39), channel_id=1, source_target_pairs={{0,34},{1,35},{2,32},{3,33},{32,2},{33,3},{34,0},{35,1},{4,38},{5,... | collective-permute-start | bytes 786440 | tf_op jit(solution)/shard_map/ppermute | solution.py:383
  12.4 2.0 %collective-permute-start.3 = (bf16[6,128,256]{2,1,0:T(8,128)(2,1)S(1)}, bf16[6,128,256]{2,1,0:T(8,128)(2,1)S(1)}, u32[]{:S(2)}, u32[]{:S(2)}) collective-permute-start(bf16[6,128,256]{2,1,0:T(8,128)(2,1)S(1)} %bitcast.7), channel_id=1, source_target_pairs={{0,32},{1,33},{2,34},{3,35},{32,0},{33,1},{34,2},{35,3},{4,36},{5,... | collective-permute-start | bytes 1179656 | tf_op jit(solution)/shard_map/ppermute | solution.py:383
  14.4 2.1 %collective-permute-start.7 = (bf16[6,128,256]{2,1,0:T(8,128)(2,1)S(1)}, bf16[6,128,256]{2,1,0:T(8,128)(2,1)S(1)}, u32[]{:S(2)}, u32[]{:S(2)}) collective-permute-start(bf16[6,128,256]{2,1,0:T(8,128)(2,1)S(1)} %bitcast.8), channel_id=1, source_target_pairs={{0,34},{1,35},{2,32},{3,33},{32,2},{33,3},{34,0},{35,1},{4,38},{5,... | collective-permute-start | bytes 1179656 | tf_op jit(solution)/shard_map/ppermute | solution.py:383
  16.5 1.9 %shard_map.38 = (f32[1024,128]{1,0:T(8,128)S(1)}, f32[512,128]{1,0:T(8,128)S(1)}) custom-call(s32[3]{0:T(128)S(1)} %pad_add_fusion.ids_ref, bf16[1024,512]{1,0:T(8,128)(2,1)S(1)} %get-tuple-element.32.xs_ref, bf16[1536,512]{1,0:T(8,128)(2,1)S(1)} %get-tuple-element.33.rest_ref, f32[5,32,128]{2,1,0:T(8,128)S(1)} %get-tuple-element.31.outer_ref, ...), custom_call_target="tpu_custom_call" | custom-call | tf_op jit(solution)/shard_map/pallas_call | solution.py:248
  18.4 0.0 collective-permute-done.1
  18.4 0.1 add_convert_fusion.1.own_ref
  18.5 0.1 collective-permute-start.2
  18.6 3.1 %collective-permute-done.5 = bf16[1024,128]{1,0:T(8,128)(2,1)S(1)} collective-permute-done((bf16[1024,128]{1,0:T(8,128)(2,1)S(1)}, bf16[1024,128]{1,0:T(8,128)(2,1)S(1)}, u32[]{:S(2)}, u32[]{:S(2)}) %collective-permute-start.5) | collective-permute-done | bytes 262176 | tf_op jit(solution)/shard_map/ppermute | solution.py:383
  21.7 0.4 collective-permute-done.4
  22.0 0.1 add_convert_fusion.cross_ref
  22.1 0.1 collective-permute-start.6
  22.2 7.8 %collective-permute-done.3.w1_ref = bf16[6,128,256]{2,1,0:T(8,128)(2,1)S(1)} collective-permute-done((bf16[6,128,256]{2,1,0:T(8,128)(2,1)S(1)}, bf16[6,128,256]{2,1,0:T(8,128)(2,1)S(1)}, u32[]{:S(2)}, u32[]{:S(2)}) %collective-permute-start.3) | collective-permute-done | bytes 393248 | tf_op jit(solution)/shard_map/ppermute | solution.py:383
  30.0 1.2 %collective-permute-start.8 = (bf16[3,128,256]{2,1,0:T(8,128)(2,1)S(1)}, bf16[3,128,256]{2,1,0:T(8,128)(2,1)S(1)}, u32[]{:S(2)}, u32[]{:S(2)}) collective-permute-start(bf16[3,128,256]{2,1,0:T(8,128)(2,1)S(1)} %slice.8), channel_id=1, source_target_pairs={{0,34},{1,35},{2,32},{3,33},{32,2},{33,3},{34,0},{35,1},{4,38},{5,... | collective-permute-start | bytes 589832 | tf_op jit(solution)/shard_map/ppermute | solution.py:383
  31.2 1.2 %collective-permute-start.9 = (bf16[3,128,256]{2,1,0:T(8,128)(2,1)S(1)}, bf16[3,128,256]{2,1,0:T(8,128)(2,1)S(1)}, u32[]{:S(2)}, u32[]{:S(2)}) collective-permute-start(bf16[3,128,256]{2,1,0:T(8,128)(2,1)S(1)} %slice.9), channel_id=1, source_target_pairs={{0,32},{1,33},{2,34},{3,35},{32,0},{33,1},{34,2},{35,3},{4,36},{5,... | collective-permute-start | bytes 589832 | tf_op jit(solution)/shard_map/ppermute | solution.py:383
  32.4 0.7 shard_map.39
  33.1 0.6 shard_map.42.p3_ref
  33.7 1.3 %shard_map.40 = (bf16[2,1024,256]{2,1,0:T(8,128)(2,1)S(1)}, f32[1024,384]{1,0:T(8,128)S(1)}) custom-call(s32[3]{0:T(128)S(1)} %pad_add_fusion.ids_ref, bf16[1024,128]{1,0:T(8,128)(2,1)S(1)} %add_convert_fusion.1.own_ref, bf16[1024,128]{1,0:T(8,128)(2,1)S(1)} %collective-permute-done.2.sib_ref, bf16[2,384,256]{2,1,0:T(8,128)(2,1)S(1)} %get-tuple-element.36.p0_ref), custom_call_target="tpu_custom_call" | custom-call | tf_op jit(solution)/shard_map/pallas_call | solution.py:341
  35.0 1.2 %shard_map.43 = (f32[1024,384]{1,0:T(8,128)S(1)}, f32[1024,384]{1,0:T(8,128)S(1)}) custom-call(s32[3]{0:T(128)S(1)} %pad_add_fusion.ids_ref, bf16[1024,128]{1,0:T(8,128)(2,1)S(1)} %add_convert_fusion.cross_ref, bf16[2,384,256]{2,1,0:T(8,128)(2,1)S(1)} %get-tuple-element.40.p1_ref, bf16[2,384,256]{2,1,0:T(8,128)(2,1)S(1)} %shard_map.42.p3_ref, ...), custom_call_target="tpu_custom_call" | custom-call | tf_op jit(solution)/shard_map/pallas_call | solution.py:345
  36.2 1.2 %shard_map.44 = (bf16[8,2,4,32,128]{4,3,2,1,0:T(8,128)(2,1)S(1)}, f32[1024,384]{1,0:T(8,128)S(1)}) custom-call(s32[3]{0:T(128)S(1)} %pad_add_fusion.ids_ref, bf16[1024,128]{1,0:T(8,128)(2,1)S(1)} %collective-permute-done.6.cross_ref, bf16[2,384,256]{2,1,0:T(8,128)(2,1)S(1)} %get-tuple-element.40.p1_ref, bf16[2,384,256]{2,1,0:T(8,128)(2,1)S(1)} %shard_map.42.p3_ref, ...), custom_call_target="tpu_custom_call" | custom-call | tf_op jit(solution)/shard_map/pallas_call | solution.py:349
  37.4 0.4 collective-permute-done.8.w2a_ref
  37.8 1.3 %shard_map.45 = bf16[8,2,4,32,128]{4,3,2,1,0:T(8,128)(2,1)S(1)} custom-call(s32[3]{0:T(128)S(1)} %pad_add_fusion.ids_ref, bf16[2,1024,256]{2,1,0:T(8,128)(2,1)S(1)} %get-tuple-element.37.l_ref, f32[1024,384]{1,0:T(8,128)S(1)} %get-tuple-element.45.acc_ref, f32[512,128]{1,0:T(8,128)S(1)} %get-tuple-element.44.group_ref, ...), custom_call_target="tpu_custom_call", output_to_operand_aliasing={{}: (6, {})} | custom-call | tf_op jit(solution)/shard_map/pallas_call | solution.py:353
  39.1 31.4 %all_to_all.5.got_ref = bf16[64,32,128]{2,1,0:T(8,128)(2,1)S(1)} all-to-all(bf16[64,32,128]{2,1,0:T(8,128)(2,1)S(1)} %bitcast.6), channel_id=1, replica_groups=mesh['y'=4,'xlo'=2,'z'=8,'xhi'=2,'core'=2] {'z','xhi','y'}, dimensions={0} | all-to-all | bytes 1048576 | tf_op jit(solution)/shard_map/all_to_all | solution.py:410
  70.5 0.7 add.15
  (9 shorter events, 0.0 us)
Async XLA Ops:
  0.0 3.0 %collective-permute-start = (bf16[256,2048]{1,0:T(8,128)(2,1)}, bf16[256,2048]{1,0:T(8,128)(2,1)S(1)}, u32[]{:S(2)}, u32[]{:S(2)}) collective-permute-start(bf16[256,2048]{1,0:T(8,128)(2,1)} %own_ref.1), channel_id=1, source_target_pairs={{0,1},{1,0},{2,3},{3,2},{32,33},{33,32},{34,35},{35,34},{4,5},{5,4... | collective-permute-start | bytes 3145736 | tf_op jit(solution)/shard_map/ppermute | solution.py:383
  5.5 6.9 %copy-start = (bf16[3,2,128,256]{3,2,1,0:T(8,128)(2,1)S(1)}, bf16[3,2,128,256]{3,2,1,0:T(8,128)(2,1)}, u32[]{:S(2)}) copy-start(bf16[3,2,128,256]{3,2,1,0:T(8,128)(2,1)} %param.4) | copy-start | bytes 1179652
  5.5 11.0 %copy-start.1 = (s32[2048]{0:T(1024)S(1)}, s32[2048]{0:T(1024)}, u32[]{:S(2)}) copy-start(s32[2048]{0:T(1024)} %param.5) | copy-start | bytes 24580
  5.5 12.9 %collective-permute-start.1 = (bf16[1024,128]{1,0:T(8,128)(2,1)S(1)}, bf16[1024,128]{1,0:T(8,128)(2,1)S(1)}, u32[]{:S(2)}, u32[]{:S(2)}) collective-permute-start(bf16[1024,128]{1,0:T(8,128)(2,1)S(1)} %get-tuple-element.35), channel_id=1, source_target_pairs={{0,2},{1,3},{2,0},{3,1},{32,34},{33,35},{34,32},{35,33},{4,6},{5,7... | collective-permute-start | bytes 786440 | tf_op jit(solution)/shard_map/ppermute | solution.py:383
  11.2 10.5 %collective-permute-start.5 = (bf16[1024,128]{1,0:T(8,128)(2,1)S(1)}, bf16[1024,128]{1,0:T(8,128)(2,1)S(1)}, u32[]{:S(2)}, u32[]{:S(2)}) collective-permute-start(bf16[1024,128]{1,0:T(8,128)(2,1)S(1)} %get-tuple-element.39), channel_id=1, source_target_pairs={{0,34},{1,35},{2,32},{3,33},{32,2},{33,3},{34,0},{35,1},{4,38},{5,... | collective-permute-start | bytes 786440 | tf_op jit(solution)/shard_map/ppermute | solution.py:383
  12.4 9.6 %collective-permute-start.4 = (bf16[1024,128]{1,0:T(8,128)(2,1)S(1)}, bf16[1024,128]{1,0:T(8,128)(2,1)S(1)}, u32[]{:S(2)}, u32[]{:S(2)}) collective-permute-start(bf16[1024,128]{1,0:T(8,128)(2,1)S(1)} %get-tuple-element.38), channel_id=1, source_target_pairs={{0,32},{1,33},{2,34},{3,35},{32,0},{33,1},{34,2},{35,3},{4,36},{5,... | collective-permute-start | bytes 786440 | tf_op jit(solution)/shard_map/ppermute | solution.py:383
  12.4 17.6 %collective-permute-start.3 = (bf16[6,128,256]{2,1,0:T(8,128)(2,1)S(1)}, bf16[6,128,256]{2,1,0:T(8,128)(2,1)S(1)}, u32[]{:S(2)}, u32[]{:S(2)}) collective-permute-start(bf16[6,128,256]{2,1,0:T(8,128)(2,1)S(1)} %bitcast.7), channel_id=1, source_target_pairs={{0,32},{1,33},{2,34},{3,35},{32,0},{33,1},{34,2},{35,3},{4,36},{5,... | collective-permute-start | bytes 1179656 | tf_op jit(solution)/shard_map/ppermute | solution.py:383
  14.4 16.8 %collective-permute-start.7 = (bf16[6,128,256]{2,1,0:T(8,128)(2,1)S(1)}, bf16[6,128,256]{2,1,0:T(8,128)(2,1)S(1)}, u32[]{:S(2)}, u32[]{:S(2)}) collective-permute-start(bf16[6,128,256]{2,1,0:T(8,128)(2,1)S(1)} %bitcast.8), channel_id=1, source_target_pairs={{0,34},{1,35},{2,32},{3,33},{32,2},{33,3},{34,0},{35,1},{4,38},{5,... | collective-permute-start | bytes 1179656 | tf_op jit(solution)/shard_map/ppermute | solution.py:383
  18.5 15.2 %collective-permute-start.2 = (bf16[1024,128]{1,0:T(8,128)(2,1)S(1)}, bf16[1024,128]{1,0:T(8,128)(2,1)S(1)}, u32[]{:S(2)}, u32[]{:S(2)}) collective-permute-start(bf16[1024,128]{1,0:T(8,128)(2,1)S(1)} %add_convert_fusion.1.own_ref), channel_id=1, source_target_pairs={{0,1},{1,0},{2,3},{3,2},{32,33},{33,32},{34,35},{35,34},{4,5},{5,4... | collective-permute-start | bytes 786440 | tf_op jit(solution)/shard_map/ppermute | solution.py:383
  22.1 14.0 %collective-permute-start.6 = (bf16[1024,128]{1,0:T(8,128)(2,1)S(1)}, bf16[1024,128]{1,0:T(8,128)(2,1)S(1)}, u32[]{:S(2)}, u32[]{:S(2)}) collective-permute-start(bf16[1024,128]{1,0:T(8,128)(2,1)S(1)} %add_convert_fusion.cross_ref), channel_id=1, source_target_pairs={{0,1},{1,0},{2,3},{3,2},{32,33},{33,32},{34,35},{35,34},{4,5},{5,4... | collective-permute-start | bytes 786440 | tf_op jit(solution)/shard_map/ppermute | solution.py:383
  30.0 7.8 %collective-permute-start.8 = (bf16[3,128,256]{2,1,0:T(8,128)(2,1)S(1)}, bf16[3,128,256]{2,1,0:T(8,128)(2,1)S(1)}, u32[]{:S(2)}, u32[]{:S(2)}) collective-permute-start(bf16[3,128,256]{2,1,0:T(8,128)(2,1)S(1)} %slice.8), channel_id=1, source_target_pairs={{0,34},{1,35},{2,32},{3,33},{32,2},{33,3},{34,0},{35,1},{4,38},{5,... | collective-permute-start | bytes 589832 | tf_op jit(solution)/shard_map/ppermute | solution.py:383
  31.2 6.6 %collective-permute-start.9 = (bf16[3,128,256]{2,1,0:T(8,128)(2,1)S(1)}, bf16[3,128,256]{2,1,0:T(8,128)(2,1)S(1)}, u32[]{:S(2)}, u32[]{:S(2)}) collective-permute-start(bf16[3,128,256]{2,1,0:T(8,128)(2,1)S(1)} %slice.9), channel_id=1, source_target_pairs={{0,32},{1,33},{2,34},{3,35},{32,0},{33,1},{34,2},{35,3},{4,36},{5,... | collective-permute-start | bytes 589832 | tf_op jit(solution)/shard_map/ppermute | solution.py:383

commit v13 on v12

--- a/solution.py
+++ b/solution.py
@@ -314,7 +314,7 @@
 
 
 def far_kernel(ids_ref, l_ref, acc_ref, group_ref, w2a_ref, w2b_ref, begun_ref, out_ref, w_ref):
-    place_weights(ids_ref[0], w_ref, 0, [w2a_ref.at[i] for i in range(3)] + [w2b_ref.at[i] for i in range(3)])
+    place_weights(ids_ref[0], w_ref, 0, [w2a_ref.at[i] for i in range(2)] + [w2b_ref.at[i] for i in range(4)])
     acc = acc_ref[...] + product(l_ref[0], w_ref[0]) + product(l_ref[1], w_ref[1])
     store_beams(1 - ids_ref[1], acc, group_ref, out_ref)
 
@@ -398,8 +398,8 @@
     same = (mine + got0.astype(F32)).astype(BF16)
     same_sib = exchange(same, 1)
     p0, p1 = pack_near(ids, blocks, w1)
-    w2a = exchange(w1[:3], 6)
-    w2b = exchange(w3[3:], 4)
+    w2a = exchange(w1[:2], 6)
+    w2b = exchange(w3[2:], 4)
     p3 = pack_side(ids, w3)
     lhs, near = form_early(ids, same, same_sib, p0)
     cross = (got1.astype(F32) + got2.astype(F32)).astype(BF16)

time: 71.3 us -> 72.7 us (1.020)
  starting transfers between devices: 11 us -> 12.6 us
    ppermute x10, starting transfers between devices: 11 us -> 12.6 us  [exchange(): return lax.ppermute(value, ring, [(i, i ^ flip) for i in range(8)])]
  transfers between devices with their start and end apart: 10 -> 10, of which waited for: 4 -> 3; matrix products, arithmetic and copies ran while one was open for 0% -> 0% of each run, Pallas kernels for 17% -> 17%
where the time goes in v13:
time: 72.7 us; the launch traced here: 72.5 us
  blocking collectives  31.6 us (43%)
  Pallas kernels  16.8 us (23%)
  starting transfers between devices  12.6 us (17%)
  waiting for transfers between devices  11.2 us (15%)
    all_to_all x1, blocking collectives, shards(): lax.all_to_all(parts.reshape(64, 32, 128), ('z', 'xhi', 'y'), 0, 0, tiled...  31.6 us
    ppermute x10, starting transfers between devices, exchange(): return lax.ppermute(value, ring, [(i, i ^ flip) for i in range(8)])  12.6 us
    ppermute x10, waiting for transfers between devices, exchange(): return lax.ppermute(value, ring, [(i, i ^ flip) for i in range(8)])  11.2 us
    pallas_call x1, Pallas kernels, prep(): pl.pallas_call(prep_kernel, grid_spec=pltpu.PrefetchScalarGridSpec(num_sc...  2.89 us
    pallas_call x1, Pallas kernels, dft_first(): return call(first_kernel, 7, outs, [pltpu.VMEM((512, 1024), F32)])(*args)  2.53 us
    pallas_call x1, Pallas kernels, dft_next(): call(next_kernel, 3, [PIECE, PIECE], [pltpu.VMEM((2, 512, 1024), F32)])  2.52 us
    pallas_call x1, Pallas kernels, dft_last(): return call(last_kernel, 4, outs, [pltpu.VMEM((512, 1024), F32)])(*args)  1.87 us
  transfers between devices with their start and end apart: 10, of which 3 were waited for; matrix products, arithmetic and copies ran while one was open for 0% of the time, Pallas kernels for 17%

profile of v13, /device:TPU:24, one launch (start us, length us, event | category | flops | bytes accessed | tf_op | source)
XLA Modules:
  0.0 72.5 jit_solution(16091828029124444755)
XLA Ops:
  0.0 0.0 collective-permute-start
  0.0 0.1 pad_add_fusion.ids_ref
  0.1 2.9 %prep.1 = (bf16[1024,256]{1,0:T(8,128)(2,1)S(1)}, bf16[1024,1024]{1,0:T(8,128)(2,1)S(1)}, bf16[512,512]{1,0:T(8,128)(2,1)S(1)}, f32[2,32,128]{2,1,0:T(8,128)S(1)...) custom-call(s32[3]{0:T(128)S(1)} %pad_add_fusion.ids_ref, bf16[256,2048]{1,0:T(8,128)(2,1)} %own_ref.1), custom_call_target="tpu_custom_call" | custom-call | tf_op jit(solution)/shard_map/prep/pallas_call | solution.py:100
  3.0 0.0 collective-permute-done.other_ref
  3.0 2.5 %shard_map.37 = (bf16[1024,128]{1,0:T(8,128)(2,1)S(1)}, bf16[1024,512]{1,0:T(8,128)(2,1)S(1)}, bf16[1536,512]{1,0:T(8,128)(2,1)S(1)}) custom-call(s32[3]{0:T(128)S(1)} %pad_add_fusion.ids_ref, bf16[256,2048]{1,0:T(8,128)(2,1)S(1)} %collective-permute-done.other_ref, bf16[1024,256]{1,0:T(8,128)(2,1)S(1)} %get-tuple-element.26.own_ref, ...), custom_call_target="tpu_custom_call" | custom-call | tf_op jit(solution)/shard_map/pallas_call | solution.py:239
  5.5 0.0 copy-start
  5.5 0.0 copy-start.1
  5.5 3.1 %collective-permute-start.1 = (bf16[1024,128]{1,0:T(8,128)(2,1)S(1)}, bf16[1024,128]{1,0:T(8,128)(2,1)S(1)}, u32[]{:S(2)}, u32[]{:S(2)}) collective-permute-start(bf16[1024,128]{1,0:T(8,128)(2,1)S(1)} %get-tuple-element.35), channel_id=1, source_target_pairs={{0,2},{1,3},{2,0},{3,1},{32,34},{33,35},{34,32},{35,33},{4,6},{5,7... | collective-permute-start | bytes 786440 | tf_op jit(solution)/shard_map/ppermute | solution.py:383
  8.7 2.5 %shard_map.41 = (bf16[1024,128]{1,0:T(8,128)(2,1)S(1)}, bf16[1024,128]{1,0:T(8,128)(2,1)S(1)}) custom-call(s32[3]{0:T(128)S(1)} %pad_add_fusion.ids_ref, bf16[1024,512]{1,0:T(8,128)(2,1)S(1)} %get-tuple-element.32.xs_ref, bf16[1536,512]{1,0:T(8,128)(2,1)S(1)} %get-tuple-element.33.rest_ref, f32[5,32,128]{2,1,0:T(8,128)S(1)} %get-tuple-element.31.outer_ref), custom_call_target="tpu_custom_call" | custom-call | tf_op jit(solution)/shard_map/pallas_call | solution.py:243
  11.2 1.2 %collective-permute-start.5 = (bf16[1024,128]{1,0:T(8,128)(2,1)S(1)}, bf16[1024,128]{1,0:T(8,128)(2,1)S(1)}, u32[]{:S(2)}, u32[]{:S(2)}) collective-permute-start(bf16[1024,128]{1,0:T(8,128)(2,1)S(1)} %get-tuple-element.39), channel_id=1, source_target_pairs={{0,34},{1,35},{2,32},{3,33},{32,2},{33,3},{34,0},{35,1},{4,38},{5,... | collective-permute-start | bytes 786440 | tf_op jit(solution)/shard_map/ppermute | solution.py:383
  12.4 2.0 %collective-permute-start.3 = (bf16[6,128,256]{2,1,0:T(8,128)(2,1)S(1)}, bf16[6,128,256]{2,1,0:T(8,128)(2,1)S(1)}, u32[]{:S(2)}, u32[]{:S(2)}) collective-permute-start(bf16[6,128,256]{2,1,0:T(8,128)(2,1)S(1)} %bitcast.7), channel_id=1, source_target_pairs={{0,32},{1,33},{2,34},{3,35},{32,0},{33,1},{34,2},{35,3},{4,36},{5,... | collective-permute-start | bytes 1179656 | tf_op jit(solution)/shard_map/ppermute | solution.py:383
  14.4 2.1 %collective-permute-start.7 = (bf16[6,128,256]{2,1,0:T(8,128)(2,1)S(1)}, bf16[6,128,256]{2,1,0:T(8,128)(2,1)S(1)}, u32[]{:S(2)}, u32[]{:S(2)}) collective-permute-start(bf16[6,128,256]{2,1,0:T(8,128)(2,1)S(1)} %bitcast.8), channel_id=1, source_target_pairs={{0,34},{1,35},{2,32},{3,33},{32,2},{33,3},{34,0},{35,1},{4,38},{5,... | collective-permute-start | bytes 1179656 | tf_op jit(solution)/shard_map/ppermute | solution.py:383
  16.5 1.9 %shard_map.38 = (f32[1024,128]{1,0:T(8,128)S(1)}, f32[512,128]{1,0:T(8,128)S(1)}) custom-call(s32[3]{0:T(128)S(1)} %pad_add_fusion.ids_ref, bf16[1024,512]{1,0:T(8,128)(2,1)S(1)} %get-tuple-element.32.xs_ref, bf16[1536,512]{1,0:T(8,128)(2,1)S(1)} %get-tuple-element.33.rest_ref, f32[5,32,128]{2,1,0:T(8,128)S(1)} %get-tuple-element.31.outer_ref, ...), custom_call_target="tpu_custom_call" | custom-call | tf_op jit(solution)/shard_map/pallas_call | solution.py:248
  18.4 0.0 collective-permute-done.1
  18.4 0.1 add_convert_fusion.1.own_ref
  18.5 0.1 collective-permute-start.2
  18.6 3.1 %collective-permute-done.5 = bf16[1024,128]{1,0:T(8,128)(2,1)S(1)} collective-permute-done((bf16[1024,128]{1,0:T(8,128)(2,1)S(1)}, bf16[1024,128]{1,0:T(8,128)(2,1)S(1)}, u32[]{:S(2)}, u32[]{:S(2)}) %collective-permute-start.5) | collective-permute-done | bytes 262176 | tf_op jit(solution)/shard_map/ppermute | solution.py:383
  21.7 0.4 collective-permute-done.4
  22.0 0.1 add_convert_fusion.cross_ref
  22.1 0.1 collective-permute-start.6
  22.2 7.7 %collective-permute-done.7.w3_ref = bf16[6,128,256]{2,1,0:T(8,128)(2,1)S(1)} collective-permute-done((bf16[6,128,256]{2,1,0:T(8,128)(2,1)S(1)}, bf16[6,128,256]{2,1,0:T(8,128)(2,1)S(1)}, u32[]{:S(2)}, u32[]{:S(2)}) %collective-permute-start.7) | collective-permute-done | bytes 393248 | tf_op jit(solution)/shard_map/ppermute | solution.py:383
  29.9 1.6 %collective-permute-start.9 = (bf16[4,128,256]{2,1,0:T(8,128)(2,1)S(1)}, bf16[4,128,256]{2,1,0:T(8,128)(2,1)S(1)}, u32[]{:S(2)}, u32[]{:S(2)}) collective-permute-start(bf16[4,128,256]{2,1,0:T(8,128)(2,1)S(1)} %slice.9), channel_id=1, source_target_pairs={{0,32},{1,33},{2,34},{3,35},{32,0},{33,1},{34,2},{35,3},{4,36},{5,... | collective-permute-start | bytes 786440 | tf_op jit(solution)/shard_map/ppermute | solution.py:383
  31.5 0.0 collective-permute-done.3.w1_ref
  31.5 2.4 %collective-permute-start.8 = (bf16[2,128,256]{2,1,0:T(8,128)(2,1)S(1)}, bf16[2,128,256]{2,1,0:T(8,128)(2,1)S(1)}, u32[]{:S(2)}, u32[]{:S(2)}) collective-permute-start(bf16[2,128,256]{2,1,0:T(8,128)(2,1)S(1)} %slice.8), channel_id=1, source_target_pairs={{0,34},{1,35},{2,32},{3,33},{32,2},{33,3},{34,0},{35,1},{4,38},{5,... | collective-permute-start | bytes 393224 | tf_op jit(solution)/shard_map/ppermute | solution.py:383
  33.9 0.7 shard_map.39
  34.6 0.6 shard_map.42.p3_ref
  35.2 1.3 %shard_map.40 = (bf16[2,1024,256]{2,1,0:T(8,128)(2,1)S(1)}, f32[1024,384]{1,0:T(8,128)S(1)}) custom-call(s32[3]{0:T(128)S(1)} %pad_add_fusion.ids_ref, bf16[1024,128]{1,0:T(8,128)(2,1)S(1)} %add_convert_fusion.1.own_ref, bf16[1024,128]{1,0:T(8,128)(2,1)S(1)} %collective-permute-done.2.sib_ref, bf16[2,384,256]{2,1,0:T(8,128)(2,1)S(1)} %get-tuple-element.36.p0_ref), custom_call_target="tpu_custom_call" | custom-call | tf_op jit(solution)/shard_map/pallas_call | solution.py:341
  36.5 1.2 %shard_map.43 = (f32[1024,384]{1,0:T(8,128)S(1)}, f32[1024,384]{1,0:T(8,128)S(1)}) custom-call(s32[3]{0:T(128)S(1)} %pad_add_fusion.ids_ref, bf16[1024,128]{1,0:T(8,128)(2,1)S(1)} %add_convert_fusion.cross_ref, bf16[2,384,256]{2,1,0:T(8,128)(2,1)S(1)} %get-tuple-element.40.p1_ref, bf16[2,384,256]{2,1,0:T(8,128)(2,1)S(1)} %shard_map.42.p3_ref, ...), custom_call_target="tpu_custom_call" | custom-call | tf_op jit(solution)/shard_map/pallas_call | solution.py:345
  37.7 1.2 %shard_map.44 = (bf16[8,2,4,32,128]{4,3,2,1,0:T(8,128)(2,1)S(1)}, f32[1024,384]{1,0:T(8,128)S(1)}) custom-call(s32[3]{0:T(128)S(1)} %pad_add_fusion.ids_ref, bf16[1024,128]{1,0:T(8,128)(2,1)S(1)} %collective-permute-done.6.cross_ref, bf16[2,384,256]{2,1,0:T(8,128)(2,1)S(1)} %get-tuple-element.40.p1_ref, bf16[2,384,256]{2,1,0:T(8,128)(2,1)S(1)} %shard_map.42.p3_ref, ...), custom_call_target="tpu_custom_call" | custom-call | tf_op jit(solution)/shard_map/pallas_call | solution.py:349
  38.9 1.3 %shard_map.45 = bf16[8,2,4,32,128]{4,3,2,1,0:T(8,128)(2,1)S(1)} custom-call(s32[3]{0:T(128)S(1)} %pad_add_fusion.ids_ref, bf16[2,1024,256]{2,1,0:T(8,128)(2,1)S(1)} %get-tuple-element.37.l_ref, f32[1024,384]{1,0:T(8,128)S(1)} %get-tuple-element.45.acc_ref, f32[512,128]{1,0:T(8,128)S(1)} %get-tuple-element.44.group_ref, ...), custom_call_target="tpu_custom_call", output_to_operand_aliasing={{}: (6, {})} | custom-call | tf_op jit(solution)/shard_map/pallas_call | solution.py:353
  40.2 31.6 %all_to_all.5.got_ref = bf16[64,32,128]{2,1,0:T(8,128)(2,1)S(1)} all-to-all(bf16[64,32,128]{2,1,0:T(8,128)(2,1)S(1)} %bitcast.6), channel_id=1, replica_groups=mesh['y'=4,'xlo'=2,'z'=8,'xhi'=2,'core'=2] {'z','xhi','y'}, dimensions={0} | all-to-all | bytes 1048576 | tf_op jit(solution)/shard_map/all_to_all | solution.py:410
  71.8 0.7 add.15
  (9 shorter events, 0.0 us)
Async XLA Ops:
  0.0 3.0 %collective-permute-start = (bf16[256,2048]{1,0:T(8,128)(2,1)}, bf16[256,2048]{1,0:T(8,128)(2,1)S(1)}, u32[]{:S(2)}, u32[]{:S(2)}) collective-permute-start(bf16[256,2048]{1,0:T(8,128)(2,1)} %own_ref.1), channel_id=1, source_target_pairs={{0,1},{1,0},{2,3},{3,2},{32,33},{33,32},{34,35},{35,34},{4,5},{5,4... | collective-permute-start | bytes 3145736 | tf_op jit(solution)/shard_map/ppermute | solution.py:383
  5.5 6.9 %copy-start = (bf16[3,2,128,256]{3,2,1,0:T(8,128)(2,1)S(1)}, bf16[3,2,128,256]{3,2,1,0:T(8,128)(2,1)}, u32[]{:S(2)}) copy-start(bf16[3,2,128,256]{3,2,1,0:T(8,128)(2,1)} %param.4) | copy-start | bytes 1179652
  5.5 11.0 %copy-start.1 = (s32[2048]{0:T(1024)S(1)}, s32[2048]{0:T(1024)}, u32[]{:S(2)}) copy-start(s32[2048]{0:T(1024)} %param.5) | copy-start | bytes 24580
  5.5 12.9 %collective-permute-start.1 = (bf16[1024,128]{1,0:T(8,128)(2,1)S(1)}, bf16[1024,128]{1,0:T(8,128)(2,1)S(1)}, u32[]{:S(2)}, u32[]{:S(2)}) collective-permute-start(bf16[1024,128]{1,0:T(8,128)(2,1)S(1)} %get-tuple-element.35), channel_id=1, source_target_pairs={{0,2},{1,3},{2,0},{3,1},{32,34},{33,35},{34,32},{35,33},{4,6},{5,7... | collective-permute-start | bytes 786440 | tf_op jit(solution)/shard_map/ppermute | solution.py:383
  11.2 10.5 %collective-permute-start.5 = (bf16[1024,128]{1,0:T(8,128)(2,1)S(1)}, bf16[1024,128]{1,0:T(8,128)(2,1)S(1)}, u32[]{:S(2)}, u32[]{:S(2)}) collective-permute-start(bf16[1024,128]{1,0:T(8,128)(2,1)S(1)} %get-tuple-element.39), channel_id=1, source_target_pairs={{0,34},{1,35},{2,32},{3,33},{32,2},{33,3},{34,0},{35,1},{4,38},{5,... | collective-permute-start | bytes 786440 | tf_op jit(solution)/shard_map/ppermute | solution.py:383
  12.4 9.6 %collective-permute-start.4 = (bf16[1024,128]{1,0:T(8,128)(2,1)S(1)}, bf16[1024,128]{1,0:T(8,128)(2,1)S(1)}, u32[]{:S(2)}, u32[]{:S(2)}) collective-permute-start(bf16[1024,128]{1,0:T(8,128)(2,1)S(1)} %get-tuple-element.38), channel_id=1, source_target_pairs={{0,32},{1,33},{2,34},{3,35},{32,0},{33,1},{34,2},{35,3},{4,36},{5,... | collective-permute-start | bytes 786440 | tf_op jit(solution)/shard_map/ppermute | solution.py:383
  12.4 19.1 %collective-permute-start.3 = (bf16[6,128,256]{2,1,0:T(8,128)(2,1)S(1)}, bf16[6,128,256]{2,1,0:T(8,128)(2,1)S(1)}, u32[]{:S(2)}, u32[]{:S(2)}) collective-permute-start(bf16[6,128,256]{2,1,0:T(8,128)(2,1)S(1)} %bitcast.7), channel_id=1, source_target_pairs={{0,32},{1,33},{2,34},{3,35},{32,0},{33,1},{34,2},{35,3},{4,36},{5,... | collective-permute-start | bytes 1179656 | tf_op jit(solution)/shard_map/ppermute | solution.py:383
  14.4 15.4 %collective-permute-start.7 = (bf16[6,128,256]{2,1,0:T(8,128)(2,1)S(1)}, bf16[6,128,256]{2,1,0:T(8,128)(2,1)S(1)}, u32[]{:S(2)}, u32[]{:S(2)}) collective-permute-start(bf16[6,128,256]{2,1,0:T(8,128)(2,1)S(1)} %bitcast.8), channel_id=1, source_target_pairs={{0,34},{1,35},{2,32},{3,33},{32,2},{33,3},{34,0},{35,1},{4,38},{5,... | collective-permute-start | bytes 1179656 | tf_op jit(solution)/shard_map/ppermute | solution.py:383
  18.5 16.7 %collective-permute-start.2 = (bf16[1024,128]{1,0:T(8,128)(2,1)S(1)}, bf16[1024,128]{1,0:T(8,128)(2,1)S(1)}, u32[]{:S(2)}, u32[]{:S(2)}) collective-permute-start(bf16[1024,128]{1,0:T(8,128)(2,1)S(1)} %add_convert_fusion.1.own_ref), channel_id=1, source_target_pairs={{0,1},{1,0},{2,3},{3,2},{32,33},{33,32},{34,35},{35,34},{4,5},{5,4... | collective-permute-start | bytes 786440 | tf_op jit(solution)/shard_map/ppermute | solution.py:383
  22.1 15.5 %collective-permute-start.6 = (bf16[1024,128]{1,0:T(8,128)(2,1)S(1)}, bf16[1024,128]{1,0:T(8,128)(2,1)S(1)}, u32[]{:S(2)}, u32[]{:S(2)}) collective-permute-start(bf16[1024,128]{1,0:T(8,128)(2,1)S(1)} %add_convert_fusion.cross_ref), channel_id=1, source_target_pairs={{0,1},{1,0},{2,3},{3,2},{32,33},{33,32},{34,35},{35,34},{4,5},{5,4... | collective-permute-start | bytes 786440 | tf_op jit(solution)/shard_map/ppermute | solution.py:383
  29.9 9.0 %collective-permute-start.9 = (bf16[4,128,256]{2,1,0:T(8,128)(2,1)S(1)}, bf16[4,128,256]{2,1,0:T(8,128)(2,1)S(1)}, u32[]{:S(2)}, u32[]{:S(2)}) collective-permute-start(bf16[4,128,256]{2,1,0:T(8,128)(2,1)S(1)} %slice.9), channel_id=1, source_target_pairs={{0,32},{1,33},{2,34},{3,35},{32,0},{33,1},{34,2},{35,3},{4,36},{5,... | collective-permute-start | bytes 786440 | tf_op jit(solution)/shard_map/ppermute | solution.py:383
  31.5 7.4 %collective-permute-start.8 = (bf16[2,128,256]{2,1,0:T(8,128)(2,1)S(1)}, bf16[2,128,256]{2,1,0:T(8,128)(2,1)S(1)}, u32[]{:S(2)}, u32[]{:S(2)}) collective-permute-start(bf16[2,128,256]{2,1,0:T(8,128)(2,1)S(1)} %slice.8), channel_id=1, source_target_pairs={{0,34},{1,35},{2,32},{3,33},{32,2},{33,3},{34,0},{35,1},{4,38},{5,... | collective-permute-start | bytes 393224 | tf_op jit(solution)/shard_map/ppermute | solution.py:383

commit v14 on v13

--- a/solution.py
+++ b/solution.py
@@ -314,7 +314,7 @@
 
 
 def far_kernel(ids_ref, l_ref, acc_ref, group_ref, w2a_ref, w2b_ref, begun_ref, out_ref, w_ref):
-    place_weights(ids_ref[0], w_ref, 0, [w2a_ref.at[i] for i in range(2)] + [w2b_ref.at[i] for i in range(4)])
+    place_weights(ids_ref[0], w_ref, 0, [w2a_ref.at[i] for i in range(1)] + [w2b_ref.at[i] for i in range(5)])
     acc = acc_ref[...] + product(l_ref[0], w_ref[0]) + product(l_ref[1], w_ref[1])
     store_beams(1 - ids_ref[1], acc, group_ref, out_ref)
 
@@ -398,8 +398,8 @@
     same = (mine + got0.astype(F32)).astype(BF16)
     same_sib = exchange(same, 1)
     p0, p1 = pack_near(ids, blocks, w1)
-    w2a = exchange(w1[:2], 6)
-    w2b = exchange(w3[2:], 4)
+    w2a = exchange(w1[:1], 6)
+    w2b = exchange(w3[1:], 4)
     p3 = pack_side(ids, w3)
     lhs, near = form_early(ids, same, same_sib, p0)
     cross = (got1.astype(F32) + got2.astype(F32)).astype(BF16)

time: 72.7 us -> 71.8 us (0.988)
  starting transfers between devices: 12.6 us -> 10.8 us
  waiting for transfers between devices: 11.2 us -> 12.8 us
    ppermute x10, starting transfers between devices: 12.6 us -> 10.8 us  [exchange(): return lax.ppermute(value, ring, [(i, i ^ flip) for i in range(8)])]
    ppermute x10, waiting for transfers between devices: 11.2 us -> 12.8 us  [exchange(): return lax.ppermute(value, ring, [(i, i ^ flip) for i in range(8)])]
  transfers between devices with their start and end apart: 10 -> 10, of which waited for: 3 -> 3; matrix products, arithmetic and copies ran while one was open for 0% -> 0% of each run, Pallas kernels for 17% -> 21%
where the time goes in v14:
time: 71.8 us; the launch traced here: 71.6 us
  blocking collectives  30.9 us (43%)
  Pallas kernels  16.7 us (23%)
  waiting for transfers between devices  12.8 us (18%)
  starting transfers between devices  10.8 us (15%)
    all_to_all x1, blocking collectives, shards(): lax.all_to_all(parts.reshape(64, 32, 128), ('z', 'xhi', 'y'), 0, 0, tiled...  30.9 us
    ppermute x10, waiting for transfers between devices, exchange(): return lax.ppermute(value, ring, [(i, i ^ flip) for i in range(8)])  12.8 us
    ppermute x10, starting transfers between devices, exchange(): return lax.ppermute(value, ring, [(i, i ^ flip) for i in range(8)])  10.8 us
    pallas_call x1, Pallas kernels, prep(): pl.pallas_call(prep_kernel, grid_spec=pltpu.PrefetchScalarGridSpec(num_sc...  2.89 us
    pallas_call x1, Pallas kernels, dft_first(): return call(first_kernel, 7, outs, [pltpu.VMEM((512, 1024), F32)])(*args)  2.53 us
    pallas_call x1, Pallas kernels, dft_next(): call(next_kernel, 3, [PIECE, PIECE], [pltpu.VMEM((2, 512, 1024), F32)])  2.51 us
    pallas_call x1, Pallas kernels, dft_last(): return call(last_kernel, 4, outs, [pltpu.VMEM((512, 1024), F32)])(*args)  1.86 us
  transfers between devices with their start and end apart: 10, of which 3 were waited for; matrix products, arithmetic and copies ran while one was open for 0% of the time, Pallas kernels for 21%

profile of v14, /device:TPU:24, one launch (start us, length us, event | category | flops | bytes accessed | tf_op | source)
XLA Modules:
  0.0 71.6 jit_solution(14465021190769869225)
XLA Ops:
  0.0 0.0 collective-permute-start
  0.0 2.8 %collective-permute-start.7 = (bf16[6,128,256]{2,1,0:T(8,128)(2,1)}, bf16[6,128,256]{2,1,0:T(8,128)(2,1)S(1)}, u32[]{:S(2)}, u32[]{:S(2)}) collective-permute-start(bf16[6,128,256]{2,1,0:T(8,128)(2,1)} %bitcast.7), channel_id=1, source_target_pairs={{0,34},{1,35},{2,32},{3,33},{32,2},{33,3},{34,0},{35,1},{4,38},{5,... | collective-permute-start | bytes 1179656 | tf_op jit(solution)/shard_map/ppermute | solution.py:383
  2.8 0.1 pad_add_fusion.ids_ref
  2.8 2.9 %prep.1 = (bf16[1024,256]{1,0:T(8,128)(2,1)S(1)}, bf16[1024,1024]{1,0:T(8,128)(2,1)S(1)}, bf16[512,512]{1,0:T(8,128)(2,1)S(1)}, f32[2,32,128]{2,1,0:T(8,128)S(1)...) custom-call(s32[3]{0:T(128)S(1)} %pad_add_fusion.ids_ref, bf16[256,2048]{1,0:T(8,128)(2,1)} %own_ref.1), custom_call_target="tpu_custom_call" | custom-call | tf_op jit(solution)/shard_map/prep/pallas_call | solution.py:100
  5.7 0.0 collective-permute-done.other_ref
  5.7 2.5 %shard_map.37 = (bf16[1024,128]{1,0:T(8,128)(2,1)S(1)}, bf16[1024,512]{1,0:T(8,128)(2,1)S(1)}, bf16[1536,512]{1,0:T(8,128)(2,1)S(1)}) custom-call(s32[3]{0:T(128)S(1)} %pad_add_fusion.ids_ref, bf16[256,2048]{1,0:T(8,128)(2,1)S(1)} %collective-permute-done.other_ref, bf16[1024,256]{1,0:T(8,128)(2,1)S(1)} %get-tuple-element.26.own_ref, ...), custom_call_target="tpu_custom_call" | custom-call | tf_op jit(solution)/shard_map/pallas_call | solution.py:239
  8.3 0.0 copy-start
  8.3 0.9 %collective-permute-start.1 = (bf16[1024,128]{1,0:T(8,128)(2,1)S(1)}, bf16[1024,128]{1,0:T(8,128)(2,1)S(1)}, u32[]{:S(2)}, u32[]{:S(2)}) collective-permute-start(bf16[1024,128]{1,0:T(8,128)(2,1)S(1)} %get-tuple-element.35), channel_id=1, source_target_pairs={{0,2},{1,3},{2,0},{3,1},{32,34},{33,35},{34,32},{35,33},{4,6},{5,7... | collective-permute-start | bytes 786440 | tf_op jit(solution)/shard_map/ppermute | solution.py:383
  9.2 2.5 %shard_map.41 = (bf16[1024,128]{1,0:T(8,128)(2,1)S(1)}, bf16[1024,128]{1,0:T(8,128)(2,1)S(1)}) custom-call(s32[3]{0:T(128)S(1)} %pad_add_fusion.ids_ref, bf16[1024,512]{1,0:T(8,128)(2,1)S(1)} %get-tuple-element.32.xs_ref, bf16[1536,512]{1,0:T(8,128)(2,1)S(1)} %get-tuple-element.33.rest_ref, f32[5,32,128]{2,1,0:T(8,128)S(1)} %get-tuple-element.31.outer_ref), custom_call_target="tpu_custom_call" | custom-call | tf_op jit(solution)/shard_map/pallas_call | solution.py:243
  11.7 2.2 %collective-permute-start.5 = (bf16[1024,128]{1,0:T(8,128)(2,1)S(1)}, bf16[1024,128]{1,0:T(8,128)(2,1)S(1)}, u32[]{:S(2)}, u32[]{:S(2)}) collective-permute-start(bf16[1024,128]{1,0:T(8,128)(2,1)S(1)} %get-tuple-element.39), channel_id=1, source_target_pairs={{0,34},{1,35},{2,32},{3,33},{32,2},{33,3},{34,0},{35,1},{4,38},{5,... | collective-permute-start | bytes 786440 | tf_op jit(solution)/shard_map/ppermute | solution.py:383
  13.9 0.6 collective-permute-start.4
  14.5 1.5 %collective-permute-start.3 = (bf16[6,128,256]{2,1,0:T(8,128)(2,1)S(1)}, bf16[6,128,256]{2,1,0:T(8,128)(2,1)S(1)}, u32[]{:S(2)}, u32[]{:S(2)}) collective-permute-start(bf16[6,128,256]{2,1,0:T(8,128)(2,1)S(1)} %bitcast.8), channel_id=1, source_target_pairs={{0,32},{1,33},{2,34},{3,35},{32,0},{33,1},{34,2},{35,3},{4,36},{5,... | collective-permute-start | bytes 1179656 | tf_op jit(solution)/shard_map/ppermute | solution.py:383
  15.9 2.4 %collective-permute-done.7.w3_ref = bf16[6,128,256]{2,1,0:T(8,128)(2,1)S(1)} collective-permute-done((bf16[6,128,256]{2,1,0:T(8,128)(2,1)}, bf16[6,128,256]{2,1,0:T(8,128)(2,1)S(1)}, u32[]{:S(2)}, u32[]{:S(2)}) %collective-permute-start.7) | collective-permute-done | bytes 393248 | tf_op jit(solution)/shard_map/ppermute | solution.py:383
  18.4 0.5 collective-permute-start.9
  18.9 1.9 %shard_map.38 = (f32[1024,128]{1,0:T(8,128)S(1)}, f32[512,128]{1,0:T(8,128)S(1)}) custom-call(s32[3]{0:T(128)S(1)} %pad_add_fusion.ids_ref, bf16[1024,512]{1,0:T(8,128)(2,1)S(1)} %get-tuple-element.32.xs_ref, bf16[1536,512]{1,0:T(8,128)(2,1)S(1)} %get-tuple-element.33.rest_ref, f32[5,32,128]{2,1,0:T(8,128)S(1)} %get-tuple-element.31.outer_ref, ...), custom_call_target="tpu_custom_call" | custom-call | tf_op jit(solution)/shard_map/pallas_call | solution.py:248
  20.8 0.0 collective-permute-done.1
  20.8 0.1 add_convert_fusion.1.own_ref
  20.8 0.1 collective-permute-start.2
  20.9 3.3 %collective-permute-done.5 = bf16[1024,128]{1,0:T(8,128)(2,1)S(1)} collective-permute-done((bf16[1024,128]{1,0:T(8,128)(2,1)S(1)}, bf16[1024,128]{1,0:T(8,128)(2,1)S(1)}, u32[]{:S(2)}, u32[]{:S(2)}) %collective-permute-start.5) | collective-permute-done | bytes 262176 | tf_op jit(solution)/shard_map/ppermute | solution.py:383
  24.2 0.1 add_convert_fusion.cross_ref
  24.3 0.1 collective-permute-start.6
  24.4 7.1 %collective-permute-done.3.w1_ref = bf16[6,128,256]{2,1,0:T(8,128)(2,1)S(1)} collective-permute-done((bf16[6,128,256]{2,1,0:T(8,128)(2,1)S(1)}, bf16[6,128,256]{2,1,0:T(8,128)(2,1)S(1)}, u32[]{:S(2)}, u32[]{:S(2)}) %collective-permute-start.3) | collective-permute-done | bytes 393248 | tf_op jit(solution)/shard_map/ppermute | solution.py:383
  31.5 2.2 %collective-permute-start.8 = (bf16[1,128,256]{2,1,0:T(8,128)(2,1)S(1)}, bf16[1,128,256]{2,1,0:T(8,128)(2,1)S(1)}, u32[]{:S(2)}, u32[]{:S(2)}) collective-permute-start(bf16[1,128,256]{2,1,0:T(8,128)(2,1)S(1)} %slice.8), channel_id=1, source_target_pairs={{0,34},{1,35},{2,32},{3,33},{32,2},{33,3},{34,0},{35,1},{4,38},{5,... | collective-permute-start | bytes 196616 | tf_op jit(solution)/shard_map/ppermute | solution.py:383
  33.7 0.7 shard_map.39
  34.4 0.6 shard_map.42.p3_ref
  35.0 1.3 %shard_map.40 = (bf16[2,1024,256]{2,1,0:T(8,128)(2,1)S(1)}, f32[1024,384]{1,0:T(8,128)S(1)}) custom-call(s32[3]{0:T(128)S(1)} %pad_add_fusion.ids_ref, bf16[1024,128]{1,0:T(8,128)(2,1)S(1)} %add_convert_fusion.1.own_ref, bf16[1024,128]{1,0:T(8,128)(2,1)S(1)} %collective-permute-done.2.sib_ref, bf16[2,384,256]{2,1,0:T(8,128)(2,1)S(1)} %get-tuple-element.36.p0_ref), custom_call_target="tpu_custom_call" | custom-call | tf_op jit(solution)/shard_map/pallas_call | solution.py:341
  36.3 1.2 %shard_map.43 = (f32[1024,384]{1,0:T(8,128)S(1)}, f32[1024,384]{1,0:T(8,128)S(1)}) custom-call(s32[3]{0:T(128)S(1)} %pad_add_fusion.ids_ref, bf16[1024,128]{1,0:T(8,128)(2,1)S(1)} %add_convert_fusion.cross_ref, bf16[2,384,256]{2,1,0:T(8,128)(2,1)S(1)} %get-tuple-element.40.p1_ref, bf16[2,384,256]{2,1,0:T(8,128)(2,1)S(1)} %shard_map.42.p3_ref, ...), custom_call_target="tpu_custom_call" | custom-call | tf_op jit(solution)/shard_map/pallas_call | solution.py:345
  37.5 1.2 %shard_map.44 = (bf16[8,2,4,32,128]{4,3,2,1,0:T(8,128)(2,1)S(1)}, f32[1024,384]{1,0:T(8,128)S(1)}) custom-call(s32[3]{0:T(128)S(1)} %pad_add_fusion.ids_ref, bf16[1024,128]{1,0:T(8,128)(2,1)S(1)} %collective-permute-done.6.cross_ref, bf16[2,384,256]{2,1,0:T(8,128)(2,1)S(1)} %get-tuple-element.40.p1_ref, bf16[2,384,256]{2,1,0:T(8,128)(2,1)S(1)} %shard_map.42.p3_ref, ...), custom_call_target="tpu_custom_call" | custom-call | tf_op jit(solution)/shard_map/pallas_call | solution.py:349
  38.7 0.0 collective-permute-done.8.w2a_ref
  38.7 1.3 %shard_map.45 = bf16[8,2,4,32,128]{4,3,2,1,0:T(8,128)(2,1)S(1)} custom-call(s32[3]{0:T(128)S(1)} %pad_add_fusion.ids_ref, bf16[2,1024,256]{2,1,0:T(8,128)(2,1)S(1)} %get-tuple-element.37.l_ref, f32[1024,384]{1,0:T(8,128)S(1)} %get-tuple-element.45.acc_ref, f32[512,128]{1,0:T(8,128)S(1)} %get-tuple-element.44.group_ref, ...), custom_call_target="tpu_custom_call", output_to_operand_aliasing={{}: (6, {})} | custom-call | tf_op jit(solution)/shard_map/pallas_call | solution.py:353
  40.0 30.9 %all_to_all.5.got_ref = bf16[64,32,128]{2,1,0:T(8,128)(2,1)S(1)} all-to-all(bf16[64,32,128]{2,1,0:T(8,128)(2,1)S(1)} %bitcast.6), channel_id=1, replica_groups=mesh['y'=4,'xlo'=2,'z'=8,'xhi'=2,'core'=2] {'z','xhi','y'}, dimensions={0} | all-to-all | bytes 1048576 | tf_op jit(solution)/shard_map/all_to_all | solution.py:410
  70.9 0.7 add.15
  (9 shorter events, 0.0 us)
Async XLA Ops:
  0.0 5.7 %collective-permute-start = (bf16[256,2048]{1,0:T(8,128)(2,1)}, bf16[256,2048]{1,0:T(8,128)(2,1)S(1)}, u32[]{:S(2)}, u32[]{:S(2)}) collective-permute-start(bf16[256,2048]{1,0:T(8,128)(2,1)} %own_ref.1), channel_id=1, source_target_pairs={{0,1},{1,0},{2,3},{3,2},{32,33},{33,32},{34,35},{35,34},{4,5},{5,4... | collective-permute-start | bytes 3145736 | tf_op jit(solution)/shard_map/ppermute | solution.py:383
  0.0 18.3 %collective-permute-start.7 = (bf16[6,128,256]{2,1,0:T(8,128)(2,1)}, bf16[6,128,256]{2,1,0:T(8,128)(2,1)S(1)}, u32[]{:S(2)}, u32[]{:S(2)}) collective-permute-start(bf16[6,128,256]{2,1,0:T(8,128)(2,1)} %bitcast.7), channel_id=1, source_target_pairs={{0,34},{1,35},{2,32},{3,33},{32,2},{33,3},{34,0},{35,1},{4,38},{5,... | collective-permute-start | bytes 1179656 | tf_op jit(solution)/shard_map/ppermute | solution.py:383
  8.3 6.2 %copy-start = (bf16[3,2,128,256]{3,2,1,0:T(8,128)(2,1)S(1)}, bf16[3,2,128,256]{3,2,1,0:T(8,128)(2,1)}, u32[]{:S(2)}) copy-start(bf16[3,2,128,256]{3,2,1,0:T(8,128)(2,1)} %param.4) | copy-start | bytes 1179652
  8.3 12.5 %collective-permute-start.1 = (bf16[1024,128]{1,0:T(8,128)(2,1)S(1)}, bf16[1024,128]{1,0:T(8,128)(2,1)S(1)}, u32[]{:S(2)}, u32[]{:S(2)}) collective-permute-start(bf16[1024,128]{1,0:T(8,128)(2,1)S(1)} %get-tuple-element.35), channel_id=1, source_target_pairs={{0,2},{1,3},{2,0},{3,1},{32,34},{33,35},{34,32},{35,33},{4,6},{5,7... | collective-permute-start | bytes 786440 | tf_op jit(solution)/shard_map/ppermute | solution.py:383
  9.2 9.7 %copy-start.1 = (s32[2048]{0:T(1024)S(1)}, s32[2048]{0:T(1024)}, u32[]{:S(2)}) copy-start(s32[2048]{0:T(1024)} %param.5) | copy-start | bytes 24580
  11.7 12.5 %collective-permute-start.5 = (bf16[1024,128]{1,0:T(8,128)(2,1)S(1)}, bf16[1024,128]{1,0:T(8,128)(2,1)S(1)}, u32[]{:S(2)}, u32[]{:S(2)}) collective-permute-start(bf16[1024,128]{1,0:T(8,128)(2,1)S(1)} %get-tuple-element.39), channel_id=1, source_target_pairs={{0,34},{1,35},{2,32},{3,33},{32,2},{33,3},{34,0},{35,1},{4,38},{5,... | collective-permute-start | bytes 786440 | tf_op jit(solution)/shard_map/ppermute | solution.py:383
  13.9 10.3 %collective-permute-start.4 = (bf16[1024,128]{1,0:T(8,128)(2,1)S(1)}, bf16[1024,128]{1,0:T(8,128)(2,1)S(1)}, u32[]{:S(2)}, u32[]{:S(2)}) collective-permute-start(bf16[1024,128]{1,0:T(8,128)(2,1)S(1)} %get-tuple-element.38), channel_id=1, source_target_pairs={{0,32},{1,33},{2,34},{3,35},{32,0},{33,1},{34,2},{35,3},{4,36},{5,... | collective-permute-start | bytes 786440 | tf_op jit(solution)/shard_map/ppermute | solution.py:383
  14.5 17.0 %collective-permute-start.3 = (bf16[6,128,256]{2,1,0:T(8,128)(2,1)S(1)}, bf16[6,128,256]{2,1,0:T(8,128)(2,1)S(1)}, u32[]{:S(2)}, u32[]{:S(2)}) collective-permute-start(bf16[6,128,256]{2,1,0:T(8,128)(2,1)S(1)} %bitcast.8), channel_id=1, source_target_pairs={{0,32},{1,33},{2,34},{3,35},{32,0},{33,1},{34,2},{35,3},{4,36},{5,... | collective-permute-start | bytes 1179656 | tf_op jit(solution)/shard_map/ppermute | solution.py:383
  18.4 20.4 %collective-permute-start.9 = (bf16[5,128,256]{2,1,0:T(8,128)(2,1)S(1)}, bf16[5,128,256]{2,1,0:T(8,128)(2,1)S(1)}, u32[]{:S(2)}, u32[]{:S(2)}) collective-permute-start(bf16[5,128,256]{2,1,0:T(8,128)(2,1)S(1)} %slice.9), channel_id=1, source_target_pairs={{0,32},{1,33},{2,34},{3,35},{32,0},{33,1},{34,2},{35,3},{4,36},{5,... | collective-permute-start | bytes 983048 | tf_op jit(solution)/shard_map/ppermute | solution.py:383
  20.8 14.2 %collective-permute-start.2 = (bf16[1024,128]{1,0:T(8,128)(2,1)S(1)}, bf16[1024,128]{1,0:T(8,128)(2,1)S(1)}, u32[]{:S(2)}, u32[]{:S(2)}) collective-permute-start(bf16[1024,128]{1,0:T(8,128)(2,1)S(1)} %add_convert_fusion.1.own_ref), channel_id=1, source_target_pairs={{0,1},{1,0},{2,3},{3,2},{32,33},{33,32},{34,35},{35,34},{4,5},{5,4... | collective-permute-start | bytes 786440 | tf_op jit(solution)/shard_map/ppermute | solution.py:383
  24.3 13.2 %collective-permute-start.6 = (bf16[1024,128]{1,0:T(8,128)(2,1)S(1)}, bf16[1024,128]{1,0:T(8,128)(2,1)S(1)}, u32[]{:S(2)}, u32[]{:S(2)}) collective-permute-start(bf16[1024,128]{1,0:T(8,128)(2,1)S(1)} %add_convert_fusion.cross_ref), channel_id=1, source_target_pairs={{0,1},{1,0},{2,3},{3,2},{32,33},{33,32},{34,35},{35,34},{4,5},{5,4... | collective-permute-start | bytes 786440 | tf_op jit(solution)/shard_map/ppermute | solution.py:383
  31.5 7.2 %collective-permute-start.8 = (bf16[1,128,256]{2,1,0:T(8,128)(2,1)S(1)}, bf16[1,128,256]{2,1,0:T(8,128)(2,1)S(1)}, u32[]{:S(2)}, u32[]{:S(2)}) collective-permute-start(bf16[1,128,256]{2,1,0:T(8,128)(2,1)S(1)} %slice.8), channel_id=1, source_target_pairs={{0,34},{1,35},{2,32},{3,33},{32,2},{33,3},{34,0},{35,1},{4,38},{5,... | collective-permute-start | bytes 196616 | tf_op jit(solution)/shard_map/ppermute | solution.py:383
